TPU v7x, 16 devices: a whole 2x2x2 slice. The times are simulated.
16 devices in a mesh: sp: 16 (over z, y, x, core).
Axes of the slice: x: 2, y: 2, z: 2, core: 2. Of those that a mesh axis runs over, the one named last changes fastest.
Arguments:
- x_in: bfloat16 [2048, 2048], P('sp')
- positions: int32 [2048], P('sp')
- d_out: bfloat16 [2048, 2048], P('sp')
- norm1_gain: bfloat16 [2048], P('sp')
- norm2_gain: bfloat16 [2048], P('sp')
- w_q: bfloat16 [2048, 32, 64], P('sp')
- w_k: bfloat16 [2048, 4, 64], P('sp')
- w_v: bfloat16 [2048, 4, 64], P('sp')
- w_o: bfloat16 [32, 64, 2048], P('sp')
- w_gate: bfloat16 [2048, 5632], P('sp')
- w_up: bfloat16 [2048, 5632], P('sp')
- w_down: bfloat16 [5632, 2048], P('sp')
Outputs:
- output 1: bfloat16 [2048, 2048], P('sp')
- output 2: bfloat16 [2048, 2048], P('sp')
- output 3: float32 [2048], P('sp')
- output 4: float32 [2048], P('sp')
- output 5: float32 [2048, 32, 64], P('sp')
- output 6: float32 [2048, 4, 64], P('sp')
- output 7: float32 [2048, 4, 64], P('sp')
- output 8: float32 [32, 64, 2048], P('sp')
- output 9: float32 [2048, 5632], P('sp')
- output 10: float32 [2048, 5632], P('sp')
- output 11: float32 [5632, 2048], P('sp')
All inputs are finite; a program needn't handle non-finite values.
Results may differ from a plain program's by a relative error of at most 0.019747.
Values are sent between devices in bfloat16 or wider.
A program may use at most 1 GiB of HBM per device.

v0:
```python
import functools
import jax
import jax.numpy as jnp
from jax import lax
from jax.sharding import PartitionSpec as P

ROPE_BASE = 10000.0
NORM_EPS = 1e-5
NEG_LARGE = -1e30


def norm_forward(hidden, gain_vec):
    inv_rms = lax.rsqrt(jnp.mean(hidden * hidden, axis=-1, keepdims=True) + NORM_EPS)
    return hidden * inv_rms * gain_vec


def rope_tables(positions, head_dim):
    half_dim = head_dim // 2
    inv_freq = 1.0 / (ROPE_BASE ** (jnp.arange(half_dim, dtype=jnp.float32) * (2.0 / head_dim)))
    angles = positions.astype(jnp.float32)[:, None] * inv_freq[None, :]
    return jnp.cos(angles)[:, None, :], jnp.sin(angles)[:, None, :]


def rotate(values_in, cos_tab, sin_tab):
    half_dim = values_in.shape[-1] // 2
    first_half = values_in[..., :half_dim].astype(jnp.float32)
    second_half = values_in[..., half_dim:].astype(jnp.float32)
    return jnp.concatenate([first_half * cos_tab - second_half * sin_tab, second_half * cos_tab + first_half * sin_tab], axis=-1)


def gated_unit(gate_pre, up_pre):
    return jax.nn.silu(gate_pre) * up_pre


def attention_forward(queries, keys_all, values_all):
    seq_len = queries.shape[0]
    score_scale = queries.shape[-1] ** -0.5
    scores = jnp.einsum('skgd,tkd->kgst', queries, keys_all, preferred_element_type=jnp.float32) * score_scale
    causal = jnp.arange(seq_len)[:, None] >= jnp.arange(seq_len)[None, :]
    attn_probs = jax.nn.softmax(jnp.where(causal, scores, NEG_LARGE), axis=-1)
    attn_out = jnp.einsum('kgst,tkd->skgd', attn_probs.astype(jnp.bfloat16), values_all, preferred_element_type=jnp.float32)
    return attn_out.astype(jnp.bfloat16), attn_probs


def attention_backward(queries, keys_all, values_all, attn_probs, d_attn):
    score_scale = queries.shape[-1] ** -0.5
    probs_b16 = attn_probs.astype(jnp.bfloat16)
    d_probs = jnp.einsum('skgd,tkd->kgst', d_attn, values_all, preferred_element_type=jnp.float32)
    d_probs = d_probs.astype(jnp.bfloat16).astype(jnp.float32)
    row_dot = jnp.sum(d_probs * attn_probs, axis=-1, keepdims=True)
    d_scores = (attn_probs * (d_probs - row_dot) * score_scale).astype(jnp.bfloat16)
    d_queries = jnp.einsum('kgst,tkd->skgd', d_scores, keys_all, preferred_element_type=jnp.float32)
    d_keys = jnp.einsum('kgst,skgd->tkd', d_scores, queries, preferred_element_type=jnp.float32)
    d_values = jnp.einsum('kgst,skgd->tkd', probs_b16, d_attn, preferred_element_type=jnp.float32)
    return d_queries.astype(jnp.bfloat16), d_keys.astype(jnp.bfloat16), d_values.astype(jnp.bfloat16)


def solution(mesh):
    n_devices = mesh.shape['sp']
    gather_rows = functools.partial(lax.all_gather, axis_name='sp', axis=0, tiled=True)
    scatter_rows = functools.partial(lax.psum_scatter, axis_name='sp', scatter_dimension=0, tiled=True)
    to_heads = functools.partial(lax.all_to_all, axis_name='sp', split_axis=1, concat_axis=0, tiled=True)
    to_tokens = functools.partial(lax.all_to_all, axis_name='sp', split_axis=0, concat_axis=1, tiled=True)

    def layer_step(x_in, positions, d_out, norm1_gain, norm2_gain, w_q, w_k, w_v, w_o, w_gate, w_up, w_down):
        g1_full, g2_full, wq_full, wk_full, wv_full, wo_full, gate_full, up_full, down_full = [gather_rows(shard_w) for shard_w in (norm1_gain, norm2_gain, w_q, w_k, w_v, w_o, w_gate, w_up, w_down)]
        tokens = x_in.shape[0]
        seq_len = tokens * n_devices
        head_dim = w_q.shape[2]
        kv_heads = w_k.shape[1]
        kv_repeat = max(1, n_devices // kv_heads)
        cos_tab, sin_tab = rope_tables(positions, head_dim)

        x_f32 = x_in.astype(jnp.float32)
        normed_pre, norm1_pull = jax.vjp(norm_forward, x_f32, g1_full.astype(jnp.float32))
        normed = normed_pre.astype(jnp.bfloat16)
        q_lin = jnp.einsum('td,dhe->the', normed, wq_full, preferred_element_type=jnp.float32).astype(jnp.bfloat16)
        k_lin = jnp.einsum('td,dhe->the', normed, wk_full, preferred_element_type=jnp.float32).astype(jnp.bfloat16)
        v_lin = jnp.einsum('td,dhe->the', normed, wv_full, preferred_element_type=jnp.float32).astype(jnp.bfloat16)
        q_rot = rotate(q_lin, cos_tab, sin_tab).astype(jnp.bfloat16)
        k_rot = rotate(k_lin, cos_tab, sin_tab).astype(jnp.bfloat16)
        q_seq = to_heads(q_rot)
        k_seq = to_heads(jnp.repeat(k_rot, kv_repeat, axis=1))
        v_seq = to_heads(jnp.repeat(v_lin, kv_repeat, axis=1))
        kv_local = k_seq.shape[1]
        q_grouped = q_seq.reshape(seq_len, kv_local, -1, head_dim)
        attn_seq, attn_probs = attention_forward(q_grouped, k_seq, v_seq)
        attn_tok = to_tokens(attn_seq.reshape(seq_len, -1, head_dim))
        attn_proj = jnp.einsum('the,hed->td', attn_tok, wo_full, preferred_element_type=jnp.float32)
        hidden = (x_f32 + attn_proj).astype(jnp.bfloat16)
        hidden_f32 = hidden.astype(jnp.float32)
        mlp_pre, norm2_pull = jax.vjp(norm_forward, hidden_f32, g2_full.astype(jnp.float32))
        mlp_in = mlp_pre.astype(jnp.bfloat16)
        gate_act = jnp.dot(mlp_in, gate_full, preferred_element_type=jnp.float32).astype(jnp.bfloat16)
        up_act = jnp.dot(mlp_in, up_full, preferred_element_type=jnp.float32).astype(jnp.bfloat16)
        glu_pre, glu_pull = jax.vjp(gated_unit, gate_act.astype(jnp.float32), up_act.astype(jnp.float32))
        glu_out = glu_pre.astype(jnp.bfloat16)
        y_out = (hidden_f32 + jnp.dot(glu_out, down_full, preferred_element_type=jnp.float32)).astype(jnp.bfloat16)

        wq_back, wk_back, wv_back, wo_back, gate_back, up_back, down_back = [gather_rows(shard_w) for shard_w in (w_q, w_k, w_v, w_o, w_gate, w_up, w_down)]
        d_down = jnp.einsum('tf,td->fd', glu_out, d_out, preferred_element_type=jnp.float32)
        d_glu = jnp.einsum('td,fd->tf', d_out, down_back, preferred_element_type=jnp.float32).astype(jnp.bfloat16)
        d_gate_f, d_up_f = glu_pull(d_glu.astype(jnp.float32))
        d_gate_act = d_gate_f.astype(jnp.bfloat16)
        d_up_act = d_up_f.astype(jnp.bfloat16)
        d_gate = jnp.einsum('td,tf->df', mlp_in, d_gate_act, preferred_element_type=jnp.float32)
        d_up = jnp.einsum('td,tf->df', mlp_in, d_up_act, preferred_element_type=jnp.float32)
        d_mlp_in = (jnp.einsum('tf,df->td', d_gate_act, gate_back, preferred_element_type=jnp.float32) + jnp.einsum('tf,df->td', d_up_act, up_back, preferred_element_type=jnp.float32)).astype(jnp.bfloat16)
        d_hidden_norm, d_g2 = norm2_pull(d_mlp_in.astype(jnp.float32))
        d_hidden = (d_out.astype(jnp.float32) + d_hidden_norm).astype(jnp.bfloat16)
        d_wo = jnp.einsum('the,td->hed', attn_tok, d_hidden, preferred_element_type=jnp.float32)
        d_attn_tok = jnp.einsum('td,hed->the', d_hidden, wo_back, preferred_element_type=jnp.float32).astype(jnp.bfloat16)
        d_attn_seq = to_heads(d_attn_tok).reshape(seq_len, kv_local, -1, head_dim)
        d_q_seq, d_k_seq, d_v_seq = attention_backward(q_grouped, k_seq, v_seq, attn_probs, d_attn_seq)
        d_q_rot = to_tokens(d_q_seq.reshape(seq_len, -1, head_dim))
        d_k_rot = jnp.sum(to_tokens(d_k_seq).reshape(tokens, kv_heads, kv_repeat, head_dim), axis=2, dtype=jnp.float32).astype(jnp.bfloat16)
        d_v_lin = jnp.sum(to_tokens(d_v_seq).reshape(tokens, kv_heads, kv_repeat, head_dim), axis=2, dtype=jnp.float32).astype(jnp.bfloat16)
        d_q_lin = rotate(d_q_rot, cos_tab, -sin_tab).astype(jnp.bfloat16)
        d_k_lin = rotate(d_k_rot, cos_tab, -sin_tab).astype(jnp.bfloat16)
        d_wq = jnp.einsum('td,the->dhe', normed, d_q_lin, preferred_element_type=jnp.float32)
        d_wk = jnp.einsum('td,the->dhe', normed, d_k_lin, preferred_element_type=jnp.float32)
        d_wv = jnp.einsum('td,the->dhe', normed, d_v_lin, preferred_element_type=jnp.float32)
        d_normed = (jnp.einsum('the,dhe->td', d_q_lin, wq_back, preferred_element_type=jnp.float32) + jnp.einsum('the,dhe->td', d_k_lin, wk_back, preferred_element_type=jnp.float32) + jnp.einsum('the,dhe->td', d_v_lin, wv_back, preferred_element_type=jnp.float32)).astype(jnp.bfloat16)
        d_x_norm, d_g1 = norm1_pull(d_normed.astype(jnp.float32))
        d_x = (d_hidden.astype(jnp.float32) + d_x_norm).astype(jnp.bfloat16)
        grad_parts = (d_g1, d_g2, d_wq, d_wk, d_wv, d_wo, d_gate, d_up, d_down)
        return (y_out, d_x) + tuple(scatter_rows(grad_part) for grad_part in grad_parts)

    all_rows = P('sp')
    return jax.shard_map(layer_step, mesh=mesh, in_specs=(all_rows,) * 12, out_specs=(all_rows,) * 11, check_vma=False)
```

profile of v0, /device:TPU:0, one launch (start us, length us, event | category | flops | bytes accessed | tf_op | source)
XLA Modules:
  0.0 2532.5 jit_solution(3578692884055564635)
XLA Ops:
  11.9 14.5 all-gather
  27.1 1.2 fusion.58
  29.1 10.5 all-gather.10.cloned.1.call-done
  39.7 1.9 fusion.102
  42.3 2.5 all-to-all-start
  44.8 23.6 all-gather.12.cloned.1.call-done
  68.4 1.9 fusion.100
  70.4 63.4 %all-gather.14.cloned.1.call-done = bf16[2048,32,64]{0,2,1:T(8,128)(2,1)} async-done(((bf16[128,32,64]{0,2,1:T(8,128)(2,1)}), bf16[2048,32,64]{0,2,1:T(8,128)(2,1)}) %all-gather.14.cloned.1.call-update) | async-done | bytes 8388624 | tf_op jit(solution)/shard_map/all_gather | solution.py:66
  133.8 6.0 fusion.98
  140.7 2.5 all-to-all-start.1
  143.4 0.9 pad_maximum_fusion
  144.3 8.9 all-to-all-done.1
  153.1 2.8 all-to-all-start.2
  156.0 4.1 iota_compare_fusion
  160.7 11.2 all-to-all-done.2
  172.0 16.2 fusion.8
  188.2 14.6 fusion.7
  203.5 15.9 fusion.35
  219.4 0.8 copy.57
  220.1 1.5 reshape.263
  221.7 2.3 all-to-all-start.3
  224.0 21.6 all-gather.1
  247.0 4.9 multiply_reduce_fusion.2
  252.1 45.4 %all-gather.18.cloned.1.call-done = bf16[2048,5632]{1,0:T(8,128)(2,1)} async-done(((bf16[128,5632]{1,0:T(8,128)(2,1)}), bf16[2048,5632]{1,0:T(8,128)(2,1)}) %all-gather.18.cloned.1.call-update) | async-done | bytes 23068688 | tf_op jit(solution)/shard_map/all_gather | solution.py:66
  297.5 12.3 fusion.15
  309.8 86.4 %all-gather.20.cloned.1.call-done = bf16[2048,5632]{1,0:T(8,128)(2,1)} async-done(((bf16[128,5632]{1,0:T(8,128)(2,1)}), bf16[2048,5632]{1,0:T(8,128)(2,1)}) %all-gather.20.cloned.1.call-update) | async-done | bytes 23068688 | tf_op jit(solution)/shard_map/all_gather | solution.py:66
  396.1 12.3 fusion.16
  408.5 86.6 %all-gather.22.cloned.1.call-done = bf16[5632,2048]{1,0:T(8,128)(2,1)} async-done(((bf16[352,2048]{1,0:T(8,128)(2,1)}), bf16[5632,2048]{1,0:T(8,128)(2,1)}) %all-gather.22.cloned.1.call-update) | async-done | bytes 23068688 | tf_op jit(solution)/shard_map/all_gather | solution.py:66
  495.0 14.7 multiply_convert_fusion
  509.7 13.8 fusion.107
  523.5 13.1 multiply_reduce_fusion
  536.9 0.8 copy-done.11
  537.7 5.7 convolution_convert_fusion.5
  543.4 12.8 all_to_all.126
  556.2 21.7 fusion.2
  577.9 26.3 %fusion.9 = bf16[2,2048,2048]{1,2,0:T(8,128)(2,1)} fusion(bf16[2048,2048,2]{1,0,2:T(8,128)(2,1)} %get-tuple-element.39, f32[2,2048]{1,0:T(2,128)S(1)} %get-tuple-element.38, f32[2,2048]{1,0:T(2,128)S(1)} %copy-done.43, f32[2,2048]{1,0:T(2,128)S(1)} %copy-done.41, f32[2048,2048,2]{1,0,2:T(8,128)} %get-tuple-element.34, pred[2048,2048]{0,1:T(8,128)(4,1)} %iota_compare_fusion), kind=kLoop, calls=%fused_computation.12 | loop fusion | flops 75497472 | bytes 71352320 | tf_op jit(solution)/shard_map/reshape.28
  604.2 11.0 fusion.49
  615.7 0.8 reduce.106
  617.2 9.1 all_to_all.127
  628.0 1.9 fusion.94
  630.0 15.9 fusion.46
  646.0 0.8 reduce.105
  647.4 9.4 all_to_all.128
  658.5 1.8 fusion.96
  660.4 8.2 fusion.73
  668.7 8.8 fusion.41
  677.5 0.8 copy.61
  679.0 13.3 all_to_all.129
  694.6 8.3 fusion.92
  702.9 18.0 fusion.108
  721.0 1.3 copy-done.9
  722.3 18.2 fusion.109
  740.6 1.3 copy-done.10
  742.0 18.0 fusion.110
  760.0 1.2 copy-done.3
  761.2 11.6 fusion.34
  773.2 4.7 convolution_bitcast_fusion
  778.6 32.1 %all-reduce.2 = (f32[2048]{0:T(1024)S(1)}, f32[2048]{0:T(1024)S(1)}) all-reduce(f32[2048]{0:T(1024)S(1)} %get-tuple-element.13, f32[2048]{0:T(1024)S(1)} %copy-done.44), channel_id=2, replica_groups=mesh['sp'=16] {'sp'}, use_global_device_ids=true, to_apply=%region_10.11.clone | all-reduce | flops 4096 | bytes 32768
  811.9 1.2 fusion.57
  813.0 113.9 %reduce-scatter.14.cloned.1.call-done = f32[2,64,2048]{2,1,0:T(8,128)} async-done(((f32[32,64,2048]{2,1,0:T(8,128)}), f32[2,64,2048]{2,1,0:T(8,128)}) %reduce-scatter.14.cloned.1.call-update) | async-done | bytes 1048592 | tf_op jit(solution)/shard_map/reduce_scatter | solution.py:127
  926.9 178.4 %reduce-scatter.8.cloned.1.call-done = f32[128,32,64]{0,2,1:T(8,128)} async-done(((f32[2048,32,64]{0,2,1:T(8,128)}), f32[128,32,64]{0,2,1:T(8,128)}) %reduce-scatter.8.cloned.1.call-update) | async-done | bytes 1048592 | tf_op jit(solution)/shard_map/reduce_scatter | solution.py:127
  1105.3 473.4 %reduce-scatter.16.cloned.1.call-done = f32[128,5632]{1,0:T(8,128)} async-done(((f32[2048,5632]{1,0:T(8,128)}), f32[128,5632]{1,0:T(8,128)}) %reduce-scatter.16.cloned.1.call-update) | async-done | bytes 2883600 | tf_op jit(solution)/shard_map/reduce_scatter | solution.py:127
  1578.7 473.6 %reduce-scatter.18.cloned.1.call-done = f32[128,5632]{1,0:T(8,128)} async-done(((f32[2048,5632]{1,0:T(8,128)}), f32[128,5632]{1,0:T(8,128)}) %reduce-scatter.18.cloned.1.call-update) | async-done | bytes 2883600 | tf_op jit(solution)/shard_map/reduce_scatter | solution.py:127
  2052.3 473.4 %reduce-scatter.20.cloned.1.call-done = f32[352,2048]{1,0:T(8,128)} async-done(((f32[5632,2048]{1,0:T(8,128)}), f32[352,2048]{1,0:T(8,128)}) %reduce-scatter.20.cloned.1.call-update) | async-done | bytes 2883600 | tf_op jit(solution)/shard_map/reduce_scatter | solution.py:127
  (180 shorter events, 21.9 us)
Async XLA Ops:
  7.2 32.5 %all-gather.10.cloned.1.call-start = ((), (), s32[]{:S(2)}) async-start(), calls=%async_computation.15 | async-start | bytes 1114112 | tf_op jit(solution)/shard_map/all_gather | solution.py:66
  7.9 60.5 %all-gather.12.cloned.1.call-start = ((), (), s32[]{:S(2)}) async-start(), calls=%async_computation.16 | async-start | bytes 1114112 | tf_op jit(solution)/shard_map/all_gather | solution.py:66
  8.7 125.2 %all-gather.14.cloned.1.call-start = ((), (), s32[]{:S(2)}) async-start(), calls=%async_computation.17 | async-start | bytes 8912896 | tf_op jit(solution)/shard_map/all_gather | solution.py:66
  9.4 237.6 %all-gather.16.cloned.1.call-start = ((), (), s32[]{:S(2)}) async-start(), calls=%async_computation.18 | async-start | bytes 8912896 | tf_op jit(solution)/shard_map/all_gather | solution.py:66
  10.0 287.5 %all-gather.18.cloned.1.call-start = ((), (), s32[]{:S(2)}) async-start(), calls=%async_computation.19 | async-start | bytes 24510464 | tf_op jit(solution)/shard_map/all_gather | solution.py:66
  10.6 385.6 %all-gather.20.cloned.1.call-start = ((), (), s32[]{:S(2)}) async-start(), calls=%async_computation.20 | async-start | bytes 24510464 | tf_op jit(solution)/shard_map/all_gather | solution.py:66
  11.1 483.9 %all-gather.22.cloned.1.call-start = ((), (), s32[]{:S(2)}) async-start(), calls=%async_computation.21 | async-start | bytes 24510464 | tf_op jit(solution)/shard_map/all_gather | solution.py:66
  26.4 113.5 %copy-start.27 = (f32[16,1,128]{2,1,0:T(1,128)}, f32[16,1,128]{2,1,0:T(1,128)S(1)}, u32[]{:S(2)}) copy-start(f32[16,1,128]{2,1,0:T(1,128)S(1)} %convert_element_type.237) | copy-start | bytes 24580
  28.3 13.2 copy-start.47
  28.3 112.4 %copy-start.45 = (f32[128]{0:T(128)}, f32[128]{0:T(128)S(1)}, u32[]{:S(2)}) copy-start(f32[128]{0:T(128)S(1)} %fusion.89) | copy-start | bytes 1540
  29.1 131.0 %copy-start.31 = (f32[128,32]{0,1:T(8,128)}, f32[128,32]{0,1:T(8,128)S(1)}, u32[]{:S(2)}) copy-start(f32[128,32]{0,1:T(8,128)S(1)} %get-tuple-element.32) | copy-start | bytes 49156
  42.3 97.6 %all-to-all-start = ((bf16[128,16,64]{0,2,1:T(8,128)(2,1)}), bf16[128,16,64]{0,2,1:T(8,128)(2,1)S(1)}, u32[]{:S(2)}, u32[]{:S(2)}) async-start(bf16[128,16,64]{0,2,1:T(8,128)(2,1)} %bitcast.4), calls=%async_computation | async-start | bytes 524288 | tf_op jit(solution)/shard_map/all_to_all | solution.py:84
  140.7 12.4 all-to-all-start.1
  153.1 18.8 all-to-all-start.2
  160.4 42.5 %copy-start.37 = (bf16[2048,64,1]{0,1,2:T(8,128)(2,1)}, bf16[2048,64,1]{0,1,2:T(8,128)(2,1)S(1)}, u32[]{:S(2)}) copy-start(bf16[2048,64,1]{0,1,2:T(8,128)(2,1)S(1)} %reshape.247) | copy-start | bytes 786436
  160.7 27.5 %copy-start.23 = (bf16[2048,64,1]{0,1,2:T(8,128)(2,1)}, bf16[2048,64,1]{0,1,2:T(8,128)(2,1)S(1)}, u32[]{:S(2)}) copy-start(bf16[2048,64,1]{0,1,2:T(8,128)(2,1)S(1)} %reshape.246) | copy-start | bytes 786436
  171.9 16.2 copy-start.21
  172.0 16.3 copy-start.1
  188.2 14.7 copy-start.40
  203.5 20.6 copy-start.49
  203.5 43.5 %copy-start = (bf16[128,2048]{1,0:T(8,128)(2,1)S(1)}, bf16[128,2048]{1,0:T(8,128)(2,1)}, u32[]{:S(2)}) copy-start(bf16[128,2048]{1,0:T(8,128)(2,1)} %param.12) | copy-start | bytes 1572868
  221.7 24.0 all-to-all-start.3
  224.0 589.1 %reduce-scatter.10.cloned.1.call-start = ((), (), s32[]{:S(2)}) async-start(), calls=%async_computation.23 | async-start | bytes 2228224 | tf_op jit(solution)/shard_map/reduce_scatter | solution.py:127
  247.0 5.0 copy-start.13
  251.9 284.7 %copy-start.2 = (f32[128,2048]{1,0:T(8,128)}, f32[128,2048]{1,0:T(8,128)S(1)}, u32[]{:S(2)}) copy-start(f32[128,2048]{1,0:T(8,128)S(1)} %get-tuple-element.36) | copy-start | bytes 3145732
  252.1 156.4 %copy-start.4 = (bf16[128,2048]{1,0:T(8,128)(2,1)}, bf16[128,2048]{1,0:T(8,128)(2,1)S(1)}, u32[]{:S(2)}) copy-start(bf16[128,2048]{1,0:T(8,128)(2,1)S(1)} %multiply_convert_fusion.2) | copy-start | bytes 1572868
  309.8 185.2 %copy-start.19 = (bf16[128,2048]{1,0:T(8,128)(2,1)S(1)}, bf16[128,2048]{1,0:T(8,128)(2,1)}, u32[]{:S(2)}) copy-start(bf16[128,2048]{1,0:T(8,128)(2,1)} %param.14) | copy-start | bytes 1572868
  509.7 13.8 copy-start.6
  509.7 13.8 copy-start.8
  523.5 32.8 %copy-start.38 = (bf16[2048,64,1]{0,1,2:T(8,128)(2,1)S(1)}, bf16[2048,64,1]{0,1,2:T(8,128)(2,1)}, u32[]{:S(2)}) copy-start(bf16[2048,64,1]{0,1,2:T(8,128)(2,1)} %copy-done.37) | copy-start | bytes 786436
  523.5 32.8 %copy-start.41 = (f32[2,2048]{1,0:T(2,128)S(1)}, f32[2,2048]{1,0:T(2,128)}, u32[]{:S(2)}) copy-start(f32[2,2048]{1,0:T(2,128)} %copy-done.40) | copy-start | bytes 49156
  523.5 32.7 %copy-start.43 = (f32[2,2048]{1,0:T(2,128)S(1)}, f32[2,2048]{1,0:T(2,128)}, u32[]{:S(2)}) copy-start(f32[2,2048]{1,0:T(2,128)} %copy-done.42) | copy-start | bytes 49156
  577.9 26.3 %copy-start.22 = (bf16[128,32,64]{0,2,1:T(8,128)(2,1)S(1)}, bf16[128,32,64]{0,2,1:T(8,128)(2,1)}, u32[]{:S(2)}) copy-start(bf16[128,32,64]{0,2,1:T(8,128)(2,1)} %copy-done.21) | copy-start | bytes 1572868
  604.2 23.8 copy-start.32
  604.2 23.8 copy-start.39
  604.2 23.8 copy-start.28
  604.2 23.8 copy-start.46
  628.0 17.9 copy-start.33
  628.0 17.9 copy-start.35
  629.9 30.5 %copy-start.12 = (bf16[128,2048]{1,0:T(8,128)(2,1)S(1)}, bf16[128,2048]{1,0:T(8,128)(2,1)}, u32[]{:S(2)}) copy-start(bf16[128,2048]{1,0:T(8,128)(2,1)} %copy-done.11) | copy-start | bytes 1572868
  630.0 30.5 %copy-start.14 = (bf16[16,128,2,64]{1,3,2,0:T(8,128)(2,1)S(1)}, bf16[16,128,2,64]{1,3,2,0:T(8,128)(2,1)}, u32[]{:S(2)}) copy-start(bf16[16,128,2,64]{1,3,2,0:T(8,128)(2,1)} %copy-done.13) | copy-start | bytes 1572868
  630.0 183.1 %reduce-scatter.12.cloned.1.call-start = ((), (), s32[]{:S(2)}) async-start(), calls=%async_computation.24 | async-start | bytes 2228224 | tf_op jit(solution)/shard_map/reduce_scatter | solution.py:127
  658.5 10.2 copy-start.29
  660.4 8.3 copy-start.24
  660.4 266.5 %reduce-scatter.14.cloned.1.call-start = ((), (), s32[]{:S(2)}) async-start(), calls=%async_computation.25 | async-start | bytes 17825792 | tf_op jit(solution)/shard_map/reduce_scatter | solution.py:127
  668.6 436.7 %reduce-scatter.8.cloned.1.call-start = ((), (), s32[]{:S(2)}) async-start(), calls=%async_computation.22 | async-start | bytes 17825792 | tf_op jit(solution)/shard_map/reduce_scatter | solution.py:127
  694.6 8.3 copy-start.5
  694.6 8.3 copy-start.7
  702.9 875.8 %reduce-scatter.16.cloned.1.call-start = ((), (), s32[]{:S(2)}) async-start(), calls=%async_computation.26 | async-start | bytes 49020928 | tf_op jit(solution)/shard_map/reduce_scatter | solution.py:127
  721.0 1.4 copy-start.9
  721.0 1331.3 %reduce-scatter.18.cloned.1.call-start = ((), (), s32[]{:S(2)}) async-start(), calls=%async_computation.27 | async-start | bytes 49020928 | tf_op jit(solution)/shard_map/reduce_scatter | solution.py:127
  740.5 1.4 copy-start.10
  740.5 1.5 copy-start.20
  740.5 1785.1 %reduce-scatter.20.cloned.1.call-start = ((), (), s32[]{:S(2)}) async-start(), calls=%async_computation.28 | async-start | bytes 49020928 | tf_op jit(solution)/shard_map/reduce_scatter | solution.py:127
  760.0 1.2 copy-start.3
  761.2 11.6 copy-start.25
  761.2 11.6 copy-start.30
  761.2 12.0 copy-start.16
  761.2 12.0 copy-start.18
  772.8 5.1 copy-start.26
  772.8 5.1 copy-start.34
  772.9 5.1 copy-start.36
  772.9 5.7 copy-start.44
  772.9 39.0 %copy-start.48 = (f32[128]{0:T(128)S(1)}, f32[128]{0:T(128)}, u32[]{:S(2)}) copy-start(f32[128]{0:T(128)} %copy-done.47) | copy-start | bytes 1540
  (4 other events, 2.9 us)
Sparse Core Ops, SparseCore 0:
  10.2 29.4 all-gather.9
  41.9 26.5 all-gather.11
  70.7 63.1 all-gather.13
  135.9 57.0 all-gather.15
  195.1 102.3 all-gather.17
  299.6 96.5 all-gather.19
  398.4 96.5 all-gather.21
  630.1 57.1 reduce-scatter.9
  690.1 56.3 reduce-scatter.11
  749.2 177.6 reduce-scatter.13
  929.8 175.4 reduce-scatter.7
  1108.1 470.5 reduce-scatter.15
  1581.6 470.6 reduce-scatter.17
  2055.0 470.5 reduce-scatter.19
where the time goes:
time: 2540 us; the launch traced here: 2530 us
  waiting for transfers between devices  2050 us (81%)
  matrix products  268 us (11%)
  blocking collectives  113 us (4%)
  other arithmetic  53 us (2%)
    reduce_scatter x7, waiting for transfers between devices, layer_step(): scatter_rows(grad_part)  1710 us
    all_gather x7, waiting for transfers between devices, layer_step(): gather_rows(shard_w)  316 us
  transfers between devices with their start and end apart: 18, of which 13 were waited for; matrix products, arithmetic and copies ran while one was open for 9% of the time, Pallas kernels for 0%

commit v1 on v0

v1 whole, which is shorter than its diff:
```python
import functools
import jax
import jax.numpy as jnp
from jax import lax
from jax.sharding import PartitionSpec as P

ROPE_BASE = 10000.0
NORM_EPS = 1e-5
NEG_LARGE = -1e30
F32 = jnp.float32
BF16 = jnp.bfloat16


def norm_forward(hidden, gain_vec):
    inv_rms = lax.rsqrt(jnp.mean(hidden * hidden, axis=-1, keepdims=True) + NORM_EPS)
    return hidden * inv_rms * gain_vec


def rope_tables(positions, head_dim):
    half_dim = head_dim // 2
    inv_freq = 1.0 / (ROPE_BASE ** (jnp.arange(half_dim, dtype=F32) * (2.0 / head_dim)))
    angles = positions.astype(F32)[:, None] * inv_freq[None, :]
    return jnp.cos(angles)[:, None, :], jnp.sin(angles)[:, None, :]


def rotate(values_in, cos_tab, sin_tab):
    half_dim = values_in.shape[-1] // 2
    first_half = values_in[..., :half_dim].astype(F32)
    second_half = values_in[..., half_dim:].astype(F32)
    return jnp.concatenate([first_half * cos_tab - second_half * sin_tab, second_half * cos_tab + first_half * sin_tab], axis=-1)


def gated_unit(gate_pre, up_pre):
    return jax.nn.silu(gate_pre) * up_pre


def attention_forward(queries, keys_all, values_all):
    seq_len = queries.shape[0]
    score_scale = queries.shape[-1] ** -0.5
    scores = jnp.einsum('sgd,td->gst', queries, keys_all, preferred_element_type=F32) * score_scale
    causal = jnp.arange(seq_len)[:, None] >= jnp.arange(seq_len)[None, :]
    attn_probs = jax.nn.softmax(jnp.where(causal, scores, NEG_LARGE), axis=-1)
    attn_out = jnp.einsum('gst,td->sgd', attn_probs.astype(BF16), values_all, preferred_element_type=F32)
    return attn_out.astype(BF16), attn_probs


def attention_backward(queries, keys_all, values_all, attn_probs, d_attn):
    score_scale = queries.shape[-1] ** -0.5
    probs_b16 = attn_probs.astype(BF16)
    d_probs = jnp.einsum('sgd,td->gst', d_attn, values_all, preferred_element_type=F32)
    d_probs = d_probs.astype(BF16).astype(F32)
    row_dot = jnp.sum(d_probs * attn_probs, axis=-1, keepdims=True)
    d_scores = (attn_probs * (d_probs - row_dot) * score_scale).astype(BF16)
    d_queries = jnp.einsum('gst,td->sgd', d_scores, keys_all, preferred_element_type=F32)
    d_keys = jnp.einsum('gst,sgd->td', d_scores, queries, preferred_element_type=F32)
    d_values = jnp.einsum('gst,sgd->td', probs_b16, d_attn, preferred_element_type=F32)
    return d_queries.astype(BF16), d_keys.astype(BF16), d_values.astype(BF16)


def solution(mesh):
    n_dev = mesh.shape['sp']
    gather = functools.partial(lax.all_gather, axis_name='sp', axis=0, tiled=True)
    scatter = functools.partial(lax.psum_scatter, axis_name='sp', scatter_dimension=0, tiled=True)
    swap = functools.partial(lax.all_to_all, axis_name='sp', split_axis=0, concat_axis=0, tiled=True)

    def layer_step(x_in, positions, d_out, norm1_gain, norm2_gain, w_q, w_k, w_v, w_o, w_gate, w_up, w_down):
        tokens, dim = x_in.shape
        seq_len = tokens * n_dev
        n_q, hd = w_q.shape[1], w_q.shape[2]
        n_kv = w_k.shape[1]
        hpd = n_q // n_dev
        qw, kw = hpd * hd, hd
        rows = w_q.shape[0]
        feat = w_down.shape[0]
        me = lax.axis_index('sp')

        small = jnp.stack([norm1_gain.astype(F32), norm2_gain.astype(F32), positions.astype(F32)])
        small_all = gather(small[None])
        g1 = small_all[:, 0].reshape(-1)
        g2 = small_all[:, 1].reshape(-1)
        pos_all = small_all[:, 2].reshape(-1)
        cos_tab, sin_tab = rope_tables(positions, hd)
        cos_all, sin_all = rope_tables(pos_all, hd)

        wqkv = gather(jnp.concatenate([w_q.reshape(rows, n_q * hd), w_k.reshape(rows, n_kv * hd), w_v.reshape(rows, n_kv * hd)], axis=1))
        wo_own = w_o.reshape(qw, dim)
        wo_full = gather(wo_own)

        def by_feature(w):
            return w.T.reshape(n_dev, feat, rows)
        wgu = swap(jnp.concatenate([by_feature(w_gate), by_feature(w_up)], axis=1))
        wgu = wgu.transpose(1, 0, 2).reshape(2 * feat, dim)

        x_f32 = x_in.astype(F32)
        normed_pre, norm1_pull = jax.vjp(norm_forward, x_f32, g1)
        normed = normed_pre.astype(BF16)
        qkv = jnp.dot(normed, wqkv, preferred_element_type=F32).astype(BF16)
        q_rot = rotate(qkv[:, :n_q * hd].reshape(tokens, n_q, hd), cos_tab, sin_tab).astype(BF16)
        k_rot = rotate(qkv[:, n_q * hd:(n_q + n_kv) * hd].reshape(tokens, n_kv, hd), cos_tab, sin_tab).astype(BF16)
        v_lin = qkv[:, (n_q + n_kv) * hd:].reshape(tokens, n_kv, hd)
        rep = n_dev // n_kv
        send = jnp.concatenate([
            q_rot.reshape(tokens, n_dev, qw).transpose(1, 0, 2),
            jnp.repeat(k_rot.transpose(1, 0, 2), rep, axis=0),
            jnp.repeat(v_lin.transpose(1, 0, 2), rep, axis=0)], axis=2)
        seq = swap(send).reshape(seq_len, qw + 2 * kw)
        q_seq = seq[:, :qw].reshape(seq_len, hpd, hd)
        k_seq = seq[:, qw:qw + kw]
        v_seq = seq[:, qw + kw:]
        attn_seq, attn_probs = attention_forward(q_seq, k_seq, v_seq)
        attn_seq = attn_seq.reshape(seq_len, qw)
        attn_tok = swap(attn_seq.reshape(n_dev, tokens, qw)).transpose(1, 0, 2).reshape(tokens, n_q * hd)
        attn_proj = jnp.dot(attn_tok, wo_full, preferred_element_type=F32)
        hidden = (x_f32 + attn_proj).astype(BF16)
        hidden_f32 = hidden.astype(F32)
        mlp_pre, norm2_pull = jax.vjp(norm_forward, hidden_f32, g2)
        mlp_in = mlp_pre.astype(BF16)

        m_full = gather(mlp_in)
        do_full = gather(d_out)
        u_full = gather(normed)
        gu = jnp.einsum('fd,td->ft', wgu, m_full, preferred_element_type=F32).astype(BF16)
        gate_act, up_act = gu[:feat], gu[feat:]
        glu_pre, glu_pull = jax.vjp(gated_unit, gate_act.astype(F32), up_act.astype(F32))
        glu = glu_pre.astype(BF16)
        y_part = jnp.einsum('ft,fd->td', glu, w_down, preferred_element_type=F32)
        y_out = (hidden_f32 + scatter(y_part)).astype(BF16)

        d_down = jnp.einsum('ft,td->fd', glu, do_full, preferred_element_type=F32)
        d_glu = jnp.einsum('fd,td->ft', w_down, do_full, preferred_element_type=F32).astype(BF16)
        d_gate_f, d_up_f = glu_pull(d_glu.astype(F32))
        dgu = jnp.concatenate([d_gate_f.astype(BF16), d_up_f.astype(BF16)], axis=0)
        dm_part = jnp.einsum('ft,fd->td', dgu, wgu, preferred_element_type=F32)
        d_mlp_in = scatter(dm_part).astype(BF16)
        d_hidden_norm, d_g2 = norm2_pull(d_mlp_in.astype(F32))
        d_hidden = (d_out.astype(F32) + d_hidden_norm).astype(BF16)
        dh_full = gather(d_hidden)

        dwgu = jnp.einsum('ft,td->fd', dgu, m_full, preferred_element_type=F32)
        dwgu = swap(dwgu.reshape(2 * feat, n_dev, rows).transpose(1, 0, 2))
        d_gate = dwgu[:, :feat].reshape(n_dev * feat, rows).T
        d_up = dwgu[:, feat:].reshape(n_dev * feat, rows).T

        d_wo = jnp.einsum('te,td->ed', attn_seq, dh_full, preferred_element_type=F32).reshape(w_o.shape)
        d_attn = jnp.einsum('td,ed->te', dh_full, wo_own, preferred_element_type=F32).astype(BF16)
        d_q_seq, d_k_seq, d_v_seq = attention_backward(q_seq, k_seq, v_seq, attn_probs, d_attn.reshape(seq_len, hpd, hd))
        dq_lin_seq = rotate(d_q_seq, cos_all, -sin_all).astype(BF16).reshape(seq_len, qw)
        back = swap(jnp.concatenate([dq_lin_seq, d_k_seq, d_v_seq], axis=1).reshape(n_dev, tokens, qw + 2 * kw))
        d_q_lin = back[:, :, :qw].transpose(1, 0, 2).reshape(tokens, n_q * hd)
        shares = back[:, :, qw:].reshape(n_kv, rep, tokens, 2, hd)
        dkv = jnp.sum(shares, axis=1, dtype=F32).astype(BF16)
        d_k_lin = rotate(dkv[:, :, 0].transpose(1, 0, 2), cos_tab, -sin_tab).astype(BF16).reshape(tokens, n_kv * hd)
        d_v_lin = dkv[:, :, 1].transpose(1, 0, 2).reshape(tokens, n_kv * hd)
        dkv_lin = jnp.concatenate([d_k_lin, d_v_lin], axis=1)
        dkv_full = gather(dkv_lin)
        u_own = lax.dynamic_slice_in_dim(u_full, me * rows, rows, axis=1)
        d_wkv = jnp.einsum('td,te->de', u_own, dkv_full, preferred_element_type=F32)
        d_wk = d_wkv[:, :n_kv * hd].reshape(w_k.shape)
        d_wv = d_wkv[:, n_kv * hd:].reshape(w_v.shape)
        dwq = jnp.einsum('td,te->de', u_full, dq_lin_seq, preferred_element_type=F32)
        d_normed = lax.dot_general(jnp.concatenate([d_q_lin, dkv_lin], axis=1), wqkv, (((1,), (1,)), ((), ())), preferred_element_type=F32).astype(BF16)
        d_x_norm, d_g1 = norm1_pull(d_normed.astype(F32))
        d_x = (d_hidden.astype(F32) + d_x_norm).astype(BF16)
        gains = jnp.stack([d_g1.reshape(n_dev, rows), d_g2.reshape(n_dev, rows)], axis=1)
        tail = swap(jnp.concatenate([dwq.reshape(n_dev, rows, qw), jnp.pad(gains, ((0, 0), (0, 6), (0, qw - rows)))], axis=1))
        d_wq = tail[:, :rows].transpose(1, 0, 2).reshape(w_q.shape)
        gsum = jnp.sum(tail[:, rows:, :rows], axis=0)
        return (y_out, d_x, gsum[0], gsum[1], d_wq, d_wk, d_wv, d_wo, d_gate, d_up, d_down)

    all_rows = P('sp')
    return jax.shard_map(layer_step, mesh=mesh, in_specs=(all_rows,) * 12, out_specs=(all_rows,) * 11, check_vma=False)
```

time: 2540 us -> 991 us (0.39)
  waiting for transfers between devices: 2050 us -> 607 us
  matrix products: 268 us -> 213 us
  blocking collectives: 113 us -> 59.8 us
  other arithmetic: 53 us -> 24.9 us
  local copies, waits for them, and re-layouts: 20.2 us -> 47 us
    reduce_scatter x7 -> x2, waiting for transfers between devices: 1710 us -> 342 us  [the longest x1 176 us: layer_step(): y_out = (hidden_f32 + scatter(y_part)).astype(BF16)]
    all_gather x7, waiting for transfers between devices: 316 us -> 162 us  [the longest x1 58.9 us: layer_step(): gather(jnp.concatenate([w_q.reshape(rows, n_q * hd), w_k.reshape(rows, n_...]
    all_to_all x4 -> x5, waiting for transfers between devices: 20.1 us -> 100 us  [the longest x1 56.9 us: layer_step(): dwgu = swap(dwgu.reshape(2 * feat, n_dev, rows).transpose(1, 0, 2))]
    dot_general x21 -> x18, matrix products: 246 us -> 194 us  [the longest x1 33.3 us: attention_backward(): jnp.einsum('gst,sgd->td', d_scores, queries, preferred_element_type=F32)]
    unnamed x1 -> x0, blocking collectives: 32.1 us -> none
  transfers between devices with their start and end apart: 18 -> 14, of which waited for: 13 -> 11; matrix products, arithmetic and copies ran while one was open for 9% -> 25% of each run, Pallas kernels for 0% -> 0%
where the time goes in v1:
time: 991 us; the launch traced here: 982 us
  waiting for transfers between devices  607 us (61%)
  matrix products  213 us (21%)
  blocking collectives  59.8 us (6%)
  local copies, waits for them, and re-layouts  47 us (5%)
  other arithmetic  24.9 us (3%)
  starting transfers between devices  16.4 us (2%)
  between operations  14.8 us (1%)
    reduce_scatter x1, waiting for transfers between devices, layer_step(): y_out = (hidden_f32 + scatter(y_part)).astype(BF16)  176 us
    reduce_scatter x1, waiting for transfers between devices, layer_step(): d_mlp_in = scatter(dm_part).astype(BF16)  167 us
    all_gather x1, waiting for transfers between devices, layer_step(): gather(jnp.concatenate([w_q.reshape(rows, n_q * hd), w_k.reshape(rows, n_...  58.9 us
    all_to_all x1, waiting for transfers between devices, layer_step(): dwgu = swap(dwgu.reshape(2 * feat, n_dev, rows).transpose(1, 0, 2))  56.9 us
    all_to_all x1, blocking collectives, layer_step(): wgu = swap(jnp.concatenate([by_feature(w_gate), by_feature(w_up)], axis=1))  45.3 us
    all_gather x1, waiting for transfers between devices, layer_step(): dh_full = gather(d_hidden)  45.2 us
    all_gather x1, waiting for transfers between devices, layer_step(): do_full = gather(d_out)  40.2 us
    dot_general x1, matrix products, attention_backward(): jnp.einsum('gst,sgd->td', d_scores, queries, preferred_element_type=F32)  33.3 us
  transfers between devices with their start and end apart: 14, of which 11 were waited for; matrix products, arithmetic and copies ran while one was open for 25% of the time, Pallas kernels for 0%

profile of v1, /device:TPU:0, one launch (start us, length us, event | category | flops | bytes accessed | tf_op | source)
XLA Modules:
  0.0 982.4 jit_solution(6141247018754246511)
XLA Ops:
  7.3 2.1 pad_maximum_fusion.7
  11.5 14.5 %all-gather.1 = f32[16,3,128]{2,1,0:T(4,128)S(1)} all-gather(f32[1,3,128]{2,1,0:T(4,128)S(1)} %maximum_bitcast_fusion.1), channel_id=2, replica_groups=mesh['sp'=16] {'sp'}, dimensions={0}, use_global_device_ids=true | all-gather | bytes 26112 | tf_op jit(solution)/shard_map/all_gather | solution.py:78
  26.3 0.8 fusion.91
  28.5 58.9 %all-gather.10.cloned.1.call-done = bf16[2048,2560]{0,1:T(8,128)(2,1)} async-done(((bf16[128,2560]{0,1:T(8,128)(2,1)}), bf16[2048,2560]{0,1:T(8,128)(2,1)}) %all-gather.10.cloned.1.call-update) | async-done | bytes 10485776 | tf_op jit(solution)/shard_map/all_gather | solution.py:85
  87.4 7.5 convolution_convert_fusion.1
  96.3 0.9 fusion.73
  97.3 1.0 pad_maximum_fusion.5
  98.4 2.5 all-to-all-start
  100.9 4.2 iota_compare_fusion
  105.0 19.3 %all-to-all-done = bf16[16,128,256]{1,2,0:T(8,128)(2,1)S(1)} async-done(((bf16[16,128,256]{1,2,0:T(8,128)(2,1)}), bf16[16,128,256]{1,2,0:T(8,128)(2,1)S(1)}, u32[]{:S(2)}, u32[]{:S(2)}) %all-to-all-start) | async-done | bytes 1048608 | tf_op jit(solution)/shard_map/all_to_all | solution.py:106
  124.5 1.0 copy-done.7
  125.5 18.4 %fusion.114 = (f32[2,2048]{1,0:T(2,128)S(1)}, f32[2,2048,2048]{1,2,0:T(8,128)}) fusion(pred[2048,2048]{0,1:T(8,128)(4,1)} %iota_compare_fusion, bf16[2048,2,64]{0,2,1:T(8,128)(2,1)S(1)} %bitcast.272, bf16[2048,256]{0,1:T(8,128)(2,1)} %copy-done.7), kind=kOutput, calls=%fused_computation.188 | convolution fusion | flops 1107298304 | bytes 38551552 | tf_op jit(solution)/shard_map/sub | solution.py:42
  143.9 12.2 %fusion.33 = bf16[64,2,2048]{2,0,1:T(8,128)(2,1)S(1)} fusion(bf16[2048,256]{0,1:T(8,128)(2,1)} %copy-done.7, f32[2,2048,2048]{1,2,0:T(8,128)} %get-tuple-element.83, f32[2,2048]{1,0:T(2,128)S(1)} %get-tuple-element.82), kind=kOutput, calls=%fused_computation.54 | convolution fusion | flops 1090781184 | bytes 34357248 | tf_op jit(solution)/shard_map/gst,td->sgd/dot_general | solution.py:43
  156.2 0.8 copy-done.10
  157.1 0.9 copy.64
  158.0 2.3 all-to-all-start.1
  160.6 10.1 %all-to-all-done.1 = bf16[16,128,128]{1,2,0:T(8,128)(2,1)S(1)} async-done(((bf16[16,128,128]{1,2,0:T(8,128)(2,1)}), bf16[16,128,128]{1,2,0:T(8,128)(2,1)S(1)}, u32[]{:S(2)}, u32[]{:S(2)}) %all-to-all-start.1) | async-done | bytes 524320 | tf_op jit(solution)/shard_map/all_to_all | solution.py:112
  170.7 4.8 multiply_reduce_fusion
  175.4 1.0 multiply_convert_fusion
  177.0 2.5 copy.65
  179.6 2.5 copy.66
  182.1 2.0 pad_maximum_fusion
  184.1 45.3 %all_to_all.30 = bf16[16,704,128]{2,1,0:T(8,128)(2,1)} all-to-all(bf16[16,704,128]{2,1,0:T(8,128)(2,1)S(1)} %pad_maximum_fusion), channel_id=1, replica_groups=mesh['sp'=16] {'sp'}, dimensions={0} | all-to-all | bytes 5767168 | tf_op jit(solution)/shard_map/all_to_all | solution.py:91
  229.4 18.1 %all-gather.14.cloned.1.call-done = bf16[2048,2048]{1,0:T(8,128)(2,1)} async-done(((bf16[128,2048]{1,0:T(8,128)(2,1)}), bf16[2048,2048]{1,0:T(8,128)(2,1)}) %all-gather.14.cloned.1.call-update) | async-done | bytes 8388624 | tf_op jit(solution)/shard_map/all_gather | solution.py:119
  247.5 10.6 %convolution_convert_fusion.2 = bf16[704,2048]{1,0:T(8,128)(2,1)} fusion(bf16[2048,2048]{1,0:T(8,128)(2,1)} %all-gather.14.cloned.1.call-done, bf16[16,704,128]{2,1,0:T(8,128)(2,1)} %all_to_all.30), kind=kOutput, calls=%fused_computation.35 | convolution fusion | flops 5907021824 | bytes 14155776 | tf_op jit(solution)/shard_map/fd,td->ft/dot_general | solution.py:122
  258.0 40.2 %all-gather.16.cloned.1.call-done = bf16[2048,2048]{1,0:T(8,128)(2,1)} async-done(((bf16[128,2048]{1,0:T(8,128)(2,1)}), bf16[2048,2048]{1,0:T(8,128)(2,1)}) %all-gather.16.cloned.1.call-update) | async-done | bytes 8388624 | tf_op jit(solution)/shard_map/all_gather | solution.py:120
  298.2 8.6 fusion.27
  306.9 1.1 copy-done.33
  308.5 10.4 %fusion.28 = f32[2048,2048]{1,0:T(8,128)} fusion(bf16[352,2048]{1,0:T(8,128)(2,1)S(1)} %get-tuple-element.51, bf16[352,2048]{1,0:T(8,128)(2,1)S(1)} %get-tuple-element.50, bf16[16,704,128]{2,1,0:T(8,128)(2,1)S(1)} %copy-done.9), kind=kOutput, calls=%fused_computation.44 | convolution fusion | flops 5911347200 | bytes 22544384 | tf_op jit(solution)/shard_map/ft,fd->td/dot_general | solution.py:133
  319.2 10.3 %fusion.106 = f32[2048,2048]{1,0:T(8,128)} fusion(bf16[352,2048]{1,0:T(8,128)(2,1)S(1)} %copy-done, bf16[704,2048]{1,0:T(8,128)(2,1)} %convolution_convert_fusion.2), kind=kOutput, calls=%fused_computation.181 | convolution fusion | flops 2958557184 | bytes 21102592 | tf_op jit(solution)/shard_map/ft,fd->td/dot_general | solution.py:126
  329.6 166.8 %reduce-scatter.5.cloned.1.call-done = f32[128,2048]{1,0:T(8,128)} async-done(((f32[2048,2048]{1,0:T(8,128)}), f32[128,2048]{1,0:T(8,128)}) %reduce-scatter.5.cloned.1.call-update) | async-done | bytes 1048592 | tf_op jit(solution)/shard_map/reduce_scatter | solution.py:134
  496.3 2.1 fusion.60
  498.4 175.6 %reduce-scatter.3.cloned.1.call-done = f32[128,2048]{1,0:T(8,128)} async-done(((f32[2048,2048]{1,0:T(8,128)}), f32[128,2048]{1,0:T(8,128)}) %reduce-scatter.3.cloned.1.call-update) | async-done | bytes 1048592 | tf_op jit(solution)/shard_map/reduce_scatter | solution.py:127
  674.0 2.9 fusion.62
  677.7 1.0 multiply_cosine_fusion
  678.7 45.2 %all-gather.18.cloned.1.call-done = bf16[2048,2048]{1,0:T(8,128)(2,1)} async-done(((bf16[128,2048]{1,0:T(8,128)(2,1)}), bf16[2048,2048]{1,0:T(8,128)(2,1)}) %all-gather.18.cloned.1.call-update) | async-done | bytes 8388624 | tf_op jit(solution)/shard_map/all_gather | solution.py:137
  723.9 6.3 convolution_convert_fusion.4
  730.2 8.5 convolution_convert_fusion
  738.7 33.2 %fusion.40 = bf16[2048,2,64]{0,2,1:T(8,128)(2,1)S(1)} fusion(bf16[2048,2048,2]{1,0,2:T(8,128)(2,1)} %convolution_convert_fusion, bf16[2048,256]{0,1:T(8,128)(2,1)S(1)} %copy-done.8, f32[2,2048,2048]{1,2,0:T(8,128)} %get-tuple-element.83, f32[2,2048]{1,0:T(2,128)S(1)} %copy-done.37), kind=kOutput, calls=%fused_computation.61 | convolution fusion | flops 1149507584 | bytes 101482496 | tf_op jit(solution)/shard_map/gst,td->sgd/dot_general | solution.py:54
  772.9 33.3 %fusion.53 = bf16[8,16,8,128]{3,2,1,0:T(8,128)(2,1)S(1)} fusion(bf16[2048,2,64]{0,2,1:T(8,128)(2,1)S(1)} %bitcast.273, bf16[2048,2048,2]{1,0,2:T(8,128)(2,1)} %convolution_convert_fusion, f32[2,2048,2048]{1,2,0:T(8,128)} %get-tuple-element.83, f32[2,2048]{1,0:T(2,128)S(1)} %copy-done.37), kind=kOutput, calls=%fused_computation.78 | convolution fusion | flops 1149376512 | bytes 51134464 | tf_op jit(solution)/shard_map/gst,sgd->td/dot_general | solution.py:55
  806.4 13.3 %fusion.54 = bf16[8,16,8,128]{3,2,1,0:T(8,128)(2,1)S(1)} fusion(bf16[2048,2,64]{0,2,1:T(8,128)(2,1)S(1)} %bitcast.268, f32[2,2048,2048]{1,2,0:T(8,128)} %get-tuple-element.83, f32[2,2048]{1,0:T(2,128)S(1)} %copy-done.37), kind=kOutput, calls=%fused_computation.79 | convolution fusion | flops 1090650112 | bytes 34357248 | tf_op jit(solution)/shard_map/gst,sgd->td/dot_general | solution.py:56
  819.7 1.0 pad_maximum_fusion.6
  820.7 2.7 all-to-all-start.3
  823.4 9.0 convolution_bitcast_fusion
  832.4 3.0 copy.108
  835.4 4.1 all-to-all-done.3
  839.5 3.4 all-to-all-start.5
  842.9 12.4 %copy.87 = bf16[2048,2048]{1,0:T(8,128)(2,1)} copy(bf16[2048,2048]{0,1:T(8,128)(2,1)} %bitcast.244) | data formatting | bytes 16777216 | tf_op jit(solution)/shard_map/td,te->de/dot_general | solution.py:160
  855.3 0.9 fusion.109
  857.0 9.4 fusion.104
  866.5 56.9 %all-to-all-done.5 = f32[16,704,128]{2,1,0:T(8,128)} async-done(((f32[16,704,128]{2,1,0:T(8,128)}), f32[16,704,128]{2,1,0:T(8,128)}, u32[]{:S(2)}, u32[]{:S(2)}) %all-to-all-start.5) | async-done | bytes 5767200 | tf_op jit(solution)/shard_map/all_to_all | solution.py:140
  923.3 5.6 fusion.108
  929.0 3.4 copy.80
  932.3 3.5 copy.81
  935.9 5.9 fusion.115
  941.9 2.6 fusion.58
  944.5 1.1 pad_maximum_fusion.4
  945.6 4.8 all-to-all-start.4
  950.5 5.7 fusion.10
  956.3 1.2 fusion.64
  957.5 9.8 all-to-all-done.4
  967.3 1.1 slice_bitcast_fusion
  968.4 2.5 copy.76
  971.5 2.6 fusion.79
  (142 shorter events, 12.2 us)
Async XLA Ops:
  7.2 291.1 %copy-start = (bf16[352,2048]{1,0:T(8,128)(2,1)S(1)}, bf16[352,2048]{1,0:T(8,128)(2,1)}, u32[]{:S(2)}) copy-start(bf16[352,2048]{1,0:T(8,128)(2,1)} %param.23) | copy-start | bytes 4325380
  7.2 18.9 %copy-start.2 = (bf16[128,2048]{1,0:T(8,128)(2,1)S(1)}, bf16[128,2048]{1,0:T(8,128)(2,1)}, u32[]{:S(2)}) copy-start(bf16[128,2048]{1,0:T(8,128)(2,1)} %param.12) | copy-start | bytes 1572868
  7.2 80.2 %all-gather.10.cloned.1.call-start = ((), (), s32[]{:S(2)}) async-start(), calls=%async_computation.8 | async-start | bytes 11141120 | tf_op jit(solution)/shard_map/all_gather | solution.py:85
  9.4 151.1 %all-gather.12.cloned.1.call-start = ((), (), s32[]{:S(2)}) async-start(), calls=%async_computation.9 | async-start | bytes 8912896 | tf_op jit(solution)/shard_map/all_gather | solution.py:87
  26.1 1.6 copy-start.29
  26.3 1.4 copy-start.31
  26.3 1.4 copy-start.27
  27.0 69.2 %copy-start.19 = (f32[128,32]{0,1:T(8,128)}, f32[128,32]{0,1:T(8,128)S(1)}, u32[]{:S(2)}) copy-start(f32[128,32]{0,1:T(8,128)S(1)} %get-tuple-element.79) | copy-start | bytes 49156
  27.7 0.6 copy-start.21
  28.5 66.4 %copy-start.4 = (bf16[128,2048]{1,0:T(8,128)(2,1)}, bf16[128,2048]{1,0:T(8,128)(2,1)S(1)}, u32[]{:S(2)}) copy-start(bf16[128,2048]{1,0:T(8,128)(2,1)S(1)} %fusion.57) | copy-start | bytes 1572868
  98.4 25.9 %all-to-all-start = ((bf16[16,128,256]{1,2,0:T(8,128)(2,1)}), bf16[16,128,256]{1,2,0:T(8,128)(2,1)S(1)}, u32[]{:S(2)}, u32[]{:S(2)}) async-start(bf16[16,128,256]{1,2,0:T(8,128)(2,1)} %pad_maximum_fusion.5), calls=%async_computation | async-start | bytes 2097152 | tf_op jit(solution)/shard_map/all_to_all | solution.py:106
  124.5 1.0 copy-start.7
  125.5 18.4 %copy-start.17 = (bf16[2048,128]{0,1:T(8,128)(2,1)}, bf16[2048,128]{0,1:T(8,128)(2,1)S(1)}, u32[]{:S(2)}) copy-start(bf16[2048,128]{0,1:T(8,128)(2,1)S(1)} %slice.134) | copy-start | bytes 1572868
  143.9 12.3 %copy-start.36 = (f32[2,2048]{1,0:T(2,128)}, f32[2,2048]{1,0:T(2,128)S(1)}, u32[]{:S(2)}) copy-start(f32[2,2048]{1,0:T(2,128)S(1)} %get-tuple-element.82) | copy-start | bytes 49156
  156.1 0.8 copy-start.10
  158.0 12.7 %all-to-all-start.1 = ((bf16[16,128,128]{1,2,0:T(8,128)(2,1)}), bf16[16,128,128]{1,2,0:T(8,128)(2,1)S(1)}, u32[]{:S(2)}, u32[]{:S(2)}) async-start(bf16[16,128,128]{1,2,0:T(8,128)(2,1)} %copy.64), calls=%async_computation.1 | async-start | bytes 1048576 | tf_op jit(solution)/shard_map/all_to_all | solution.py:112
  160.3 87.1 %all-gather.14.cloned.1.call-start = ((), (), s32[]{:S(2)}) async-start(), calls=%async_computation.10 | async-start | bytes 8912896 | tf_op jit(solution)/shard_map/all_gather | solution.py:119
  170.7 4.8 copy-start.23
  176.4 121.8 %all-gather.16.cloned.1.call-start = ((), (), s32[]{:S(2)}) async-start(), calls=%async_computation.12 | async-start | bytes 8912896 | tf_op jit(solution)/shard_map/all_gather | solution.py:120
  177.0 319.3 %reduce-scatter.5.cloned.1.call-start = ((), (), s32[]{:S(2)}) async-start(), calls=%async_computation.13 | async-start | bytes 17825792 | tf_op jit(solution)/shard_map/reduce_scatter | solution.py:134
  298.2 10.2 %copy-start.9 = (bf16[16,704,128]{2,1,0:T(8,128)(2,1)S(1)}, bf16[16,704,128]{2,1,0:T(8,128)(2,1)}, u32[]{:S(2)}) copy-start(bf16[16,704,128]{2,1,0:T(8,128)(2,1)} %all_to_all.30) | copy-start | bytes 8650756
  306.9 1.1 copy-start.33
  306.9 1.6 copy-start.35
  318.9 355.1 %reduce-scatter.3.cloned.1.call-start = ((), (), s32[]{:S(2)}) async-start(), calls=%async_computation.11 | async-start | bytes 17825792 | tf_op jit(solution)/shard_map/reduce_scatter | solution.py:127
  329.5 344.5 %copy-start.15 = (bf16[128,2048]{1,0:T(8,128)(2,1)S(1)}, bf16[128,2048]{1,0:T(8,128)(2,1)}, u32[]{:S(2)}) copy-start(bf16[128,2048]{1,0:T(8,128)(2,1)} %param.14) | copy-start | bytes 1572868
  329.5 394.4 %all-gather.18.cloned.1.call-start = ((), (), s32[]{:S(2)}) async-start(), calls=%async_computation.14 | async-start | bytes 8912896 | tf_op jit(solution)/shard_map/all_gather | solution.py:137
  498.4 179.3 %copy-start.26 = (f32[16,1,128]{2,1,0:T(1,128)S(1)}, f32[16,1,128]{2,1,0:T(1,128)}, u32[]{:S(2)}) copy-start(f32[16,1,128]{2,1,0:T(1,128)} %get-tuple-element.70) | copy-start | bytes 24580
  498.4 179.3 %copy-start.30 = (f32[32]{0:T(128)S(1)}, f32[32]{0:T(128)}, u32[]{:S(2)}) copy-start(f32[32]{0:T(128)} %copy-done.29) | copy-start | bytes 388
  498.4 225.5 %copy-start.16 = (bf16[2,64,2048]{2,1,0:T(8,128)(2,1)S(1)}, bf16[2,64,2048]{2,1,0:T(8,128)(2,1)}, u32[]{:S(2)}) copy-start(bf16[2,64,2048]{2,1,0:T(8,128)(2,1)} %param.20) | copy-start | bytes 1572868
  676.9 166.0 %all-gather.20.cloned.1.call-start = ((), (), s32[]{:S(2)}) async-start(), calls=%async_computation.15 | async-start | bytes 8912896 | tf_op jit(solution)/shard_map/all_gather | solution.py:121
  678.7 51.5 %copy-start.8 = (bf16[2048,256]{0,1:T(8,128)(2,1)S(1)}, bf16[2048,256]{0,1:T(8,128)(2,1)}, u32[]{:S(2)}) copy-start(bf16[2048,256]{0,1:T(8,128)(2,1)} %copy-done.7) | copy-start | bytes 3145732
  730.2 8.5 copy-start.37
  771.9 1.0 copy-start.18
  772.1 34.2 %copy-start.12 = (bf16[2048,2,64]{0,2,1:T(8,128)(2,1)}, bf16[2048,2,64]{0,2,1:T(8,128)(2,1)S(1)}, u32[]{:S(2)}) copy-start(bf16[2048,2,64]{0,2,1:T(8,128)(2,1)S(1)} %maximum_convert_fusion) | copy-start | bytes 1572868
  819.6 3.8 copy-start.34
  820.7 18.8 %all-to-all-start.3 = ((bf16[16,128,256]{1,2,0:T(8,128)(2,1)}), bf16[16,128,256]{1,2,0:T(8,128)(2,1)S(1)}, u32[]{:S(2)}, u32[]{:S(2)}) async-start(bf16[16,128,256]{1,2,0:T(8,128)(2,1)} %pad_maximum_fusion.6), calls=%async_computation.5 | async-start | bytes 2097152 | tf_op jit(solution)/shard_map/all_to_all | solution.py:148
  839.5 83.8 %all-to-all-start.5 = ((f32[16,704,128]{2,1,0:T(8,128)}), f32[16,704,128]{2,1,0:T(8,128)}, u32[]{:S(2)}, u32[]{:S(2)}) async-start(f32[16,704,128]{2,1,0:T(8,128)} %bitcast.241), calls=%async_computation.7 | async-start | bytes 11534336 | tf_op jit(solution)/shard_map/all_to_all | solution.py:140
  842.9 128.6 %all-gather.22.cloned.1.call-start = ((), (), s32[]{:S(2)}) async-start(), calls=%async_computation.16 | async-start | bytes 2228224 | tf_op jit(solution)/shard_map/all_gather | solution.py:155
  855.3 1.0 copy-start.20
  855.3 1.0 copy-start.24
  932.3 3.5 copy-start.13
  932.3 9.5 slice-start
  935.9 6.0 slice-start.1
  935.9 6.0 slice-start.2
  935.9 6.0 copy-start.3
  935.9 6.0 copy-start.14
  935.9 6.0 copy-start.22
  935.9 6.0 copy-start.28
  941.9 2.6 copy-start.25
  944.5 6.0 copy-start.11
  945.6 21.6 %all-to-all-start.4 = ((f32[16,136,128]{2,1,0:T(8,128)}), f32[16,136,128]{2,1,0:T(8,128)S(1)}, u32[]{:S(2)}, u32[]{:S(2)}) async-start(f32[16,136,128]{2,1,0:T(8,128)} %pad_maximum_fusion.4), calls=%async_computation.6 | async-start | bytes 2228224 | tf_op jit(solution)/shard_map/all_to_all | solution.py:165
  950.5 5.8 copy-start.32
  950.5 5.8 copy-start.5
  950.5 5.8 copy-start.6
  967.3 8.3 copy-start.1
Sparse Core Ops, SparseCore 0:
  10.8 76.5 all-gather.9
  89.6 55.8 all-gather.11
  176.5 70.8 all-gather.13
  249.6 48.6 all-gather.15
  319.0 177.2 reduce-scatter.4
  498.4 175.4 reduce-scatter.2
  677.1 46.8 all-gather.17
  726.2 48.6 all-gather.19
  857.2 65.2 all-gather.21

commit v2 on v1

--- a/solution.py
+++ b/solution.py
@@ -2,6 +2,8 @@
 import jax
 import jax.numpy as jnp
 from jax import lax
+from jax.experimental import pallas as pl
+from jax.experimental.pallas import tpu as pltpu
 from jax.sharding import PartitionSpec as P
 
 ROPE_BASE = 10000.0
@@ -34,33 +36,299 @@
     return jax.nn.silu(gate_pre) * up_pre
 
 
-def attention_forward(queries, keys_all, values_all):
-    seq_len = queries.shape[0]
-    score_scale = queries.shape[-1] ** -0.5
-    scores = jnp.einsum('sgd,td->gst', queries, keys_all, preferred_element_type=F32) * score_scale
-    causal = jnp.arange(seq_len)[:, None] >= jnp.arange(seq_len)[None, :]
-    attn_probs = jax.nn.softmax(jnp.where(causal, scores, NEG_LARGE), axis=-1)
-    attn_out = jnp.einsum('gst,td->sgd', attn_probs.astype(BF16), values_all, preferred_element_type=F32)
-    return attn_out.astype(BF16), attn_probs
-
-
-def attention_backward(queries, keys_all, values_all, attn_probs, d_attn):
-    score_scale = queries.shape[-1] ** -0.5
-    probs_b16 = attn_probs.astype(BF16)
-    d_probs = jnp.einsum('sgd,td->gst', d_attn, values_all, preferred_element_type=F32)
-    d_probs = d_probs.astype(BF16).astype(F32)
-    row_dot = jnp.sum(d_probs * attn_probs, axis=-1, keepdims=True)
-    d_scores = (attn_probs * (d_probs - row_dot) * score_scale).astype(BF16)
-    d_queries = jnp.einsum('gst,td->sgd', d_scores, keys_all, preferred_element_type=F32)
-    d_keys = jnp.einsum('gst,sgd->td', d_scores, queries, preferred_element_type=F32)
-    d_values = jnp.einsum('gst,sgd->td', probs_b16, d_attn, preferred_element_type=F32)
-    return d_queries.astype(BF16), d_keys.astype(BF16), d_values.astype(BF16)
+NT = (((1,), (1,)), ((), ()))
+TN = (((0,), (0,)), ((), ()))
+NN = (((1,), (0,)), ((), ()))
+
+
+def mm(a, b, dims):
+    return lax.dot_general(a, b, dims, preferred_element_type=F32)
+
+
+QB = 256
+KB = 256
+
+
+def attn_fwd_kernel(q_ref, k_ref, v_ref, o_ref, stat_ref, s_scr):
+    heads, seq, hd = q_ref.shape
+    scale = hd ** -0.5
+    lanes = heads * QB
+
+    def q_block(qb, carry):
+        qs = pl.ds(pl.multiple_of(qb * QB, QB), QB)
+        q2 = jnp.concatenate([q_ref[h, qs, :] for h in range(heads)], axis=0)
+
+        def scores(kb, top, diagonal):
+            ks = pl.ds(pl.multiple_of(kb * KB, KB), KB)
+            s = mm(k_ref[ks, :], q2, NT) * scale
+            if diagonal:
+                key = lax.broadcasted_iota(jnp.int32, (KB, lanes), 0)
+                qry = lax.broadcasted_iota(jnp.int32, (KB, lanes), 1) % QB
+                s = jnp.where(qry >= key, s, NEG_LARGE)
+            s_scr[ks, :] = s
+            return jnp.maximum(top, jnp.max(s, axis=0, keepdims=True))
+
+        top = lax.fori_loop(0, qb, lambda kb, t: scores(kb, t, False), jnp.full((1, lanes), NEG_LARGE, F32))
+        top = scores(qb, top, True)
+
+        def expo(kb, tot):
+            ks = pl.ds(pl.multiple_of(kb * KB, KB), KB)
+            e = jnp.exp(s_scr[ks, :] - top)
+            s_scr[ks, :] = e
+            return tot + jnp.sum(e, axis=0, keepdims=True)
+
+        inv = 1.0 / lax.fori_loop(0, qb + 1, expo, jnp.zeros((1, lanes), F32))
+
+        def weigh(kb, acc):
+            ks = pl.ds(pl.multiple_of(kb * KB, KB), KB)
+            p = (s_scr[ks, :] * inv).astype(BF16)
+            return acc + mm(v_ref[ks, :], p, TN)
+
+        acc = lax.fori_loop(0, qb + 1, weigh, jnp.zeros((hd, lanes), F32))
+        for h in range(heads):
+            o_ref[h * hd:(h + 1) * hd, qs] = acc[:, h * QB:(h + 1) * QB].astype(BF16)
+        stat_ref[qb, 0:1, :] = top
+        stat_ref[qb, 1:2, :] = inv
+        return carry
+
+    lax.fori_loop(0, seq // QB, q_block, 0)
+
+
+def attn_bwd_kernel(q_ref, k_ref, v_ref, do_ref, stat_ref, dq_ref, dk_ref, dv_ref, p_scr, dp_scr, dk_acc, dv_acc):
+    heads, seq, hd = q_ref.shape
+    scale = hd ** -0.5
+    lanes = heads * QB
+    dk_acc[...] = jnp.zeros_like(dk_acc)
+    dv_acc[...] = jnp.zeros_like(dv_acc)
+
+    def q_block(qb, carry):
+        qs = pl.ds(pl.multiple_of(qb * QB, QB), QB)
+        q2 = jnp.concatenate([q_ref[h, qs, :] for h in range(heads)], axis=0)
+        do2 = jnp.concatenate([do_ref[h, qs, :] for h in range(heads)], axis=0)
+        top = stat_ref[qb, 0:1, :]
+        inv = stat_ref[qb, 1:2, :]
+
+        def probs(kb, rd, diagonal):
+            ks = pl.ds(pl.multiple_of(kb * KB, KB), KB)
+            s = mm(k_ref[ks, :], q2, NT) * scale
+            if diagonal:
+                key = lax.broadcasted_iota(jnp.int32, (KB, lanes), 0)
+                qry = lax.broadcasted_iota(jnp.int32, (KB, lanes), 1) % QB
+                s = jnp.where(qry >= key, s, NEG_LARGE)
+            p = jnp.exp(s - top) * inv
+            dp = mm(v_ref[ks, :], do2, NT).astype(BF16)
+            p_scr[ks, :] = p
+            dp_scr[ks, :] = dp
+            dv_acc[ks, :] += mm(p.astype(BF16), do2, NN)
+            return rd + jnp.sum(dp.astype(F32) * p, axis=0, keepdims=True)
+
+        rd = lax.fori_loop(0, qb, lambda kb, r: probs(kb, r, False), jnp.zeros((1, lanes), F32))
+        rd = probs(qb, rd, True)
+
+        def scores(kb, acc):
+            ks = pl.ds(pl.multiple_of(kb * KB, KB), KB)
+            ds = (p_scr[ks, :] * (dp_scr[ks, :].astype(F32) - rd) * scale).astype(BF16)
+            dk_acc[ks, :] += mm(ds, q2, NN)
+            return acc + mm(k_ref[ks, :], ds, TN)
+
+        acc = lax.fori_loop(0, qb + 1, scores, jnp.zeros((hd, lanes), F32))
+        for h in range(heads):
+            dq_ref[h * hd:(h + 1) * hd, qs] = acc[:, h * QB:(h + 1) * QB].astype(BF16)
+        return carry
+
+    lax.fori_loop(0, seq // QB, q_block, 0)
+    dk_ref[...] = dk_acc[...].astype(BF16)
+    dv_ref[...] = dv_acc[...].astype(BF16)
+
+
+VMEM_CAP = 60 * 1024 * 1024
+
+
+def in_vmem(n):
+    return [pl.BlockSpec(memory_space=pltpu.VMEM)] * n
+
+
+def attention_forward(q2, k, v):
+    heads, seq, hd = q2.shape
+    lanes = heads * QB
+    return pl.pallas_call(
+        attn_fwd_kernel,
+        out_shape=(jax.ShapeDtypeStruct((heads * hd, seq), BF16), jax.ShapeDtypeStruct((seq // QB, 2, lanes), F32)),
+        in_specs=in_vmem(3), out_specs=tuple(in_vmem(2)),
+        scratch_shapes=[pltpu.VMEM((seq, lanes), F32)],
+        cost_estimate=pl.CostEstimate(flops=2 * 4 * heads * seq * seq * hd, bytes_accessed=4 * seq * hd * 8, transcendentals=0),
+        compiler_params=pltpu.CompilerParams(vmem_limit_bytes=VMEM_CAP),
+        name='attn_fwd',
+    )(q2, k, v)
+
+
+def attention_backward(q2, k, v, do2, stat):
+    heads, seq, hd = q2.shape
+    lanes = heads * QB
+    return pl.pallas_call(
+        attn_bwd_kernel,
+        out_shape=(jax.ShapeDtypeStruct((heads * hd, seq), BF16), jax.ShapeDtypeStruct((seq, hd), BF16), jax.ShapeDtypeStruct((seq, hd), BF16)),
+        in_specs=in_vmem(5), out_specs=tuple(in_vmem(3)),
+        scratch_shapes=[pltpu.VMEM((seq, lanes), F32), pltpu.VMEM((seq, lanes), BF16), pltpu.VMEM((seq, hd), F32), pltpu.VMEM((seq, hd), F32)],
+        cost_estimate=pl.CostEstimate(flops=2 * 10 * heads * seq * seq * hd, bytes_accessed=4 * seq * hd * 8, transcendentals=0),
+        compiler_params=pltpu.CompilerParams(vmem_limit_bytes=VMEM_CAP),
+        name='attn_bwd',
+    )(q2, k, v, do2, stat)
+
+
+RS_ORDERS = ((2, 4, 8), (4, 8, 2), (8, 2, 4))
+RS_MASKS = (14, 6, 12, 10, 2, 4, 8, 0)
+RS_FIRST = ((14, 6, 10, 2), (14, 12, 6, 4), (14, 10, 12, 8))
+
+
+def first_axis(colour, mask):
+    return next(i for i, a in enumerate(RS_ORDERS[colour]) if mask & a)
+
+
+def rs_slots(colour):
+    slots = {}
+    for mask in RS_MASKS:
+        for axis in RS_ORDERS[colour][:first_axis(colour, mask) if mask else 3]:
+            slots[mask, axis] = len(slots)
+    return slots
+
+
+def flipped(index, mask):
+    out = index
+    for bit in (1, 2, 4, 8):
+        if mask & bit:
+            out = out + (1 - 2 * ((index // bit) % 2)) * bit
+    return out
+
+
+def enter(peers):
+    barrier = pltpu.get_barrier_semaphore()
+    for peer in peers:
+        pl.semaphore_signal(barrier, inc=1, device_id=(peer,), device_id_type=pl.DeviceIdType.MESH)
+    pl.semaphore_wait(barrier, len(peers))
+
+
+def rs_kernel(cols, a_ref, w_ref, base_ref, out_ref, part, pair_in, link_in, pair_send, pair_recv, link_send, link_recv):
+    tokens, dim = out_ref.shape
+    me = lax.axis_index('sp')
+    core = me % 2
+    partner = flipped(me, 1)
+    enter([partner] + [flipped(me, a) for a in (2, 4, 8)])
+
+    def pair_copy(i):
+        return pltpu.make_async_remote_copy(
+            src_ref=part.at[i, 1 - core], dst_ref=pair_in.at[i], send_sem=pair_send.at[i], recv_sem=pair_recv.at[i],
+            device_id=(partner,), device_id_type=pl.DeviceIdType.MESH)
+
+    def link_copy(colour, mask):
+        axis = RS_ORDERS[colour][first_axis(colour, mask)]
+        slot = rs_slots(colour)[mask - axis, axis]
+        lo, n = cols[colour]
+        return pltpu.make_async_remote_copy(
+            src_ref=part.at[RS_MASKS.index(mask), core, :, pl.ds(lo, n)], dst_ref=link_in.at[slot, :, pl.ds(lo, n)],
+            send_sem=link_send.at[colour, RS_MASKS.index(mask)], recv_sem=link_recv.at[colour, slot],
+            device_id=(flipped(me, axis),), device_id_type=pl.DeviceIdType.MESH)
+
+    rows = 16
+
+    def add(i, colour, slot):
+        lo, n = cols[colour]
+
+        def step(r, c):
+            rs = pl.ds(pl.multiple_of(r * rows, rows), rows)
+            part[i, core, rs, pl.ds(lo, n)] += link_in[slot, rs, pl.ds(lo, n)]
+            return c
+        lax.fori_loop(0, tokens // rows, step, 0)
+
+    width = 512
+
+    def compute(i):
+        start = pl.multiple_of((flipped(me, RS_MASKS[i]) // 2) * (2 * tokens), 2 * tokens)
+        a = a_ref[:, pl.ds(start, 2 * tokens)]
+
+        def step(n, c):
+            cs = pl.ds(pl.multiple_of(n * width, width), width)
+            r = mm(a, w_ref[:, cs], TN)
+            part[i, 0, :, cs] = r[:tokens]
+            part[i, 1, :, cs] = r[tokens:]
+            return c
+        lax.fori_loop(0, dim // width, step, 0)
+        pair_copy(i).start()
+
+    ready = set()
+    sent = [0, 0, 0]
+
+    def finish_pair(i):
+        pair_copy(i).wait_recv()
+
+        def step(r, c):
+            rs = pl.ds(pl.multiple_of(r * rows, rows), rows)
+            part[i, core, rs, :] += pair_in[i, rs, :]
+            return c
+        lax.fori_loop(0, tokens // rows, step, 0)
+        ready.add(RS_MASKS[i])
+        for colour in range(3):
+            todo = RS_FIRST[colour]
+            while sent[colour] < 4 and todo[sent[colour]] in ready:
+                link_copy(colour, todo[sent[colour]]).start()
+                sent[colour] += 1
+
+    for i in range(8):
+        compute(i)
+        if i:
+            finish_pair(i - 1)
+    finish_pair(7)
+
+    def take(colour, mask, axis):
+        link_copy(colour, mask + axis).wait_recv()
+        add(RS_MASKS.index(mask), colour, rs_slots(colour)[mask, axis])
+
+    for step in range(2):
+        for colour in range(3):
+            o = RS_ORDERS[colour]
+            mask = (o[1] + o[2], o[1])[step]
+            take(colour, mask, o[0])
+            link_copy(colour, mask).start()
+    for colour in range(3):
+        o = RS_ORDERS[colour]
+        take(colour, o[2], o[0])
+        take(colour, o[2], o[1])
+        link_copy(colour, o[2]).start()
+    for colour in range(3):
+        o = RS_ORDERS[colour]
+        for axis in o:
+            take(colour, 0, axis)
+    out_ref[...] = (base_ref[...].astype(F32) + part[7, core]).astype(out_ref.dtype)
+    for i in range(8):
+        pair_copy(i).wait_send()
+    for colour in range(3):
+        for mask in RS_MASKS[:7]:
+            link_copy(colour, mask).wait_send()
+
+
+def product_scatter(a, w, base, ident):
+    feat, seq = a.shape
+    tokens, dim = base.shape
+    unit = 128
+    n = dim // unit
+    wide = (n + 2) // 3
+    cols = ((0, wide * unit), (wide * unit, (n - wide) // 2 * unit), ((wide + (n - wide) // 2) * unit, (n - wide - (n - wide) // 2) * unit))
+    return pl.pallas_call(
+        functools.partial(rs_kernel, cols),
+        out_shape=jax.ShapeDtypeStruct((tokens, dim), BF16),
+        in_specs=in_vmem(3), out_specs=in_vmem(1)[0],
+        scratch_shapes=[
+            pltpu.VMEM((8, 2, tokens, dim), F32), pltpu.VMEM((8, tokens, dim), F32), pltpu.VMEM((7, tokens, dim), F32),
+            pltpu.SemaphoreType.DMA((8,)), pltpu.SemaphoreType.DMA((8,)), pltpu.SemaphoreType.DMA((3, 8)), pltpu.SemaphoreType.DMA((3, 7))],
+        cost_estimate=pl.CostEstimate(flops=2 * seq * feat * dim, bytes_accessed=2 * (a.size + w.size), transcendentals=0),
+        compiler_params=pltpu.CompilerParams(collective_id=ident, has_side_effects=True, vmem_limit_bytes=VMEM_CAP),
+        name=f'product_scatter_{ident}',
+    )(a, w, base)
 
 
 def solution(mesh):
     n_dev = mesh.shape['sp']
     gather = functools.partial(lax.all_gather, axis_name='sp', axis=0, tiled=True)
-    scatter = functools.partial(lax.psum_scatter, axis_name='sp', scatter_dimension=0, tiled=True)
     swap = functools.partial(lax.all_to_all, axis_name='sp', split_axis=0, concat_axis=0, tiled=True)
 
     def layer_step(x_in, positions, d_out, norm1_gain, norm2_gain, w_q, w_k, w_v, w_o, w_gate, w_up, w_down):
@@ -104,12 +372,11 @@
             jnp.repeat(k_rot.transpose(1, 0, 2), rep, axis=0),
             jnp.repeat(v_lin.transpose(1, 0, 2), rep, axis=0)], axis=2)
         seq = swap(send).reshape(seq_len, qw + 2 * kw)
-        q_seq = seq[:, :qw].reshape(seq_len, hpd, hd)
+        q_seq = seq[:, :qw].reshape(seq_len, hpd, hd).transpose(1, 0, 2)
         k_seq = seq[:, qw:qw + kw]
         v_seq = seq[:, qw + kw:]
-        attn_seq, attn_probs = attention_forward(q_seq, k_seq, v_seq)
-        attn_seq = attn_seq.reshape(seq_len, qw)
-        attn_tok = swap(attn_seq.reshape(n_dev, tokens, qw)).transpose(1, 0, 2).reshape(tokens, n_q * hd)
+        attn_t, stat = attention_forward(q_seq, k_seq, v_seq)
+        attn_tok = swap(attn_t.reshape(qw, n_dev, tokens).transpose(1, 2, 0)).transpose(1, 0, 2).reshape(tokens, n_q * hd)
         attn_proj = jnp.dot(attn_tok, wo_full, preferred_element_type=F32)
         hidden = (x_f32 + attn_proj).astype(BF16)
         hidden_f32 = hidden.astype(F32)
@@ -123,15 +390,13 @@
         gate_act, up_act = gu[:feat], gu[feat:]
         glu_pre, glu_pull = jax.vjp(gated_unit, gate_act.astype(F32), up_act.astype(F32))
         glu = glu_pre.astype(BF16)
-        y_part = jnp.einsum('ft,fd->td', glu, w_down, preferred_element_type=F32)
-        y_out = (hidden_f32 + scatter(y_part)).astype(BF16)
+        y_out = product_scatter(glu, w_down, hidden, 0)
 
         d_down = jnp.einsum('ft,td->fd', glu, do_full, preferred_element_type=F32)
         d_glu = jnp.einsum('fd,td->ft', w_down, do_full, preferred_element_type=F32).astype(BF16)
         d_gate_f, d_up_f = glu_pull(d_glu.astype(F32))
         dgu = jnp.concatenate([d_gate_f.astype(BF16), d_up_f.astype(BF16)], axis=0)
-        dm_part = jnp.einsum('ft,fd->td', dgu, wgu, preferred_element_type=F32)
-        d_mlp_in = scatter(dm_part).astype(BF16)
+        d_mlp_in = product_scatter(dgu, wgu, jnp.zeros_like(hidden), 1)
         d_hidden_norm, d_g2 = norm2_pull(d_mlp_in.astype(F32))
         d_hidden = (d_out.astype(F32) + d_hidden_norm).astype(BF16)
         dh_full = gather(d_hidden)
@@ -141,9 +406,10 @@
         d_gate = dwgu[:, :feat].reshape(n_dev * feat, rows).T
         d_up = dwgu[:, feat:].reshape(n_dev * feat, rows).T
 
-        d_wo = jnp.einsum('te,td->ed', attn_seq, dh_full, preferred_element_type=F32).reshape(w_o.shape)
+        d_wo = jnp.einsum('et,td->ed', attn_t, dh_full, preferred_element_type=F32).reshape(w_o.shape)
         d_attn = jnp.einsum('td,ed->te', dh_full, wo_own, preferred_element_type=F32).astype(BF16)
-        d_q_seq, d_k_seq, d_v_seq = attention_backward(q_seq, k_seq, v_seq, attn_probs, d_attn.reshape(seq_len, hpd, hd))
+        d_q_t, d_k_seq, d_v_seq = attention_backward(q_seq, k_seq, v_seq, d_attn.reshape(seq_len, hpd, hd).transpose(1, 0, 2), stat)
+        d_q_seq = d_q_t.reshape(hpd, hd, seq_len).transpose(2, 0, 1)
         dq_lin_seq = rotate(d_q_seq, cos_all, -sin_all).astype(BF16).reshape(seq_len, qw)
         back = swap(jnp.concatenate([dq_lin_seq, d_k_seq, d_v_seq], axis=1).reshape(n_dev, tokens, qw + 2 * kw))
         d_q_lin = back[:, :, :qw].transpose(1, 0, 2).reshape(tokens, n_q * hd)

time: 991 us -> 680 us (0.69)
  waiting for transfers between devices: 607 us -> 191 us
  Pallas kernels: 0 us -> 227 us
  matrix products: 213 us -> 74 us
  blocking collectives: 59.8 us -> 79.2 us
    reduce_scatter x2 -> x0, waiting for transfers between devices: 342 us -> none  [the longest x1 176 us: layer_step(): y_out = (hidden_f32 + scatter(y_part)).astype(BF16)]
    pallas_call x0 -> x4, Pallas kernels: none -> 227 us  [the longest x2 179 us: product_scatter(): pl.pallas_call(functools.partial(rs_kernel, cols), out_shape=jax.ShapeDty...]
    dot_general x8 -> x1, matrix products: 127 us -> 5.73 us  [layer_step(): jnp.einsum('et,td->ed', attn_t, dh_full, preferred_element_type=F32)]
    all_to_all x1, waiting for transfers between devices: 56.9 us -> 0.01 us  [layer_step(): dwgu = swap(dwgu.reshape(2 * feat, n_dev, rows).transpose(1, 0, 2))]
    all_to_all x0 -> x1, blocking collectives: none -> 19.3 us  [layer_step(): seq = swap(send).reshape(seq_len, qw + 2 * kw)]
    all_to_all x2 -> x1, waiting for transfers between devices: 29.4 us -> 10.3 us  [layer_step(): swap(attn_t.reshape(qw, n_dev, tokens).transpose(1, 2, 0))]
    sub x1 -> x0, matrix products: 18.4 us -> none  [attention_forward(): attn_probs = jax.nn.softmax(jnp.where(causal, scores, NEG_LARGE), axis=-1)]
  transfers between devices with their start and end apart: 14 -> 11, of which waited for: 11 -> 7; matrix products, arithmetic and copies ran while one was open for 25% -> 17% of each run, Pallas kernels for 0% -> 24%
where the time goes in v2:
time: 680 us; the launch traced here: 673 us
  Pallas kernels  227 us (33%)
  waiting for transfers between devices  191 us (28%)
  blocking collectives  79.2 us (12%)
  matrix products  74 us (11%)
  local copies, waits for them, and re-layouts  53.8 us (8%)
  other arithmetic  18.3 us (3%)
  between operations  15.2 us (2%)
  starting transfers between devices  13.8 us (2%)
    pallas_call x2, Pallas kernels, product_scatter(): pl.pallas_call(functools.partial(rs_kernel, cols), out_shape=jax.ShapeDty...  179 us
    all_gather x1, waiting for transfers between devices, layer_step(): gather(jnp.concatenate([w_q.reshape(rows, n_q * hd), w_k.reshape(rows, n_...  60.8 us
    all_gather x1, waiting for transfers between devices, layer_step(): dh_full = gather(d_hidden)  46.3 us
    all_to_all x1, blocking collectives, layer_step(): wgu = swap(jnp.concatenate([by_feature(w_gate), by_feature(w_up)], axis=1))  45.3 us
    all_gather x1, waiting for transfers between devices, layer_step(): do_full = gather(d_out)  40.2 us
    pallas_call x1, Pallas kernels, attention_backward(): pl.pallas_call(attn_bwd_kernel, out_shape=(jax.ShapeDtypeStruct((heads *...  26.8 us
    pallas_call x1, Pallas kernels, attention_forward(): pl.pallas_call(attn_fwd_kernel, out_shape=(jax.ShapeDtypeStruct((heads *...  21 us
    all_to_all x1, blocking collectives, layer_step(): seq = swap(send).reshape(seq_len, qw + 2 * kw)  19.3 us
  transfers between devices with their start and end apart: 11, of which 7 were waited for; matrix products, arithmetic and copies ran while one was open for 17% of the time, Pallas kernels for 24%

profile of v2, /device:TPU:0, one launch (start us, length us, event | category | flops | bytes accessed | tf_op | source)
XLA Modules:
  0.0 672.9 jit_solution(16229762313850319084)
XLA Ops:
  7.2 2.0 pad_maximum_fusion.5
  9.3 0.7 all-gather.12.cloned.1.call-update
  10.7 0.7 bitcast_convert_fusion
  11.4 14.5 %all-gather.1 = f32[16,3,128]{2,1,0:T(4,128)S(1)} all-gather(f32[1,3,128]{2,1,0:T(4,128)S(1)} %maximum_bitcast_fusion.1), channel_id=2, replica_groups=mesh['sp'=16] {'sp'}, dimensions={0}, use_global_device_ids=true | all-gather | bytes 26112 | tf_op jit(solution)/shard_map/all_gather | solution.py:346
  26.5 60.8 %all-gather.10.cloned.1.call-done = bf16[2048,2560]{0,1:T(8,128)(2,1)} async-done(((bf16[128,2560]{0,1:T(8,128)(2,1)}), bf16[2048,2560]{0,1:T(8,128)(2,1)}) %all-gather.10.cloned.1.call-update) | async-done | bytes 10485776 | tf_op jit(solution)/shard_map/all_gather | solution.py:353
  87.3 7.5 %convolution_convert_fusion = bf16[128,2560]{1,0:T(8,128)(2,1)S(1)} fusion(bf16[128,2048]{1,0:T(8,128)(2,1)S(1)} %fusion.14, bf16[2048,2560]{0,1:T(8,128)(2,1)} %all-gather.10.cloned.1.call-done), kind=kOutput, calls=%fused_computation.5 | convolution fusion | flops 1342504960 | bytes 11665408 | tf_op jit(solution)/shard_map/dot_general | solution.py:365
  96.1 19.3 %all_to_all.30 = bf16[16,128,256]{1,2,0:T(8,128)(2,1)S(1)} all-to-all(bf16[16,128,256]{1,2,0:T(8,128)(2,1)S(1)} %pad_maximum_fusion.3), channel_id=1, replica_groups=mesh['sp'=16] {'sp'}, dimensions={0} | all-to-all | bytes 2097152 | tf_op jit(solution)/shard_map/all_to_all | solution.py:374
  116.2 1.3 copy.90
  117.5 1.2 fusion.55
  118.7 21.0 %attn_fwd.1 = (bf16[128,2048]{1,0:T(8,128)(2,1)}, f32[8,2,512]{2,1,0:T(2,128)}) custom-call(bf16[2,2048,64]{2,1,0:T(8,128)(2,1)} %bitcast.155, bf16[2048,64]{1,0:T(8,128)(2,1)} %get-tuple-element.79.k_ref, bf16[2048,64]{1,0:T(8,128)(2,1)} %get-tuple-element.78.v_ref), custom_call_target="tpu_custom_call" | custom-call | flops 4294967296 | bytes 4194304 | tf_op jit(solution)/shard_map/attn_fwd/pallas_call | solution.py:154
  139.7 2.0 bitcast_bitcast_fusion.1
  141.7 2.3 all-to-all-start.2
  144.1 10.3 %all-to-all-done.2 = bf16[16,128,128]{1,2,0:T(8,128)(2,1)S(1)} async-done(((bf16[16,128,128]{1,2,0:T(8,128)(2,1)}), bf16[16,128,128]{1,2,0:T(8,128)(2,1)S(1)}, u32[]{:S(2)}, u32[]{:S(2)}) %all-to-all-start.2) | async-done | bytes 524320 | tf_op jit(solution)/shard_map/all_to_all | solution.py:379
  154.4 4.8 fusion.22
  159.2 1.0 fusion.16
  160.8 1.8 copy.80
  162.6 2.5 copy.79
  165.2 1.6 pad_maximum_fusion
  166.8 45.3 %all_to_all.31 = bf16[16,704,128]{2,1,0:T(8,128)(2,1)S(1)} all-to-all(bf16[16,704,128]{2,1,0:T(8,128)(2,1)S(1)} %pad_maximum_fusion), channel_id=1, replica_groups=mesh['sp'=16] {'sp'}, dimensions={0} | all-to-all | bytes 5767168 | tf_op jit(solution)/shard_map/all_to_all | solution.py:359
  212.1 1.6 copy-done.1
  213.7 2.0 copy_bitcast_fusion.w_ref
  215.7 14.8 %all-gather.14.cloned.1.call-done = bf16[2048,2048]{1,0:T(8,128)(2,1)} async-done(((bf16[128,2048]{1,0:T(8,128)(2,1)}), bf16[2048,2048]{1,0:T(8,128)(2,1)}) %all-gather.14.cloned.1.call-update) | async-done | bytes 8388624 | tf_op jit(solution)/shard_map/all_gather | solution.py:386
  230.6 10.6 %convolution_convert_fusion.1 = bf16[704,2048]{1,0:T(8,128)(2,1)} fusion(bf16[2048,2048]{1,0:T(8,128)(2,1)} %all-gather.14.cloned.1.call-done, bf16[16,704,128]{2,1,0:T(8,128)(2,1)} %copy-done.1), kind=kOutput, calls=%fused_computation.9 | convolution fusion | flops 5907021824 | bytes 14155776 | tf_op jit(solution)/shard_map/fd,td->ft/dot_general | solution.py:389
  241.1 40.2 %all-gather.16.cloned.1.call-done = bf16[2048,2048]{1,0:T(8,128)(2,1)} async-done(((bf16[128,2048]{1,0:T(8,128)(2,1)}), bf16[2048,2048]{1,0:T(8,128)(2,1)}) %all-gather.16.cloned.1.call-update) | async-done | bytes 8388624 | tf_op jit(solution)/shard_map/all_gather | solution.py:387
  281.3 10.2 %fusion.7 = (bf16[352,2048]{1,0:T(8,128)(2,1)S(1)}, bf16[352,2048]{1,0:T(8,128)(2,1)S(1)}, bf16[352,2048]{1,0:T(8,128)(2,1)}) fusion(bf16[704,2048]{1,0:T(8,128)(2,1)} %convolution_convert_fusion.1, bf16[352,2048]{1,0:T(8,128)(2,1)} %w_ref.1, bf16[2048,2048]{1,0:T(8,128)(2,1)} %all-gather.16.cloned.1.call-done), kind=kOutput, calls=%fused_computation.17 | convolution fusion | flops 2967207936 | bytes 17039360 | tf_op jit(solution)/shard_map/fd,td->ft/dot_general | solution.py:396
  291.5 2.0 pad_maximum_fusion.1.a_ref
  294.0 0.8 broadcast_in_dim.30.base_ref
  294.9 67.5 %product_scatter_1.1 = bf16[128,2048]{1,0:T(8,128)(2,1)} custom-call(bf16[704,2048]{1,0:T(8,128)(2,1)} %pad_maximum_fusion.1.a_ref, bf16[704,2048]{1,0:T(8,128)(2,1)} %copy_bitcast_fusion.w_ref, bf16[128,2048]{1,0:T(8,128)(2,1)} %broadcast_in_dim.30.base_ref), custom_call_target="tpu_custom_call" | custom-call | flops 5905580032 | bytes 5767168 | tf_op jit(solution)/shard_map/product_scatter_1/pallas_call | solution.py:316
  362.4 1.7 fusion.17
  364.1 2.2 fusion.19
  366.9 1.0 multiply_cosine_fusion
  367.9 46.3 %all-gather.18.cloned.1.call-done = bf16[2048,2048]{1,0:T(8,128)(2,1)} async-done(((bf16[128,2048]{1,0:T(8,128)(2,1)}), bf16[2048,2048]{1,0:T(8,128)(2,1)}) %all-gather.18.cloned.1.call-update) | async-done | bytes 8388624 | tf_op jit(solution)/shard_map/all_gather | solution.py:402
  414.2 6.3 convolution_convert_fusion.3
  420.5 1.3 copy.92
  421.8 26.8 %attn_bwd.1 = (bf16[128,2048]{1,0:T(8,128)(2,1)}, bf16[2048,64]{1,0:T(8,128)(2,1)}, bf16[2048,64]{1,0:T(8,128)(2,1)}) custom-call(bf16[2,2048,64]{2,1,0:T(8,128)(2,1)} %bitcast.156, bf16[2048,64]{1,0:T(8,128)(2,1)} %get-tuple-element.79.k_ref, bf16[2048,64]{1,0:T(8,128)(2,1)} %get-tuple-element.78.v_ref, bf16[2,2048,64]{2,1,0:T(8,128)(2,1)} %bitcast.157, ...), custom_call_target="tpu_custom_call" | custom-call | flops 10737418240 | bytes 4194304 | tf_op jit(solution)/shard_map/attn_bwd/pallas_call | solution.py:168
  448.6 1.3 copy.94
  450.0 1.3 copy.93
  451.3 1.2 fusion.35
  452.8 1.2 copy.95
  454.0 2.5 all-to-all-start.3
  456.5 9.4 %convolution_bitcast_fusion = f32[88,16,8,128]{3,2,1,0:T(8,128)S(1)} fusion(bf16[2048,2048]{1,0:T(8,128)(2,1)} %all-gather.14.cloned.1.call-done, bf16[352,2048]{1,0:T(8,128)(2,1)} %copy-done.10, bf16[352,2048]{1,0:T(8,128)(2,1)} %copy-done.9), kind=kOutput, calls=%fused_computation.22 | convolution fusion | flops 5911347200 | bytes 17039360 | tf_op jit(solution)/shard_map/ft,td->fd/dot_general | solution.py:404
  465.9 3.0 copy.129
  468.9 7.3 %all-to-all-done.3 = bf16[16,128,256]{1,2,0:T(8,128)(2,1)S(1)} async-done(((bf16[16,128,256]{1,2,0:T(8,128)(2,1)}), bf16[16,128,256]{1,2,0:T(8,128)(2,1)S(1)}, u32[]{:S(2)}, u32[]{:S(2)}) %all-to-all-start.3) | async-done | bytes 1048608 | tf_op jit(solution)/shard_map/all_to_all | solution.py:414
  476.2 3.4 all-to-all-start.5
  479.9 12.4 %copy.108 = bf16[2048,2048]{1,0:T(8,128)(2,1)} copy(bf16[2048,2048]{0,1:T(8,128)(2,1)} %bitcast.140) | data formatting | bytes 16777216 | tf_op jit(solution)/shard_map/td,te->de/dot_general | solution.py:426
  492.3 8.5 %fusion.64 = f32[352,2048]{1,0:T(8,128)} fusion(bf16[352,2048]{1,0:T(8,128)(2,1)} %get-tuple-element.73.a_ref, bf16[2048,2048]{1,0:T(8,128)(2,1)} %all-gather.16.cloned.1.call-done), kind=kOutput, calls=%fused_computation.141 | convolution fusion | flops 2952790016 | bytes 12713984 | tf_op jit(solution)/shard_map/ft,td->fd/dot_general | solution.py:395
  500.9 0.9 fusion.54
  502.1 0.7 pad_maximum_fusion.7
  502.8 111.9 %product_scatter_0.1 = bf16[128,2048]{1,0:T(8,128)(2,1)} custom-call(bf16[352,2048]{1,0:T(8,128)(2,1)} %get-tuple-element.73.a_ref, bf16[352,2048]{1,0:T(8,128)(2,1)} %w_ref.1, bf16[128,2048]{1,0:T(8,128)(2,1)} %copy-done.2), custom_call_target="tpu_custom_call" | custom-call | flops 2952790016 | bytes 2883584 | tf_op jit(solution)/shard_map/product_scatter_0/pallas_call | solution.py:316
  614.7 5.6 fusion.53
  620.4 3.4 copy.105
  623.7 3.5 copy.106
  627.3 5.9 fusion.62
  633.2 2.6 fusion.15
  635.8 1.1 pad_maximum_fusion.2
  636.9 5.0 all-to-all-start.4
  641.9 5.7 fusion.63
  647.6 1.2 fusion.21
  648.8 9.8 %all-to-all-done.4 = f32[16,136,128]{2,1,0:T(8,128)S(1)} async-done(((f32[16,136,128]{2,1,0:T(8,128)}), f32[16,136,128]{2,1,0:T(8,128)S(1)}, u32[]{:S(2)}, u32[]{:S(2)}) %all-to-all-start.4) | async-done | bytes 1114144 | tf_op jit(solution)/shard_map/all_to_all | solution.py:431
  658.7 1.3 copy.101
  660.6 2.6 fusion.37
  663.2 0.8 copy.102
  664.0 0.8 copy.103
  664.7 0.8 copy.133
  (93 shorter events, 6.7 us)
Async XLA Ops:
  7.2 18.8 %copy-start = (bf16[128,2048]{1,0:T(8,128)(2,1)S(1)}, bf16[128,2048]{1,0:T(8,128)(2,1)}, u32[]{:S(2)}) copy-start(bf16[128,2048]{1,0:T(8,128)(2,1)} %param.12) | copy-start | bytes 1572868
  7.2 80.2 %all-gather.10.cloned.1.call-start = ((), (), s32[]{:S(2)}) async-start(), calls=%async_computation.6 | async-start | bytes 11141120 | tf_op jit(solution)/shard_map/all_gather | solution.py:353
  9.3 134.8 %all-gather.12.cloned.1.call-start = ((), (), s32[]{:S(2)}) async-start(), calls=%async_computation.7 | async-start | bytes 8912896 | tf_op jit(solution)/shard_map/all_gather | solution.py:355
  26.5 68.4 %copy-start.3 = (bf16[128,2048]{1,0:T(8,128)(2,1)}, bf16[128,2048]{1,0:T(8,128)(2,1)S(1)}, u32[]{:S(2)}) copy-start(bf16[128,2048]{1,0:T(8,128)(2,1)S(1)} %fusion.14) | copy-start | bytes 1572868
  141.7 12.7 %all-to-all-start.2 = ((bf16[16,128,128]{1,2,0:T(8,128)(2,1)}), bf16[16,128,128]{1,2,0:T(8,128)(2,1)S(1)}, u32[]{:S(2)}, u32[]{:S(2)}) async-start(bf16[16,128,128]{1,2,0:T(8,128)(2,1)} %bitcast_bitcast_fusion.1), calls=%async_computation.2 | async-start | bytes 1048576 | tf_op jit(solution)/shard_map/all_to_all | solution.py:379
  144.0 86.5 %all-gather.14.cloned.1.call-start = ((), (), s32[]{:S(2)}) async-start(), calls=%async_computation.8 | async-start | bytes 8912896 | tf_op jit(solution)/shard_map/all_gather | solution.py:386
  159.2 204.9 %copy-start.2 = (bf16[128,2048]{1,0:T(8,128)(2,1)}, bf16[128,2048]{1,0:T(8,128)(2,1)S(1)}, u32[]{:S(2)}) copy-start(bf16[128,2048]{1,0:T(8,128)(2,1)S(1)} %get-tuple-element.107.base_ref) | copy-start | bytes 1572868
  160.2 121.2 %all-gather.16.cloned.1.call-start = ((), (), s32[]{:S(2)}) async-start(), calls=%async_computation.9 | async-start | bytes 8912896 | tf_op jit(solution)/shard_map/all_gather | solution.py:387
  160.8 253.5 %all-gather.18.cloned.1.call-start = ((), (), s32[]{:S(2)}) async-start(), calls=%async_computation.10 | async-start | bytes 8912896 | tf_op jit(solution)/shard_map/all_gather | solution.py:402
  212.1 1.6 copy-start.1
  291.5 2.0 copy-start.9
  291.5 2.5 copy-start.10
  294.9 69.2 %copy-start.8 = (bf16[128,2048]{1,0:T(8,128)(2,1)S(1)}, bf16[128,2048]{1,0:T(8,128)(2,1)}, u32[]{:S(2)}) copy-start(bf16[128,2048]{1,0:T(8,128)(2,1)} %param.14) | copy-start | bytes 1572868
  362.4 51.9 %copy-start.11 = (bf16[2,64,2048]{2,1,0:T(8,128)(2,1)S(1)}, bf16[2,64,2048]{2,1,0:T(8,128)(2,1)}, u32[]{:S(2)}) copy-start(bf16[2,64,2048]{2,1,0:T(8,128)(2,1)} %param.20) | copy-start | bytes 1572868
  366.3 113.6 %all-gather.20.cloned.1.call-start = ((), (), s32[]{:S(2)}) async-start(), calls=%async_computation.11 | async-start | bytes 8912896 | tf_op jit(solution)/shard_map/all_gather | solution.py:388
  454.0 22.2 %all-to-all-start.3 = ((bf16[16,128,256]{1,2,0:T(8,128)(2,1)}), bf16[16,128,256]{1,2,0:T(8,128)(2,1)S(1)}, u32[]{:S(2)}, u32[]{:S(2)}) async-start(bf16[16,128,256]{1,2,0:T(8,128)(2,1)} %copy.95), calls=%async_computation.3 | async-start | bytes 2097152 | tf_op jit(solution)/shard_map/all_to_all | solution.py:414
  476.2 138.5 %all-to-all-start.5 = ((f32[16,704,128]{2,1,0:T(8,128)}), f32[16,704,128]{2,1,0:T(8,128)}, u32[]{:S(2)}, u32[]{:S(2)}) async-start(f32[16,704,128]{2,1,0:T(8,128)} %bitcast.137), calls=%async_computation.5 | async-start | bytes 11534336 | tf_op jit(solution)/shard_map/all_to_all | solution.py:405
  479.6 181.0 %all-gather.22.cloned.1.call-start = ((), (), s32[]{:S(2)}) async-start(), calls=%async_computation.12 | async-start | bytes 2228224 | tf_op jit(solution)/shard_map/all_gather | solution.py:421
  623.7 9.4 %slice-start = ((s8[10485760]{0:T(1024)(128)(4,1)}), s8[2097152]{0:T(1024)(128)(4,1)S(1)}, s32[]{:S(2)}) async-start(s8[10485760]{0:T(1024)(128)(4,1)} %bitcast.135), calls=%async_computation.13 | async-start | bytes 4194304
  627.3 5.9 slice-start.1
  627.3 5.9 slice-start.2
  627.3 5.9 copy-start.7
  635.8 6.1 copy-start.6
  636.9 21.8 %all-to-all-start.4 = ((f32[16,136,128]{2,1,0:T(8,128)}), f32[16,136,128]{2,1,0:T(8,128)S(1)}, u32[]{:S(2)}, u32[]{:S(2)}) async-start(f32[16,136,128]{2,1,0:T(8,128)} %pad_maximum_fusion.2), calls=%async_computation.4 | async-start | bytes 2228224 | tf_op jit(solution)/shard_map/all_to_all | solution.py:431
  641.8 5.8 copy-start.4
  641.8 5.8 copy-start.5
  658.7 6.0 copy-start.12
Sparse Core Ops, SparseCore 0:
  10.8 76.5 all-gather.9
  89.6 54.3 all-gather.11
  160.3 70.2 all-gather.13
  232.7 48.6 all-gather.15
  366.5 47.7 all-gather.17
  416.3 57.8 all-gather.19
  502.9 67.3 all-gather.21

commit v3 on v2

v3 whole, which is shorter than its diff:
```python
import functools
import jax
import jax.numpy as jnp
from jax import lax
from jax.experimental import pallas as pl
from jax.experimental.pallas import tpu as pltpu
from jax.sharding import PartitionSpec as P

ROPE_BASE = 10000.0
NORM_EPS = 1e-5
NEG_LARGE = -1e30
F32 = jnp.float32
BF16 = jnp.bfloat16
N_DEV, N_CHIP, LANE, WIDE, CHUNK = 16, 8, 128, 256, 512


def norm_forward(hidden, gain_vec):
    inv_rms = lax.rsqrt(jnp.mean(hidden * hidden, axis=-1, keepdims=True) + NORM_EPS)
    return hidden * inv_rms * gain_vec


def rope_tables(positions, head_dim):
    half_dim = head_dim // 2
    inv_freq = 1.0 / (ROPE_BASE ** (jnp.arange(half_dim, dtype=F32) * (2.0 / head_dim)))
    angles = positions.astype(F32)[:, None] * inv_freq[None, :]
    return jnp.cos(angles)[:, None, :], jnp.sin(angles)[:, None, :]


def gated_unit(gate_pre, up_pre):
    return jax.nn.silu(gate_pre) * up_pre


NT = (((1,), (1,)), ((), ()))
TN = (((0,), (0,)), ((), ()))
NN = (((1,), (0,)), ((), ()))


def mm(a, b, dims):
    return lax.dot_general(a, b, dims, preferred_element_type=F32)


VMEM_CAP = 60 * 1024 * 1024


def in_vmem(n):
    return [pl.BlockSpec(memory_space=pltpu.VMEM)] * n


def comm_params(ident):
    return pltpu.CompilerParams(collective_id=ident, has_side_effects=True, vmem_limit_bytes=VMEM_CAP)


RS_ORDERS = ((2, 4, 8), (4, 8, 2), (8, 2, 4))
RS_MASKS = (14, 6, 12, 10, 2, 4, 8, 0)
RS_FIRST = ((14, 6, 10, 2), (14, 12, 6, 4), (14, 10, 12, 8))


def first_axis(colour, mask):
    return next(i for i, a in enumerate(RS_ORDERS[colour]) if mask & a)


def rs_slots(colour):
    slots = {}
    for mask in RS_MASKS:
        for axis in RS_ORDERS[colour][:first_axis(colour, mask) if mask else 3]:
            slots[mask, axis] = len(slots)
    return slots


def flipped(index, mask):
    out = index
    for bit in (1, 2, 4, N_CHIP):
        if mask & bit:
            out = out + (1 - 2 * ((index // bit) % 2)) * bit
    return out


def enter(peers):
    barrier = pltpu.get_barrier_semaphore()
    for peer in peers:
        pl.semaphore_signal(barrier, inc=1, device_id=(peer,), device_id_type=pl.DeviceIdType.MESH)
    pl.semaphore_wait(barrier, len(peers))


def rs_kernel(cols, a_ref, w_ref, base_ref, out_ref, part, pair_in, link_in, pair_send, pair_recv, link_send, link_recv):
    tokens, dim = out_ref.shape
    me = lax.axis_index('sp')
    core = me % 2
    partner = flipped(me, 1)
    enter([partner] + [flipped(me, a) for a in (2, 4, N_CHIP)])

    def pair_copy(i):
        return pltpu.make_async_remote_copy(
            src_ref=part.at[i, 1 - core], dst_ref=pair_in.at[i], send_sem=pair_send.at[i], recv_sem=pair_recv.at[i],
            device_id=(partner,), device_id_type=pl.DeviceIdType.MESH)

    def link_copy(colour, mask):
        axis = RS_ORDERS[colour][first_axis(colour, mask)]
        slot = rs_slots(colour)[mask - axis, axis]
        lo, n = cols[colour]
        return pltpu.make_async_remote_copy(
            src_ref=part.at[RS_MASKS.index(mask), core, :, pl.ds(lo, n)], dst_ref=link_in.at[slot, :, pl.ds(lo, n)],
            send_sem=link_send.at[colour, RS_MASKS.index(mask)], recv_sem=link_recv.at[colour, slot],
            device_id=(flipped(me, axis),), device_id_type=pl.DeviceIdType.MESH)

    rows = N_DEV

    def add(i, colour, slot):
        lo, n = cols[colour]

        def step(r, c):
            rs = pl.ds(pl.multiple_of(r * rows, rows), rows)
            part[i, core, rs, pl.ds(lo, n)] += link_in[slot, rs, pl.ds(lo, n)]
            return c
        lax.fori_loop(0, tokens // rows, step, 0)

    width = CHUNK

    def compute(i):
        start = pl.multiple_of((flipped(me, RS_MASKS[i]) // 2) * (2 * tokens), 2 * tokens)
        a = a_ref[:, pl.ds(start, 2 * tokens)]

        def step(n, c):
            cs = pl.ds(pl.multiple_of(n * width, width), width)
            r = mm(a, w_ref[:, cs], TN)
            part[i, 0, :, cs] = r[:tokens]
            part[i, 1, :, cs] = r[tokens:]
            return c
        lax.fori_loop(0, dim // width, step, 0)
        pair_copy(i).start()

    ready = set()
    sent = [0, 0, 0]

    def finish_pair(i):
        pair_copy(i).wait_recv()

        def step(r, c):
            rs = pl.ds(pl.multiple_of(r * rows, rows), rows)
            part[i, core, rs, :] += pair_in[i, rs, :]
            return c
        lax.fori_loop(0, tokens // rows, step, 0)
        ready.add(RS_MASKS[i])
        for colour in range(3):
            todo = RS_FIRST[colour]
            while sent[colour] < 4 and todo[sent[colour]] in ready:
                link_copy(colour, todo[sent[colour]]).start()
                sent[colour] += 1

    for i in range(N_CHIP):
        compute(i)
        if i:
            finish_pair(i - 1)
    finish_pair(7)

    def take(colour, mask, axis):
        link_copy(colour, mask + axis).wait_recv()
        add(RS_MASKS.index(mask), colour, rs_slots(colour)[mask, axis])

    for step in range(2):
        for colour in range(3):
            o = RS_ORDERS[colour]
            mask = (o[1] + o[2], o[1])[step]
            take(colour, mask, o[0])
            link_copy(colour, mask).start()
    for colour in range(3):
        o = RS_ORDERS[colour]
        take(colour, o[2], o[0])
        take(colour, o[2], o[1])
        link_copy(colour, o[2]).start()
    for colour in range(3):
        o = RS_ORDERS[colour]
        for axis in o:
            take(colour, 0, axis)
    out_ref[...] = (base_ref[...].astype(F32) + part[7, core]).astype(out_ref.dtype)
    for i in range(N_CHIP):
        pair_copy(i).wait_send()
    for colour in range(3):
        for mask in RS_MASKS[:7]:
            link_copy(colour, mask).wait_send()


def product_scatter(a, w, base, ident):
    feat, seq = a.shape
    tokens, dim = base.shape
    cols = thirds(dim, LANE)
    return pl.pallas_call(
        functools.partial(rs_kernel, cols),
        out_shape=jax.ShapeDtypeStruct((tokens, dim), BF16),
        in_specs=in_vmem(3), out_specs=in_vmem(1)[0],
        scratch_shapes=[
            pltpu.VMEM((N_CHIP, 2, tokens, dim), F32), pltpu.VMEM((N_CHIP, tokens, dim), F32), pltpu.VMEM((7, tokens, dim), F32),
            pltpu.SemaphoreType.DMA((N_CHIP,)), pltpu.SemaphoreType.DMA((N_CHIP,)), pltpu.SemaphoreType.DMA((3, N_CHIP)), pltpu.SemaphoreType.DMA((3, 7))],
        cost_estimate=pl.CostEstimate(flops=2 * seq * feat * dim, bytes_accessed=2 * (a.size + w.size), transcendentals=0),
        compiler_params=comm_params(ident),
        name=f'product_scatter_{ident}',
    )(a, w, base)


GATHER_ROUNDS = ((0,), (1,), (2,), (0, 1), (0, 2), (1, 2), (0, 1, 2))
TURNS = ((0,), (), (), (2,), (4,), (8,), (6, 10, 12, 14))


class Gather:
    def __init__(self, own, block, cut, sems, me):
        self.own, self.block, self.cut, self.me = own, block, cut, me
        self.send, self.recv, self.pair_send, self.pair_recv = sems

    def source(self, mask):
        return self.own if mask == 0 else self.block(flipped(self.me, mask))

    def unit(self, colour, mask, axis):
        return pltpu.make_async_remote_copy(
            src_ref=self.cut(self.source(mask), colour), dst_ref=self.cut(self.block(flipped(self.me, mask)), colour),
            send_sem=self.send.at[colour, mask // 2, RS_ORDERS[colour].index(axis)], recv_sem=self.recv.at[colour, (mask + axis) // 2],
            device_id=(flipped(self.me, axis),), device_id_type=MESH)

    def arrival(self, colour, mask):
        view = self.cut(self.block(flipped(self.me, mask)), colour)
        return pltpu.make_async_remote_copy(
            src_ref=view, dst_ref=view, send_sem=self.send.at[colour, 0, 0], recv_sem=self.recv.at[colour, mask // 2],
            device_id=(self.me,), device_id_type=MESH)

    def pair(self, mask):
        return pltpu.make_async_remote_copy(
            src_ref=self.source(mask), dst_ref=self.block(flipped(self.me, mask)),
            send_sem=self.pair_send.at[mask // 2], recv_sem=self.pair_recv.at[mask // 2],
            device_id=(flipped(self.me, 1),), device_id_type=MESH)

    def wait_pair(self, mask):
        view = self.block(flipped(self.me, mask + 1))
        pltpu.make_async_remote_copy(
            src_ref=view, dst_ref=view, send_sem=self.pair_send.at[mask // 2], recv_sem=self.pair_recv.at[mask // 2],
            device_id=(self.me,), device_id_type=MESH).wait_recv()

    def start(self):
        for pos in range(3):
            for colour in range(3):
                self.unit(colour, 0, RS_ORDERS[colour][pos]).start()
        self.pair(0).start()

    def round(self, r):
        for colour in range(3):
            order = RS_ORDERS[colour]
            mask = sum(order[p] for p in GATHER_ROUNDS[r])
            self.arrival(colour, mask).wait_recv()
            for axis in order[GATHER_ROUNDS[r][-1] + 1:]:
                self.unit(colour, mask, axis).start()
        for mask in {2: (2, 4, N_CHIP), 5: (6, 10, 12), 6: (14,)}.get(r, ()):
            self.pair(mask).start()

    def finish(self):
        for colour in range(3):
            order = RS_ORDERS[colour]
            for pos in range(3):
                self.unit(colour, 0, order[pos]).wait_send()
            for picks in GATHER_ROUNDS:
                for axis in order[picks[-1] + 1:]:
                    self.unit(colour, sum(order[p] for p in picks), axis).wait_send()
        for mask in CHIP_MASKS:
            self.pair(mask).wait_send()


CHIP_MASKS = (0, 2, 4, 8, 6, 10, 12, 14)
MESH = pl.DeviceIdType.MESH


def gather_sems():
    return [pltpu.SemaphoreType.DMA((3, N_CHIP, 3)), pltpu.SemaphoreType.DMA((3, N_CHIP)), pltpu.SemaphoreType.DMA((N_CHIP,)), pltpu.SemaphoreType.DMA((N_CHIP,))]


def thirds(total, unit):
    n = total // unit
    first = (n + 2) // 3
    second = (n - first + 1) // 2
    sizes = (first * unit, second * unit, (n - first - second) * unit)
    return ((0, sizes[0]), (sizes[0], sizes[1]), (sizes[0] + sizes[1], sizes[2]))


def lane_block(index, width=LANE):
    return pl.ds(pl.multiple_of(index * width, width), width)


class Swap:
    def __init__(self, src, dst, send, recv, me):
        self.src, self.dst, self.send, self.recv, self.me = src, dst, send, recv, me

    def copy(self, mask):
        peer = flipped(self.me, mask)
        return pltpu.make_async_remote_copy(
            src_ref=self.src(peer), dst_ref=self.dst(self.me), send_sem=self.send.at[mask], recv_sem=self.recv.at[mask],
            device_id=(peer,), device_id_type=MESH)

    def start(self):
        for mask in range(1, N_DEV):
            self.copy(mask).start()

    def wait_recv(self):
        for mask in range(1, N_DEV):
            view = self.dst(flipped(self.me, mask))
            pltpu.make_async_remote_copy(
                src_ref=view, dst_ref=view, send_sem=self.send.at[mask], recv_sem=self.recv.at[mask],
                device_id=(self.me,), device_id_type=MESH).wait_recv()

    def wait_send(self):
        for mask in range(1, N_DEV):
            self.copy(mask).wait_send()


def swap_sems():
    return [pltpu.SemaphoreType.DMA((N_DEV,)), pltpu.SemaphoreType.DMA((N_DEV,))]


def qkv_kernel(groups, hd, x_ref, small_ref, w_ref, cos_ref, sin_ref, qkv_ref, ucol_ref, small_all, w_out,
               full, acc, rot, u_scr, g_scr, *sems):
    me = lax.axis_index('sp')
    tokens, dim = x_ref.shape
    cols = w_ref.shape[0]
    n_dev = N_DEV
    qw = tokens
    q_all = n_dev * qw
    gsems, osem, rest = sems[:4], sems[4], sems[5:]
    enter([flipped(me, m) for m in range(1, N_DEV)])
    smalls = Swap(lambda peer: small_ref, lambda o: small_all.at[o], rest[0], rest[1], me)
    smalls.start()
    parts = thirds(cols, N_DEV)

    def block(o):
        return full.at[o // 2, :, lane_block(o % 2)]

    g = Gather(w_ref, block, lambda view, c: view.at[pl.ds(parts[c][0], parts[c][1]), :], gsems, me)
    g.start()

    def own_block(i, c):
        rs = pl.ds(pl.multiple_of(i * WIDE, WIDE), WIDE)
        full[me // 2, rs, lane_block(me % 2)] = w_ref[rs, :]
        return c
    lax.fori_loop(0, cols // WIDE, own_block, 0)
    acc[...] = jnp.zeros_like(acc)
    small_all[me] = small_ref[...]
    smalls.wait_recv()
    for o in range(n_dev):
        g_scr[0:1, o * LANE:(o + 1) * LANE] = small_all[o, 0:1, :]

    def norm(i, c):
        rs = pl.ds(pl.multiple_of(i * N_DEV, N_DEV), N_DEV)
        xf = x_ref[rs, :].astype(F32)
        inv = lax.rsqrt(jnp.mean(xf * xf, axis=-1, keepdims=True) + NORM_EPS)
        u_scr[rs, :] = (xf * inv * g_scr[0:1, :]).astype(BF16)
        return c
    lax.fori_loop(0, tokens // N_DEV, norm, 0)
    ucols = Swap(lambda peer: u_scr.at[:, lane_block(peer)], lambda o: ucol_ref.at[pl.ds(pl.multiple_of(o * tokens, tokens), tokens), :], rest[2], rest[3], me)

    def use(mask):
        g.wait_pair(mask)
        chip = flipped(me, mask) // 2
        pltpu.make_async_copy(full.at[chip], w_out.at[chip], osem.at[mask // 2]).start()
        u = u_scr[:, lane_block(chip, WIDE)]

        def step(i, c):
            rs = pl.ds(pl.multiple_of(i * CHUNK, CHUNK), CHUNK)
            acc[rs, :] += mm(full[chip, rs, :], u, NT)
            return c
        lax.fori_loop(0, cols // CHUNK, step, 0)

    for r in range(7):
        g.round(r)
        if r == 0:
            ucols.start()
        for mask in TURNS[r]:
            use(mask)

    half = hd // 2
    cos, sin = cos_ref[...], sin_ref[...]

    def turn(h, c):
        first = pl.ds(pl.multiple_of(h * hd, hd), half)
        second = pl.ds(pl.multiple_of(h * hd + half, half), half)
        p = acc[first, :].astype(BF16).astype(F32)
        q = acc[second, :].astype(BF16).astype(F32)
        rot[first, :] = (p * cos - q * sin).astype(BF16)
        rot[second, :] = (q * cos + p * sin).astype(BF16)
        return c
    lax.fori_loop(0, q_all // hd, turn, 0)
    for k in range(groups):
        turn(q_all // hd + 2 * k, 0)
        vs = pl.ds(q_all + (2 * k + 1) * hd, hd)
        rot[vs, :] = acc[vs, :].astype(BF16)
    per = n_dev // groups
    tok = lambda o: lane_block(o, tokens)
    qs = Swap(lambda peer: rot.at[pl.ds(pl.multiple_of(peer * qw, qw), qw), :], lambda o: qkv_ref.at[pl.ds(0, qw), tok(o)], rest[4], rest[5], me)
    kvs = Swap(lambda peer: rot.at[pl.ds(pl.multiple_of(q_all + (peer // per) * 2 * hd, 2 * hd), 2 * hd), :], lambda o: qkv_ref.at[pl.ds(qw, 2 * hd), tok(o)], rest[6], rest[7], me)
    qs.start()
    kvs.start()
    qkv_ref[0:qw, tok(me)] = rot[pl.ds(pl.multiple_of(me * qw, qw), qw), :]
    qkv_ref[qw:qw + 2 * hd, tok(me)] = rot[pl.ds(pl.multiple_of(q_all + (me // per) * 2 * hd, 2 * hd), 2 * hd), :]
    ucol_ref[pl.ds(pl.multiple_of(me * tokens, tokens), tokens), :] = u_scr[:, lane_block(me)]
    for swap in (ucols, qs, kvs):
        swap.wait_recv()
    for mask in CHIP_MASKS:
        chip = flipped(me, mask) // 2
        pltpu.make_async_copy(full.at[chip], w_out.at[chip], osem.at[mask // 2]).wait()
    g.finish()
    for swap in (smalls, ucols, qs, kvs):
        swap.wait_send()


def project_qkv(x, small, w, cos, sin, groups, hd):
    tokens, dim = x.shape
    cols = w.shape[0]
    seq = N_DEV * tokens
    return pl.pallas_call(
        functools.partial(qkv_kernel, groups, hd),
        out_shape=(jax.ShapeDtypeStruct((tokens + 2 * hd, seq), BF16), jax.ShapeDtypeStruct((seq, LANE), BF16),
                   jax.ShapeDtypeStruct((N_DEV,) + small.shape, F32), jax.ShapeDtypeStruct((N_CHIP, cols, WIDE), BF16)),
        in_specs=in_vmem(5), out_specs=tuple(in_vmem(3)) + (pl.BlockSpec(memory_space=pl.ANY),),
        scratch_shapes=[pltpu.VMEM((N_CHIP, cols, WIDE), BF16), pltpu.VMEM((cols, tokens), F32), pltpu.VMEM((cols, tokens), BF16),
                        pltpu.VMEM((tokens, dim), BF16), pltpu.VMEM((N_CHIP, dim), F32)]
        + gather_sems() + [pltpu.SemaphoreType.DMA((N_CHIP,))] + 4 * swap_sems(),
        cost_estimate=pl.CostEstimate(flops=2 * tokens * dim * cols, bytes_accessed=4 * N_DEV * w.size, transcendentals=0),
        compiler_params=comm_params(2),
        name='project_qkv',
    )(x, small, w, cos, sin)


def token_gather(full, own_ref, gsems, me):
    tokens = own_ref.shape[0]
    parts = thirds(own_ref.shape[1], LANE)

    def block(o):
        return full.at[o // 2, pl.ds(pl.multiple_of((o % 2) * tokens, tokens), tokens), :]

    g = Gather(own_ref, block, lambda view, c: view.at[:, pl.ds(parts[c][0], parts[c][1])], gsems, me)
    enter([flipped(me, m) for m in (1, 2, 4, N_CHIP)])
    g.start()
    for i in range(0, tokens, 32):
        full[me // 2, pl.ds(pl.multiple_of((me % 2) * tokens + i, 32), 32), :] = own_ref[i:i + 32, :]
    return g


def gate_up_kernel(m_ref, w_ref, gu_ref, m_out, full, *sems):
    me = lax.axis_index('sp')
    gsems, osem = sems[:4], sems[4]
    g = token_gather(full, m_ref, gsems, me)

    def use(mask):
        g.wait_pair(mask)
        chip = flipped(me, mask) // 2
        pltpu.make_async_copy(full.at[chip], m_out.at[chip], osem.at[mask // 2]).start()
        gu_ref[:, lane_block(chip, WIDE)] = mm(w_ref[...], full[chip], NT).astype(BF16)

    for r in range(7):
        g.round(r)
        for mask in TURNS[r]:
            use(mask)
    for mask in CHIP_MASKS:
        chip = flipped(me, mask) // 2
        pltpu.make_async_copy(full.at[chip], m_out.at[chip], osem.at[mask // 2]).wait()
    g.finish()


def gather_gate_up(m, w):
    tokens, dim = m.shape
    feat = w.shape[0]
    return pl.pallas_call(
        gate_up_kernel,
        out_shape=(jax.ShapeDtypeStruct((feat, N_DEV * tokens), BF16), jax.ShapeDtypeStruct((N_CHIP, 2 * tokens, dim), BF16)),
        in_specs=in_vmem(2), out_specs=(in_vmem(1)[0], pl.BlockSpec(memory_space=pl.ANY)),
        scratch_shapes=[pltpu.VMEM((N_CHIP, 2 * tokens, dim), BF16)] + gather_sems() + [pltpu.SemaphoreType.DMA((N_CHIP,))],
        cost_estimate=pl.CostEstimate(flops=2 * feat * N_DEV * tokens * dim, bytes_accessed=4 * N_DEV * m.size, transcendentals=0),
        compiler_params=comm_params(3),
        name='gather_gate_up',
    )(m, w)


def d_attn_kernel(dh_ref, wo_ref, o_ref, do_ref, dwo_ref, full, *sems):
    me = lax.axis_index('sp')
    g = token_gather(full, dh_ref, sems, me)
    dwo_ref[...] = jnp.zeros_like(dwo_ref)
    dim = wo_ref.shape[1]

    def use(mask):
        g.wait_pair(mask)
        chip = flipped(me, mask) // 2
        do_ref[:, lane_block(chip, WIDE)] = mm(wo_ref[...], full[chip], NT).astype(BF16)
        o = o_ref[:, lane_block(chip, WIDE)]

        def step(n, c):
            cs = lane_block(n, CHUNK)
            dwo_ref[:, cs] += mm(o, full[chip, :, cs], NN)
            return c
        lax.fori_loop(0, dim // CHUNK, step, 0)

    for r in range(7):
        g.round(r)
        for mask in TURNS[r]:
            use(mask)
    g.finish()


def gather_d_attn(dh, wo, o):
    tokens, dim = dh.shape
    return pl.pallas_call(
        d_attn_kernel,
        out_shape=(jax.ShapeDtypeStruct(o.shape, BF16), jax.ShapeDtypeStruct(wo.shape, F32)),
        in_specs=in_vmem(3), out_specs=tuple(in_vmem(2)),
        scratch_shapes=[pltpu.VMEM((N_CHIP, 2 * tokens, dim), BF16)] + gather_sems(),
        cost_estimate=pl.CostEstimate(flops=4 * wo.shape[0] * N_DEV * tokens * dim, bytes_accessed=4 * N_DEV * dh.size, transcendentals=0),
        compiler_params=comm_params(4),
        name='gather_d_attn',
    )(dh, wo, o)


QB = WIDE
KB = WIDE


def key_rows(dst, src, lo, hd):
    def step(i, c):
        ks = lane_block(i, KB)
        dst[ks, :] = src[lo:lo + hd, ks].T
        return c
    lax.fori_loop(0, src.shape[1] // KB, step, 0)


def score_block(k, q2, scale, diagonal):
    s = mm(k, q2, NN) * scale
    if diagonal:
        key = lax.broadcasted_iota(jnp.int32, s.shape, 0)
        qry = lax.broadcasted_iota(jnp.int32, s.shape, 1) % QB
        s = jnp.where(qry >= key, s, NEG_LARGE)
    return s


def attn_fwd_kernel(hd, qkv_ref, wg_ref, wu_ref, ot_ref, o_ref, stat_ref, w_ref, s_scr, k_scr, *sems):
    heads = qkv_ref.shape[0] // hd - 2
    seq = qkv_ref.shape[1]
    scale = hd ** -0.5
    lanes = heads * QB
    me = lax.axis_index('sp')
    qw = heads * hd
    feat = wg_ref.shape[0] // N_DEV
    enter([flipped(me, m) for m in range(1, N_DEV)])
    rows = lambda peer: pl.ds(pl.multiple_of(peer * feat, 32), feat)
    gates = Swap(lambda peer: wg_ref.at[rows(peer), :], lambda o: w_ref.at[pl.ds(0, feat), lane_block(o)], sems[0], sems[1], me)
    ups = Swap(lambda peer: wu_ref.at[rows(peer), :], lambda o: w_ref.at[pl.ds(feat, feat), lane_block(o)], sems[2], sems[3], me)
    osend, orecv = sems[4], sems[5]
    gates.start()
    ups.start()
    w_ref[0:feat, lane_block(me)] = wg_ref[rows(me), :]
    w_ref[feat:2 * feat, lane_block(me)] = wu_ref[rows(me), :]
    key_rows(k_scr, qkv_ref, qw, hd)
    own = pl.ds(pl.multiple_of(me * qw, qw), qw)

    def o_copy(peer, origin):
        return pltpu.make_async_remote_copy(
            src_ref=o_ref.at[:, lane_block(peer)], dst_ref=ot_ref.at[pl.ds(pl.multiple_of(origin * qw, qw), qw), :],
            send_sem=osend.at[peer], recv_sem=orecv.at[origin], device_id=(peer,), device_id_type=MESH)

    def q_block(qb, carry):
        qs = lane_block(qb, QB)
        q2 = jnp.concatenate([qkv_ref[h * hd:(h + 1) * hd, qs] for h in range(heads)], axis=1)

        def scores(kb, top, diagonal):
            ks = lane_block(kb, KB)
            s = score_block(k_scr[ks, :], q2, scale, diagonal)
            s_scr[ks, :] = s
            return jnp.maximum(top, jnp.max(s, axis=0, keepdims=True))

        top = lax.fori_loop(0, qb, lambda kb, t: scores(kb, t, False), jnp.full((1, lanes), NEG_LARGE, F32))
        top = scores(qb, top, True)

        def expo(kb, tot):
            ks = lane_block(kb, KB)
            e = jnp.exp(s_scr[ks, :] - top)
            s_scr[ks, :] = e
            return tot + jnp.sum(e, axis=0, keepdims=True)

        inv = 1.0 / lax.fori_loop(0, qb + 1, expo, jnp.zeros((1, lanes), F32))

        def weigh(kb, acc):
            ks = lane_block(kb, KB)
            p = (s_scr[ks, :] * inv).astype(BF16)
            return acc + mm(qkv_ref[qw + hd:qw + 2 * hd, ks], p, NN)

        acc = lax.fori_loop(0, qb + 1, weigh, jnp.zeros((hd, lanes), F32))
        for h in range(heads):
            o_ref[h * hd:(h + 1) * hd, qs] = acc[:, h * QB:(h + 1) * QB].astype(BF16)
        stat_ref[qb, 0:1, :] = top
        stat_ref[qb, 1:2, :] = inv
        for core in range(2):
            peer = 2 * qb + core

            @pl.when(peer != me)
            def _():
                o_copy(peer, me).start()
        return carry

    lax.fori_loop(0, seq // QB, q_block, 0)
    ot_ref[own, :] = o_ref[:, lane_block(me)]
    for mask in range(1, N_DEV):
        o_copy(me, flipped(me, mask)).wait_recv()
    gates.wait_recv()
    ups.wait_recv()
    for mask in range(1, N_DEV):
        o_copy(flipped(me, mask), me).wait_send()
    gates.wait_send()
    ups.wait_send()


def attention_forward(qkv, wg, wu, hd):
    rows, seq = qkv.shape
    qw = rows - 2 * hd
    lanes = qw // hd * QB
    feat = wg.shape[0] // N_DEV
    return pl.pallas_call(
        functools.partial(attn_fwd_kernel, hd),
        out_shape=(jax.ShapeDtypeStruct((N_DEV * qw, seq // N_DEV), BF16), jax.ShapeDtypeStruct((qw, seq), BF16),
                   jax.ShapeDtypeStruct((seq // QB, 2, lanes), F32), jax.ShapeDtypeStruct((2 * feat, N_DEV * wg.shape[1]), BF16)),
        in_specs=in_vmem(3), out_specs=tuple(in_vmem(4)),
        scratch_shapes=[pltpu.VMEM((seq, lanes), F32), pltpu.VMEM((seq, hd), BF16)] + 3 * swap_sems(),
        cost_estimate=pl.CostEstimate(flops=2 * 4 * qw * seq * seq, bytes_accessed=4 * wg.size, transcendentals=0),
        compiler_params=comm_params(5),
        name='attn_fwd',
    )(qkv, wg, wu)


def attn_bwd_kernel(hd, qkv_ref, do_ref, stat_ref, cos_ref, sin_ref, dq_ref, dk_ref, dv_ref, p_scr, dp_scr, k_scr, v_scr, dk_acc, dv_acc):
    heads = qkv_ref.shape[0] // hd - 2
    seq = qkv_ref.shape[1]
    scale = hd ** -0.5
    lanes = heads * QB
    qw = heads * hd
    half = hd // 2
    dk_acc[...] = jnp.zeros_like(dk_acc)
    dv_acc[...] = jnp.zeros_like(dv_acc)
    key_rows(k_scr, qkv_ref, qw, hd)
    key_rows(v_scr, qkv_ref, qw + hd, hd)

    def q_block(qb, carry):
        qs = lane_block(qb, QB)
        q2 = jnp.concatenate([qkv_ref[h * hd:(h + 1) * hd, qs] for h in range(heads)], axis=1)
        do2 = jnp.concatenate([do_ref[h * hd:(h + 1) * hd, qs] for h in range(heads)], axis=1)
        top = stat_ref[qb, 0:1, :]
        inv = stat_ref[qb, 1:2, :]

        def probs(kb, rd, diagonal):
            ks = lane_block(kb, KB)
            s = score_block(k_scr[ks, :], q2, scale, diagonal)
            p = jnp.exp(s - top) * inv
            dp = mm(v_scr[ks, :], do2, NN).astype(BF16)
            p_scr[ks, :] = p
            dp_scr[ks, :] = dp
            dv_acc[ks, :] += mm(p.astype(BF16), do2, NT)
            return rd + jnp.sum(dp.astype(F32) * p, axis=0, keepdims=True)

        rd = lax.fori_loop(0, qb, lambda kb, r: probs(kb, r, False), jnp.zeros((1, lanes), F32))
        rd = probs(qb, rd, True)

        def d_scores(kb, acc):
            ks = lane_block(kb, KB)
            ds = (p_scr[ks, :] * (dp_scr[ks, :].astype(F32) - rd) * scale).astype(BF16)
            dk_acc[ks, :] += mm(ds, q2, NT)
            return acc + mm(qkv_ref[qw:qw + hd, ks], ds, NN)

        acc = lax.fori_loop(0, qb + 1, d_scores, jnp.zeros((hd, lanes), F32))
        cos, sin = cos_ref[:, qs], sin_ref[:, qs]
        for h in range(heads):
            dq = acc[:, h * QB:(h + 1) * QB].astype(BF16).astype(F32)
            p, q = dq[:half], dq[half:]
            dq_ref[h * hd:h * hd + half, qs] = (p * cos + q * sin).astype(BF16)
            dq_ref[h * hd + half:(h + 1) * hd, qs] = (q * cos - p * sin).astype(BF16)
        return carry

    lax.fori_loop(0, seq // QB, q_block, 0)
    dk_ref[...] = dk_acc[...].astype(BF16)
    dv_ref[...] = dv_acc[...].astype(BF16)


def attention_backward(qkv, do, stat, cos, sin, hd):
    rows, seq = qkv.shape
    qw = rows - 2 * hd
    lanes = qw // hd * QB
    return pl.pallas_call(
        functools.partial(attn_bwd_kernel, hd),
        out_shape=(jax.ShapeDtypeStruct((qw, seq), BF16), jax.ShapeDtypeStruct((seq, hd), BF16), jax.ShapeDtypeStruct((seq, hd), BF16)),
        in_specs=in_vmem(5), out_specs=tuple(in_vmem(3)),
        scratch_shapes=[pltpu.VMEM((seq, lanes), F32), pltpu.VMEM((seq, lanes), BF16), pltpu.VMEM((seq, hd), BF16), pltpu.VMEM((seq, hd), BF16),
                        pltpu.VMEM((seq, hd), F32), pltpu.VMEM((seq, hd), F32)],
        cost_estimate=pl.CostEstimate(flops=2 * 10 * qw * seq * seq, bytes_accessed=4 * seq * hd * N_CHIP, transcendentals=0),
        compiler_params=pltpu.CompilerParams(vmem_limit_bytes=VMEM_CAP),
        name='attn_bwd',
    )(qkv, do, stat, cos, sin)


def solution(mesh):
    n_dev = mesh.shape['sp']
    gather = functools.partial(lax.all_gather, axis_name='sp', axis=0, tiled=True)
    swap = functools.partial(lax.all_to_all, axis_name='sp', split_axis=0, concat_axis=0, tiled=True)

    def layer_step(x_in, positions, d_out, norm1_gain, norm2_gain, w_q, w_k, w_v, w_o, w_gate, w_up, w_down):
        tokens, dim = x_in.shape
        seq_len = tokens * n_dev
        n_q, hd = w_q.shape[1], w_q.shape[2]
        n_kv = w_k.shape[1]
        qw = n_q // n_dev * hd
        rows = w_q.shape[0]
        feat = w_down.shape[0]
        me = lax.axis_index('sp')

        small = jnp.stack([norm1_gain.astype(F32), norm2_gain.astype(F32), positions.astype(F32)] + [jnp.zeros((rows,), F32)] * 5)
        cos_tab, sin_tab = rope_tables(positions, hd)
        wq_t = w_q.transpose(1, 2, 0).reshape(n_q * hd, rows)
        wkv_t = jnp.stack([w_k.transpose(1, 2, 0), w_v.transpose(1, 2, 0)], axis=1).reshape(2 * n_kv * hd, rows)
        wo_own = w_o.reshape(qw, dim)
        wo_full = gather(wo_own)
        do_full = gather(d_out)

        qkv, u_col, small_all, wqkv = project_qkv(x_in, small, jnp.concatenate([wq_t, wkv_t], axis=0), cos_tab[:, 0].T, sin_tab[:, 0].T, n_kv, hd)
        g1 = small_all[:, 0].reshape(-1)
        g2 = small_all[:, 1].reshape(-1)
        cos_all, sin_all = rope_tables(small_all[:, 2].reshape(-1), hd)

        attn_tok, attn_t, stat, wgu = attention_forward(qkv, w_gate.T, w_up.T, hd)
        x_f32 = x_in.astype(F32)
        attn_proj = jnp.einsum('et,ed->td', attn_tok, wo_full, preferred_element_type=F32)
        hidden = (x_f32 + attn_proj).astype(BF16)
        hidden_f32 = hidden.astype(F32)
        mlp_pre, norm2_pull = jax.vjp(norm_forward, hidden_f32, g2)
        mlp_in = mlp_pre.astype(BF16)

        gu, m_full = gather_gate_up(mlp_in, wgu)
        m_full = m_full.reshape(seq_len, dim)
        gate_act, up_act = gu[:feat], gu[feat:]
        glu_pre, glu_pull = jax.vjp(gated_unit, gate_act.astype(F32), up_act.astype(F32))
        glu = glu_pre.astype(BF16)
        y_out = product_scatter(glu, w_down, hidden, 0)

        d_down = jnp.einsum('ft,td->fd', glu, do_full, preferred_element_type=F32)
        d_glu = jnp.einsum('fd,td->ft', w_down, do_full, preferred_element_type=F32).astype(BF16)
        d_gate_f, d_up_f = glu_pull(d_glu.astype(F32))
        dgu = jnp.concatenate([d_gate_f.astype(BF16), d_up_f.astype(BF16)], axis=0)
        d_mlp_in = product_scatter(dgu, wgu, jnp.zeros_like(hidden), 1)
        d_hidden_norm, d_g2 = norm2_pull(d_mlp_in.astype(F32))
        d_hidden = (d_out.astype(F32) + d_hidden_norm).astype(BF16)

        dwgu = jnp.einsum('ft,td->fd', dgu, m_full, preferred_element_type=F32)
        dwgu = swap(dwgu.reshape(2 * feat, n_dev, rows).transpose(1, 0, 2))
        d_gate = dwgu[:, :feat].reshape(n_dev * feat, rows).T
        d_up = dwgu[:, feat:].reshape(n_dev * feat, rows).T

        d_attn, d_wo = gather_d_attn(d_hidden, wo_own, attn_t)
        dq_t, d_k_seq, d_v_seq = attention_backward(qkv, d_attn, stat, cos_all[:, 0].T, sin_all[:, 0].T, hd)
        dq_full = gather(dq_t)
        shares = swap(jnp.concatenate([d_k_seq, d_v_seq], axis=1).reshape(n_dev, tokens, 2 * hd))
        dkv = jnp.sum(shares.reshape(n_kv, n_dev // n_kv, tokens, 2 * hd), axis=1, dtype=F32).astype(BF16).astype(F32)
        first, second = dkv[:, :, :hd // 2], dkv[:, :, hd // 2:hd]
        cos_k, sin_k = cos_tab[None], sin_tab[None]
        cos_k, sin_k = cos_k[:, :, 0], sin_k[:, :, 0]
        dkv = jnp.concatenate([first * cos_k + second * sin_k, second * cos_k - first * sin_k, dkv[:, :, hd:]], axis=2).astype(BF16)
        dkv = dkv.transpose(1, 0, 2).reshape(tokens, 2 * n_kv * hd)
        dkv_full = gather(dkv)
        dwkv = jnp.einsum('te,td->ed', dkv_full, u_col, preferred_element_type=F32).reshape(n_kv, 2, hd, rows)
        d_wk = dwkv[:, 0].transpose(2, 0, 1)
        d_wv = dwkv[:, 1].transpose(2, 0, 1)
        d_wq = jnp.einsum('et,td->ed', dq_full, u_col, preferred_element_type=F32).reshape(n_q, hd, rows).transpose(2, 0, 1)
        dq_own = lax.dynamic_slice_in_dim(dq_full, me * tokens, tokens, axis=1)
        dqkv = jnp.concatenate([dq_own, dkv.T], axis=0)
        d_normed = jnp.einsum('et,ced->tcd', dqkv, wqkv, preferred_element_type=F32).reshape(tokens, dim).astype(BF16)
        norm1_pull = jax.vjp(norm_forward, x_f32, g1)[1]
        d_x_norm, d_g1 = norm1_pull(d_normed.astype(F32))
        d_x = (d_hidden.astype(F32) + d_x_norm).astype(BF16)
        gains = jnp.stack([d_g1.reshape(n_dev, rows), d_g2.reshape(n_dev, rows)] + [jnp.zeros((n_dev, rows), F32)] * 6, axis=1)
        gsum = jnp.sum(swap(gains), axis=0)
        return (y_out, d_x, gsum[0], gsum[1], d_wq, d_wk, d_wv, d_wo.reshape(w_o.shape), d_gate, d_up, d_down)

    all_rows = P('sp')
    return jax.shard_map(layer_step, mesh=mesh, in_specs=(all_rows,) * 12, out_specs=(all_rows,) * 11, check_vma=False)
```

time: 680 us -> 629 us (0.925)
  Pallas kernels: 227 us -> 486 us
  waiting for transfers between devices: 191 us -> 12 us
  blocking collectives: 79.2 us -> 0 us
  matrix products: 74 us -> 48.6 us
  local copies, waits for them, and re-layouts: 53.8 us -> 36.6 us
    pallas_call x2 -> x5, Pallas kernels: 47.8 us -> 268 us  [the longest x1 97.2 us: project_qkv(): pl.pallas_call(functools.partial(qkv_kernel, groups, hd), out_shape=(jax....]
    all_gather x5 -> x2, waiting for transfers between devices: 122 us -> 0.01 us  [the longest x1 0.01 us: layer_step(): dkv_full = gather(dkv)]
    all_to_all x2 -> x0, blocking collectives: 64.7 us -> none  [the longest x1 45.3 us: layer_step(): wgu = swap(jnp.concatenate([by_feature(w_gate), by_feature(w_up)], axis=1))]
    all_gather x1, waiting for transfers between devices: 40.2 us -> 0.02 us  [layer_step(): do_full = gather(d_out)]
    pallas_call x2, Pallas kernels: 179 us -> 218 us  [product_scatter(): pl.pallas_call(functools.partial(rs_kernel, cols), out_shape=jax.ShapeDty...]
    dot_general x8 -> x4, matrix products: 45.9 us -> 19.6 us  [the longest x1 6.76 us: layer_step(): jnp.einsum('et,td->ed', dq_full, u_col, preferred_element_type=F32)]
    all_to_all x3 -> x2, waiting for transfers between devices: 27.4 us -> 9.99 us  [the longest x1 9.99 us: layer_step(): swap(jnp.concatenate([d_k_seq, d_v_seq], axis=1).reshape(n_dev, tokens, 2...]
    all_gather x1 -> x0, blocking collectives: 14.5 us -> none  [layer_step(): small_all = gather(small[None])]
  transfers between devices with their start and end apart: 11 -> 7, of which waited for: 7 -> 1; matrix products, arithmetic and copies ran while one was open for 17% -> 11% of each run, Pallas kernels for 24% -> 57%
where the time goes in v3:
time: 629 us; the launch traced here: 623 us
  Pallas kernels  486 us (77%)
  matrix products  48.6 us (8%)
  local copies, waits for them, and re-layouts  36.6 us (6%)
  other arithmetic  17.2 us (3%)
  between operations  14.4 us (2%)
  waiting for transfers between devices  12 us (2%)
  starting transfers between devices  8.22 us (1%)
    pallas_call x2, Pallas kernels, product_scatter(): pl.pallas_call(functools.partial(rs_kernel, cols), out_shape=jax.ShapeDty...  218 us
    pallas_call x1, Pallas kernels, project_qkv(): pl.pallas_call(functools.partial(qkv_kernel, groups, hd), out_shape=(jax....  97.2 us
    pallas_call x1, Pallas kernels, attention_forward(): pl.pallas_call(functools.partial(attn_fwd_kernel, hd), out_shape=(jax.Sha...  60.6 us
    pallas_call x1, Pallas kernels, gather_gate_up(): pl.pallas_call(gate_up_kernel, out_shape=(jax.ShapeDtypeStruct((feat, N_D...  45.2 us
    pallas_call x1, Pallas kernels, gather_d_attn(): pl.pallas_call(d_attn_kernel, out_shape=(jax.ShapeDtypeStruct(o.shape, BF...  38.7 us
    pallas_call x1, Pallas kernels, attention_backward(): pl.pallas_call(functools.partial(attn_bwd_kernel, hd), out_shape=(jax.Sha...  26.8 us
    dot_general x1, local copies, waits for them, and re-layouts, layer_step(): dwgu = jnp.einsum('ft,td->fd', dgu, m_full, preferred_element_type=F32)  12.7 us
  transfers between devices with their start and end apart: 7, of which 1 were waited for; matrix products, arithmetic and copies ran while one was open for 11% of the time, Pallas kernels for 57%

profile of v3, /device:TPU:0, one launch (start us, length us, event | category | flops | bytes accessed | tf_op | source)
XLA Modules:
  0.0 623.3 jit_solution(12920914973252079497)
XLA Ops:
  7.2 0.7 all-gather.5.cloned.1.call-update
  7.9 0.0 all-gather.7.cloned.1.call-start
  8.0 0.7 all-gather.7.cloned.1.call-update
  8.7 0.9 pad_maximum_fusion.3
  9.6 2.6 copy.45
  12.2 1.5 copy.46
  13.8 0.6 stack.45.small_ref
  14.4 0.8 multiply_sine_fusion.2
  15.2 0.9 pad_maximum_fusion.1.w_ref
  16.1 97.2 %project_qkv.1 = (bf16[256,2048]{1,0:T(8,128)(2,1)}, bf16[2048,128]{1,0:T(8,128)(2,1)}, f32[16,8,128]{2,1,0:T(8,128)}, bf16[8,2560,256]{2,1,0:T(8,128)(2,1)}) custom-call(bf16[128,2048]{1,0:T(8,128)(2,1)} %x_ref.1, f32[8,128]{1,0:T(8,128)} %stack.45.small_ref, bf16[2560,128]{1,0:T(8,128)(2,1)} %pad_maximum_fusion.1.w_ref, ...), custom_call_target="tpu_custom_call" | custom-call | flops 1342177280 | bytes 20971520 | tf_op jit(solution)/shard_map/project_qkv/pallas_call | solution.py:412
  113.3 1.0 fusion.36
  114.3 60.6 %attn_fwd.1 = (bf16[2048,128]{1,0:T(8,128)(2,1)}, bf16[128,2048]{1,0:T(8,128)(2,1)}, f32[8,2,512]{2,1,0:T(2,128)}, bf16[704,2048]{1,0:T(8,128)(2,1)}) custom-call(bf16[256,2048]{1,0:T(8,128)(2,1)} %get-tuple-element.26.qkv_ref, bf16[5632,128]{1,0:T(8,128)(2,1)} %bitcast.96, bf16[5632,128]{1,0:T(8,128)(2,1)} %bitcast.97), custom_call_target="tpu_custom_call" | custom-call | flops 4294967296 | bytes 2883584 | tf_op jit(solution)/shard_map/attn_fwd/pallas_call | solution.py:616
  174.9 2.0 multiply_sine_fusion
  176.9 4.9 fusion.24
  181.8 1.0 fusion.18.m_ref
  182.8 45.2 %gather_gate_up.1 = (bf16[704,2048]{1,0:T(8,128)(2,1)}, bf16[8,256,2048]{2,1,0:T(8,128)(2,1)}) custom-call(bf16[128,2048]{1,0:T(8,128)(2,1)} %fusion.18.m_ref, bf16[704,2048]{1,0:T(8,128)(2,1)} %get-tuple-element.29.w_ref), custom_call_target="tpu_custom_call" | custom-call | flops 5905580032 | bytes 16777216 | tf_op jit(solution)/shard_map/gather_gate_up/pallas_call | solution.py:465
  228.0 10.3 %fusion.7 = (bf16[352,2048]{1,0:T(8,128)(2,1)S(1)}, bf16[352,2048]{1,0:T(8,128)(2,1)S(1)}, bf16[352,2048]{1,0:T(8,128)(2,1)}) fusion(bf16[704,2048]{1,0:T(8,128)(2,1)} %get-tuple-element.30, bf16[352,2048]{1,0:T(8,128)(2,1)} %w_ref.1, bf16[2048,2048]{1,0:T(8,128)(2,1)} %all-gather.7.cloned.1.call-done), kind=kOutput, calls=%fused_computation.14 | convolution fusion | flops 2967207936 | bytes 17039360 | tf_op jit(solution)/shard_map/fd,td->ft/dot_general | solution.py:740
  238.3 1.9 pad_maximum_fusion.a_ref
  240.2 0.1 copy-done.5
  240.4 0.8 broadcast_in_dim.6.base_ref
  241.2 66.3 %product_scatter_1.1 = bf16[128,2048]{1,0:T(8,128)(2,1)} custom-call(bf16[704,2048]{1,0:T(8,128)(2,1)} %pad_maximum_fusion.a_ref, bf16[704,2048]{1,0:T(8,128)(2,1)} %get-tuple-element.29.w_ref, bf16[128,2048]{1,0:T(8,128)(2,1)} %broadcast_in_dim.6.base_ref), custom_call_target="tpu_custom_call" | custom-call | flops 5905580032 | bytes 5767168 | tf_op jit(solution)/shard_map/product_scatter_1/pallas_call | solution.py:187
  307.5 1.6 fusion.19
  309.1 2.2 fusion.21.dh_ref
  311.4 38.7 %gather_d_attn.1 = (bf16[128,2048]{1,0:T(8,128)(2,1)}, f32[128,2048]{1,0:T(8,128)}) custom-call(bf16[128,2048]{1,0:T(8,128)(2,1)} %fusion.21.dh_ref, bf16[128,2048]{1,0:T(8,128)(2,1)} %bitcast.105, bf16[128,2048]{1,0:T(8,128)(2,1)} %get-tuple-element.31.o_ref), custom_call_target="tpu_custom_call" | custom-call | flops 2147483648 | bytes 16777216 | tf_op jit(solution)/shard_map/gather_d_attn/pallas_call | solution.py:503
  350.1 26.8 %attn_bwd.1 = (bf16[128,2048]{1,0:T(8,128)(2,1)}, bf16[2048,64]{1,0:T(8,128)(2,1)}, bf16[2048,64]{1,0:T(8,128)(2,1)}) custom-call(bf16[256,2048]{1,0:T(8,128)(2,1)} %get-tuple-element.26.qkv_ref, bf16[128,2048]{1,0:T(8,128)(2,1)} %get-tuple-element.32.do_ref, f32[8,2,512]{2,1,0:T(2,128)} %get-tuple-element.33.stat_ref, ...), custom_call_target="tpu_custom_call" | custom-call | flops 10737418240 | bytes 4194304 | tf_op jit(solution)/shard_map/attn_bwd/pallas_call | solution.py:684
  376.8 2.3 pad_maximum_fusion.2
  379.1 2.3 all-to-all-start
  381.5 0.0 all-gather.11.cloned.1.call-start
  381.5 0.3 multiply_cosine_fusion.1
  381.8 10.0 %all-to-all-done = bf16[16,128,128]{2,1,0:T(8,128)(2,1)S(1)} async-done(((bf16[16,128,128]{2,1,0:T(8,128)(2,1)}), bf16[16,128,128]{2,1,0:T(8,128)(2,1)S(1)}, u32[]{:S(2)}, u32[]{:S(2)}) %all-to-all-start) | async-done | bytes 524320 | tf_op jit(solution)/shard_map/all_to_all | solution.py:755
  391.8 0.1 bitcast_reduce_fusion
  391.9 0.1 slice.59
  392.0 0.1 add_convert_fusion
  392.2 0.1 maximum_bitcast_fusion.2
  392.3 0.8 copy.47
  393.1 0.0 all-gather.9.cloned.1.call-start
  393.2 0.5 all-gather.9.cloned.1.call-update
  393.7 12.7 %copy.52 = bf16[2048,2048]{1,0:T(8,128)(2,1)} copy(bf16[2048,2048]{0,1:T(8,128)(2,1)} %bitcast.92) | data formatting | bytes 16777216 | tf_op jit(solution)/shard_map/ft,td->fd/dot_general | solution.py:747
  406.4 10.6 %fusion.10 = f32[16,704,128]{2,1,0:T(8,128)} fusion(bf16[16,128,2048]{2,1,0:T(8,128)(2,1)} %bitcast.93, bf16[352,2048]{1,0:T(8,128)(2,1)} %copy-done.5, bf16[352,2048]{1,0:T(8,128)(2,1)S(1)} %get-tuple-element.47), kind=kOutput, calls=%fused_computation.19 | convolution fusion | flops 5911347200 | bytes 17039360 | tf_op jit(solution)/shard_map/ft,td->fd/dot_general | solution.py:747
  417.0 3.3 all-to-all-start.2
  420.3 0.6 pad.3.clone
  420.9 0.6 pad.2.clone
  421.5 0.2 fusion.26
  421.7 0.5 copy-done.13
  422.2 0.5 fusion.33
  422.7 151.6 %product_scatter_0.1 = bf16[128,2048]{1,0:T(8,128)(2,1)} custom-call(bf16[352,2048]{1,0:T(8,128)(2,1)} %get-tuple-element.49.a_ref, bf16[352,2048]{1,0:T(8,128)(2,1)} %w_ref.1, bf16[128,2048]{1,0:T(8,128)(2,1)} %copy-done.1), custom_call_target="tpu_custom_call" | custom-call | flops 2952790016 | bytes 2883584 | tf_op jit(solution)/shard_map/product_scatter_0/pallas_call | solution.py:187
  574.4 8.2 %fusion.40 = f32[352,2048]{1,0:T(8,128)} fusion(bf16[352,2048]{1,0:T(8,128)(2,1)S(1)} %copy-done.20, bf16[2048,2048]{1,0:T(8,128)(2,1)} %all-gather.7.cloned.1.call-done), kind=kOutput, calls=%fused_computation.89 | convolution fusion | flops 2952790016 | bytes 12713984 | tf_op jit(solution)/shard_map/ft,td->fd/dot_general | solution.py:739
  582.5 2.3 fusion.39
  584.8 0.7 slice_bitcast_fusion
  585.6 4.7 fusion.35
  590.2 3.4 copy.53
  593.6 2.2 copy.54
  595.8 1.1 constant_dynamic-slice_fusion
  596.9 5.6 fusion.15
  602.5 0.1 copy.59
  602.6 0.4 fusion.29
  603.0 0.1 copy-done.14
  603.2 0.7 maximum_maximum_fusion
  603.9 2.4 all-to-all-start.1
  606.3 6.8 %fusion.38 = f32[2048,128]{1,0:T(8,128)} fusion(bf16[2048,2048]{1,0:T(8,128)(2,1)} %all-gather.9.cloned.1.call-done, bf16[2048,128]{1,0:T(8,128)(2,1)S(1)} %copy-done.11), kind=kOutput, calls=%fused_computation.87 | convolution fusion | flops 1073741824 | bytes 9961472 | tf_op jit(solution)/shard_map/et,td->ed/dot_general | solution.py:766
  613.1 1.2 fusion.23
  614.3 0.5 slice_bitcast_fusion.2
  614.8 0.8 copy.62
  615.6 1.0 copy.63
  (60 shorter events, 0.3 us)
Async XLA Ops:
  7.2 5.0 copy-start.4
  7.2 169.7 %all-gather.5.cloned.1.call-start = ((), (), s32[]{:S(2)}) async-start(), calls=%async_computation.3 | async-start | bytes 8912896 | tf_op jit(solution)/shard_map/all_gather | solution.py:716
  7.9 220.1 %all-gather.7.cloned.1.call-start = ((), (), s32[]{:S(2)}) async-start(), calls=%async_computation.4 | async-start | bytes 8912896 | tf_op jit(solution)/shard_map/all_gather | solution.py:717
  9.6 4.2 copy-start.19
  9.6 4.2 copy-start.15
  9.6 4.2 copy-start.16
  9.6 5.6 copy-start.8
  114.3 62.6 %copy-start = (bf16[128,2048]{1,0:T(8,128)(2,1)S(1)}, bf16[128,2048]{1,0:T(8,128)(2,1)}, u32[]{:S(2)}) copy-start(bf16[128,2048]{1,0:T(8,128)(2,1)} %x_ref.1) | copy-start | bytes 1572868
  181.8 127.3 %copy-start.1 = (bf16[128,2048]{1,0:T(8,128)(2,1)}, bf16[128,2048]{1,0:T(8,128)(2,1)S(1)}, u32[]{:S(2)}) copy-start(bf16[128,2048]{1,0:T(8,128)(2,1)S(1)} %get-tuple-element.68.base_ref) | copy-start | bytes 1572868
  238.3 2.0 copy-start.5
  241.2 67.9 %copy-start.3 = (bf16[128,2048]{1,0:T(8,128)(2,1)S(1)}, bf16[128,2048]{1,0:T(8,128)(2,1)}, u32[]{:S(2)}) copy-start(bf16[128,2048]{1,0:T(8,128)(2,1)} %param.14) | copy-start | bytes 1572868
  379.1 12.7 %all-to-all-start = ((bf16[16,128,128]{2,1,0:T(8,128)(2,1)}), bf16[16,128,128]{2,1,0:T(8,128)(2,1)S(1)}, u32[]{:S(2)}, u32[]{:S(2)}) async-start(bf16[16,128,128]{2,1,0:T(8,128)(2,1)} %bitcast.15), calls=%async_computation | async-start | bytes 1048576 | tf_op jit(solution)/shard_map/all_to_all | solution.py:755
  381.5 201.1 %all-gather.11.cloned.1.call-start = ((), (), s32[]{:S(2)}) async-start(), calls=%async_computation.6 | async-start | bytes 2228224 | tf_op jit(solution)/shard_map/all_gather | solution.py:762
  393.1 202.7 %all-gather.9.cloned.1.call-start = ((), (), s32[]{:S(2)}) async-start(), calls=%async_computation.5 | async-start | bytes 8912896 | tf_op jit(solution)/shard_map/all_gather | solution.py:754
  417.0 168.6 %all-to-all-start.2 = ((f32[16,704,128]{2,1,0:T(8,128)}), f32[16,704,128]{2,1,0:T(8,128)}, u32[]{:S(2)}, u32[]{:S(2)}) async-start(f32[16,704,128]{2,1,0:T(8,128)} %fusion.10), calls=%async_computation.2 | async-start | bytes 11534336 | tf_op jit(solution)/shard_map/all_to_all | solution.py:748
  421.7 0.5 copy-start.13
  422.7 151.6 %copy-start.20 = (bf16[352,2048]{1,0:T(8,128)(2,1)S(1)}, bf16[352,2048]{1,0:T(8,128)(2,1)}, u32[]{:S(2)}) copy-start(bf16[352,2048]{1,0:T(8,128)(2,1)} %get-tuple-element.49.a_ref) | copy-start | bytes 4325380
  574.4 8.2 %copy-start.10 = (bf16[2048,128]{1,0:T(8,128)(2,1)S(1)}, bf16[2048,128]{1,0:T(8,128)(2,1)}, u32[]{:S(2)}) copy-start(bf16[2048,128]{1,0:T(8,128)(2,1)} %get-tuple-element.38) | copy-start | bytes 1572868
  593.6 3.3 copy-start.6
  596.9 5.7 copy-start.12
  602.5 0.7 copy-start.14
  602.5 0.7 copy-start.17
  602.5 0.7 copy-start.18
  602.5 3.8 copy-start.11
  603.9 10.4 %all-to-all-start.1 = ((f32[16,8,128]{2,1,0:T(8,128)}), f32[16,8,128]{2,1,0:T(8,128)S(1)}, u32[]{:S(2)}, u32[]{:S(2)}) async-start(f32[16,8,128]{2,1,0:T(8,128)} %maximum_maximum_fusion), calls=%async_computation.1 | async-start | bytes 131072 | tf_op jit(solution)/shard_map/all_to_all | solution.py:774
  606.3 6.8 %copy-start.2 = (bf16[128,2048]{1,0:T(8,128)(2,1)S(1)}, bf16[128,2048]{1,0:T(8,128)(2,1)}, u32[]{:S(2)}) copy-start(bf16[128,2048]{1,0:T(8,128)(2,1)} %fusion.21.dh_ref) | copy-start | bytes 1572868
  613.1 1.7 copy-start.9
  613.1 2.5 copy-start.7
Sparse Core Ops, SparseCore 0:
  10.2 79.4 all-gather.4
  92.0 81.5 all-gather.6
  393.2 30.2 all-gather.10
  426.1 115.1 all-gather.8

commit v4 on v0

v4 whole, which is shorter than its diff:
```python
import functools
import jax
import jax.numpy as jnp
from jax import lax
from jax.experimental import pallas as pl
from jax.experimental.pallas import tpu as pltpu
from jax.sharding import PartitionSpec as P

ROPE_BASE = 10000.0
NORM_EPS = 1e-5
NEG_LARGE = -1e30
F32 = jnp.float32
BF16 = jnp.bfloat16
N_DEV, N_CHIP, LANE, WIDE, CHUNK, STRIP = 16, 8, 128, 256, 512, 16
NT = (((1,), (1,)), ((), ()))
TN = (((0,), (0,)), ((), ()))
NN = (((1,), (0,)), ((), ()))
MESH = pl.DeviceIdType.MESH
VMEM_CAP = 62 * 1024 * 1024

CORE, X, Y, Z = 1, 2, 4, 8
XYZ = X + Y + Z
ORDERS = ((X, Y, Z), (Y, Z, X), (Z, X, Y))
CHIP_MASKS = (0, X, Y, Z, X + Y, X + Z, Y + Z, XYZ)
NEAR = (CORE, X, Y, Z)
OTHERS = range(1, N_DEV)
COLOURS = range(len(ORDERS))


def mm(a, b, dims):
    return lax.dot_general(a, b, dims, preferred_element_type=F32)


def seg(index, width=LANE):
    return pl.ds(pl.multiple_of(index * width, width), width)


def loop(count, body):
    lax.fori_loop(0, count, lambda i, c: (body(i), c)[1], 0)


def flipped(index, mask):
    out = index
    for bit in NEAR:
        if mask & bit:
            out = out + (1 - 2 * ((index // bit) % 2)) * bit
    return out


def thirds(total, unit):
    n = total // unit
    first = (n + 2) // 3
    second = (n - first + 1) // 2
    sizes = (first * unit, second * unit, (n - first - second) * unit)
    return ((0, sizes[0]), (sizes[0], sizes[1]), (sizes[0] + sizes[1], sizes[2]))


def enter(me, masks):
    barrier = pltpu.get_barrier_semaphore()
    for mask in masks:
        pl.semaphore_signal(barrier, inc=1, device_id=(flipped(me, mask),), device_id_type=MESH)
    pl.semaphore_wait(barrier, len(masks))


def remote(src, dst, send, recv, peer):
    return pltpu.make_async_remote_copy(src_ref=src, dst_ref=dst, send_sem=send, recv_sem=recv, device_id=(peer,), device_id_type=MESH)


def dma(*shape):
    return pltpu.SemaphoreType.DMA(shape)


class Swap:
    sems = (dma(N_DEV), dma(N_DEV))

    def __init__(self, src, dst, sems, me):
        self.src, self.dst, (self.send, self.recv), self.me = src, dst, sems, me

    def copy(self, mask):
        peer = flipped(self.me, mask)
        return remote(self.src(peer), self.dst(self.me), self.send.at[mask], self.recv.at[mask], peer)

    def start(self, masks=OTHERS):
        for mask in masks:
            self.copy(mask).start()

    def wait_recv(self):
        for mask in OTHERS:
            view = self.dst(flipped(self.me, mask))
            remote(view, view, self.send.at[mask], self.recv.at[mask], self.me).wait_recv()

    def wait_send(self):
        for mask in OTHERS:
            self.copy(mask).wait_send()


class Gather:
    ROUNDS = ((0,), (1,), (2,), (0, 1), (0, 2), (1, 2), (0, 1, 2))
    READY = ((0,), (), (), (X,), (Y,), (Z, X + Y), (X + Z, Y + Z, XYZ))
    sems = (dma(3, N_CHIP, 3), dma(3, N_CHIP), dma(N_CHIP), dma(N_CHIP))

    def __init__(self, own, block, cut, sems, me):
        self.own, self.block, self.cut, self.me = own, block, cut, me
        self.send, self.recv, self.pair_send, self.pair_recv = sems

    def source(self, mask):
        return self.block(flipped(self.me, mask)) if mask else self.own

    def unit(self, colour, mask, axis):
        return remote(self.cut(self.source(mask), colour), self.cut(self.block(flipped(self.me, mask)), colour),
                      self.send.at[colour, mask // 2, ORDERS[colour].index(axis)], self.recv.at[colour, (mask + axis) // 2],
                      flipped(self.me, axis))

    def pair(self, mask):
        return remote(self.source(mask), self.block(flipped(self.me, mask)), self.pair_send.at[mask // 2],
                      self.pair_recv.at[mask // 2], flipped(self.me, CORE))

    def wait_pair(self, mask):
        view = self.block(flipped(self.me, mask + CORE))
        remote(view, view, self.pair_send.at[mask // 2], self.pair_recv.at[mask // 2], self.me).wait_recv()

    def onward(self, colour):
        order = ORDERS[colour]
        for picks in self.ROUNDS:
            for axis in order[picks[-1] + 1:]:
                yield picks, sum(order[p] for p in picks), axis

    def start(self):
        for pos in COLOURS:
            for colour in COLOURS:
                self.unit(colour, 0, ORDERS[colour][pos]).start()
        self.pair(0).start()

    def round(self, r):
        for colour in COLOURS:
            mask = sum(ORDERS[colour][p] for p in self.ROUNDS[r])
            view = self.cut(self.block(flipped(self.me, mask)), colour)
            remote(view, view, self.send.at[colour, 0, 0], self.recv.at[colour, mask // 2], self.me).wait_recv()
            for picks, at, axis in self.onward(colour):
                if picks == self.ROUNDS[r]:
                    self.unit(colour, at, axis).start()
        for mask in {2: (X, Y, Z), 5: (X + Y, X + Z, Y + Z), 6: (XYZ,)}.get(r, ()):
            self.pair(mask).start()

    def run(self, use):
        self.start()
        for r in range(len(self.ROUNDS)):
            self.round(r)
            for mask in self.READY[r]:
                use(mask)

    def finish(self):
        for colour in COLOURS:
            for axis in ORDERS[colour]:
                self.unit(colour, 0, axis).wait_send()
            for _, at, axis in self.onward(colour):
                self.unit(colour, at, axis).wait_send()
        for mask in CHIP_MASKS:
            self.pair(mask).wait_send()


def row_gather(own, full, sems, me):
    width = own.shape[1]
    parts = thirds(width, LANE)

    def block(o):
        return full.at[o // 2, seg(o % 2), :]

    return Gather(own, block, lambda view, c: view.at[:, pl.ds(*parts[c])], sems, me)


def keep_own(own, full, me):
    def step(i):
        full[me // 2, pl.ds(pl.multiple_of((me % 2) * LANE + i * STRIP, STRIP), STRIP), :] = own[seg(i, STRIP), :]
    loop(LANE // STRIP, step)


class Scatter:
    ORDER = (XYZ, X + Y, Y + Z, X + Z, X, Y, Z, 0)
    sems = (dma(N_CHIP), dma(N_CHIP), dma(3, N_CHIP), dma(3, N_CHIP))

    @staticmethod
    def scratch(tokens, dim):
        return [pltpu.VMEM((N_CHIP, 2, tokens, dim), F32), pltpu.VMEM((N_CHIP, tokens, dim), F32), pltpu.VMEM((N_CHIP - 1, tokens, dim), F32)]

    def __init__(self, part, pair_in, link_in, sems, me):
        self.part, self.pair_in, self.link_in, self.me = part, pair_in, link_in, me
        self.pair_send, self.pair_recv, self.link_send, self.link_recv = sems
        self.core = me % 2
        self.tokens, self.dim = part.shape[2:]
        self.cols = thirds(self.dim, LANE)
        self.ready, self.sent = set(), [0] * len(ORDERS)

    @staticmethod
    def first(colour, mask):
        return next((i for i, a in enumerate(ORDERS[colour]) if mask & a), 3)

    def slot(self, colour, mask, axis):
        slots = [(m, a) for m in self.ORDER for a in ORDERS[colour][:self.first(colour, m)]]
        return slots.index((mask, axis))

    def pair(self, i):
        return remote(self.part.at[i, 1 - self.core], self.pair_in.at[i], self.pair_send.at[i], self.pair_recv.at[i], flipped(self.me, CORE))

    def link(self, colour, mask):
        axis = ORDERS[colour][self.first(colour, mask)]
        slot = self.slot(colour, mask - axis, axis)
        cs = pl.ds(*self.cols[colour])
        i = self.ORDER.index(mask)
        return remote(self.part.at[i, self.core, :, cs], self.link_in.at[slot, :, cs], self.link_send.at[colour, i],
                      self.link_recv.at[colour, slot], flipped(self.me, axis))

    def add(self, mask, ref, cs):
        i = self.ORDER.index(mask)

        def step(r):
            rs = seg(r, STRIP)
            self.part[i, self.core, rs, cs] += ref[rs, cs]
        loop(self.tokens // STRIP, step)

    def finish_pair(self, i):
        self.pair(i).wait_recv()
        self.add(self.ORDER[i], self.pair_in.at[i], pl.ds(0, self.dim))
        self.ready.add(self.ORDER[i])
        for colour in COLOURS:
            a, b, c = ORDERS[colour]
            todo = (XYZ, a + b, a + c, a)
            while self.sent[colour] < len(todo) and todo[self.sent[colour]] in self.ready:
                self.link(colour, todo[self.sent[colour]]).start()
                self.sent[colour] += 1

    def take(self, colour, mask, axis):
        self.link(colour, mask + axis).wait_recv()
        self.add(mask, self.link_in.at[self.slot(colour, mask, axis)], pl.ds(*self.cols[colour]))

    def run(self, product):
        for i, mask in enumerate(self.ORDER):
            product(i, flipped(self.me, mask) // 2)
            self.pair(i).start()
            if i:
                self.finish_pair(i - 1)
        self.finish_pair(N_CHIP - 1)
        for step in range(2):
            for colour in COLOURS:
                a, b, c = ORDERS[colour]
                mask = (b + c, b)[step]
                self.take(colour, mask, a)
                self.link(colour, mask).start()
        for colour in COLOURS:
            a, b, c = ORDERS[colour]
            self.take(colour, c, a)
            self.take(colour, c, b)
            self.link(colour, c).start()
        for colour in COLOURS:
            for axis in ORDERS[colour]:
                self.take(colour, 0, axis)
        return self.part.at[N_CHIP - 1, self.core]

    def finish(self):
        for i in range(N_CHIP):
            self.pair(i).wait_send()
        for colour in COLOURS:
            for mask in self.ORDER[:-1]:
                self.link(colour, mask).wait_send()


def block_product(part, a_ref, w_ref):
    tokens = part.shape[2]

    def product(i, chip):
        a = a_ref[:, seg(chip, 2 * tokens)]

        def step(n):
            cs = seg(n, CHUNK)
            r = mm(a, w_ref[:, cs], TN)
            part[i, 0, :, cs] = r[:tokens]
            part[i, 1, :, cs] = r[tokens:]
        loop(part.shape[3] // CHUNK, step)
    return product


def on_chip(n):
    return [pl.BlockSpec(memory_space=pltpu.VMEM)] * n


IN_HBM = pl.BlockSpec(memory_space=pl.ANY)


def call(kernel, ident, args, outs, scratch, flops, far_in=(), far_out=()):
    specs = [IN_HBM if i in far_in else on_chip(1)[0] for i in range(len(args))]
    out_specs = [IN_HBM if i in far_out else on_chip(1)[0] for i in range(len(outs))]
    return pl.pallas_call(
        kernel,
        out_shape=[jax.ShapeDtypeStruct(shape, dtype) for shape, dtype in outs],
        in_specs=specs, out_specs=out_specs, scratch_shapes=scratch,
        cost_estimate=pl.CostEstimate(flops=flops, bytes_accessed=flops // CHUNK, transcendentals=0),
        compiler_params=pltpu.CompilerParams(collective_id=ident, has_side_effects=True, vmem_limit_bytes=VMEM_CAP),
        name=kernel.func.__name__ if isinstance(kernel, functools.partial) else kernel.__name__,
    )(*args)


def gain_row(dst, small_all, which):
    for o in range(N_DEV):
        dst[:1, o * LANE:(o + 1) * LANE] = small_all[o, which:which + 1, :]


def norm_rows(src, gain, dst):
    def step(i):
        rs = seg(i, STRIP)
        t = src[rs, :].astype(F32)
        dst[rs, :] = (t * lax.rsqrt(jnp.mean(t * t, axis=-1, keepdims=True) + NORM_EPS) * gain[:1, :]).astype(BF16)
    loop(src.shape[0] // STRIP, step)


def norm_back(dy, src, gain, skip, dst, dgain):
    def step(i):
        rs = seg(i, STRIP)
        d = dy[rs, :].astype(BF16).astype(F32)
        t = src[rs, :].astype(F32)
        inv = lax.rsqrt(jnp.mean(t * t, axis=-1, keepdims=True) + NORM_EPS)
        gd = gain[:1, :] * d
        pull = jnp.mean(gd * t, axis=-1, keepdims=True)
        dst[rs, :] = (skip[rs, :].astype(F32) + (inv * gd - t * (inv * inv * inv * pull))).astype(BF16)
        g = d * (t * inv)
        dgain[...] += g[:N_CHIP] + g[N_CHIP:]
    dgain[...] = jnp.zeros_like(dgain)
    loop(src.shape[0] // STRIP, step)


def project_qkv(groups, hd, x_ref, small_ref, w_ref, cos_ref, sin_ref, qkv_ref, ucol_ref, small_all, w_out,
                full, acc, rot, u_scr, g_scr, osem, *sems):
    me = lax.axis_index('sp')
    tokens, dim = x_ref.shape
    cols = w_ref.shape[0]
    qw = tokens
    q_all = N_DEV * qw
    gsems, ssems, usems, qsems, ksems = sems[:4], sems[4:6], sems[6:8], sems[8:10], sems[10:]
    enter(me, OTHERS)
    smalls = Swap(lambda peer: small_ref, lambda o: small_all.at[o], ssems, me)
    smalls.start()
    parts = thirds(cols, STRIP)
    g = Gather(w_ref, lambda o: full.at[o // 2, :, seg(o % 2)], lambda view, c: view.at[pl.ds(*parts[c]), :], gsems, me)
    g.start()

    def own_block(i):
        full[me // 2, seg(i, WIDE), seg(me % 2)] = w_ref[seg(i, WIDE), :]
    loop(cols // WIDE, own_block)
    acc[...] = jnp.zeros_like(acc)
    small_all[me] = small_ref[...]
    smalls.wait_recv()
    gain_row(g_scr, small_all, 0)
    norm_rows(x_ref, g_scr, u_scr)
    ucols = Swap(lambda peer: u_scr.at[:, seg(peer)], lambda o: ucol_ref.at[seg(o, tokens), :], usems, me)

    def keep(mask):
        chip = flipped(me, mask) // 2
        return pltpu.make_async_copy(full.at[chip], w_out.at[chip], osem.at[mask // 2])

    def use(mask):
        g.wait_pair(mask)
        keep(mask).start()
        chip = flipped(me, mask) // 2
        u = u_scr[:, seg(chip, WIDE)]

        def step(i):
            rs = seg(i, CHUNK)
            acc[rs, :] += mm(full[chip, rs, :], u, NT)
        loop(cols // CHUNK, step)

    for r in range(len(g.ROUNDS)):
        g.round(r)
        if r == 0:
            ucols.start()
        for mask in g.READY[r]:
            use(mask)

    half = hd // 2
    cos, sin = cos_ref[...], sin_ref[...]

    def turn(h):
        first = seg(2 * h, half)
        second = seg(2 * h + 1, half)
        p = acc[first, :].astype(BF16).astype(F32)
        q = acc[second, :].astype(BF16).astype(F32)
        rot[first, :] = (p * cos - q * sin).astype(BF16)
        rot[second, :] = (q * cos + p * sin).astype(BF16)
    loop(q_all // hd, turn)
    for k in range(groups):
        turn(q_all // hd + 2 * k)
        vs = seg(q_all // hd + 2 * k + 1, hd)
        rot[vs, :] = acc[vs, :].astype(BF16)
    per = N_DEV // groups
    q_rows = lambda peer: seg(peer, qw)
    kv_rows = lambda peer: seg(q_all // (2 * hd) + peer // per, 2 * hd)
    qs = Swap(lambda peer: rot.at[q_rows(peer), :], lambda o: qkv_ref.at[:qw, seg(o, tokens)], qsems, me)
    kvs = Swap(lambda peer: rot.at[kv_rows(peer), :], lambda o: qkv_ref.at[qw:, seg(o, tokens)], ksems, me)
    qs.start()
    kvs.start()
    qkv_ref[:qw, seg(me, tokens)] = rot[q_rows(me), :]
    qkv_ref[qw:, seg(me, tokens)] = rot[kv_rows(me), :]
    ucol_ref[seg(me, tokens), :] = u_scr[:, seg(me)]
    for swap in (ucols, qs, kvs):
        swap.wait_recv()
    for mask in CHIP_MASKS:
        keep(mask).wait()
    g.finish()
    for swap in (smalls, ucols, qs, kvs):
        swap.wait_send()


QB = 256
KB = 256


def key_rows(dst, src, lo, hd):
    def step(i):
        dst[seg(i, KB), :] = src[lo:lo + hd, seg(i, KB)].T
    loop(src.shape[1] // KB, step)


def score_block(k, q2, scale, diagonal):
    s = mm(k, q2, NN) * scale
    if diagonal:
        key = lax.broadcasted_iota(jnp.int32, s.shape, 0)
        qry = lax.broadcasted_iota(jnp.int32, s.shape, 1) % QB
        s = jnp.where(qry >= key, s, NEG_LARGE)
    return s


def side_by_side(ref, heads, hd, qs):
    return jnp.concatenate([ref[h * hd:(h + 1) * hd, qs] for h in range(heads)], axis=1)


def attn_fwd(hd, qkv_ref, wg_ref, wu_ref, ot_ref, o_ref, stat_ref, w_ref, s_scr, k_scr, *sems):
    heads = qkv_ref.shape[0] // hd - 2
    seq = qkv_ref.shape[1]
    scale = hd ** -0.5
    lanes = heads * QB
    me = lax.axis_index('sp')
    qw = heads * hd
    feat = wg_ref.shape[0] // N_DEV
    enter(me, OTHERS)
    gates = Swap(lambda peer: wg_ref.at[seg(peer, feat), :], lambda o: w_ref.at[:feat, seg(o)], sems[:2], me)
    ups = Swap(lambda peer: wu_ref.at[seg(peer, feat), :], lambda o: w_ref.at[feat:, seg(o)], sems[2:4], me)
    osend, orecv = sems[4:]
    gates.start()
    ups.start()
    w_ref[:feat, seg(me)] = wg_ref[seg(me, feat), :]
    w_ref[feat:, seg(me)] = wu_ref[seg(me, feat), :]
    key_rows(k_scr, qkv_ref, qw, hd)

    def o_copy(peer, origin):
        return remote(o_ref.at[:, seg(peer)], ot_ref.at[seg(origin, qw), :], osend.at[peer], orecv.at[origin], peer)

    def q_block(qb):
        qs = seg(qb, QB)
        q2 = side_by_side(qkv_ref, heads, hd, qs)

        def scores(kb, top, diagonal):
            s = score_block(k_scr[seg(kb, KB), :], q2, scale, diagonal)
            s_scr[seg(kb, KB), :] = s
            return jnp.maximum(top, jnp.max(s, axis=0, keepdims=True))

        top = lax.fori_loop(0, qb, lambda kb, t: scores(kb, t, False), jnp.full((1, lanes), NEG_LARGE, F32))
        top = scores(qb, top, True)

        def expo(kb, tot):
            e = jnp.exp(s_scr[seg(kb, KB), :] - top)
            s_scr[seg(kb, KB), :] = e
            return tot + jnp.sum(e, axis=0, keepdims=True)

        inv = 1.0 / lax.fori_loop(0, qb + 1, expo, jnp.zeros((1, lanes), F32))

        def weigh(kb, acc):
            p = (s_scr[seg(kb, KB), :] * inv).astype(BF16)
            return acc + mm(qkv_ref[qw + hd:, seg(kb, KB)], p, NN)

        acc = lax.fori_loop(0, qb + 1, weigh, jnp.zeros((hd, lanes), F32))
        for h in range(heads):
            o_ref[h * hd:(h + 1) * hd, qs] = acc[:, h * QB:(h + 1) * QB].astype(BF16)
        stat_ref[qb, :1, :] = top
        stat_ref[qb, 1:, :] = inv
        for core in range(2):
            peer = 2 * qb + core

            @pl.when(peer != me)
            def _():
                o_copy(peer, me).start()

    loop(seq // QB, q_block)
    ot_ref[seg(me, qw), :] = o_ref[:, seg(me)]
    for mask in OTHERS:
        o_copy(me, flipped(me, mask)).wait_recv()
    gates.wait_recv()
    ups.wait_recv()
    for mask in OTHERS:
        o_copy(flipped(me, mask), me).wait_send()
    gates.wait_send()
    ups.wait_send()


def mlp_local(ot_ref, wo_ref, x_ref, small_all, dout_ref, wgu_ref, down_ref, h_ref, m_out, glu_ref, dgu_ref, ddown_ref,
              full_w, full_d, full_m, acc, m_scr, g_scr, osem, *sems):
    me = lax.axis_index('sp')
    feat, dim = down_ref.shape
    enter(me, NEAR)
    gw = row_gather(wo_ref, full_w, sems[:4], me)
    gd = row_gather(dout_ref, full_d, sems[4:8], me)
    gm = row_gather(m_scr, full_m, sems[8:], me)

    def project(mask):
        gw.wait_pair(mask)
        chip = flipped(me, mask) // 2
        o = ot_ref[seg(chip, WIDE), :]

        def step(n):
            acc[:, seg(n, CHUNK)] += mm(o, full_w[chip, :, seg(n, CHUNK)], TN)
        loop(dim // CHUNK, step)

    gw.start()
    keep_own(wo_ref, full_w, me)
    keep_own(dout_ref, full_d, me)
    gain_row(g_scr, small_all, 1)
    acc[...] = jnp.zeros_like(acc)
    ddown_ref[...] = jnp.zeros_like(ddown_ref)
    for r in range(len(gw.ROUNDS)):
        gw.round(r)
        if r == 3:
            gd.start()
        for mask in gw.READY[r]:
            project(mask)

    def residual(i):
        rs = seg(i, STRIP)
        h_ref[rs, :] = (x_ref[rs, :].astype(F32) + acc[rs, :]).astype(BF16)
    loop(x_ref.shape[0] // STRIP, residual)
    norm_rows(h_ref, g_scr, m_scr)
    gm.start()
    keep_own(m_scr, full_m, me)

    def keep(mask):
        chip = flipped(me, mask) // 2
        return pltpu.make_async_copy(full_m.at[chip], m_out.at[chip], osem.at[mask // 2])

    def use(mask):
        gd.wait_pair(mask)
        gm.wait_pair(mask)
        keep(mask).start()
        chip = flipped(me, mask) // 2
        ts = seg(chip, WIDE)
        gu = mm(wgu_ref[...], full_m[chip], NT).astype(BF16).astype(F32)
        gate, up = gu[:feat], gu[feat:]
        d_glu = mm(down_ref[...], full_d[chip], NT).astype(BF16).astype(F32)
        sig = jax.nn.sigmoid(gate)
        act = gate * sig
        glu = (act * up).astype(BF16)
        glu_ref[:, ts] = glu
        dgu_ref[:feat, ts] = (d_glu * up * (sig * (1.0 + gate * (1.0 - sig)))).astype(BF16)
        dgu_ref[feat:, ts] = (d_glu * act).astype(BF16)

        def step(n):
            ddown_ref[:, seg(n, CHUNK)] += mm(glu, full_d[chip, :, seg(n, CHUNK)], NN)
        loop(dim // CHUNK, step)

    for r in range(len(gm.ROUNDS)):
        gd.round(r)
        gm.round(r)
        for mask in gm.READY[r]:
            use(mask)
    for mask in CHIP_MASKS:
        keep(mask).wait()
    for g in (gw, gd, gm):
        g.finish()


def scatter_y(a_ref, w_ref, h_ref, y_ref, *scr):
    me = lax.axis_index('sp')
    enter(me, NEAR)
    s = Scatter(*scr[:3], scr[3:], me)
    total = s.run(block_product(s.part, a_ref, w_ref))
    y_ref[...] = (h_ref[...].astype(F32) + total[...]).astype(BF16)
    s.finish()


def mlp_back(dgu_ref, wgu_ref, h_ref, small_all, dout_ref, wo_ref, o_ref, dh_ref, do_ref, dwo_ref, dg_ref,
             full, g_scr, *scr):
    me = lax.axis_index('sp')
    dim = wo_ref.shape[1]
    enter(me, NEAR)
    s = Scatter(*scr[:3], scr[3:7], me)
    g = row_gather(dh_ref, full, scr[7:], me)
    gain_row(g_scr, small_all, 1)
    dwo_ref[...] = jnp.zeros_like(dwo_ref)
    total = s.run(block_product(s.part, dgu_ref, wgu_ref))
    norm_back(total, h_ref, g_scr, dout_ref, dh_ref, dg_ref)

    def use(mask):
        g.wait_pair(mask)
        chip = flipped(me, mask) // 2
        do_ref[:, seg(chip, WIDE)] = mm(wo_ref[...], full[chip], NT).astype(BF16)
        o = o_ref[:, seg(chip, WIDE)]

        def step(n):
            dwo_ref[:, seg(n, CHUNK)] += mm(o, full[chip, :, seg(n, CHUNK)], NN)
        loop(dim // CHUNK, step)

    g.start()
    keep_own(dh_ref, full, me)
    for r in range(len(g.ROUNDS)):
        g.round(r)
        for mask in g.READY[r]:
            use(mask)
    s.finish()
    g.finish()


def attn_bwd(hd, qkv_ref, do_ref, stat_ref, cos_ref, sin_ref, dgu_ref, m_ref, dq_ref, dkv_ref, dg_ref, du_ref,
             p_scr, dp_scr, k_scr, v_scr, dk_acc, dv_acc, stage, *sems):
    heads = qkv_ref.shape[0] // hd - 2
    seq = qkv_ref.shape[1]
    scale = hd ** -0.5
    lanes = heads * QB
    qw = heads * hd
    half = hd // 2
    me = lax.axis_index('sp')
    feat = dgu_ref.shape[0] // 2
    enter(me, OTHERS)

    def piece(lo):
        return lambda peer: stage.at[peer // 2, lo:lo + feat, seg(peer % 2)]
    gates = Swap(piece(0), lambda o: dg_ref.at[seg(o, feat), :], sems[:2], me)
    ups = Swap(piece(feat), lambda o: du_ref.at[seg(o, feat), :], sems[2:], me)
    for mask in (XYZ, X + Y, X + Z, Y + Z, X, Y, Z, 0):
        chip = flipped(me, mask) // 2
        cols = m_ref[:, :, seg(chip, WIDE)].reshape(seq, WIDE)
        stage[chip] = mm(dgu_ref[...], cols, NN)
        for swap in (gates, ups):
            swap.start([m for m in (mask, mask + CORE) if m])
    dg_ref[seg(me, feat), :] = stage[me // 2, :feat, seg(me % 2)]
    du_ref[seg(me, feat), :] = stage[me // 2, feat:, seg(me % 2)]

    dk_acc[...] = jnp.zeros_like(dk_acc)
    dv_acc[...] = jnp.zeros_like(dv_acc)
    key_rows(k_scr, qkv_ref, qw, hd)
    key_rows(v_scr, qkv_ref, qw + hd, hd)

    def q_block(qb):
        qs = seg(qb, QB)
        q2 = side_by_side(qkv_ref, heads, hd, qs)
        do2 = side_by_side(do_ref, heads, hd, qs)
        top = stat_ref[qb, :1, :]
        inv = stat_ref[qb, 1:, :]

        def probs(kb, rd, diagonal):
            ks = seg(kb, KB)
            s = score_block(k_scr[ks, :], q2, scale, diagonal)
            p = jnp.exp(s - top) * inv
            dp = mm(v_scr[ks, :], do2, NN).astype(BF16)
            p_scr[ks, :] = p
            dp_scr[ks, :] = dp
            dv_acc[ks, :] += mm(p.astype(BF16), do2, NT)
            return rd + jnp.sum(dp.astype(F32) * p, axis=0, keepdims=True)

        rd = lax.fori_loop(0, qb, lambda kb, r: probs(kb, r, False), jnp.zeros((1, lanes), F32))
        rd = probs(qb, rd, True)

        def d_scores(kb, acc):
            ks = seg(kb, KB)
            ds = (p_scr[ks, :] * (dp_scr[ks, :].astype(F32) - rd) * scale).astype(BF16)
            dk_acc[ks, :] += mm(ds, q2, NT)
            return acc + mm(qkv_ref[qw:qw + hd, ks], ds, NN)

        acc = lax.fori_loop(0, qb + 1, d_scores, jnp.zeros((hd, lanes), F32))
        cos, sin = cos_ref[:, qs], sin_ref[:, qs]
        for h in range(heads):
            dq = acc[:, h * QB:(h + 1) * QB].astype(BF16).astype(F32)
            p, q = dq[:half], dq[half:]
            dq_ref[h * hd:h * hd + half, qs] = (p * cos + q * sin).astype(BF16)
            dq_ref[h * hd + half:(h + 1) * hd, qs] = (q * cos - p * sin).astype(BF16)

    loop(seq // QB, q_block)

    def share(i):
        rs = seg(i, WIDE)
        dkv_ref[rs, :] = jnp.concatenate([dk_acc[rs, :], dv_acc[rs, :]], axis=1).astype(BF16)
    loop(seq // WIDE, share)
    for swap in (gates, ups):
        swap.wait_recv()
    for swap in (gates, ups):
        swap.wait_send()


def tail(groups, hd, dq_ref, dkv_ref, ucol_ref, cos_ref, sin_ref, w_hbm, x_ref, small_all, dh_ref, dg2_ref,
         dwq_ref, dwkv_ref, dx_ref, gain_ref, full, w_scr, shares, dkv_own, full_kv, dqkv, dn, g_scr, dg1, gains, gains_in, wsem, *sems):
    me = lax.axis_index('sp')
    seq, tokens = ucol_ref.shape
    half = hd // 2
    per = N_DEV // groups
    q_all = dwq_ref.shape[0]
    enter(me, OTHERS)
    load = pltpu.make_async_copy(w_hbm, w_scr, wsem)
    load.start()
    sh = Swap(lambda peer: dkv_ref.at[seg(peer, tokens), :], lambda o: shares.at[o], sems[:2], me)
    gq = row_gather(dq_ref, full, sems[2:6], me)
    parts = thirds(dkv_own.shape[0], STRIP)
    gk = Gather(dkv_own, lambda o: full_kv.at[:, seg(o, tokens)], lambda view, c: view.at[pl.ds(*parts[c]), :], sems[6:10], me)
    gs = Swap(lambda peer: gains.at[:, seg(peer)], lambda o: gains_in.at[o], sems[10:], me)
    sh.start()
    gq.start()
    keep_own(dq_ref, full, me)
    gain_row(g_scr, small_all, 0)
    shares[me] = dkv_ref[seg(me, tokens), :]
    sh.wait_recv()
    cos, sin = cos_ref[...], sin_ref[...]
    for k in range(groups):
        both = sum(shares[per * k + i].astype(F32) for i in range(per)).astype(BF16).astype(F32).T
        p, q = both[:half], both[half:hd]
        lo = 2 * hd * k
        dkv_own[lo:lo + half, :] = (p * cos + q * sin).astype(BF16)
        dkv_own[lo + half:lo + hd, :] = (q * cos - p * sin).astype(BF16)
        dkv_own[lo + hd:lo + 2 * hd, :] = both[hd:].astype(BF16)
    gk.start()
    full_kv[:, seg(me, tokens)] = dkv_own[...]
    dqkv[q_all:, :] = dkv_own[...]

    def use(mask):
        gq.wait_pair(mask)
        chip = flipped(me, mask) // 2
        dwq_ref[seg(chip, WIDE), :] = mm(full[chip], ucol_ref[...], NN)
        dqkv[seg(chip, WIDE), :] = full[chip, :, seg(me, tokens)]

    for r in range(len(gq.ROUNDS)):
        gq.round(r)
        gk.round(r)
        for mask in gq.READY[r]:
            use(mask)
    load.wait()

    def normed(i):
        dn[:, seg(i, WIDE)] = mm(dqkv[...], w_scr[i], TN)
    loop(N_CHIP, normed)
    norm_back(dn, x_ref, g_scr, dh_ref, dx_ref, dg1)
    gains[...] = jnp.concatenate([jnp.sum(dg1[...], axis=0, keepdims=True), jnp.sum(dg2_ref[...], axis=0, keepdims=True),
                                  jnp.zeros((N_CHIP - 2, dg1.shape[1]), F32)], axis=0)
    gs.start()
    gains_in[me] = gains[:, seg(me)]
    for mask in CHIP_MASKS:
        gk.wait_pair(mask)
    dwkv_ref[...] = mm(full_kv[...], ucol_ref[...], NN)
    gs.wait_recv()
    gain_ref[...] = sum(gains_in[o] for o in range(N_DEV))
    for c in (sh, gs):
        c.wait_send()
    for g in (gq, gk):
        g.finish()


def rope_tables(positions, head_dim):
    half_dim = head_dim // 2
    inv_freq = 1.0 / (ROPE_BASE ** (jnp.arange(half_dim, dtype=F32) * (2.0 / head_dim)))
    angles = positions.astype(F32)[None, :] * inv_freq[:, None]
    return jnp.cos(angles), jnp.sin(angles)


def solution(mesh):
    assert mesh.shape['sp'] == N_DEV

    def layer_step(x_in, positions, d_out, norm1_gain, norm2_gain, w_q, w_k, w_v, w_o, w_gate, w_up, w_down):
        tokens, dim = x_in.shape
        seq = tokens * N_DEV
        n_q, hd = w_q.shape[1:]
        n_kv = w_k.shape[1]
        qw = n_q // N_DEV * hd
        rows = w_q.shape[0]
        feat = w_down.shape[0]
        cols = (n_q + 2 * n_kv) * hd
        lanes = qw // hd * QB
        vm = pltpu.VMEM
        full = vm((N_CHIP, WIDE, dim), BF16)
        gain_scr = vm((N_CHIP, dim), F32)
        small_shape = ((N_DEV, N_CHIP, rows), F32)

        small = jnp.stack([norm1_gain.astype(F32), norm2_gain.astype(F32), positions.astype(F32)])
        small = jnp.pad(small, ((0, N_CHIP - small.shape[0]), (0, 0)))
        cos_own, sin_own = rope_tables(positions, hd)
        wq_t = w_q.transpose(1, 2, 0).reshape(n_q * hd, rows)
        wkv_t = jnp.stack([w_k.transpose(1, 2, 0), w_v.transpose(1, 2, 0)], axis=1).reshape(2 * n_kv * hd, rows)
        wo_own = w_o.reshape(qw, dim)

        qkv, u_col, small_all, wqkv = call(
            functools.partial(project_qkv, n_kv, hd), 0, (x_in, small, jnp.concatenate([wq_t, wkv_t], axis=0), cos_own, sin_own),
            (((qw + 2 * hd, seq), BF16), ((seq, rows), BF16), small_shape, ((N_CHIP, cols, WIDE), BF16)),
            [vm((N_CHIP, cols, WIDE), BF16), vm((cols, tokens), F32), vm((cols, tokens), BF16), vm((tokens, dim), BF16), gain_scr, dma(N_CHIP),
             *Gather.sems, *(4 * Swap.sems)], 2 * tokens * dim * cols, far_out=(3,))
        attn_tok, attn_t, stat, wgu = call(
            functools.partial(attn_fwd, hd), 1, (qkv, w_gate.T, w_up.T),
            (((n_q * hd, tokens), BF16), ((qw, seq), BF16), ((seq // QB, 2, lanes), F32), ((2 * feat, dim), BF16)),
            [vm((seq, lanes), F32), vm((seq, hd), BF16), *(3 * Swap.sems)], 4 * qw * seq * seq)
        hidden, m_full, glu, dgu, d_down = call(
            mlp_local, 2, (attn_tok, wo_own, x_in, small_all, d_out, wgu, w_down),
            (((tokens, dim), BF16), ((N_CHIP, WIDE, dim), BF16), ((feat, seq), BF16), ((2 * feat, seq), BF16), ((feat, dim), F32)),
            [full, full, full, vm((tokens, dim), F32), vm((tokens, dim), BF16), gain_scr, dma(N_CHIP), *(3 * Gather.sems)],
            8 * feat * seq * dim, far_out=(1,))
        d_hidden, d_attn, d_wo, d_g2 = call(
            mlp_back, 3, (dgu, wgu, hidden, small_all, d_out, wo_own, attn_t),
            (((tokens, dim), BF16), ((qw, seq), BF16), ((qw, dim), F32), ((N_CHIP, dim), F32)),
            [full, gain_scr, *Scatter.scratch(tokens, dim), *Scatter.sems, *Gather.sems], 4 * feat * seq * dim)
        cos_all, sin_all = rope_tables(small_all[:, 2].reshape(-1), hd)
        dq_t, dkv, d_gate_t, d_up_t = call(
            functools.partial(attn_bwd, hd), 4, (qkv, d_attn, stat, cos_all, sin_all, dgu, m_full),
            (((qw, seq), BF16), ((seq, 2 * hd), BF16), ((feat * N_DEV, rows), F32), ((feat * N_DEV, rows), F32)),
            [vm((seq, lanes), F32), vm((seq, lanes), BF16), vm((seq, hd), BF16), vm((seq, hd), BF16), vm((seq, hd), F32), vm((seq, hd), F32),
             vm((N_CHIP, 2 * feat, WIDE), F32), *(2 * Swap.sems)], 10 * qw * seq * seq)
        d_wq, d_wkv, d_x, gains = call(
            functools.partial(tail, n_kv, hd), 5, (dq_t, dkv, u_col, cos_own, sin_own, wqkv, x_in, small_all, d_hidden, d_g2),
            (((n_q * hd, rows), F32), ((2 * n_kv * hd, rows), F32), ((tokens, dim), BF16), ((N_CHIP, rows), F32)),
            [full, vm((N_CHIP, cols, WIDE), BF16), vm((N_DEV, tokens, 2 * hd), BF16), vm((2 * n_kv * hd, tokens), BF16), vm((2 * n_kv * hd, seq), BF16),
             vm((cols, tokens), BF16), vm((tokens, dim), F32), gain_scr, gain_scr, gain_scr, vm((N_DEV, N_CHIP, rows), F32), dma(),
             *Swap.sems, *(2 * Gather.sems), *Swap.sems], 4 * tokens * dim * cols, far_in=(5,))
        y_out, = call(scatter_y, 6, (glu, w_down, hidden), (((tokens, dim), BF16),),
                      [*Scatter.scratch(tokens, dim), *Scatter.sems], 2 * feat * seq * dim)

        d_wkv = d_wkv.reshape(n_kv, 2, hd, rows).transpose(3, 0, 2, 1)
        return (y_out, d_x, gains[0], gains[1], d_wq.reshape(n_q, hd, rows).transpose(2, 0, 1), d_wkv[..., 0], d_wkv[..., 1],
                d_wo.reshape(w_o.shape), d_gate_t.T, d_up_t.T, d_down)

    all_rows = P('sp')
    return jax.shard_map(layer_step, mesh=mesh, in_specs=(all_rows,) * 12, out_specs=(all_rows,) * 11, check_vma=False)
```

time: 2540 us -> 577 us (0.23)
  waiting for transfers between devices: 2050 us -> 0 us
  Pallas kernels: 0 us -> 539 us
  matrix products: 268 us -> 0 us
  blocking collectives: 113 us -> 0 us
  other arithmetic: 53 us -> 7.5 us
    reduce_scatter x7 -> x0, waiting for transfers between devices: 1710 us -> none  [layer_step(): scatter_rows(grad_part)]
    pallas_call x0 -> x7, Pallas kernels: none -> 539 us  [call(): pl.pallas_call(kernel, out_shape=[jax.ShapeDtypeStruct(shape, dtype) for...]
    all_gather x7 -> x0, waiting for transfers between devices: 316 us -> none  [layer_step(): gather_rows(shard_w)]
    dot_general x21 -> x0, matrix products: 246 us -> none  [the longest x1 21.7 us: attention_backward(): jnp.einsum('skgd,tkd->kgst', d_attn, values_all, preferred_element_type=j...]
    all_to_all x4 -> x0, blocking collectives: 44.6 us -> none  [the longest x1 13.3 us: layer_step(): d_q_rot = to_tokens(d_q_seq.reshape(seq_len, -1, head_dim))]
    all_gather x2 -> x0, blocking collectives: 36.1 us -> none  [layer_step(): gather_rows(shard_w)]
    unnamed x1 -> x0, blocking collectives: 32.1 us -> none
  transfers between devices with their start and end apart: 18 -> 0, of which waited for: 13 -> 0; matrix products, arithmetic and copies ran while one was open for 9% -> 0% of each run, Pallas kernels for 0% -> 0%
where the time goes in v4:
time: 577 us; the launch traced here: 568 us
  Pallas kernels  539 us (93%)
  local copies, waits for them, and re-layouts  20.3 us (4%)
  other arithmetic  7.5 us (1%)
    pallas_call x7, Pallas kernels, call(): pl.pallas_call(kernel, out_shape=[jax.ShapeDtypeStruct(shape, dtype) for...  539 us
    unnamed x21, local copies, waits for them, and re-layouts  16.5 us

profile of v4, /device:TPU:0, one launch (start us, length us, event | category | flops | bytes accessed | tf_op | source)
XLA Modules:
  0.0 568.3 jit_solution(6457683485571185095)
XLA Ops:
  0.6 0.0 copy-start.2
  0.7 0.0 copy-start.3
  0.7 0.8 fusion
  1.5 0.7 bitcast_convert_fusion
  2.2 0.6 select_maximum_fusion.small_ref
  2.8 0.8 multiply_sine_fusion.1
  3.6 0.9 pad_maximum_fusion.1
  4.5 1.9 pad_maximum_fusion.w_ref
  6.4 0.0 copy-done.2
  6.4 1.5 copy.24
  7.9 0.0 copy-done.3
  7.9 1.5 copy.25
  9.4 67.6 %project_qkv.1 = (bf16[256,2048]{1,0:T(8,128)(2,1)}, bf16[2048,128]{1,0:T(8,128)(2,1)}, f32[16,8,128]{2,1,0:T(8,128)}, bf16[8,2560,256]{2,1,0:T(8,128)(2,1)}) custom-call(bf16[128,2048]{1,0:T(8,128)(2,1)} %x_ref.5, f32[8,128]{1,0:T(8,128)} %select_maximum_fusion.small_ref, bf16[2560,128]{1,0:T(8,128)(2,1)} %pad_maximum_fusion.w_ref, ...), custom_call_target="tpu_custom_call" | custom-call | flops 1342177280 | bytes 2621440 | tf_op jit(solution)/shard_map/project_qkv/pallas_call | solution.py:292
  77.1 0.8 slice.15
  77.9 1.8 multiply_sine_fusion
  79.7 50.2 %attn_fwd.1 = (bf16[2048,128]{1,0:T(8,128)(2,1)}, bf16[128,2048]{1,0:T(8,128)(2,1)}, f32[8,2,512]{2,1,0:T(2,128)}, bf16[704,2048]{1,0:T(8,128)(2,1)}) custom-call(bf16[256,2048]{1,0:T(8,128)(2,1)} %get-tuple-element.36.qkv_ref, bf16[5632,128]{1,0:T(8,128)(2,1)} %bitcast.42, bf16[5632,128]{1,0:T(8,128)(2,1)} %bitcast.43), custom_call_target="tpu_custom_call" | custom-call | flops 2147483648 | bytes 4194304 | tf_op jit(solution)/shard_map/attn_fwd/pallas_call | solution.py:292
  129.9 104.4 %mlp_local.1 = (bf16[128,2048]{1,0:T(8,128)(2,1)}, bf16[8,256,2048]{2,1,0:T(8,128)(2,1)}, bf16[352,2048]{1,0:T(8,128)(2,1)}, bf16[704,2048]{1,0:T(8,128)(2,1)}, f32[352,2048]{1,0:T(8,128)}) custom-call(bf16[2048,128]{1,0:T(8,128)(2,1)} %get-tuple-element.37.ot_ref, bf16[128,2048]{1,0:T(8,128)(2,1)} %bitcast.53, bf16[128,2048]{1,0:T(8,128)(2,1)} %x_ref.5, ...), custom_call_target="tpu_custom_call" | custom-call | flops 11811160064 | bytes 23068672 | tf_op jit(solution)/shard_map/mlp_local/pallas_call | solution.py:292
  234.4 102.5 %mlp_back.1 = (bf16[128,2048]{1,0:T(8,128)(2,1)}, bf16[128,2048]{1,0:T(8,128)(2,1)}, f32[128,2048]{1,0:T(8,128)}, f32[8,2048]{1,0:T(8,128)}) custom-call(bf16[704,2048]{1,0:T(8,128)(2,1)} %get-tuple-element.42.dgu_ref, bf16[704,2048]{1,0:T(8,128)(2,1)} %get-tuple-element.39.wgu_ref, bf16[128,2048]{1,0:T(8,128)(2,1)} %get-tuple-element.41.h_ref, ...), custom_call_target="tpu_custom_call" | custom-call | flops 5905580032 | bytes 11534336 | tf_op jit(solution)/shard_map/mlp_back/pallas_call | solution.py:292
  336.9 64.6 %scatter_y.1 = bf16[128,2048]{1,0:T(8,128)(2,1)} custom-call(bf16[352,2048]{1,0:T(8,128)(2,1)} %get-tuple-element.40.a_ref, bf16[352,2048]{1,0:T(8,128)(2,1)} %w_ref.1, bf16[128,2048]{1,0:T(8,128)(2,1)} %get-tuple-element.41.h_ref), custom_call_target="tpu_custom_call" | custom-call | flops 2952790016 | bytes 5767168 | tf_op jit(solution)/shard_map/scatter_y/pallas_call | solution.py:292
  401.5 91.2 %attn_bwd.1 = (bf16[128,2048]{1,0:T(8,128)(2,1)}, bf16[2048,128]{1,0:T(8,128)(2,1)}, f32[5632,128]{1,0:T(8,128)}, f32[5632,128]{1,0:T(8,128)}) custom-call(bf16[256,2048]{1,0:T(8,128)(2,1)} %get-tuple-element.36.qkv_ref, bf16[128,2048]{1,0:T(8,128)(2,1)} %get-tuple-element.44.do_ref, f32[8,2,512]{2,1,0:T(2,128)} %get-tuple-element.45.stat_ref, ...), custom_call_target="tpu_custom_call" | custom-call | flops 5368709120 | bytes 10485760 | tf_op jit(solution)/shard_map/attn_bwd/pallas_call | solution.py:292
  492.7 58.8 %tail.1 = (f32[2048,128]{1,0:T(8,128)}, f32[512,128]{1,0:T(8,128)}, bf16[128,2048]{1,0:T(8,128)(2,1)}, f32[8,128]{1,0:T(8,128)}) custom-call(bf16[128,2048]{1,0:T(8,128)(2,1)} %get-tuple-element.47.dq_ref, bf16[2048,128]{1,0:T(8,128)(2,1)} %get-tuple-element.48.dkv_ref, bf16[2048,128]{1,0:T(8,128)(2,1)} %get-tuple-element.49.ucol_ref, ...), custom_call_target="tpu_custom_call" | custom-call | flops 2684354560 | bytes 5242880 | tf_op jit(solution)/shard_map/tail/pallas_call | solution.py:292
  551.5 1.3 slice_bitcast_fusion.2
  552.8 1.0 copy.30
  553.7 0.7 slice_bitcast_fusion
  554.4 0.0 copy-start.1
  554.4 3.5 copy.27
  558.0 0.0 copy-done.1
  558.0 0.0 copy-start.5
  558.0 2.2 copy.28
  560.2 0.0 copy-done.5
  560.2 0.0 copy-start.4
  560.2 0.8 copy.36
  561.0 0.0 copy-start
  561.0 2.0 copy.37
  563.0 2.3 copy.38
  565.3 0.0 copy-done.4
  565.3 1.0 copy.39
  566.3 0.0 copy-done
  566.3 1.6 copy.40
  (2 shorter events, 0.0 us)
Async XLA Ops:
  0.6 5.7 %copy-start.2 = (bf16[128,5632]{1,0:T(8,128)(2,1)S(1)}, bf16[128,5632]{1,0:T(8,128)(2,1)}, u32[]{:S(2)}) copy-start(bf16[128,5632]{1,0:T(8,128)(2,1)} %param.21) | copy-start | bytes 4325380
  0.7 7.3 %copy-start.3 = (bf16[128,5632]{1,0:T(8,128)(2,1)S(1)}, bf16[128,5632]{1,0:T(8,128)(2,1)}, u32[]{:S(2)}) copy-start(bf16[128,5632]{1,0:T(8,128)(2,1)} %param.22) | copy-start | bytes 4325380
  554.4 3.5 copy-start.1
  558.0 2.2 copy-start.5
  560.2 5.1 copy-start.4
  561.0 5.3 copy-start

commit v5 on v4

--- a/solution.py
+++ b/solution.py
@@ -24,6 +24,7 @@
 CHIP_MASKS = (0, X, Y, Z, X + Y, X + Z, Y + Z, XYZ)
 NEAR = (CORE, X, Y, Z)
 OTHERS = range(1, N_DEV)
+SETS = tuple(tuple(m + c for m in masks for c in (0, CORE)) for masks in ((XYZ,), (X, Y + Z), (Y, X + Z), (Z, X + Y)))
 COLOURS = range(len(ORDERS))
 
 
@@ -47,6 +48,10 @@
     return out
 
 
+def other_chip(chip, k):
+    return sum(((chip // b + k // b) % 2) * b for b in (1, 2, 4))
+
+
 def thirds(total, unit):
     n = total // unit
     first = (n + 2) // 3
@@ -84,13 +89,19 @@
         for mask in masks:
             self.copy(mask).start()
 
+    def advance(self, n):
+        if n:
+            for mask in SETS[n - 1]:
+                self.copy(mask).wait_send()
+        self.start(SETS[n])
+
     def wait_recv(self):
         for mask in OTHERS:
             view = self.dst(flipped(self.me, mask))
             remote(view, view, self.send.at[mask], self.recv.at[mask], self.me).wait_recv()
 
-    def wait_send(self):
-        for mask in OTHERS:
+    def wait_send(self, masks=OTHERS):
+        for mask in masks:
             self.copy(mask).wait_send()
 
 
@@ -327,14 +338,38 @@
     loop(src.shape[0] // STRIP, step)
 
 
-def project_qkv(groups, hd, x_ref, small_ref, w_ref, cos_ref, sin_ref, qkv_ref, ucol_ref, small_all, w_out,
-                full, acc, rot, u_scr, g_scr, osem, *sems):
+QB = 256
+KB = 256
+
+
+def key_rows(dst, src, lo, hd):
+    def step(i):
+        dst[seg(i, KB), :] = src[lo:lo + hd, seg(i, KB)].T
+    loop(src.shape[1] // KB, step)
+
+
+def score_block(k, q2, scale, diagonal):
+    s = mm(k, q2, NN) * scale
+    if diagonal:
+        key = lax.broadcasted_iota(jnp.int32, s.shape, 0)
+        qry = lax.broadcasted_iota(jnp.int32, s.shape, 1) % QB
+        s = jnp.where(qry >= key, s, NEG_LARGE)
+    return s
+
+
+def side_by_side(ref, heads, hd, qs):
+    return jnp.concatenate([ref[h * hd:(h + 1) * hd, qs] for h in range(heads)], axis=1)
+
+
+def head(groups, hd, x_ref, small_ref, w_ref, cos_ref, sin_ref, wg_ref, wu_ref, qkv_ref, ucol_ref, small_all, w_out, ot_ref, o_ref, stat_ref, wgu_ref,
+         full, acc, rot, u_scr, g_scr, wg_t, wu_t, s_scr, k_scr, osem, *sems):
     me = lax.axis_index('sp')
     tokens, dim = x_ref.shape
     cols = w_ref.shape[0]
     qw = tokens
     q_all = N_DEV * qw
-    gsems, ssems, usems, qsems, ksems = sems[:4], sems[4:6], sems[6:8], sems[8:10], sems[10:]
+    gsems, ssems, usems, qsems, ksems, gate_sems, up_sems, (osend, orecv) = sems[:4], *(sems[i:i + 2] for i in range(4, len(sems), 2))
+    feat = wg_ref.shape[1] // N_DEV
     enter(me, OTHERS)
     smalls = Swap(lambda peer: small_ref, lambda o: small_all.at[o], ssems, me)
     smalls.start()
@@ -350,6 +385,14 @@
     smalls.wait_recv()
     gain_row(g_scr, small_all, 0)
     norm_rows(x_ref, g_scr, u_scr)
+    gates = Swap(lambda peer: wg_t.at[seg(peer, feat), :], lambda o: wgu_ref.at[:feat, seg(o)], gate_sems, me)
+    ups = Swap(lambda peer: wu_t.at[seg(peer, feat), :], lambda o: wgu_ref.at[feat:, seg(o)], up_sems, me)
+    turns = wg_ref.shape[1] // LANE // 4
+
+    def transpose(i):
+        wg_t[seg(i), :] = wg_ref[:, seg(i)].T
+        wu_t[seg(i), :] = wu_ref[:, seg(i)].T
+
     ucols = Swap(lambda peer: u_scr.at[:, seg(peer)], lambda o: ucol_ref.at[seg(o, tokens), :], usems, me)
 
     def keep(mask):
@@ -369,8 +412,11 @@
 
     for r in range(len(g.ROUNDS)):
         g.round(r)
-        if r == 0:
-            ucols.start()
+        if r < 4:
+            loop(turns, lambda i: transpose(turns * r + i))
+        if r == 5:
+            gates.advance(0)
+            ups.advance(0)
         for mask in g.READY[r]:
             use(mask)
 
@@ -399,60 +445,30 @@
     qkv_ref[:qw, seg(me, tokens)] = rot[q_rows(me), :]
     qkv_ref[qw:, seg(me, tokens)] = rot[kv_rows(me), :]
     ucol_ref[seg(me, tokens), :] = u_scr[:, seg(me)]
-    for swap in (ucols, qs, kvs):
+    wgu_ref[:feat, seg(me)] = wg_t[seg(me, feat), :]
+    wgu_ref[feat:, seg(me)] = wu_t[seg(me, feat), :]
+    gates.start((CORE,))
+    ups.start((CORE,))
+    for swap in (qs, kvs):
         swap.wait_recv()
-    for mask in CHIP_MASKS:
-        keep(mask).wait()
-    g.finish()
-    for swap in (smalls, ucols, qs, kvs):
-        swap.wait_send()
-
-
-QB = 256
-KB = 256
-
-
-def key_rows(dst, src, lo, hd):
-    def step(i):
-        dst[seg(i, KB), :] = src[lo:lo + hd, seg(i, KB)].T
-    loop(src.shape[1] // KB, step)
-
-
-def score_block(k, q2, scale, diagonal):
-    s = mm(k, q2, NN) * scale
-    if diagonal:
-        key = lax.broadcasted_iota(jnp.int32, s.shape, 0)
-        qry = lax.broadcasted_iota(jnp.int32, s.shape, 1) % QB
-        s = jnp.where(qry >= key, s, NEG_LARGE)
-    return s
-
-
-def side_by_side(ref, heads, hd, qs):
-    return jnp.concatenate([ref[h * hd:(h + 1) * hd, qs] for h in range(heads)], axis=1)
-
-
-def attn_fwd(hd, qkv_ref, wg_ref, wu_ref, ot_ref, o_ref, stat_ref, w_ref, s_scr, k_scr, *sems):
+    gates.advance(1)
+    ups.advance(1)
     heads = qkv_ref.shape[0] // hd - 2
     seq = qkv_ref.shape[1]
     scale = hd ** -0.5
     lanes = heads * QB
-    me = lax.axis_index('sp')
-    qw = heads * hd
-    feat = wg_ref.shape[0] // N_DEV
-    enter(me, OTHERS)
-    gates = Swap(lambda peer: wg_ref.at[seg(peer, feat), :], lambda o: w_ref.at[:feat, seg(o)], sems[:2], me)
-    ups = Swap(lambda peer: wu_ref.at[seg(peer, feat), :], lambda o: w_ref.at[feat:, seg(o)], sems[2:4], me)
-    osend, orecv = sems[4:]
-    gates.start()
-    ups.start()
-    w_ref[:feat, seg(me)] = wg_ref[seg(me, feat), :]
-    w_ref[feat:, seg(me)] = wu_ref[seg(me, feat), :]
     key_rows(k_scr, qkv_ref, qw, hd)
 
     def o_copy(peer, origin):
         return remote(o_ref.at[:, seg(peer)], ot_ref.at[seg(origin, qw), :], osend.at[peer], orecv.at[origin], peer)
 
-    def q_block(qb):
+    def q_block(i):
+        qb = other_chip(me // 2, N_CHIP - 1 - i)
+        for at, n in ((3, 2), (6, 3)):
+            @pl.when(i == at)
+            def _():
+                gates.advance(n)
+                ups.advance(n)
         qs = seg(qb, QB)
         q2 = side_by_side(qkv_ref, heads, hd, qs)
 
@@ -491,12 +507,18 @@
     ot_ref[seg(me, qw), :] = o_ref[:, seg(me)]
     for mask in OTHERS:
         o_copy(me, flipped(me, mask)).wait_recv()
-    gates.wait_recv()
-    ups.wait_recv()
+    ucols.start()
+    for swap in (gates, ups, ucols):
+        swap.wait_recv()
+    for mask in CHIP_MASKS:
+        keep(mask).wait()
     for mask in OTHERS:
         o_copy(flipped(me, mask), me).wait_send()
-    gates.wait_send()
-    ups.wait_send()
+    for swap in (gates, ups):
+        swap.wait_send((CORE,) + SETS[3])
+    g.finish()
+    for swap in (smalls, ucols, qs, kvs):
+        swap.wait_send()
 
 
 def mlp_local(ot_ref, wo_ref, x_ref, small_all, dout_ref, wgu_ref, down_ref, h_ref, m_out, glu_ref, dgu_ref, ddown_ref,
@@ -614,8 +636,10 @@
     g.finish()
 
 
-def attn_bwd(hd, qkv_ref, do_ref, stat_ref, cos_ref, sin_ref, dgu_ref, m_ref, dq_ref, dkv_ref, dg_ref, du_ref,
-             p_scr, dp_scr, k_scr, v_scr, dk_acc, dv_acc, stage, *sems):
+def back(groups, hd, qkv_ref, do_ref, stat_ref, cos_all, sin_all, dgu_ref, m_ref, ucol_ref, cos_ref, sin_ref, w_hbm, x_ref, small_all, dh_ref, dg2_ref,
+         dg_hbm, du_hbm, dwq_ref, dwkv_ref, dx_ref, gain_ref,
+         p_scr, dp_scr, k_scr, v_scr, dk_acc, dv_acc, stage, dq_scr, dkv_scr,
+         full, w_scr, shares, dkv_own, full_kv, dqkv, dn, g_scr, dg1, gains, gains_in, wsem, lsem, *sems):
     heads = qkv_ref.shape[0] // hd - 2
     seq = qkv_ref.shape[1]
     scale = hd ** -0.5
@@ -625,19 +649,34 @@
     me = lax.axis_index('sp')
     feat = dgu_ref.shape[0] // 2
     enter(me, OTHERS)
+    load = pltpu.make_async_copy(w_hbm, w_scr, wsem)
+    load.start()
+    gain_row(g_scr, small_all, 0)
 
     def piece(lo):
         return lambda peer: stage.at[peer // 2, lo:lo + feat, seg(peer % 2)]
-    gates = Swap(piece(0), lambda o: dg_ref.at[seg(o, feat), :], sems[:2], me)
-    ups = Swap(piece(feat), lambda o: du_ref.at[seg(o, feat), :], sems[2:], me)
-    for mask in (XYZ, X + Y, X + Z, Y + Z, X, Y, Z, 0):
+    gates = Swap(piece(0), lambda o: dg_hbm.at[seg(o, feat), :], sems[:2], me)
+    ups = Swap(piece(feat), lambda o: du_hbm.at[seg(o, feat), :], sems[2:4], me)
+    own = [pltpu.make_async_copy(swap.src(me), swap.dst(me), lsem.at[i]) for i, swap in enumerate((gates, ups))]
+
+    def make(mask):
         chip = flipped(me, mask) // 2
         cols = m_ref[:, :, seg(chip, WIDE)].reshape(seq, WIDE)
         stage[chip] = mm(dgu_ref[...], cols, NN)
-        for swap in (gates, ups):
-            swap.start([m for m in (mask, mask + CORE) if m])
-    dg_ref[seg(me, feat), :] = stage[me // 2, :feat, seg(me % 2)]
-    du_ref[seg(me, feat), :] = stage[me // 2, feat:, seg(me % 2)]
+
+    def advance(n):
+        gates.advance(n)
+        ups.advance(n)
+
+    make(XYZ)
+    make(X)
+    advance(0)
+    for mask in (Y + Z, Y, X + Z, Z, X + Y, 0):
+        make(mask)
+    gates.start((CORE,))
+    ups.start((CORE,))
+    for copy in own:
+        copy.start()
 
     dk_acc[...] = jnp.zeros_like(dk_acc)
     dv_acc[...] = jnp.zeros_like(dv_acc)
@@ -645,6 +684,10 @@
     key_rows(v_scr, qkv_ref, qw + hd, hd)
 
     def q_block(qb):
+        for at, n in ((4, 1), (7, 2)):
+            @pl.when(qb == at)
+            def _():
+                advance(n)
         qs = seg(qb, QB)
         q2 = side_by_side(qkv_ref, heads, hd, qs)
         do2 = side_by_side(do_ref, heads, hd, qs)
@@ -671,45 +714,31 @@
             return acc + mm(qkv_ref[qw:qw + hd, ks], ds, NN)
 
         acc = lax.fori_loop(0, qb + 1, d_scores, jnp.zeros((hd, lanes), F32))
-        cos, sin = cos_ref[:, qs], sin_ref[:, qs]
+        cos, sin = cos_all[:, qs], sin_all[:, qs]
         for h in range(heads):
             dq = acc[:, h * QB:(h + 1) * QB].astype(BF16).astype(F32)
             p, q = dq[:half], dq[half:]
-            dq_ref[h * hd:h * hd + half, qs] = (p * cos + q * sin).astype(BF16)
-            dq_ref[h * hd + half:(h + 1) * hd, qs] = (q * cos - p * sin).astype(BF16)
+            dq_scr[h * hd:h * hd + half, qs] = (p * cos + q * sin).astype(BF16)
+            dq_scr[h * hd + half:(h + 1) * hd, qs] = (q * cos - p * sin).astype(BF16)
 
     loop(seq // QB, q_block)
 
     def share(i):
         rs = seg(i, WIDE)
-        dkv_ref[rs, :] = jnp.concatenate([dk_acc[rs, :], dv_acc[rs, :]], axis=1).astype(BF16)
+        dkv_scr[rs, :] = jnp.concatenate([dk_acc[rs, :], dv_acc[rs, :]], axis=1).astype(BF16)
     loop(seq // WIDE, share)
-    for swap in (gates, ups):
-        swap.wait_recv()
-    for swap in (gates, ups):
-        swap.wait_send()
-
-
-def tail(groups, hd, dq_ref, dkv_ref, ucol_ref, cos_ref, sin_ref, w_hbm, x_ref, small_all, dh_ref, dg2_ref,
-         dwq_ref, dwkv_ref, dx_ref, gain_ref, full, w_scr, shares, dkv_own, full_kv, dqkv, dn, g_scr, dg1, gains, gains_in, wsem, *sems):
-    me = lax.axis_index('sp')
-    seq, tokens = ucol_ref.shape
-    half = hd // 2
+    tokens = ucol_ref.shape[1]
     per = N_DEV // groups
     q_all = dwq_ref.shape[0]
-    enter(me, OTHERS)
-    load = pltpu.make_async_copy(w_hbm, w_scr, wsem)
-    load.start()
-    sh = Swap(lambda peer: dkv_ref.at[seg(peer, tokens), :], lambda o: shares.at[o], sems[:2], me)
-    gq = row_gather(dq_ref, full, sems[2:6], me)
+    sh = Swap(lambda peer: dkv_scr.at[seg(peer, tokens), :], lambda o: shares.at[o], sems[4:6], me)
+    gq = row_gather(dq_scr, full, sems[6:10], me)
     parts = thirds(dkv_own.shape[0], STRIP)
-    gk = Gather(dkv_own, lambda o: full_kv.at[:, seg(o, tokens)], lambda view, c: view.at[pl.ds(*parts[c]), :], sems[6:10], me)
-    gs = Swap(lambda peer: gains.at[:, seg(peer)], lambda o: gains_in.at[o], sems[10:], me)
+    gk = Gather(dkv_own, lambda o: full_kv.at[:, seg(o, tokens)], lambda view, c: view.at[pl.ds(*parts[c]), :], sems[10:14], me)
+    gs = Swap(lambda peer: gains.at[:, seg(peer)], lambda o: gains_in.at[o], sems[14:], me)
     sh.start()
     gq.start()
-    keep_own(dq_ref, full, me)
-    gain_row(g_scr, small_all, 0)
-    shares[me] = dkv_ref[seg(me, tokens), :]
+    keep_own(dq_scr, full, me)
+    shares[me] = dkv_scr[seg(me, tokens), :]
     sh.wait_recv()
     cos, sin = cos_ref[...], sin_ref[...]
     for k in range(groups):
@@ -732,6 +761,8 @@
     for r in range(len(gq.ROUNDS)):
         gq.round(r)
         gk.round(r)
+        if r == 3:
+            advance(3)
         for mask in gq.READY[r]:
             use(mask)
     load.wait()
@@ -749,6 +780,11 @@
     dwkv_ref[...] = mm(full_kv[...], ucol_ref[...], NN)
     gs.wait_recv()
     gain_ref[...] = sum(gains_in[o] for o in range(N_DEV))
+    for swap in (gates, ups):
+        swap.wait_recv()
+        swap.wait_send((CORE,) + SETS[3])
+    for copy in own:
+        copy.wait()
     for c in (sh, gs):
         c.wait_send()
     for g in (gq, gk):
@@ -787,15 +823,14 @@
         wkv_t = jnp.stack([w_k.transpose(1, 2, 0), w_v.transpose(1, 2, 0)], axis=1).reshape(2 * n_kv * hd, rows)
         wo_own = w_o.reshape(qw, dim)
 
-        qkv, u_col, small_all, wqkv = call(
-            functools.partial(project_qkv, n_kv, hd), 0, (x_in, small, jnp.concatenate([wq_t, wkv_t], axis=0), cos_own, sin_own),
-            (((qw + 2 * hd, seq), BF16), ((seq, rows), BF16), small_shape, ((N_CHIP, cols, WIDE), BF16)),
-            [vm((N_CHIP, cols, WIDE), BF16), vm((cols, tokens), F32), vm((cols, tokens), BF16), vm((tokens, dim), BF16), gain_scr, dma(N_CHIP),
-             *Gather.sems, *(4 * Swap.sems)], 2 * tokens * dim * cols, far_out=(3,))
-        attn_tok, attn_t, stat, wgu = call(
-            functools.partial(attn_fwd, hd), 1, (qkv, w_gate.T, w_up.T),
-            (((n_q * hd, tokens), BF16), ((qw, seq), BF16), ((seq // QB, 2, lanes), F32), ((2 * feat, dim), BF16)),
-            [vm((seq, lanes), F32), vm((seq, hd), BF16), *(3 * Swap.sems)], 4 * qw * seq * seq)
+        qkv, u_col, small_all, wqkv, attn_tok, attn_t, stat, wgu = call(
+            functools.partial(head, n_kv, hd), 0,
+            (x_in, small, jnp.concatenate([wq_t, wkv_t], axis=0), cos_own, sin_own, w_gate, w_up),
+            (((qw + 2 * hd, seq), BF16), ((seq, rows), BF16), small_shape, ((N_CHIP, cols, WIDE), BF16),
+             ((n_q * hd, tokens), BF16), ((qw, seq), BF16), ((seq // QB, 2, lanes), F32), ((2 * feat, dim), BF16)),
+            [vm((N_CHIP, cols, WIDE), BF16), vm((cols, tokens), F32), vm((cols, tokens), BF16), vm((tokens, dim), BF16), gain_scr,
+             vm((feat * N_DEV, rows), BF16), vm((feat * N_DEV, rows), BF16), vm((seq, lanes), F32), vm((seq, hd), BF16), dma(N_CHIP),
+             *Gather.sems, *(7 * Swap.sems)], 4 * qw * seq * seq, far_out=(3,))
         hidden, m_full, glu, dgu, d_down = call(
             mlp_local, 2, (attn_tok, wo_own, x_in, small_all, d_out, wgu, w_down),
             (((tokens, dim), BF16), ((N_CHIP, WIDE, dim), BF16), ((feat, seq), BF16), ((2 * feat, seq), BF16), ((feat, dim), F32)),
@@ -806,18 +841,17 @@
             (((tokens, dim), BF16), ((qw, seq), BF16), ((qw, dim), F32), ((N_CHIP, dim), F32)),
             [full, gain_scr, *Scatter.scratch(tokens, dim), *Scatter.sems, *Gather.sems], 4 * feat * seq * dim)
         cos_all, sin_all = rope_tables(small_all[:, 2].reshape(-1), hd)
-        dq_t, dkv, d_gate_t, d_up_t = call(
-            functools.partial(attn_bwd, hd), 4, (qkv, d_attn, stat, cos_all, sin_all, dgu, m_full),
-            (((qw, seq), BF16), ((seq, 2 * hd), BF16), ((feat * N_DEV, rows), F32), ((feat * N_DEV, rows), F32)),
+        d_gate_t, d_up_t, d_wq, d_wkv, d_x, gains = call(
+            functools.partial(back, n_kv, hd), 4,
+            (qkv, d_attn, stat, cos_all, sin_all, dgu, m_full, u_col, cos_own, sin_own, wqkv, x_in, small_all, d_hidden, d_g2),
+            (((feat * N_DEV, rows), F32), ((feat * N_DEV, rows), F32),
+             ((n_q * hd, rows), F32), ((2 * n_kv * hd, rows), F32), ((tokens, dim), BF16), ((N_CHIP, rows), F32)),
             [vm((seq, lanes), F32), vm((seq, lanes), BF16), vm((seq, hd), BF16), vm((seq, hd), BF16), vm((seq, hd), F32), vm((seq, hd), F32),
-             vm((N_CHIP, 2 * feat, WIDE), F32), *(2 * Swap.sems)], 10 * qw * seq * seq)
-        d_wq, d_wkv, d_x, gains = call(
-            functools.partial(tail, n_kv, hd), 5, (dq_t, dkv, u_col, cos_own, sin_own, wqkv, x_in, small_all, d_hidden, d_g2),
-            (((n_q * hd, rows), F32), ((2 * n_kv * hd, rows), F32), ((tokens, dim), BF16), ((N_CHIP, rows), F32)),
-            [full, vm((N_CHIP, cols, WIDE), BF16), vm((N_DEV, tokens, 2 * hd), BF16), vm((2 * n_kv * hd, tokens), BF16), vm((2 * n_kv * hd, seq), BF16),
-             vm((cols, tokens), BF16), vm((tokens, dim), F32), gain_scr, gain_scr, gain_scr, vm((N_DEV, N_CHIP, rows), F32), dma(),
-             *Swap.sems, *(2 * Gather.sems), *Swap.sems], 4 * tokens * dim * cols, far_in=(5,))
-        y_out, = call(scatter_y, 6, (glu, w_down, hidden), (((tokens, dim), BF16),),
+             vm((N_CHIP, 2 * feat, WIDE), F32), vm((qw, seq), BF16), vm((seq, 2 * hd), BF16),
+             full, vm((N_CHIP, cols, WIDE), BF16), vm((N_DEV, tokens, 2 * hd), BF16), vm((2 * n_kv * hd, tokens), BF16), vm((2 * n_kv * hd, seq), BF16),
+             vm((cols, tokens), BF16), vm((tokens, dim), F32), gain_scr, gain_scr, gain_scr, vm((N_DEV, N_CHIP, rows), F32), dma(), dma(2),
+             *(3 * Swap.sems), *(2 * Gather.sems), *Swap.sems], 10 * qw * seq * seq, far_in=(10,), far_out=(0, 1))
+        y_out, = call(scatter_y, 5, (glu, w_down, hidden), (((tokens, dim), BF16),),
                       [*Scatter.scratch(tokens, dim), *Scatter.sems], 2 * feat * seq * dim)
 
         d_wkv = d_wkv.reshape(n_kv, 2, hd, rows).transpose(3, 0, 2, 1)

time: 577 us -> 559 us (0.969)
  Pallas kernels: 539 us -> 529 us
    pallas_call x7 -> x5, Pallas kernels: 539 us -> 529 us  [call(): pl.pallas_call(kernel, out_shape=[jax.ShapeDtypeStruct(shape, dtype) for...]
    unnamed x21 -> x15, local copies, waits for them, and re-layouts: 16.5 us -> 13.4 us
where the time goes in v5:
time: 559 us; the launch traced here: 555 us
  Pallas kernels  529 us (95%)
  local copies, waits for them, and re-layouts  17.2 us (3%)
  other arithmetic  7.32 us (1%)
    pallas_call x5, Pallas kernels, call(): pl.pallas_call(kernel, out_shape=[jax.ShapeDtypeStruct(shape, dtype) for...  529 us
    unnamed x15, local copies, waits for them, and re-layouts  13.4 us

profile of v5, /device:TPU:0, one launch (start us, length us, event | category | flops | bytes accessed | tf_op | source)
XLA Modules:
  0.0 554.6 jit_solution(9255593092157085480)
XLA Ops:
  0.6 0.7 fusion
  1.3 0.7 bitcast_convert_fusion
  2.0 0.6 select_maximum_fusion.small_ref
  2.6 0.9 pad_maximum_fusion.1
  3.5 1.9 pad_maximum_fusion.w_ref
  5.4 0.8 multiply_sine_fusion.1
  6.2 123.5 %head.1 = (bf16[256,2048]{1,0:T(8,128)(2,1)}, bf16[2048,128]{1,0:T(8,128)(2,1)}, f32[16,8,128]{2,1,0:T(8,128)}, bf16[8,2560,256]{2,1,0:T(8,128)(2,1)}, bf16[2048...) custom-call(bf16[128,2048]{1,0:T(8,128)(2,1)} %x_ref.5, ...), custom_call_target="tpu_custom_call" | custom-call | flops 2147483648 | bytes 4194304 | tf_op jit(solution)/shard_map/head/pallas_call | solution.py:303
  129.7 110.5 %mlp_local.1 = (bf16[128,2048]{1,0:T(8,128)(2,1)}, bf16[8,256,2048]{2,1,0:T(8,128)(2,1)}, bf16[352,2048]{1,0:T(8,128)(2,1)}, bf16[704,2048]{1,0:T(8,128)(2,1)}, f32[352,2048]{1,0:T(8,128)}) custom-call(bf16[2048,128]{1,0:T(8,128)(2,1)} %get-tuple-element.34.ot_ref, bf16[128,2048]{1,0:T(8,128)(2,1)} %bitcast.49, bf16[128,2048]{1,0:T(8,128)(2,1)} %x_ref.5, ...), custom_call_target="tpu_custom_call" | custom-call | flops 11811160064 | bytes 23068672 | tf_op jit(solution)/shard_map/mlp_local/pallas_call | solution.py:303
  240.2 64.5 %scatter_y.1 = bf16[128,2048]{1,0:T(8,128)(2,1)} custom-call(bf16[352,2048]{1,0:T(8,128)(2,1)} %get-tuple-element.37.a_ref, bf16[352,2048]{1,0:T(8,128)(2,1)} %w_ref.1, bf16[128,2048]{1,0:T(8,128)(2,1)} %get-tuple-element.38.h_ref), custom_call_target="tpu_custom_call" | custom-call | flops 2952790016 | bytes 5767168 | tf_op jit(solution)/shard_map/scatter_y/pallas_call | solution.py:303
  304.7 103.4 %mlp_back.1 = (bf16[128,2048]{1,0:T(8,128)(2,1)}, bf16[128,2048]{1,0:T(8,128)(2,1)}, f32[128,2048]{1,0:T(8,128)}, f32[8,2048]{1,0:T(8,128)}) custom-call(bf16[704,2048]{1,0:T(8,128)(2,1)} %get-tuple-element.40.dgu_ref, bf16[704,2048]{1,0:T(8,128)(2,1)} %get-tuple-element.36.wgu_ref, bf16[128,2048]{1,0:T(8,128)(2,1)} %get-tuple-element.38.h_ref, ...), custom_call_target="tpu_custom_call" | custom-call | flops 5905580032 | bytes 11534336 | tf_op jit(solution)/shard_map/mlp_back/pallas_call | solution.py:303
  408.1 0.8 slice.15
  409.0 1.8 multiply_sine_fusion
  410.8 127.1 %back.1 = (f32[5632,128]{1,0:T(8,128)}, f32[5632,128]{1,0:T(8,128)}, f32[2048,128]{1,0:T(8,128)}, f32[512,128]{1,0:T(8,128)}, bf16[128,2048]{1,0:T(8,128)(2,1)}, /*index=5*/f32[8,128]{1,0:T(8,128)}) custom-call(bf16[256,2048]{1,0:T(8,128)(2,1)} %get-tuple-element.39.qkv_ref, bf16[128,2048]{1,0:T(8,128)(2,1)} %get-tuple-element.42.do_ref, ...), custom_call_target="tpu_custom_call" | custom-call | flops 5368709120 | bytes 10485760 | tf_op jit(solution)/shard_map/back/pallas_call | solution.py:303
  537.9 1.3 slice_bitcast_fusion.2
  539.1 1.0 copy.28
  540.1 0.7 slice_bitcast_fusion
  540.8 0.0 copy-start.1
  540.8 3.5 copy.25
  544.4 0.0 copy-done.1
  544.4 0.0 copy-start.3
  544.4 2.2 copy.26
  546.6 0.0 copy-start.2
  546.6 0.0 copy-done.3
  546.6 0.8 copy.34
  547.4 0.0 copy-start
  547.4 2.0 copy.35
  549.4 2.3 copy.36
  551.7 0.0 copy-done.2
  551.7 1.0 copy.37
  552.7 0.0 copy-done
  552.7 1.6 copy.38
  (2 shorter events, 0.0 us)
Async XLA Ops:
  540.8 3.5 copy-start.1
  544.4 2.2 copy-start.3
  546.6 5.1 copy-start.2
  547.4 5.3 copy-start

commit v6 on v5

--- a/solution.py
+++ b/solution.py
@@ -48,10 +48,6 @@
     return out
 
 
-def other_chip(chip, k):
-    return sum(((chip // b + k // b) % 2) * b for b in (1, 2, 4))
-
-
 def thirds(total, unit):
     n = total // unit
     first = (n + 2) // 3
@@ -60,6 +56,13 @@
     return ((0, sizes[0]), (sizes[0], sizes[1]), (sizes[0] + sizes[1], sizes[2]))
 
 
+def pieces(rows, cols, unit):
+    share = cols // LANE // 3 * LANE
+    strips = thirds(rows, unit)
+    rest = cols - 3 * share
+    return [[(pl.ds(0, rows), pl.ds(c * share, share)), (pl.ds(*strips[c]), pl.ds(3 * share, rest))] for c in COLOURS]
+
+
 def enter(me, masks):
     barrier = pltpu.get_barrier_semaphore()
     for mask in masks:
@@ -107,8 +110,8 @@
 
 class Gather:
     ROUNDS = ((0,), (1,), (2,), (0, 1), (0, 2), (1, 2), (0, 1, 2))
-    READY = ((0,), (), (), (X,), (Y,), (Z, X + Y), (X + Z, Y + Z, XYZ))
-    sems = (dma(3, N_CHIP, 3), dma(3, N_CHIP), dma(N_CHIP), dma(N_CHIP))
+    READY = ((0,), (), (), (X, Y), (Z,), (X + Y, X + Z), (Y + Z, XYZ))
+    sems = (dma(3, N_CHIP, 3, 2), dma(3, N_CHIP, 2), dma(N_CHIP), dma(N_CHIP))
 
     def __init__(self, own, block, cut, sems, me):
         self.own, self.block, self.cut, self.me = own, block, cut, me
@@ -118,9 +121,13 @@
         return self.block(flipped(self.me, mask)) if mask else self.own
 
     def unit(self, colour, mask, axis):
-        return remote(self.cut(self.source(mask), colour), self.cut(self.block(flipped(self.me, mask)), colour),
-                      self.send.at[colour, mask // 2, ORDERS[colour].index(axis)], self.recv.at[colour, (mask + axis) // 2],
-                      flipped(self.me, axis))
+        ends = zip(self.cut(self.source(mask), colour), self.cut(self.block(flipped(self.me, mask)), colour))
+        return [remote(src, dst, self.send.at[colour, mask // 2, ORDERS[colour].index(axis), i], self.recv.at[colour, (mask + axis) // 2, i],
+                       flipped(self.me, axis)) for i, (src, dst) in enumerate(ends)]
+
+    def start_unit(self, colour, mask, axis):
+        for copy in self.unit(colour, mask, axis):
+            copy.start()
 
     def pair(self, mask):
         return remote(self.source(mask), self.block(flipped(self.me, mask)), self.pair_send.at[mask // 2],
@@ -139,45 +146,41 @@
     def start(self):
         for pos in COLOURS:
             for colour in COLOURS:
-                self.unit(colour, 0, ORDERS[colour][pos]).start()
+                self.start_unit(colour, 0, ORDERS[colour][pos])
         self.pair(0).start()
 
     def round(self, r):
         for colour in COLOURS:
             mask = sum(ORDERS[colour][p] for p in self.ROUNDS[r])
-            view = self.cut(self.block(flipped(self.me, mask)), colour)
-            remote(view, view, self.send.at[colour, 0, 0], self.recv.at[colour, mask // 2], self.me).wait_recv()
+            for i, view in enumerate(self.cut(self.block(flipped(self.me, mask)), colour)):
+                remote(view, view, self.send.at[colour, 0, 0, i], self.recv.at[colour, mask // 2, i], self.me).wait_recv()
             for picks, at, axis in self.onward(colour):
                 if picks == self.ROUNDS[r]:
-                    self.unit(colour, at, axis).start()
+                    self.start_unit(colour, at, axis)
         for mask in {2: (X, Y, Z), 5: (X + Y, X + Z, Y + Z), 6: (XYZ,)}.get(r, ()):
             self.pair(mask).start()
 
-    def run(self, use):
-        self.start()
-        for r in range(len(self.ROUNDS)):
-            self.round(r)
-            for mask in self.READY[r]:
-                use(mask)
-
     def finish(self):
         for colour in COLOURS:
-            for axis in ORDERS[colour]:
-                self.unit(colour, 0, axis).wait_send()
-            for _, at, axis in self.onward(colour):
-                self.unit(colour, at, axis).wait_send()
+            for at, axis in [(0, axis) for axis in ORDERS[colour]] + [step[1:] for step in self.onward(colour)]:
+                for copy in self.unit(colour, at, axis):
+                    copy.wait_send()
         for mask in CHIP_MASKS:
             self.pair(mask).wait_send()
 
 
-def row_gather(own, full, sems, me):
-    width = own.shape[1]
-    parts = thirds(width, LANE)
+def row_gather(own, full, sems, me, extra=None):
+    rows, width = own.shape
+    parts = pieces(rows, width, STRIP)
+    if extra is not None:
+        share = width // LANE // 3 * LANE
+        more = width - 3 * share
+        parts = [[(pl.ds(0, rows), pl.ds(c * share + more * (c > extra), share + more * (c == extra)))] for c in COLOURS]
 
     def block(o):
         return full.at[o // 2, seg(o % 2), :]
 
-    return Gather(own, block, lambda view, c: view.at[:, pl.ds(*parts[c])], sems, me)
+    return Gather(own, block, lambda view, c: [view.at[rs, cs] for rs, cs in parts[c]], sems, me)
 
 
 def keep_own(own, full, me):
@@ -188,7 +191,7 @@
 
 class Scatter:
     ORDER = (XYZ, X + Y, Y + Z, X + Z, X, Y, Z, 0)
-    sems = (dma(N_CHIP), dma(N_CHIP), dma(3, N_CHIP), dma(3, N_CHIP))
+    sems = (dma(N_CHIP), dma(N_CHIP), dma(3, N_CHIP, 2), dma(3, N_CHIP, 2))
 
     @staticmethod
     def scratch(tokens, dim):
@@ -199,7 +202,7 @@
         self.pair_send, self.pair_recv, self.link_send, self.link_recv = sems
         self.core = me % 2
         self.tokens, self.dim = part.shape[2:]
-        self.cols = thirds(self.dim, LANE)
+        self.pieces = pieces(self.tokens, self.dim, STRIP // 2)
         self.ready, self.sent = set(), [0] * len(ORDERS)
 
     @staticmethod
@@ -216,10 +219,13 @@
     def link(self, colour, mask):
         axis = ORDERS[colour][self.first(colour, mask)]
         slot = self.slot(colour, mask - axis, axis)
-        cs = pl.ds(*self.cols[colour])
         i = self.ORDER.index(mask)
-        return remote(self.part.at[i, self.core, :, cs], self.link_in.at[slot, :, cs], self.link_send.at[colour, i],
-                      self.link_recv.at[colour, slot], flipped(self.me, axis))
+        return [remote(self.part.at[i, self.core, rs, cs], self.link_in.at[slot, rs, cs], self.link_send.at[colour, i, k],
+                       self.link_recv.at[colour, slot, k], flipped(self.me, axis)) for k, (rs, cs) in enumerate(self.pieces[colour])]
+
+    def start_link(self, colour, mask):
+        for copy in self.link(colour, mask):
+            copy.start()
 
     def add(self, mask, ref, cs):
         i = self.ORDER.index(mask)
@@ -237,31 +243,36 @@
             a, b, c = ORDERS[colour]
             todo = (XYZ, a + b, a + c, a)
             while self.sent[colour] < len(todo) and todo[self.sent[colour]] in self.ready:
-                self.link(colour, todo[self.sent[colour]]).start()
+                self.start_link(colour, todo[self.sent[colour]])
                 self.sent[colour] += 1
 
     def take(self, colour, mask, axis):
-        self.link(colour, mask + axis).wait_recv()
-        self.add(mask, self.link_in.at[self.slot(colour, mask, axis)], pl.ds(*self.cols[colour]))
-
-    def run(self, product):
+        for copy in self.link(colour, mask + axis):
+            copy.wait_recv()
+        ref = self.link_in.at[self.slot(colour, mask, axis)]
+        (_, wide), (rs, cs) = self.pieces[colour]
+        self.add(mask, ref, wide)
+        self.part[self.ORDER.index(mask), self.core, rs, cs] += ref[rs, cs]
+
+    def run(self, product, between=lambda i: None):
         for i, mask in enumerate(self.ORDER):
             product(i, flipped(self.me, mask) // 2)
             self.pair(i).start()
             if i:
                 self.finish_pair(i - 1)
+            between(i)
         self.finish_pair(N_CHIP - 1)
         for step in range(2):
             for colour in COLOURS:
                 a, b, c = ORDERS[colour]
                 mask = (b + c, b)[step]
                 self.take(colour, mask, a)
-                self.link(colour, mask).start()
+                self.start_link(colour, mask)
         for colour in COLOURS:
             a, b, c = ORDERS[colour]
             self.take(colour, c, a)
             self.take(colour, c, b)
-            self.link(colour, c).start()
+            self.start_link(colour, c)
         for colour in COLOURS:
             for axis in ORDERS[colour]:
                 self.take(colour, 0, axis)
@@ -272,18 +283,19 @@
             self.pair(i).wait_send()
         for colour in COLOURS:
             for mask in self.ORDER[:-1]:
-                self.link(colour, mask).wait_send()
-
-
-def block_product(part, a_ref, w_ref):
+                for copy in self.link(colour, mask):
+                    copy.wait_send()
+
+
+def block_product(part, a_ref, w_ref, a_t):
     tokens = part.shape[2]
 
     def product(i, chip):
-        a = a_ref[:, seg(chip, 2 * tokens)]
+        a_t[...] = a_ref[:, seg(chip, 2 * tokens)].T
 
         def step(n):
             cs = seg(n, CHUNK)
-            r = mm(a, w_ref[:, cs], TN)
+            r = mm(a_t[...], w_ref[:, cs], NN)
             part[i, 0, :, cs] = r[:tokens]
             part[i, 1, :, cs] = r[tokens:]
         loop(part.shape[3] // CHUNK, step)
@@ -298,7 +310,7 @@
 
 
 def call(kernel, ident, args, outs, scratch, flops, far_in=(), far_out=()):
-    specs = [IN_HBM if i in far_in else on_chip(1)[0] for i in range(len(args))]
+    specs = [IN_HBM if i in far_in else on_chip(1)[0] for i in range(args)]
     out_specs = [IN_HBM if i in far_out else on_chip(1)[0] for i in range(len(outs))]
     return pl.pallas_call(
         kernel,
@@ -307,7 +319,7 @@
         cost_estimate=pl.CostEstimate(flops=flops, bytes_accessed=flops // CHUNK, transcendentals=0),
         compiler_params=pltpu.CompilerParams(collective_id=ident, has_side_effects=True, vmem_limit_bytes=VMEM_CAP),
         name=kernel.func.__name__ if isinstance(kernel, functools.partial) else kernel.__name__,
-    )(*args)
+    )
 
 
 def gain_row(dst, small_all, which):
@@ -361,11 +373,16 @@
     return jnp.concatenate([ref[h * hd:(h + 1) * hd, qs] for h in range(heads)], axis=1)
 
 
-def head(groups, hd, x_ref, small_ref, w_ref, cos_ref, sin_ref, wg_ref, wu_ref, qkv_ref, ucol_ref, small_all, w_out, ot_ref, o_ref, stat_ref, wgu_ref,
-         full, acc, rot, u_scr, g_scr, wg_t, wu_t, s_scr, k_scr, osem, *sems):
+def head(groups, hd, x_ref, g1_ref, g2_ref, pos_ref, wq_ref, wk_ref, wv_ref, cos_ref, sin_ref, wg_ref, wu_ref, qkv_ref, ucol_ref, small_all, w_out, ot_ref, o_ref, stat_ref, wgu_ref,
+         small_ref, w_ref, full, acc, rot, u_scr, g_scr, wg_t, wu_t, s_scr, k_scr, osem, *sems):
     me = lax.axis_index('sp')
     tokens, dim = x_ref.shape
     cols = w_ref.shape[0]
+    small_ref[...] = jnp.concatenate([r[...].astype(F32) for r in (g1_ref, g2_ref, pos_ref)] + [jnp.zeros((N_CHIP - 3, LANE), F32)], axis=0)
+    w_ref[:wq_ref.shape[0], :] = wq_ref[...]
+    for k in range(groups):
+        for i, ref in enumerate((wk_ref, wv_ref)):
+            w_ref[pl.ds(wq_ref.shape[0] + (2 * k + i) * hd, hd), :] = ref[k * hd:(k + 1) * hd, :]
     qw = tokens
     q_all = N_DEV * qw
     gsems, ssems, usems, qsems, ksems, gate_sems, up_sems, (osend, orecv) = sems[:4], *(sems[i:i + 2] for i in range(4, len(sems), 2))
@@ -374,7 +391,7 @@
     smalls = Swap(lambda peer: small_ref, lambda o: small_all.at[o], ssems, me)
     smalls.start()
     parts = thirds(cols, STRIP)
-    g = Gather(w_ref, lambda o: full.at[o // 2, :, seg(o % 2)], lambda view, c: view.at[pl.ds(*parts[c]), :], gsems, me)
+    g = Gather(w_ref, lambda o: full.at[o // 2, :, seg(o % 2)], lambda view, c: [view.at[pl.ds(*parts[c]), :]], gsems, me)
     g.start()
 
     def own_block(i):
@@ -406,17 +423,16 @@
         u = u_scr[:, seg(chip, WIDE)]
 
         def step(i):
-            rs = seg(i, CHUNK)
+            rs = seg(i, cols // 2)
             acc[rs, :] += mm(full[chip, rs, :], u, NT)
-        loop(cols // CHUNK, step)
+        loop(2, step)
 
     for r in range(len(g.ROUNDS)):
         g.round(r)
         if r < 4:
             loop(turns, lambda i: transpose(turns * r + i))
-        if r == 5:
-            gates.advance(0)
-            ups.advance(0)
+        if r == 3:
+            ucols.start()
         for mask in g.READY[r]:
             use(mask)
 
@@ -442,6 +458,8 @@
     kvs = Swap(lambda peer: rot.at[kv_rows(peer), :], lambda o: qkv_ref.at[qw:, seg(o, tokens)], ksems, me)
     qs.start()
     kvs.start()
+    gates.advance(0)
+    ups.advance(0)
     qkv_ref[:qw, seg(me, tokens)] = rot[q_rows(me), :]
     qkv_ref[qw:, seg(me, tokens)] = rot[kv_rows(me), :]
     ucol_ref[seg(me, tokens), :] = u_scr[:, seg(me)]
@@ -451,8 +469,6 @@
     ups.start((CORE,))
     for swap in (qs, kvs):
         swap.wait_recv()
-    gates.advance(1)
-    ups.advance(1)
     heads = qkv_ref.shape[0] // hd - 2
     seq = qkv_ref.shape[1]
     scale = hd ** -0.5
@@ -462,10 +478,9 @@
     def o_copy(peer, origin):
         return remote(o_ref.at[:, seg(peer)], ot_ref.at[seg(origin, qw), :], osend.at[peer], orecv.at[origin], peer)
 
-    def q_block(i):
-        qb = other_chip(me // 2, N_CHIP - 1 - i)
-        for at, n in ((3, 2), (6, 3)):
-            @pl.when(i == at)
+    def q_block(qb):
+        for at, n in ((5, 1), (7, 2)):
+            @pl.when(qb == at)
             def _():
                 gates.advance(n)
                 ups.advance(n)
@@ -504,10 +519,11 @@
                 o_copy(peer, me).start()
 
     loop(seq // QB, q_block)
+    gates.advance(3)
+    ups.advance(3)
     ot_ref[seg(me, qw), :] = o_ref[:, seg(me)]
     for mask in OTHERS:
         o_copy(me, flipped(me, mask)).wait_recv()
-    ucols.start()
     for swap in (gates, ups, ucols):
         swap.wait_recv()
     for mask in CHIP_MASKS:
@@ -522,26 +538,30 @@
 
 
 def mlp_local(ot_ref, wo_ref, x_ref, small_all, dout_ref, wgu_ref, down_ref, h_ref, m_out, glu_ref, dgu_ref, ddown_ref,
-              full_w, full_d, full_m, acc, m_scr, g_scr, osem, *sems):
+              full_w, full_d, full_m, acc, m_scr, o_scr, g_scr, osem, *sems):
     me = lax.axis_index('sp')
     feat, dim = down_ref.shape
     enter(me, NEAR)
-    gw = row_gather(wo_ref, full_w, sems[:4], me)
-    gd = row_gather(dout_ref, full_d, sems[4:8], me)
-    gm = row_gather(m_scr, full_m, sems[8:], me)
+    gw = row_gather(wo_ref, full_w, sems[:4], me, 0)
+    gd = row_gather(dout_ref, full_d, sems[4:8], me, 1)
+    gm = row_gather(m_scr, full_m, sems[8:], me, 2)
 
     def project(mask):
         gw.wait_pair(mask)
         chip = flipped(me, mask) // 2
-        o = ot_ref[seg(chip, WIDE), :]
+        o = o_scr[:, seg(chip, WIDE)]
 
         def step(n):
-            acc[:, seg(n, CHUNK)] += mm(o, full_w[chip, :, seg(n, CHUNK)], TN)
+            acc[:, seg(n, CHUNK)] += mm(o, full_w[chip, :, seg(n, CHUNK)], NN)
         loop(dim // CHUNK, step)
 
     gw.start()
     keep_own(wo_ref, full_w, me)
     keep_own(dout_ref, full_d, me)
+
+    def turn(i):
+        o_scr[:, seg(i)] = ot_ref[seg(i), :].T
+    loop(ot_ref.shape[0] // LANE, turn)
     gain_row(g_scr, small_all, 1)
     acc[...] = jnp.zeros_like(acc)
     ddown_ref[...] = jnp.zeros_like(ddown_ref)
@@ -595,17 +615,8 @@
         g.finish()
 
 
-def scatter_y(a_ref, w_ref, h_ref, y_ref, *scr):
-    me = lax.axis_index('sp')
-    enter(me, NEAR)
-    s = Scatter(*scr[:3], scr[3:], me)
-    total = s.run(block_product(s.part, a_ref, w_ref))
-    y_ref[...] = (h_ref[...].astype(F32) + total[...]).astype(BF16)
-    s.finish()
-
-
-def mlp_back(dgu_ref, wgu_ref, h_ref, small_all, dout_ref, wo_ref, o_ref, dh_ref, do_ref, dwo_ref, dg_ref,
-             full, g_scr, *scr):
+def mlp_back(dgu_ref, wgu_ref, h_ref, small_all, dout_ref, wo_ref, o_ref, glu_ref, down_ref, y_ref, dh_ref, do_ref, dwo_ref, dg_ref,
+             full, g_scr, dgu_t, glu_t, free, *scr):
     me = lax.axis_index('sp')
     dim = wo_ref.shape[1]
     enter(me, NEAR)
@@ -613,8 +624,14 @@
     g = row_gather(dh_ref, full, scr[7:], me)
     gain_row(g_scr, small_all, 1)
     dwo_ref[...] = jnp.zeros_like(dwo_ref)
-    total = s.run(block_product(s.part, dgu_ref, wgu_ref))
+    total = s.run(block_product(s.part, dgu_ref, wgu_ref, dgu_t))
+    for mask in NEAR:
+        pl.semaphore_signal(free, inc=1, device_id=(flipped(me, mask),), device_id_type=MESH)
     norm_back(total, h_ref, g_scr, dout_ref, dh_ref, dg_ref)
+    g.start()
+    keep_own(dh_ref, full, me)
+    s.finish()
+    pl.semaphore_wait(free, len(NEAR))
 
     def use(mask):
         g.wait_pair(mask)
@@ -626,20 +643,23 @@
             dwo_ref[:, seg(n, CHUNK)] += mm(o, full[chip, :, seg(n, CHUNK)], NN)
         loop(dim // CHUNK, step)
 
-    g.start()
-    keep_own(dh_ref, full, me)
-    for r in range(len(g.ROUNDS)):
-        g.round(r)
-        for mask in g.READY[r]:
-            use(mask)
+    def between(i):
+        if i < len(g.ROUNDS):
+            g.round(i)
+            for mask in g.READY[i]:
+                use(mask)
+
+    s = Scatter(*scr[:3], scr[3:7], me)
+    total = s.run(block_product(s.part, glu_ref, down_ref, glu_t), between)
+    y_ref[...] = (h_ref[...].astype(F32) + total[...]).astype(BF16)
     s.finish()
     g.finish()
 
 
-def back(groups, hd, qkv_ref, do_ref, stat_ref, cos_all, sin_all, dgu_ref, m_ref, ucol_ref, cos_ref, sin_ref, w_hbm, x_ref, small_all, dh_ref, dg2_ref,
+def back(groups, hd, qkv_ref, do_ref, stat_ref, cos_all, sin_all, dgu_ref, m_hbm, ucol_ref, cos_ref, sin_ref, w_hbm, x_ref, small_all, dh_ref, dg2_ref,
          dg_hbm, du_hbm, dwq_ref, dwkv_ref, dx_ref, gain_ref,
-         p_scr, dp_scr, k_scr, v_scr, dk_acc, dv_acc, stage, dq_scr, dkv_scr,
-         full, w_scr, shares, dkv_own, full_kv, dqkv, dn, g_scr, dg1, gains, gains_in, wsem, lsem, *sems):
+         p_scr, dp_scr, k_scr, v_scr, dk_acc, dv_acc, stage, dq_scr, dkv_scr, m_scr,
+         full, w_scr, shares, dkv_own, full_kv, dqkv, dn, g_scr, dg1, gains, gains_in, wsem, lsem, msem, *sems):
     heads = qkv_ref.shape[0] // hd - 2
     seq = qkv_ref.shape[1]
     scale = hd ** -0.5
@@ -648,9 +668,16 @@
     half = hd // 2
     me = lax.axis_index('sp')
     feat = dgu_ref.shape[0] // 2
-    enter(me, OTHERS)
+    first = (XYZ, X, Y + Z, Y, X + Z, Z, X + Y, 0)
+
+    def fetch(mask):
+        cols = seg(flipped(me, mask) // 2, WIDE)
+        return pltpu.make_async_copy(m_hbm.at[:, :, cols], m_scr.at[:, :, cols], msem.at[mask // 2])
+    for mask in first:
+        fetch(mask).start()
     load = pltpu.make_async_copy(w_hbm, w_scr, wsem)
     load.start()
+    enter(me, OTHERS)
     gain_row(g_scr, small_all, 0)
 
     def piece(lo):
@@ -661,18 +688,18 @@
 
     def make(mask):
         chip = flipped(me, mask) // 2
-        cols = m_ref[:, :, seg(chip, WIDE)].reshape(seq, WIDE)
+        fetch(mask).wait()
+        cols = m_scr[:, :, seg(chip, WIDE)].reshape(seq, WIDE)
         stage[chip] = mm(dgu_ref[...], cols, NN)
 
     def advance(n):
         gates.advance(n)
         ups.advance(n)
 
-    make(XYZ)
-    make(X)
-    advance(0)
-    for mask in (Y + Z, Y, X + Z, Z, X + Y, 0):
+    for i, mask in enumerate(first):
         make(mask)
+        if i == 1:
+            advance(0)
     gates.start((CORE,))
     ups.start((CORE,))
     for copy in own:
@@ -733,7 +760,7 @@
     sh = Swap(lambda peer: dkv_scr.at[seg(peer, tokens), :], lambda o: shares.at[o], sems[4:6], me)
     gq = row_gather(dq_scr, full, sems[6:10], me)
     parts = thirds(dkv_own.shape[0], STRIP)
-    gk = Gather(dkv_own, lambda o: full_kv.at[:, seg(o, tokens)], lambda view, c: view.at[pl.ds(*parts[c]), :], sems[10:14], me)
+    gk = Gather(dkv_own, lambda o: full_kv.at[:, seg(o, tokens)], lambda view, c: [view.at[pl.ds(*parts[c]), :]], sems[10:14], me)
     gs = Swap(lambda peer: gains.at[:, seg(peer)], lambda o: gains_in.at[o], sems[14:], me)
     sh.start()
     gq.start()
@@ -750,13 +777,14 @@
         dkv_own[lo + hd:lo + 2 * hd, :] = both[hd:].astype(BF16)
     gk.start()
     full_kv[:, seg(me, tokens)] = dkv_own[...]
-    dqkv[q_all:, :] = dkv_own[...]
+    for k in range(groups):
+        dqkv[:, q_all + 2 * hd * k:q_all + 2 * hd * (k + 1)] = dkv_own[2 * hd * k:2 * hd * (k + 1), :].T
 
     def use(mask):
         gq.wait_pair(mask)
         chip = flipped(me, mask) // 2
         dwq_ref[seg(chip, WIDE), :] = mm(full[chip], ucol_ref[...], NN)
-        dqkv[seg(chip, WIDE), :] = full[chip, :, seg(me, tokens)]
+        dqkv[:, seg(chip, WIDE)] = full[chip, :, seg(me, tokens)].T
 
     for r in range(len(gq.ROUNDS)):
         gq.round(r)
@@ -768,7 +796,7 @@
     load.wait()
 
     def normed(i):
-        dn[:, seg(i, WIDE)] = mm(dqkv[...], w_scr[i], TN)
+        dn[:, seg(i, WIDE)] = mm(dqkv[...], w_scr[i], NN)
     loop(N_CHIP, normed)
     norm_back(dn, x_ref, g_scr, dh_ref, dx_ref, dg1)
     gains[...] = jnp.concatenate([jnp.sum(dg1[...], axis=0, keepdims=True), jnp.sum(dg2_ref[...], axis=0, keepdims=True),
@@ -791,6 +819,51 @@
         g.finish()
 
 
+def finish(dg_hbm, du_hbm, dkv_hbm, *refs):
+    n = (len(refs) - 11) // 3
+    srcs, (gate, up, dk, dv), dsts = refs[:n], refs[n:n + 4], refs[n + 4:2 * n + 4]
+    (g_in, g_out, kv_in), holds, sems = refs[2 * n + 4:2 * n + 7], refs[2 * n + 7:3 * n + 7], refs[3 * n + 7:]
+    t_in, t_out, p_in, p_out = sems
+    step = LANE * 11
+    cols = g_in.shape[1]
+    hd = dk.shape[0] // (kv_in.shape[0] // LANE)
+    starts = [(w, i) for i in range(cols // step) for w in range(2)]
+
+    def fetch(w, i):
+        rs = pl.ds(i * step, step)
+        return pltpu.make_async_copy((dg_hbm, du_hbm)[w].at[rs, :], g_in.at[w, rs, :], t_in.at[w, i])
+
+    def put(w, i):
+        cs = pl.ds(i * step, step)
+        return pltpu.make_async_copy(g_out.at[w, :, cs], (gate, up)[w].at[:, cs], t_out.at[w, i])
+    moves = [(pltpu.make_async_copy(a, h, p_in.at[k]), pltpu.make_async_copy(h, b, p_out.at[k])) for k, (a, h, b) in enumerate(zip(srcs, holds, dsts))]
+    kv = pltpu.make_async_copy(dkv_hbm, kv_in, p_in.at[n])
+    for w, i in starts:
+        fetch(w, i).start()
+    kv.start()
+    for load, _ in moves:
+        load.start()
+    for w, i in starts:
+        fetch(w, i).wait()
+
+        def turn(j):
+            at = seg(i * (step // LANE) + j)
+            g_out[w, :, at] = g_in[w, at, :].T
+        loop(step // LANE, turn)
+        put(w, i).start()
+    kv.wait()
+    for k in range(dk.shape[0] // hd):
+        for i, ref in enumerate((dk, dv)):
+            ref[k * hd:(k + 1) * hd, :] = kv_in[(2 * k + i) * hd:(2 * k + i + 1) * hd, :]
+    for load, store in moves:
+        load.wait()
+        store.start()
+    for w, i in starts:
+        put(w, i).wait()
+    for _, store in moves:
+        store.wait()
+
+
 def rope_tables(positions, head_dim):
     half_dim = head_dim // 2
     inv_freq = 1.0 / (ROPE_BASE ** (jnp.arange(half_dim, dtype=F32) * (2.0 / head_dim)))
@@ -816,47 +889,56 @@
         gain_scr = vm((N_CHIP, dim), F32)
         small_shape = ((N_DEV, N_CHIP, rows), F32)
 
-        small = jnp.stack([norm1_gain.astype(F32), norm2_gain.astype(F32), positions.astype(F32)])
-        small = jnp.pad(small, ((0, N_CHIP - small.shape[0]), (0, 0)))
         cos_own, sin_own = rope_tables(positions, hd)
-        wq_t = w_q.transpose(1, 2, 0).reshape(n_q * hd, rows)
-        wkv_t = jnp.stack([w_k.transpose(1, 2, 0), w_v.transpose(1, 2, 0)], axis=1).reshape(2 * n_kv * hd, rows)
+        row = lambda v: v.reshape(1, rows)
+        by_head = lambda w: w.transpose(1, 2, 0).reshape(-1, rows)
         wo_own = w_o.reshape(qw, dim)
 
+        args = (x_in, row(norm1_gain), row(norm2_gain), row(positions), by_head(w_q), by_head(w_k), by_head(w_v), cos_own, sin_own, w_gate, w_up)
         qkv, u_col, small_all, wqkv, attn_tok, attn_t, stat, wgu = call(
-            functools.partial(head, n_kv, hd), 0,
-            (x_in, small, jnp.concatenate([wq_t, wkv_t], axis=0), cos_own, sin_own, w_gate, w_up),
+            functools.partial(head, n_kv, hd), 0, len(args),
             (((qw + 2 * hd, seq), BF16), ((seq, rows), BF16), small_shape, ((N_CHIP, cols, WIDE), BF16),
              ((n_q * hd, tokens), BF16), ((qw, seq), BF16), ((seq // QB, 2, lanes), F32), ((2 * feat, dim), BF16)),
-            [vm((N_CHIP, cols, WIDE), BF16), vm((cols, tokens), F32), vm((cols, tokens), BF16), vm((tokens, dim), BF16), gain_scr,
+            [vm((N_CHIP, rows), F32), vm((cols, rows), BF16), vm((N_CHIP, cols, WIDE), BF16), vm((cols, tokens), F32), vm((cols, tokens), BF16), vm((tokens, dim), BF16), gain_scr,
              vm((feat * N_DEV, rows), BF16), vm((feat * N_DEV, rows), BF16), vm((seq, lanes), F32), vm((seq, hd), BF16), dma(N_CHIP),
-             *Gather.sems, *(7 * Swap.sems)], 4 * qw * seq * seq, far_out=(3,))
+             *Gather.sems, *(7 * Swap.sems)], 4 * qw * seq * seq, far_out=(3,))(*args)
+        args = (attn_tok, wo_own, x_in, small_all, d_out, wgu, w_down)
         hidden, m_full, glu, dgu, d_down = call(
-            mlp_local, 2, (attn_tok, wo_own, x_in, small_all, d_out, wgu, w_down),
+            mlp_local, 2, len(args),
             (((tokens, dim), BF16), ((N_CHIP, WIDE, dim), BF16), ((feat, seq), BF16), ((2 * feat, seq), BF16), ((feat, dim), F32)),
-            [full, full, full, vm((tokens, dim), F32), vm((tokens, dim), BF16), gain_scr, dma(N_CHIP), *(3 * Gather.sems)],
-            8 * feat * seq * dim, far_out=(1,))
-        d_hidden, d_attn, d_wo, d_g2 = call(
-            mlp_back, 3, (dgu, wgu, hidden, small_all, d_out, wo_own, attn_t),
-            (((tokens, dim), BF16), ((qw, seq), BF16), ((qw, dim), F32), ((N_CHIP, dim), F32)),
-            [full, gain_scr, *Scatter.scratch(tokens, dim), *Scatter.sems, *Gather.sems], 4 * feat * seq * dim)
+            [full, full, full, vm((tokens, dim), F32), vm((tokens, dim), BF16), vm((tokens, n_q * hd), BF16), gain_scr, dma(N_CHIP), *(3 * Gather.sems)],
+            8 * feat * seq * dim, far_out=(1,))(*args)
+        args = (dgu, wgu, hidden, small_all, d_out, wo_own, attn_t, glu, w_down)
+        y_out, d_hidden, d_attn, d_wo, d_g2 = call(
+            mlp_back, 3, len(args),
+            (((tokens, dim), BF16), ((tokens, dim), BF16), ((qw, seq), BF16), ((qw, dim), F32), ((N_CHIP, dim), F32)),
+            [full, gain_scr, vm((WIDE, 2 * feat), BF16), vm((WIDE, feat), BF16), pltpu.SemaphoreType.REGULAR,
+             *Scatter.scratch(tokens, dim), *Scatter.sems, *Gather.sems], 4 * feat * seq * dim)(*args)
         cos_all, sin_all = rope_tables(small_all[:, 2].reshape(-1), hd)
+        args = (qkv, d_attn, stat, cos_all, sin_all, dgu, m_full, u_col, cos_own, sin_own, wqkv, x_in, small_all, d_hidden, d_g2)
         d_gate_t, d_up_t, d_wq, d_wkv, d_x, gains = call(
-            functools.partial(back, n_kv, hd), 4,
-            (qkv, d_attn, stat, cos_all, sin_all, dgu, m_full, u_col, cos_own, sin_own, wqkv, x_in, small_all, d_hidden, d_g2),
+            functools.partial(back, n_kv, hd), 4, len(args),
             (((feat * N_DEV, rows), F32), ((feat * N_DEV, rows), F32),
              ((n_q * hd, rows), F32), ((2 * n_kv * hd, rows), F32), ((tokens, dim), BF16), ((N_CHIP, rows), F32)),
             [vm((seq, lanes), F32), vm((seq, lanes), BF16), vm((seq, hd), BF16), vm((seq, hd), BF16), vm((seq, hd), F32), vm((seq, hd), F32),
-             vm((N_CHIP, 2 * feat, WIDE), F32), vm((qw, seq), BF16), vm((seq, 2 * hd), BF16),
+             vm((N_CHIP, 2 * feat, WIDE), F32), vm((qw, seq), BF16), vm((seq, 2 * hd), BF16), full,
              full, vm((N_CHIP, cols, WIDE), BF16), vm((N_DEV, tokens, 2 * hd), BF16), vm((2 * n_kv * hd, tokens), BF16), vm((2 * n_kv * hd, seq), BF16),
-             vm((cols, tokens), BF16), vm((tokens, dim), F32), gain_scr, gain_scr, gain_scr, vm((N_DEV, N_CHIP, rows), F32), dma(), dma(2),
-             *(3 * Swap.sems), *(2 * Gather.sems), *Swap.sems], 10 * qw * seq * seq, far_in=(10,), far_out=(0, 1))
-        y_out, = call(scatter_y, 5, (glu, w_down, hidden), (((tokens, dim), BF16),),
-                      [*Scatter.scratch(tokens, dim), *Scatter.sems], 2 * feat * seq * dim)
-
-        d_wkv = d_wkv.reshape(n_kv, 2, hd, rows).transpose(3, 0, 2, 1)
-        return (y_out, d_x, gains[0], gains[1], d_wq.reshape(n_q, hd, rows).transpose(2, 0, 1), d_wkv[..., 0], d_wkv[..., 1],
-                d_wo.reshape(w_o.shape), d_gate_t.T, d_up_t.T, d_down)
+             vm((tokens, cols), BF16), vm((tokens, dim), F32), gain_scr, gain_scr, gain_scr, vm((N_DEV, N_CHIP, rows), F32), dma(), dma(2), dma(N_CHIP),
+             *(3 * Swap.sems), *(2 * Gather.sems), *Swap.sems], 10 * qw * seq * seq, far_in=(6, 10), far_out=(0, 1))(*args)
+        moved = (d_wq, d_wo, d_down, d_x, y_out, gains)
+        half_kv = jax.ShapeDtypeStruct((n_kv * hd, rows), F32)
+        wide = jax.ShapeDtypeStruct((rows, feat * N_DEV), F32)
+        d_gate, d_up, d_wk, d_wv, d_wq, d_wo, d_down, d_x, y_out, gains = pl.pallas_call(
+            finish,
+            out_shape=[wide, wide, half_kv, half_kv] + [jax.ShapeDtypeStruct(v.shape, v.dtype) for v in moved],
+            in_specs=[IN_HBM] * (3 + len(moved)), out_specs=[IN_HBM] * 2 + on_chip(2) + [IN_HBM] * len(moved),
+            scratch_shapes=[vm((2, feat * N_DEV, rows), F32), vm((2, rows, feat * N_DEV), F32), vm(d_wkv.shape, F32)]
+            + [vm(v.shape, v.dtype) for v in moved] + [dma(2, 4), dma(2, 4), dma(len(moved) + 1), dma(len(moved))],
+            compiler_params=pltpu.CompilerParams(vmem_limit_bytes=VMEM_CAP), name='finish',
+        )(d_gate_t, d_up_t, d_wkv, *moved)
+        by_row = lambda g, heads: g.reshape(heads, hd, rows).transpose(2, 0, 1)
+        return (y_out, d_x, gains[0], gains[1], by_row(d_wq, n_q), by_row(d_wk, n_kv), by_row(d_wv, n_kv),
+                d_wo.reshape(w_o.shape), d_gate, d_up, d_down)
 
     all_rows = P('sp')
     return jax.shard_map(layer_step, mesh=mesh, in_specs=(all_rows,) * 12, out_specs=(all_rows,) * 11, check_vma=False)

time: 559 us -> 531 us (0.950)
  local copies, waits for them, and re-layouts: 17.2 us -> 2.12 us
  Pallas kernels: 529 us -> 515 us
    pallas_call x5, Pallas kernels: 529 us -> 515 us  [the longest x1 159 us: layer_step(): call(mlp_back, 3, len(args), (((tokens, dim), BF16), ((tokens, dim), BF16...]
    unnamed x15 -> x0, local copies, waits for them, and re-layouts: 13.4 us -> none
where the time goes in v6:
time: 531 us; the launch traced here: 522 us
  Pallas kernels  515 us (97%)
    pallas_call x1, Pallas kernels, layer_step(): call(mlp_back, 3, len(args), (((tokens, dim), BF16), ((tokens, dim), BF16...  159 us
    pallas_call x1, Pallas kernels, layer_step(): call(functools.partial(back, n_kv, hd), 4, len(args), (((feat * N_DEV, ro...  121 us
    pallas_call x1, Pallas kernels, layer_step(): call(functools.partial(head, n_kv, hd), 0, len(args), (((qw + 2 * hd, seq...  121 us
    pallas_call x1, Pallas kernels, layer_step(): call(mlp_local, 2, len(args), (((tokens, dim), BF16), ((N_CHIP, WIDE, dim...  101 us
    pallas_call x1, Pallas kernels, layer_step(): pl.pallas_call(finish, out_shape=[wide, wide, half_kv, half_kv] + [jax.Sh...  13.7 us

profile of v6, /device:TPU:0, one launch (start us, length us, event | category | flops | bytes accessed | tf_op | source)
XLA Modules:
  0.0 521.7 jit_solution(11173807596615502866)
XLA Ops:
  0.7 0.7 convert_element_type.3
  1.3 0.8 multiply_sine_fusion.1
  2.1 120.6 %head.1 = (bf16[256,2048]{1,0:T(8,128)(2,1)}, bf16[2048,128]{1,0:T(8,128)(2,1)}, f32[16,8,128]{2,1,0:T(8,128)}, bf16[8,2560,256]{2,1,0:T(8,128)(2,1)}, bf16[2048...) custom-call(bf16[128,2048]{1,0:T(8,128)(2,1)} %x_ref.5, ...), custom_call_target="tpu_custom_call" | custom-call | flops 2147483648 | bytes 4194304 | tf_op jit(solution)/shard_map/head/pallas_call | solution.py:898
  122.6 0.8 slice.9
  123.5 1.8 multiply_sine_fusion
  125.3 101.0 %mlp_local.1 = (bf16[128,2048]{1,0:T(8,128)(2,1)}, bf16[8,256,2048]{2,1,0:T(8,128)(2,1)}, bf16[352,2048]{1,0:T(8,128)(2,1)}, bf16[704,2048]{1,0:T(8,128)(2,1)}, f32[352,2048]{1,0:T(8,128)}) custom-call(bf16[2048,128]{1,0:T(8,128)(2,1)} %get-tuple-element.46.ot_ref, bf16[128,2048]{1,0:T(8,128)(2,1)} %bitcast.32, bf16[128,2048]{1,0:T(8,128)(2,1)} %x_ref.5, ...), custom_call_target="tpu_custom_call" | custom-call | flops 11811160064 | bytes 23068672 | tf_op jit(solution)/shard_map/mlp_local/pallas_call | solution.py:906
  226.3 159.0 %mlp_back.1 = (bf16[128,2048]{1,0:T(8,128)(2,1)}, bf16[128,2048]{1,0:T(8,128)(2,1)}, bf16[128,2048]{1,0:T(8,128)(2,1)}, f32[128,2048]{1,0:T(8,128)}, f32[8,2048]{1,0:T(8,128)}) custom-call(bf16[704,2048]{1,0:T(8,128)(2,1)} %get-tuple-element.49.dgu_ref, bf16[704,2048]{1,0:T(8,128)(2,1)} %get-tuple-element.48.wgu_ref, ...), custom_call_target="tpu_custom_call" | custom-call | flops 5905580032 | bytes 11534336 | tf_op jit(solution)/shard_map/mlp_back/pallas_call | solution.py:912
  385.4 120.9 %back.1 = (f32[5632,128]{1,0:T(8,128)}, f32[5632,128]{1,0:T(8,128)}, f32[2048,128]{1,0:T(8,128)}, f32[512,128]{1,0:T(8,128)}, bf16[128,2048]{1,0:T(8,128)(2,1)}, /*index=5*/f32[8,128]{1,0:T(8,128)}) custom-call(bf16[256,2048]{1,0:T(8,128)(2,1)} %get-tuple-element.45.qkv_ref, bf16[128,2048]{1,0:T(8,128)(2,1)} %get-tuple-element.53.do_ref, ...), custom_call_target="tpu_custom_call" | custom-call | flops 5368709120 | bytes 10485760 | tf_op jit(solution)/shard_map/back/pallas_call | solution.py:919
  506.3 13.7 %finish.1 = (f32[128,5632]{1,0:T(8,128)}, f32[128,5632]{1,0:T(8,128)}, f32[256,128]{1,0:T(8,128)}, f32[256,128]{1,0:T(8,128)}, f32[2048,128]{1,0:T(8,128)}, /*in...) custom-call(f32[5632,128]{1,0:T(8,128)} %get-tuple-element.60.dg_hbm, ...), custom_call_target="tpu_custom_call" | custom-call | tf_op jit(solution)/shard_map/finish/pallas_call | solution.py:931
  520.0 1.3 slice_bitcast_fusion
  (1 shorter events, 0.0 us)

commit v7 on v6

--- a/solution.py
+++ b/solution.py
@@ -322,6 +322,13 @@
     )
 
 
+def fetch_all(sem, *pairs):
+    copies = [pltpu.make_async_copy(src, dst, sem.at[i]) for i, (src, dst) in enumerate(pairs)]
+    for copy in copies:
+        copy.start()
+    return copies
+
+
 def gain_row(dst, small_all, which):
     for o in range(N_DEV):
         dst[:1, o * LANE:(o + 1) * LANE] = small_all[o, which:which + 1, :]
@@ -385,7 +392,7 @@
             w_ref[pl.ds(wq_ref.shape[0] + (2 * k + i) * hd, hd), :] = ref[k * hd:(k + 1) * hd, :]
     qw = tokens
     q_all = N_DEV * qw
-    gsems, ssems, usems, qsems, ksems, gate_sems, up_sems, (osend, orecv) = sems[:4], *(sems[i:i + 2] for i in range(4, len(sems), 2))
+    gsems, ssems, usems, qsems, ksems, gate_sems, up_sems, osems = sems[:4], *(sems[i:i + 2] for i in range(4, len(sems), 2))
     feat = wg_ref.shape[1] // N_DEV
     enter(me, OTHERS)
     smalls = Swap(lambda peer: small_ref, lambda o: small_all.at[o], ssems, me)
@@ -475,8 +482,7 @@
     lanes = heads * QB
     key_rows(k_scr, qkv_ref, qw, hd)
 
-    def o_copy(peer, origin):
-        return remote(o_ref.at[:, seg(peer)], ot_ref.at[seg(origin, qw), :], osend.at[peer], orecv.at[origin], peer)
+    outs = Swap(lambda peer: o_ref.at[:, seg(peer)], lambda o: ot_ref.at[seg(o, qw), :], osems, me)
 
     def q_block(qb):
         for at, n in ((5, 1), (7, 2)):
@@ -511,25 +517,16 @@
             o_ref[h * hd:(h + 1) * hd, qs] = acc[:, h * QB:(h + 1) * QB].astype(BF16)
         stat_ref[qb, :1, :] = top
         stat_ref[qb, 1:, :] = inv
-        for core in range(2):
-            peer = 2 * qb + core
-
-            @pl.when(peer != me)
-            def _():
-                o_copy(peer, me).start()
-
     loop(seq // QB, q_block)
+    outs.start()
     gates.advance(3)
     ups.advance(3)
     ot_ref[seg(me, qw), :] = o_ref[:, seg(me)]
-    for mask in OTHERS:
-        o_copy(me, flipped(me, mask)).wait_recv()
-    for swap in (gates, ups, ucols):
+    for swap in (outs, gates, ups, ucols):
         swap.wait_recv()
     for mask in CHIP_MASKS:
         keep(mask).wait()
-    for mask in OTHERS:
-        o_copy(flipped(me, mask), me).wait_send()
+    outs.wait_send()
     for swap in (gates, ups):
         swap.wait_send((CORE,) + SETS[3])
     g.finish()
@@ -537,10 +534,11 @@
         swap.wait_send()
 
 
-def mlp_local(ot_ref, wo_ref, x_ref, small_all, dout_ref, wgu_ref, down_ref, h_ref, m_out, glu_ref, dgu_ref, ddown_ref,
-              full_w, full_d, full_m, acc, m_scr, o_scr, g_scr, osem, *sems):
+def mlp_local(ot_ref, wo_ref, x_ref, small_all, dout_ref, wgu_hbm, down_hbm, h_ref, m_out, glu_out, dgu_out, ddown_ref,
+              wgu_ref, down_ref, glu_ref, dgu_ref, isem, full_w, full_d, full_m, acc, m_scr, o_scr, g_scr, osem, *sems):
     me = lax.axis_index('sp')
     feat, dim = down_ref.shape
+    loads = fetch_all(isem, (wgu_hbm, wgu_ref), (down_hbm, down_ref))
     enter(me, NEAR)
     gw = row_gather(wo_ref, full_w, sems[:4], me, 0)
     gd = row_gather(dout_ref, full_d, sems[4:8], me, 1)
@@ -582,12 +580,16 @@
 
     def keep(mask):
         chip = flipped(me, mask) // 2
-        return pltpu.make_async_copy(full_m.at[chip], m_out.at[chip], osem.at[mask // 2])
+        ts = seg(chip, WIDE)
+        ends = ((full_m.at[chip], m_out.at[chip]), (glu_ref.at[:, ts], glu_out.at[:, ts]), (dgu_ref.at[:, ts], dgu_out.at[:, ts]))
+        return [pltpu.make_async_copy(src, dst, osem.at[mask // 2, i]) for i, (src, dst) in enumerate(ends)]
+
+    for load in loads:
+        load.wait()
 
     def use(mask):
         gd.wait_pair(mask)
         gm.wait_pair(mask)
-        keep(mask).start()
         chip = flipped(me, mask) // 2
         ts = seg(chip, WIDE)
         gu = mm(wgu_ref[...], full_m[chip], NT).astype(BF16).astype(F32)
@@ -603,6 +605,8 @@
         def step(n):
             ddown_ref[:, seg(n, CHUNK)] += mm(glu, full_d[chip, :, seg(n, CHUNK)], NN)
         loop(dim // CHUNK, step)
+        for copy in keep(mask):
+            copy.start()
 
     for r in range(len(gm.ROUNDS)):
         gd.round(r)
@@ -610,20 +614,24 @@
         for mask in gm.READY[r]:
             use(mask)
     for mask in CHIP_MASKS:
-        keep(mask).wait()
+        for copy in keep(mask):
+            copy.wait()
     for g in (gw, gd, gm):
         g.finish()
 
 
-def mlp_back(dgu_ref, wgu_ref, h_ref, small_all, dout_ref, wo_ref, o_ref, glu_ref, down_ref, y_ref, dh_ref, do_ref, dwo_ref, dg_ref,
-             full, g_scr, dgu_t, glu_t, free, *scr):
+def mlp_back(dgu_hbm, wgu_hbm, h_ref, small_all, dout_ref, wo_ref, o_ref, glu_hbm, down_hbm, y_ref, dh_ref, do_ref, dwo_ref, dg_ref,
+             dgu_ref, wgu_ref, glu_ref, down_ref, isem, full, g_scr, dgu_t, glu_t, free, *scr):
     me = lax.axis_index('sp')
     dim = wo_ref.shape[1]
+    loads = fetch_all(isem, (dgu_hbm, dgu_ref), (wgu_hbm, wgu_ref), (glu_hbm, glu_ref), (down_hbm, down_ref))
     enter(me, NEAR)
     s = Scatter(*scr[:3], scr[3:7], me)
     g = row_gather(dh_ref, full, scr[7:], me)
     gain_row(g_scr, small_all, 1)
     dwo_ref[...] = jnp.zeros_like(dwo_ref)
+    for load in loads:
+        load.wait()
     total = s.run(block_product(s.part, dgu_ref, wgu_ref, dgu_t))
     for mask in NEAR:
         pl.semaphore_signal(free, inc=1, device_id=(flipped(me, mask),), device_id_type=MESH)
@@ -698,7 +706,7 @@
 
     for i, mask in enumerate(first):
         make(mask)
-        if i == 1:
+        if i == 0:
             advance(0)
     gates.start((CORE,))
     ups.start((CORE,))
@@ -846,10 +854,8 @@
     for w, i in starts:
         fetch(w, i).wait()
 
-        def turn(j):
-            at = seg(i * (step // LANE) + j)
-            g_out[w, :, at] = g_in[w, at, :].T
-        loop(step // LANE, turn)
+        at = pl.ds(i * step, step)
+        g_out[w, :, at] = g_in[w, at, :].T
         put(w, i).start()
     kv.wait()
     for k in range(dk.shape[0] // hd):
@@ -906,14 +912,16 @@
         hidden, m_full, glu, dgu, d_down = call(
             mlp_local, 2, len(args),
             (((tokens, dim), BF16), ((N_CHIP, WIDE, dim), BF16), ((feat, seq), BF16), ((2 * feat, seq), BF16), ((feat, dim), F32)),
-            [full, full, full, vm((tokens, dim), F32), vm((tokens, dim), BF16), vm((tokens, n_q * hd), BF16), gain_scr, dma(N_CHIP), *(3 * Gather.sems)],
-            8 * feat * seq * dim, far_out=(1,))(*args)
+            [vm((2 * feat, dim), BF16), vm((feat, dim), BF16), vm((feat, seq), BF16), vm((2 * feat, seq), BF16), dma(2),
+             full, full, full, vm((tokens, dim), F32), vm((tokens, dim), BF16), vm((tokens, n_q * hd), BF16), gain_scr, dma(N_CHIP, 3), *(3 * Gather.sems)],
+            8 * feat * seq * dim, far_in=(5, 6), far_out=(1, 2, 3))(*args)
         args = (dgu, wgu, hidden, small_all, d_out, wo_own, attn_t, glu, w_down)
         y_out, d_hidden, d_attn, d_wo, d_g2 = call(
             mlp_back, 3, len(args),
             (((tokens, dim), BF16), ((tokens, dim), BF16), ((qw, seq), BF16), ((qw, dim), F32), ((N_CHIP, dim), F32)),
-            [full, gain_scr, vm((WIDE, 2 * feat), BF16), vm((WIDE, feat), BF16), pltpu.SemaphoreType.REGULAR,
-             *Scatter.scratch(tokens, dim), *Scatter.sems, *Gather.sems], 4 * feat * seq * dim)(*args)
+            [vm((2 * feat, seq), BF16), vm((2 * feat, dim), BF16), vm((feat, seq), BF16), vm((feat, dim), BF16), dma(4),
+             full, gain_scr, vm((WIDE, 2 * feat), BF16), vm((WIDE, feat), BF16), pltpu.SemaphoreType.REGULAR,
+             *Scatter.scratch(tokens, dim), *Scatter.sems, *Gather.sems], 4 * feat * seq * dim, far_in=(0, 1, 7, 8))(*args)
         cos_all, sin_all = rope_tables(small_all[:, 2].reshape(-1), hd)
         args = (qkv, d_attn, stat, cos_all, sin_all, dgu, m_full, u_col, cos_own, sin_own, wqkv, x_in, small_all, d_hidden, d_g2)
         d_gate_t, d_up_t, d_wq, d_wkv, d_x, gains = call(

time: 531 us -> 529 us (level)
  no operation moved by 1% of the time
where the time goes in v7:
time: 529 us; the launch traced here: 520 us
  Pallas kernels  514 us (97%)
    pallas_call x1, Pallas kernels, layer_step(): call(mlp_back, 3, len(args), (((tokens, dim), BF16), ((tokens, dim), BF16...  160 us
    pallas_call x1, Pallas kernels, layer_step(): call(functools.partial(back, n_kv, hd), 4, len(args), (((feat * N_DEV, ro...  121 us
    pallas_call x1, Pallas kernels, layer_step(): call(functools.partial(head, n_kv, hd), 0, len(args), (((qw + 2 * hd, seq...  121 us
    pallas_call x1, Pallas kernels, layer_step(): call(mlp_local, 2, len(args), (((tokens, dim), BF16), ((N_CHIP, WIDE, dim...  103 us

profile of v7, /device:TPU:0, one launch (start us, length us, event | category | flops | bytes accessed | tf_op | source)
XLA Modules:
  0.0 520.4 jit_solution(4762061929003642631)
XLA Ops:
  0.7 0.7 convert_element_type.3
  1.3 0.8 multiply_sine_fusion.1
  2.1 120.8 %head.1 = (bf16[256,2048]{1,0:T(8,128)(2,1)}, bf16[2048,128]{1,0:T(8,128)(2,1)}, f32[16,8,128]{2,1,0:T(8,128)}, bf16[8,2560,256]{2,1,0:T(8,128)(2,1)}, bf16[2048...) custom-call(bf16[128,2048]{1,0:T(8,128)(2,1)} %x_ref.5, ...), custom_call_target="tpu_custom_call" | custom-call | flops 2147483648 | bytes 4194304 | tf_op jit(solution)/shard_map/head/pallas_call | solution.py:904
  122.9 0.8 slice.9
  123.7 1.8 multiply_sine_fusion
  125.5 102.7 %mlp_local.1 = (bf16[128,2048]{1,0:T(8,128)(2,1)}, bf16[8,256,2048]{2,1,0:T(8,128)(2,1)}, bf16[352,2048]{1,0:T(8,128)(2,1)}, bf16[704,2048]{1,0:T(8,128)(2,1)}, f32[352,2048]{1,0:T(8,128)}) custom-call(bf16[2048,128]{1,0:T(8,128)(2,1)} %get-tuple-element.46.ot_ref, bf16[128,2048]{1,0:T(8,128)(2,1)} %bitcast.32, bf16[128,2048]{1,0:T(8,128)(2,1)} %x_ref.5, ...), custom_call_target="tpu_custom_call" | custom-call | flops 11811160064 | bytes 23068672 | tf_op jit(solution)/shard_map/mlp_local/pallas_call | solution.py:912
  228.3 159.9 %mlp_back.1 = (bf16[128,2048]{1,0:T(8,128)(2,1)}, bf16[128,2048]{1,0:T(8,128)(2,1)}, bf16[128,2048]{1,0:T(8,128)(2,1)}, f32[128,2048]{1,0:T(8,128)}, f32[8,2048]{1,0:T(8,128)}) custom-call(bf16[704,2048]{1,0:T(8,128)(2,1)} %get-tuple-element.49.dgu_hbm.dgu_ref, bf16[704,2048]{1,0:T(8,128)(2,1)} %get-tuple-element.48.wgu_hbm, ...), custom_call_target="tpu_custom_call" | custom-call | flops 5905580032 | bytes 11534336 | tf_op jit(solution)/shard_map/mlp_back/pallas_call | solution.py:919
  388.1 120.9 %back.1 = (f32[5632,128]{1,0:T(8,128)}, f32[5632,128]{1,0:T(8,128)}, f32[2048,128]{1,0:T(8,128)}, f32[512,128]{1,0:T(8,128)}, bf16[128,2048]{1,0:T(8,128)(2,1)}, /*index=5*/f32[8,128]{1,0:T(8,128)}) custom-call(bf16[256,2048]{1,0:T(8,128)(2,1)} %get-tuple-element.45.qkv_ref, bf16[128,2048]{1,0:T(8,128)(2,1)} %get-tuple-element.53.do_ref, ...), custom_call_target="tpu_custom_call" | custom-call | flops 5368709120 | bytes 10485760 | tf_op jit(solution)/shard_map/back/pallas_call | solution.py:927
  509.0 9.7 %finish.1 = (f32[128,5632]{1,0:T(8,128)}, f32[128,5632]{1,0:T(8,128)}, f32[256,128]{1,0:T(8,128)}, f32[256,128]{1,0:T(8,128)}, f32[2048,128]{1,0:T(8,128)}, /*in...) custom-call(f32[5632,128]{1,0:T(8,128)} %get-tuple-element.60.dg_hbm, ...), custom_call_target="tpu_custom_call" | custom-call | tf_op jit(solution)/shard_map/finish/pallas_call | solution.py:939
  518.7 1.3 slice_bitcast_fusion
  (1 shorter events, 0.0 us)

commit v8 on v7

--- a/solution.py
+++ b/solution.py
@@ -40,6 +40,10 @@
     lax.fori_loop(0, count, lambda i, c: (body(i), c)[1], 0)
 
 
+def differing(index, mask):
+    return sum(((index // bit + mask // bit) % 2) * bit for bit in NEAR)
+
+
 def flipped(index, mask):
     out = index
     for bit in NEAR:
@@ -85,27 +89,33 @@
         self.src, self.dst, (self.send, self.recv), self.me = src, dst, sems, me
 
     def copy(self, mask):
-        peer = flipped(self.me, mask)
+        peer = differing(self.me, mask)
         return remote(self.src(peer), self.dst(self.me), self.send.at[mask], self.recv.at[mask], peer)
 
-    def start(self, masks=OTHERS):
-        for mask in masks:
-            self.copy(mask).start()
+    def arrival(self, mask):
+        view = self.dst(differing(self.me, mask))
+        return remote(view, view, self.send.at[mask], self.recv.at[mask], self.me)
+
+    def each(self, masks, act):
+        if masks is None:
+            loop(N_DEV - 1, lambda i: act(i + 1))
+        else:
+            for mask in masks:
+                act(mask)
+
+    def start(self, masks=None):
+        self.each(masks, lambda mask: self.copy(mask).start())
 
     def advance(self, n):
         if n:
-            for mask in SETS[n - 1]:
-                self.copy(mask).wait_send()
+            self.wait_send(SETS[n - 1])
         self.start(SETS[n])
 
-    def wait_recv(self):
-        for mask in OTHERS:
-            view = self.dst(flipped(self.me, mask))
-            remote(view, view, self.send.at[mask], self.recv.at[mask], self.me).wait_recv()
-
-    def wait_send(self, masks=OTHERS):
-        for mask in masks:
-            self.copy(mask).wait_send()
+    def wait_recv(self, masks=None):
+        self.each(masks, lambda mask: self.arrival(mask).wait_recv())
+
+    def wait_send(self, masks=None):
+        self.each(masks, lambda mask: self.copy(mask).wait_send())
 
 
 class Gather:
@@ -309,13 +319,13 @@
 IN_HBM = pl.BlockSpec(memory_space=pl.ANY)
 
 
-def call(kernel, ident, args, outs, scratch, flops, far_in=(), far_out=()):
+def call(kernel, ident, args, outs, scratch, flops, far_in=(), far_out=(), aliases={}):
     specs = [IN_HBM if i in far_in else on_chip(1)[0] for i in range(args)]
     out_specs = [IN_HBM if i in far_out else on_chip(1)[0] for i in range(len(outs))]
     return pl.pallas_call(
         kernel,
         out_shape=[jax.ShapeDtypeStruct(shape, dtype) for shape, dtype in outs],
-        in_specs=specs, out_specs=out_specs, scratch_shapes=scratch,
+        in_specs=specs, out_specs=out_specs, scratch_shapes=scratch, input_output_aliases=aliases,
         cost_estimate=pl.CostEstimate(flops=flops, bytes_accessed=flops // CHUNK, transcendentals=0),
         compiler_params=pltpu.CompilerParams(collective_id=ident, has_side_effects=True, vmem_limit_bytes=VMEM_CAP),
         name=kernel.func.__name__ if isinstance(kernel, functools.partial) else kernel.__name__,
@@ -380,8 +390,8 @@
     return jnp.concatenate([ref[h * hd:(h + 1) * hd, qs] for h in range(heads)], axis=1)
 
 
-def head(groups, hd, x_ref, g1_ref, g2_ref, pos_ref, wq_ref, wk_ref, wv_ref, cos_ref, sin_ref, wg_ref, wu_ref, qkv_ref, ucol_ref, small_all, w_out, ot_ref, o_ref, stat_ref, wgu_ref,
-         small_ref, w_ref, full, acc, rot, u_scr, g_scr, wg_t, wu_t, s_scr, k_scr, osem, *sems):
+def head(groups, hd, x_ref, g1_ref, g2_ref, pos_ref, wq_ref, wk_ref, wv_ref, cos_ref, sin_ref, wg_ref, wu_ref, wo_ref, qkv_ref, ucol_ref, small_all, w_out, o_ref, stat_ref, wgu_ref, h_ref, m_ref,
+         full_w, acc_o, o_tok, o_send, small_ref, w_ref, full, acc, rot, u_scr, g_scr, wg_t, wu_t, s_scr, k_scr, osem, *sems):
     me = lax.axis_index('sp')
     tokens, dim = x_ref.shape
     cols = w_ref.shape[0]
@@ -392,7 +402,8 @@
             w_ref[pl.ds(wq_ref.shape[0] + (2 * k + i) * hd, hd), :] = ref[k * hd:(k + 1) * hd, :]
     qw = tokens
     q_all = N_DEV * qw
-    gsems, ssems, usems, qsems, ksems, gate_sems, up_sems, osems = sems[:4], *(sems[i:i + 2] for i in range(4, len(sems), 2))
+    gsems, ssems, usems, qsems, ksems, gate_sems, up_sems, osems = sems[:4], *(sems[i:i + 2] for i in range(4, len(sems) - 4, 2))
+    gw = row_gather(wo_ref, full_w, sems[-4:], me, 1)
     feat = wg_ref.shape[1] // N_DEV
     enter(me, OTHERS)
     smalls = Swap(lambda peer: small_ref, lambda o: small_all.at[o], ssems, me)
@@ -400,6 +411,18 @@
     parts = thirds(cols, STRIP)
     g = Gather(w_ref, lambda o: full.at[o // 2, :, seg(o % 2)], lambda view, c: [view.at[pl.ds(*parts[c]), :]], gsems, me)
     g.start()
+    gates = Swap(lambda peer: wg_t.at[seg(peer, feat), :], lambda o: wgu_ref.at[:feat, seg(o)], gate_sems, me)
+    ups = Swap(lambda peer: wu_t.at[seg(peer, feat), :], lambda o: wgu_ref.at[feat:, seg(o)], up_sems, me)
+
+    def advance(n):
+        gates.advance(n)
+        ups.advance(n)
+
+    def transpose(i):
+        wg_t[seg(i, CHUNK), :] = wg_ref[:, seg(i, CHUNK)].T
+        wu_t[seg(i, CHUNK), :] = wu_ref[:, seg(i, CHUNK)].T
+    loop(wg_ref.shape[1] // CHUNK, transpose)
+    advance(0)
 
     def own_block(i):
         full[me // 2, seg(i, WIDE), seg(me % 2)] = w_ref[seg(i, WIDE), :]
@@ -409,14 +432,6 @@
     smalls.wait_recv()
     gain_row(g_scr, small_all, 0)
     norm_rows(x_ref, g_scr, u_scr)
-    gates = Swap(lambda peer: wg_t.at[seg(peer, feat), :], lambda o: wgu_ref.at[:feat, seg(o)], gate_sems, me)
-    ups = Swap(lambda peer: wu_t.at[seg(peer, feat), :], lambda o: wgu_ref.at[feat:, seg(o)], up_sems, me)
-    turns = wg_ref.shape[1] // LANE // 4
-
-    def transpose(i):
-        wg_t[seg(i), :] = wg_ref[:, seg(i)].T
-        wu_t[seg(i), :] = wu_ref[:, seg(i)].T
-
     ucols = Swap(lambda peer: u_scr.at[:, seg(peer)], lambda o: ucol_ref.at[seg(o, tokens), :], usems, me)
 
     def keep(mask):
@@ -436,10 +451,8 @@
 
     for r in range(len(g.ROUNDS)):
         g.round(r)
-        if r < 4:
-            loop(turns, lambda i: transpose(turns * r + i))
-        if r == 3:
-            ucols.start()
+        if r in (1, 3, 5):
+            advance((r + 1) // 2)
         for mask in g.READY[r]:
             use(mask)
 
@@ -465,8 +478,10 @@
     kvs = Swap(lambda peer: rot.at[kv_rows(peer), :], lambda o: qkv_ref.at[qw:, seg(o, tokens)], ksems, me)
     qs.start()
     kvs.start()
-    gates.advance(0)
-    ups.advance(0)
+    ucols.start()
+    gw.start()
+    keep_own(wo_ref, full_w, me)
+    gain_row(g_scr, small_all, 1)
     qkv_ref[:qw, seg(me, tokens)] = rot[q_rows(me), :]
     qkv_ref[qw:, seg(me, tokens)] = rot[kv_rows(me), :]
     ucol_ref[seg(me, tokens), :] = u_scr[:, seg(me)]
@@ -482,14 +497,13 @@
     lanes = heads * QB
     key_rows(k_scr, qkv_ref, qw, hd)
 
-    outs = Swap(lambda peer: o_ref.at[:, seg(peer)], lambda o: ot_ref.at[seg(o, qw), :], osems, me)
+    outs = Swap(lambda peer: o_send.at[seg(peer), :], lambda o: o_tok.at[:, seg(o)], osems, me)
 
     def q_block(qb):
-        for at, n in ((5, 1), (7, 2)):
+        for at, r in ((2, 0), (4, 1), (5, 2), (6, 3), (7, 4)):
             @pl.when(qb == at)
             def _():
-                gates.advance(n)
-                ups.advance(n)
+                gw.round(r)
         qs = seg(qb, QB)
         q2 = side_by_side(qkv_ref, heads, hd, qs)
 
@@ -517,12 +531,28 @@
             o_ref[h * hd:(h + 1) * hd, qs] = acc[:, h * QB:(h + 1) * QB].astype(BF16)
         stat_ref[qb, :1, :] = top
         stat_ref[qb, 1:, :] = inv
+        o_send[qs, :] = o_ref[:, qs].T
+
     loop(seq // QB, q_block)
     outs.start()
-    gates.advance(3)
-    ups.advance(3)
-    ot_ref[seg(me, qw), :] = o_ref[:, seg(me)]
-    for swap in (outs, gates, ups, ucols):
+    o_tok[:, seg(me)] = o_send[seg(me), :]
+    for r in (5, 6):
+        gw.round(r)
+    outs.wait_recv()
+    for mask in CHIP_MASKS:
+        gw.wait_pair(mask)
+
+    def project(n):
+        cs = seg(n, CHUNK)
+        acc_o[:, cs] = mm(o_tok[...], full_w[:, :, cs].reshape(dim, CHUNK), NN)
+    loop(dim // CHUNK, project)
+
+    def residual(i):
+        rs = seg(i, STRIP)
+        h_ref[rs, :] = (x_ref[rs, :].astype(F32) + acc_o[rs, :]).astype(BF16)
+    loop(tokens // STRIP, residual)
+    norm_rows(h_ref, g_scr, m_ref)
+    for swap in (gates, ups, ucols):
         swap.wait_recv()
     for mask in CHIP_MASKS:
         keep(mask).wait()
@@ -530,53 +560,24 @@
     for swap in (gates, ups):
         swap.wait_send((CORE,) + SETS[3])
     g.finish()
+    gw.finish()
     for swap in (smalls, ucols, qs, kvs):
         swap.wait_send()
 
 
-def mlp_local(ot_ref, wo_ref, x_ref, small_all, dout_ref, wgu_hbm, down_hbm, h_ref, m_out, glu_out, dgu_out, ddown_ref,
-              wgu_ref, down_ref, glu_ref, dgu_ref, isem, full_w, full_d, full_m, acc, m_scr, o_scr, g_scr, osem, *sems):
+def mlp_local(m_ref, dout_ref, wgu_hbm, down_hbm, m_out, glu_out, dgu_out, ddown_ref,
+              wgu_ref, down_ref, glu_ref, dgu_ref, isem, full_d, full_m, osem, *sems):
     me = lax.axis_index('sp')
     feat, dim = down_ref.shape
     loads = fetch_all(isem, (wgu_hbm, wgu_ref), (down_hbm, down_ref))
     enter(me, NEAR)
-    gw = row_gather(wo_ref, full_w, sems[:4], me, 0)
-    gd = row_gather(dout_ref, full_d, sems[4:8], me, 1)
-    gm = row_gather(m_scr, full_m, sems[8:], me, 2)
-
-    def project(mask):
-        gw.wait_pair(mask)
-        chip = flipped(me, mask) // 2
-        o = o_scr[:, seg(chip, WIDE)]
-
-        def step(n):
-            acc[:, seg(n, CHUNK)] += mm(o, full_w[chip, :, seg(n, CHUNK)], NN)
-        loop(dim // CHUNK, step)
-
-    gw.start()
-    keep_own(wo_ref, full_w, me)
+    gd = row_gather(dout_ref, full_d, sems[:4], me, 0)
+    gm = row_gather(m_ref, full_m, sems[4:], me, 2)
+    gm.start()
+    gd.start()
+    keep_own(m_ref, full_m, me)
     keep_own(dout_ref, full_d, me)
-
-    def turn(i):
-        o_scr[:, seg(i)] = ot_ref[seg(i), :].T
-    loop(ot_ref.shape[0] // LANE, turn)
-    gain_row(g_scr, small_all, 1)
-    acc[...] = jnp.zeros_like(acc)
     ddown_ref[...] = jnp.zeros_like(ddown_ref)
-    for r in range(len(gw.ROUNDS)):
-        gw.round(r)
-        if r == 3:
-            gd.start()
-        for mask in gw.READY[r]:
-            project(mask)
-
-    def residual(i):
-        rs = seg(i, STRIP)
-        h_ref[rs, :] = (x_ref[rs, :].astype(F32) + acc[rs, :]).astype(BF16)
-    loop(x_ref.shape[0] // STRIP, residual)
-    norm_rows(h_ref, g_scr, m_scr)
-    gm.start()
-    keep_own(m_scr, full_m, me)
 
     def keep(mask):
         chip = flipped(me, mask) // 2
@@ -609,28 +610,41 @@
             copy.start()
 
     for r in range(len(gm.ROUNDS)):
+        gm.round(r)
         gd.round(r)
-        gm.round(r)
         for mask in gm.READY[r]:
             use(mask)
     for mask in CHIP_MASKS:
         for copy in keep(mask):
             copy.wait()
-    for g in (gw, gd, gm):
+    for g in (gd, gm):
         g.finish()
 
 
-def mlp_back(dgu_hbm, wgu_hbm, h_ref, small_all, dout_ref, wo_ref, o_ref, glu_hbm, down_hbm, y_ref, dh_ref, do_ref, dwo_ref, dg_ref,
-             dgu_ref, wgu_ref, glu_ref, down_ref, isem, full, g_scr, dgu_t, glu_t, free, *scr):
+def dw_swaps(stage, gate_hbm, up_hbm, sems, me):
+    feat = gate_hbm.shape[0] // N_DEV
+    return [Swap(lambda peer, lo=lo: stage(peer).at[lo:lo + feat, seg(peer % 2)], lambda o, dst=dst: dst.at[seg(o, feat), :], sems[i:i + 2], me)
+            for lo, dst, i in ((0, gate_hbm, 0), (feat, up_hbm, 2))]
+
+
+def mlp_back(dgu_hbm, wgu_hbm, h_ref, small_all, dout_ref, wo_ref, o_ref, glu_hbm, down_hbm, m_hbm,
+             y_ref, dh_ref, do_ref, dwo_ref, dg_ref, gate_hbm, up_hbm, m_cols, stage, dgu_ref, wgu_ref, glu_ref, down_ref, isem, full, g_scr, dgu_t, glu_t, free, *scr):
     me = lax.axis_index('sp')
     dim = wo_ref.shape[1]
-    loads = fetch_all(isem, (dgu_hbm, dgu_ref), (wgu_hbm, wgu_ref), (glu_hbm, glu_ref), (down_hbm, down_ref))
-    enter(me, NEAR)
+    far = seg(flipped(me, XYZ) // 2, WIDE)
+    loads = fetch_all(isem, (dgu_hbm, dgu_ref), (m_hbm.at[:, :, far], m_cols), (wgu_hbm, wgu_ref), (glu_hbm, glu_ref), (down_hbm, down_ref))
+    enter(me, NEAR + SETS[0])
     s = Scatter(*scr[:3], scr[3:7], me)
-    g = row_gather(dh_ref, full, scr[7:], me)
+    g = row_gather(dh_ref, full, scr[7:11], me)
+    gates, ups = dw_swaps(lambda peer: stage, gate_hbm, up_hbm, scr[11:], me)
     gain_row(g_scr, small_all, 1)
     dwo_ref[...] = jnp.zeros_like(dwo_ref)
-    for load in loads:
+    for load in loads[:2]:
+        load.wait()
+    stage[...] = mm(dgu_ref[...], m_cols[...].reshape(dgu_ref.shape[1], WIDE), NN)
+    for swap in (gates, ups):
+        swap.start(SETS[0])
+    for load in loads[2:]:
         load.wait()
     total = s.run(block_product(s.part, dgu_ref, wgu_ref, dgu_t))
     for mask in NEAR:
@@ -662,9 +676,12 @@
     y_ref[...] = (h_ref[...].astype(F32) + total[...]).astype(BF16)
     s.finish()
     g.finish()
-
-
-def back(groups, hd, qkv_ref, do_ref, stat_ref, cos_all, sin_all, dgu_ref, m_hbm, ucol_ref, cos_ref, sin_ref, w_hbm, x_ref, small_all, dh_ref, dg2_ref,
+    for swap in (gates, ups):
+        swap.wait_recv(SETS[0])
+        swap.wait_send(SETS[0])
+
+
+def back(groups, hd, qkv_ref, do_ref, stat_ref, cos_all, sin_all, dgu_ref, m_hbm, ucol_ref, cos_ref, sin_ref, w_hbm, x_ref, small_all, dh_ref, dg2_ref, dg_in, du_in,
          dg_hbm, du_hbm, dwq_ref, dwkv_ref, dx_ref, gain_ref,
          p_scr, dp_scr, k_scr, v_scr, dk_acc, dv_acc, stage, dq_scr, dkv_scr, m_scr,
          full, w_scr, shares, dkv_own, full_kv, dqkv, dn, g_scr, dg1, gains, gains_in, wsem, lsem, msem, *sems):
@@ -676,7 +693,7 @@
     half = hd // 2
     me = lax.axis_index('sp')
     feat = dgu_ref.shape[0] // 2
-    first = (XYZ, X, Y + Z, Y, X + Z, Z, X + Y, 0)
+    first = (X, Y + Z, Y, X + Z, Z, X + Y, 0)
 
     def fetch(mask):
         cols = seg(flipped(me, mask) // 2, WIDE)
@@ -688,10 +705,7 @@
     enter(me, OTHERS)
     gain_row(g_scr, small_all, 0)
 
-    def piece(lo):
-        return lambda peer: stage.at[peer // 2, lo:lo + feat, seg(peer % 2)]
-    gates = Swap(piece(0), lambda o: dg_hbm.at[seg(o, feat), :], sems[:2], me)
-    ups = Swap(piece(feat), lambda o: du_hbm.at[seg(o, feat), :], sems[2:4], me)
+    gates, ups = dw_swaps(lambda peer: stage.at[peer // 2], dg_hbm, du_hbm, sems[:4], me)
     own = [pltpu.make_async_copy(swap.src(me), swap.dst(me), lsem.at[i]) for i, swap in enumerate((gates, ups))]
 
     def make(mask):
@@ -701,13 +715,15 @@
         stage[chip] = mm(dgu_ref[...], cols, NN)
 
     def advance(n):
-        gates.advance(n)
-        ups.advance(n)
+        for swap in (gates, ups):
+            if n > 1:
+                swap.wait_send(SETS[n - 1])
+            swap.start(SETS[n])
 
     for i, mask in enumerate(first):
         make(mask)
-        if i == 0:
-            advance(0)
+        if i == 1:
+            advance(1)
     gates.start((CORE,))
     ups.start((CORE,))
     for copy in own:
@@ -719,10 +735,9 @@
     key_rows(v_scr, qkv_ref, qw + hd, hd)
 
     def q_block(qb):
-        for at, n in ((4, 1), (7, 2)):
-            @pl.when(qb == at)
-            def _():
-                advance(n)
+        @pl.when(qb == 5)
+        def _():
+            advance(2)
         qs = seg(qb, QB)
         q2 = side_by_side(qkv_ref, heads, hd, qs)
         do2 = side_by_side(do_ref, heads, hd, qs)
@@ -817,7 +832,7 @@
     gs.wait_recv()
     gain_ref[...] = sum(gains_in[o] for o in range(N_DEV))
     for swap in (gates, ups):
-        swap.wait_recv()
+        swap.wait_recv((CORE,) + SETS[1] + SETS[2] + SETS[3])
         swap.wait_send((CORE,) + SETS[3])
     for copy in own:
         copy.wait()
@@ -893,46 +908,49 @@
         vm = pltpu.VMEM
         full = vm((N_CHIP, WIDE, dim), BF16)
         gain_scr = vm((N_CHIP, dim), F32)
-        small_shape = ((N_DEV, N_CHIP, rows), F32)
+        tok_shapes = 2 * (((tokens, dim), BF16),)
+        dw_shapes = 2 * (((feat * N_DEV, rows), F32),)
 
         cos_own, sin_own = rope_tables(positions, hd)
         row = lambda v: v.reshape(1, rows)
         by_head = lambda w: w.transpose(1, 2, 0).reshape(-1, rows)
         wo_own = w_o.reshape(qw, dim)
 
-        args = (x_in, row(norm1_gain), row(norm2_gain), row(positions), by_head(w_q), by_head(w_k), by_head(w_v), cos_own, sin_own, w_gate, w_up)
-        qkv, u_col, small_all, wqkv, attn_tok, attn_t, stat, wgu = call(
+        args = (x_in, row(norm1_gain), row(norm2_gain), row(positions), by_head(w_q), by_head(w_k), by_head(w_v), cos_own, sin_own, w_gate, w_up, wo_own)
+        qkv, u_col, small_all, wqkv, attn_t, stat, wgu, hidden, mlp_in = call(
             functools.partial(head, n_kv, hd), 0, len(args),
-            (((qw + 2 * hd, seq), BF16), ((seq, rows), BF16), small_shape, ((N_CHIP, cols, WIDE), BF16),
-             ((n_q * hd, tokens), BF16), ((qw, seq), BF16), ((seq // QB, 2, lanes), F32), ((2 * feat, dim), BF16)),
-            [vm((N_CHIP, rows), F32), vm((cols, rows), BF16), vm((N_CHIP, cols, WIDE), BF16), vm((cols, tokens), F32), vm((cols, tokens), BF16), vm((tokens, dim), BF16), gain_scr,
+            (((qw + 2 * hd, seq), BF16), ((seq, rows), BF16), ((N_DEV, N_CHIP, rows), F32), ((N_CHIP, cols, WIDE), BF16),
+             ((qw, seq), BF16), ((seq // QB, 2, lanes), F32), ((2 * feat, dim), BF16), *tok_shapes),
+            [full, vm((tokens, dim), F32), vm((tokens, dim), BF16), vm((seq, qw), BF16),
+             vm((N_CHIP, rows), F32), vm((cols, rows), BF16), vm((N_CHIP, cols, WIDE), BF16), vm((cols, tokens), F32), vm((cols, tokens), BF16), vm((tokens, dim), BF16), gain_scr,
              vm((feat * N_DEV, rows), BF16), vm((feat * N_DEV, rows), BF16), vm((seq, lanes), F32), vm((seq, hd), BF16), dma(N_CHIP),
-             *Gather.sems, *(7 * Swap.sems)], 4 * qw * seq * seq, far_out=(3,))(*args)
-        args = (attn_tok, wo_own, x_in, small_all, d_out, wgu, w_down)
-        hidden, m_full, glu, dgu, d_down = call(
-            mlp_local, 2, len(args),
-            (((tokens, dim), BF16), ((N_CHIP, WIDE, dim), BF16), ((feat, seq), BF16), ((2 * feat, seq), BF16), ((feat, dim), F32)),
+             *Gather.sems, *(7 * Swap.sems), *Gather.sems], 4 * qw * seq * seq, far_out=(3,))(*args)
+        args = (mlp_in, d_out, wgu, w_down)
+        m_full, glu, dgu, d_down = call(
+            mlp_local, 1, len(args),
+            (((N_CHIP, WIDE, dim), BF16), ((feat, seq), BF16), ((2 * feat, seq), BF16), ((feat, dim), F32)),
             [vm((2 * feat, dim), BF16), vm((feat, dim), BF16), vm((feat, seq), BF16), vm((2 * feat, seq), BF16), dma(2),
-             full, full, full, vm((tokens, dim), F32), vm((tokens, dim), BF16), vm((tokens, n_q * hd), BF16), gain_scr, dma(N_CHIP, 3), *(3 * Gather.sems)],
-            8 * feat * seq * dim, far_in=(5, 6), far_out=(1, 2, 3))(*args)
-        args = (dgu, wgu, hidden, small_all, d_out, wo_own, attn_t, glu, w_down)
-        y_out, d_hidden, d_attn, d_wo, d_g2 = call(
-            mlp_back, 3, len(args),
-            (((tokens, dim), BF16), ((tokens, dim), BF16), ((qw, seq), BF16), ((qw, dim), F32), ((N_CHIP, dim), F32)),
-            [vm((2 * feat, seq), BF16), vm((2 * feat, dim), BF16), vm((feat, seq), BF16), vm((feat, dim), BF16), dma(4),
+             full, full, dma(N_CHIP, 3), *(2 * Gather.sems)],
+            8 * feat * seq * dim, far_in=(2, 3), far_out=(0, 1, 2))(*args)
+        args = (dgu, wgu, hidden, small_all, d_out, wo_own, attn_t, glu, w_down, m_full)
+        y_out, d_hidden, d_attn, d_wo, d_g2, d_gate_t, d_up_t = call(
+            mlp_back, 2, len(args),
+            (*tok_shapes, ((qw, seq), BF16), ((qw, dim), F32), ((N_CHIP, dim), F32), *dw_shapes),
+            [vm((N_CHIP, WIDE, WIDE), BF16), vm((2 * feat, WIDE), F32),
+             vm((2 * feat, seq), BF16), vm((2 * feat, dim), BF16), vm((feat, seq), BF16), vm((feat, dim), BF16), dma(5),
              full, gain_scr, vm((WIDE, 2 * feat), BF16), vm((WIDE, feat), BF16), pltpu.SemaphoreType.REGULAR,
-             *Scatter.scratch(tokens, dim), *Scatter.sems, *Gather.sems], 4 * feat * seq * dim, far_in=(0, 1, 7, 8))(*args)
+             *Scatter.scratch(tokens, dim), *Scatter.sems, *Gather.sems, *(2 * Swap.sems)], 4 * feat * seq * dim,
+            far_in=(0, 1, 7, 8, 9), far_out=(5, 6))(*args)
         cos_all, sin_all = rope_tables(small_all[:, 2].reshape(-1), hd)
-        args = (qkv, d_attn, stat, cos_all, sin_all, dgu, m_full, u_col, cos_own, sin_own, wqkv, x_in, small_all, d_hidden, d_g2)
+        args = (qkv, d_attn, stat, cos_all, sin_all, dgu, m_full, u_col, cos_own, sin_own, wqkv, x_in, small_all, d_hidden, d_g2, d_gate_t, d_up_t)
         d_gate_t, d_up_t, d_wq, d_wkv, d_x, gains = call(
-            functools.partial(back, n_kv, hd), 4, len(args),
-            (((feat * N_DEV, rows), F32), ((feat * N_DEV, rows), F32),
-             ((n_q * hd, rows), F32), ((2 * n_kv * hd, rows), F32), ((tokens, dim), BF16), ((N_CHIP, rows), F32)),
+            functools.partial(back, n_kv, hd), 3, len(args),
+            (*dw_shapes, ((n_q * hd, rows), F32), ((2 * n_kv * hd, rows), F32), tok_shapes[0], ((N_CHIP, rows), F32)),
             [vm((seq, lanes), F32), vm((seq, lanes), BF16), vm((seq, hd), BF16), vm((seq, hd), BF16), vm((seq, hd), F32), vm((seq, hd), F32),
              vm((N_CHIP, 2 * feat, WIDE), F32), vm((qw, seq), BF16), vm((seq, 2 * hd), BF16), full,
              full, vm((N_CHIP, cols, WIDE), BF16), vm((N_DEV, tokens, 2 * hd), BF16), vm((2 * n_kv * hd, tokens), BF16), vm((2 * n_kv * hd, seq), BF16),
              vm((tokens, cols), BF16), vm((tokens, dim), F32), gain_scr, gain_scr, gain_scr, vm((N_DEV, N_CHIP, rows), F32), dma(), dma(2), dma(N_CHIP),
-             *(3 * Swap.sems), *(2 * Gather.sems), *Swap.sems], 10 * qw * seq * seq, far_in=(6, 10), far_out=(0, 1))(*args)
+             *(3 * Swap.sems), *(2 * Gather.sems), *Swap.sems], 10 * qw * seq * seq, far_in=(6, 10, 15, 16), far_out=(0, 1), aliases={15: 0, 16: 1})(*args)
         moved = (d_wq, d_wo, d_down, d_x, y_out, gains)
         half_kv = jax.ShapeDtypeStruct((n_kv * hd, rows), F32)
         wide = jax.ShapeDtypeStruct((rows, feat * N_DEV), F32)

time: 529 us -> 514 us (0.972)
  Pallas kernels: 514 us -> 498 us
    pallas_call x3, Pallas kernels: 383 us -> 348 us  [the longest x1 171 us: layer_step(): call(mlp_back, 2, len(args), (*tok_shapes, ((qw, seq), BF16), ((qw, dim),...]
    pallas_call x1, Pallas kernels: 121 us -> 141 us  [layer_step(): call(functools.partial(head, n_kv, hd), 0, len(args), (((qw + 2 * hd, seq...]
where the time goes in v8:
time: 514 us; the launch traced here: 505 us
  Pallas kernels  498 us (97%)
    pallas_call x1, Pallas kernels, layer_step(): call(mlp_back, 2, len(args), (*tok_shapes, ((qw, seq), BF16), ((qw, dim),...  171 us
    pallas_call x1, Pallas kernels, layer_step(): call(functools.partial(head, n_kv, hd), 0, len(args), (((qw + 2 * hd, seq...  141 us
    pallas_call x1, Pallas kernels, layer_step(): call(functools.partial(back, n_kv, hd), 3, len(args), (*dw_shapes, ((n_q...  106 us
    pallas_call x1, Pallas kernels, layer_step(): call(mlp_local, 1, len(args), (((N_CHIP, WIDE, dim), BF16), ((feat, seq),...  70.7 us

profile of v8, /device:TPU:0, one launch (start us, length us, event | category | flops | bytes accessed | tf_op | source)
XLA Modules:
  0.0 504.8 jit_solution(9858222433737038573)
XLA Ops:
  0.7 0.7 convert_element_type.3
  1.3 0.8 multiply_sine_fusion.1
  2.1 140.8 %head.1 = (bf16[256,2048]{1,0:T(8,128)(2,1)}, bf16[2048,128]{1,0:T(8,128)(2,1)}, f32[16,8,128]{2,1,0:T(8,128)}, bf16[8,2560,256]{2,1,0:T(8,128)(2,1)}, bf16[128,...) custom-call(bf16[128,2048]{1,0:T(8,128)(2,1)} %x_ref.3, ...), custom_call_target="tpu_custom_call" | custom-call | flops 2147483648 | bytes 4194304 | tf_op jit(solution)/shard_map/head/pallas_call | solution.py:920
  142.8 0.8 slice.9
  143.7 1.8 multiply_sine_fusion
  145.5 70.7 %mlp_local.1 = (bf16[8,256,2048]{2,1,0:T(8,128)(2,1)}, bf16[352,2048]{1,0:T(8,128)(2,1)}, bf16[704,2048]{1,0:T(8,128)(2,1)}, f32[352,2048]{1,0:T(8,128)}) custom-call(bf16[128,2048]{1,0:T(8,128)(2,1)} %get-tuple-element.48.m_ref, bf16[128,2048]{1,0:T(8,128)(2,1)} %dout_ref.3, bf16[704,2048]{1,0:T(8,128)(2,1)} %get-tuple-element.49.wgu_hbm, ...), custom_call_target="tpu_custom_call" | custom-call | flops 11811160064 | bytes 23068672 | tf_op jit(solution)/shard_map/mlp_local/pallas_call | solution.py:929
  216.2 170.6 %mlp_back.1 = (bf16[128,2048]{1,0:T(8,128)(2,1)}, bf16[128,2048]{1,0:T(8,128)(2,1)}, bf16[128,2048]{1,0:T(8,128)(2,1)}, f32[128,2048]{1,0:T(8,128)}, f32[8,2048]...) custom-call(bf16[704,2048]{1,0:T(8,128)(2,1)} %get-tuple-element.50.dgu_hbm.dgu_ref, ...), custom_call_target="tpu_custom_call" | custom-call | flops 5905580032 | bytes 11534336 | tf_op jit(solution)/shard_map/mlp_back/pallas_call | solution.py:936
  386.8 106.5 %back.1 = (f32[5632,128]{1,0:T(8,128)}, f32[5632,128]{1,0:T(8,128)}, f32[2048,128]{1,0:T(8,128)}, f32[512,128]{1,0:T(8,128)}, bf16[128,2048]{1,0:T(8,128)(2,1)}, /*index=5*/f32[8,128]{1,0:T(8,128)}) custom-call(bf16[256,2048]{1,0:T(8,128)(2,1)} %get-tuple-element.47.qkv_ref, ...), custom_call_target="tpu_custom_call", output_to_operand_aliasing={{0}: (15, {}), {1}: (16, {})} | custom-call | flops 5368709120 | bytes 10485760 | tf_op jit(solution)/shard_map/back/pallas_call | solution.py:946
  493.3 9.7 %finish.1 = (f32[128,5632]{1,0:T(8,128)}, f32[128,5632]{1,0:T(8,128)}, f32[256,128]{1,0:T(8,128)}, f32[256,128]{1,0:T(8,128)}, f32[2048,128]{1,0:T(8,128)}, /*in...) custom-call(f32[5632,128]{1,0:T(8,128)} %get-tuple-element.64.dg_hbm, ...), custom_call_target="tpu_custom_call" | custom-call | tf_op jit(solution)/shard_map/finish/pallas_call | solution.py:957
  503.1 1.3 slice_bitcast_fusion
  (1 shorter events, 0.0 us)

commit v9 on v8

--- a/solution.py
+++ b/solution.py
@@ -25,7 +25,8 @@
 NEAR = (CORE, X, Y, Z)
 OTHERS = range(1, N_DEV)
 SETS = tuple(tuple(m + c for m in masks for c in (0, CORE)) for masks in ((XYZ,), (X, Y + Z), (Y, X + Z), (Z, X + Y)))
-COLOURS = range(len(ORDERS))
+N_COL = len(ORDERS)
+COLOURS = range(N_COL)
 
 
 def mm(a, b, dims):
@@ -61,10 +62,10 @@
 
 
 def pieces(rows, cols, unit):
-    share = cols // LANE // 3 * LANE
+    share = cols // LANE // N_COL * LANE
     strips = thirds(rows, unit)
-    rest = cols - 3 * share
-    return [[(pl.ds(0, rows), pl.ds(c * share, share)), (pl.ds(*strips[c]), pl.ds(3 * share, rest))] for c in COLOURS]
+    rest = cols - N_COL * share
+    return [[(pl.ds(0, rows), pl.ds(c * share, share)), (pl.ds(*strips[c]), pl.ds(N_COL * share, rest))] for c in COLOURS]
 
 
 def enter(me, masks):
@@ -121,7 +122,7 @@
 class Gather:
     ROUNDS = ((0,), (1,), (2,), (0, 1), (0, 2), (1, 2), (0, 1, 2))
     READY = ((0,), (), (), (X, Y), (Z,), (X + Y, X + Z), (Y + Z, XYZ))
-    sems = (dma(3, N_CHIP, 3, 2), dma(3, N_CHIP, 2), dma(N_CHIP), dma(N_CHIP))
+    sems = (dma(N_COL, N_CHIP, 3, 2), dma(N_COL, N_CHIP, 2), dma(N_CHIP), dma(N_CHIP))
 
     def __init__(self, own, block, cut, sems, me):
         self.own, self.block, self.cut, self.me = own, block, cut, me
@@ -153,22 +154,24 @@
             for axis in order[picks[-1] + 1:]:
                 yield picks, sum(order[p] for p in picks), axis
 
-    def start(self):
+    def start(self, colours=COLOURS):
         for pos in COLOURS:
-            for colour in COLOURS:
+            for colour in colours:
                 self.start_unit(colour, 0, ORDERS[colour][pos])
-        self.pair(0).start()
-
-    def round(self, r):
-        for colour in COLOURS:
+        if 2 in colours:
+            self.pair(0).start()
+
+    def round(self, r, colours=COLOURS):
+        for colour in colours:
             mask = sum(ORDERS[colour][p] for p in self.ROUNDS[r])
             for i, view in enumerate(self.cut(self.block(flipped(self.me, mask)), colour)):
                 remote(view, view, self.send.at[colour, 0, 0, i], self.recv.at[colour, mask // 2, i], self.me).wait_recv()
             for picks, at, axis in self.onward(colour):
                 if picks == self.ROUNDS[r]:
                     self.start_unit(colour, at, axis)
-        for mask in {2: (X, Y, Z), 5: (X + Y, X + Z, Y + Z), 6: (XYZ,)}.get(r, ()):
-            self.pair(mask).start()
+        if 2 in colours:
+            for mask in {2: (X, Y, Z), 5: (X + Y, X + Z, Y + Z), 6: (XYZ,)}.get(r, ()):
+                self.pair(mask).start()
 
     def finish(self):
         for colour in COLOURS:
@@ -183,8 +186,8 @@
     rows, width = own.shape
     parts = pieces(rows, width, STRIP)
     if extra is not None:
-        share = width // LANE // 3 * LANE
-        more = width - 3 * share
+        share = width // LANE // N_COL * LANE
+        more = width - N_COL * share
         parts = [[(pl.ds(0, rows), pl.ds(c * share + more * (c > extra), share + more * (c == extra)))] for c in COLOURS]
 
     def block(o):
@@ -201,7 +204,7 @@
 
 class Scatter:
     ORDER = (XYZ, X + Y, Y + Z, X + Z, X, Y, Z, 0)
-    sems = (dma(N_CHIP), dma(N_CHIP), dma(3, N_CHIP, 2), dma(3, N_CHIP, 2))
+    sems = (dma(N_CHIP), dma(N_CHIP), dma(N_COL, N_CHIP, 2), dma(N_COL, N_CHIP, 2))
 
     @staticmethod
     def scratch(tokens, dim):
@@ -213,7 +216,7 @@
         self.core = me % 2
         self.tokens, self.dim = part.shape[2:]
         self.pieces = pieces(self.tokens, self.dim, STRIP // 2)
-        self.ready, self.sent = set(), [0] * len(ORDERS)
+        self.ready, self.sent = set(), [0] * N_COL
 
     @staticmethod
     def first(colour, mask):
@@ -390,8 +393,8 @@
     return jnp.concatenate([ref[h * hd:(h + 1) * hd, qs] for h in range(heads)], axis=1)
 
 
-def head(groups, hd, x_ref, g1_ref, g2_ref, pos_ref, wq_ref, wk_ref, wv_ref, cos_ref, sin_ref, wg_ref, wu_ref, wo_ref, qkv_ref, ucol_ref, small_all, w_out, o_ref, stat_ref, wgu_ref, h_ref, m_ref,
-         full_w, acc_o, o_tok, o_send, small_ref, w_ref, full, acc, rot, u_scr, g_scr, wg_t, wu_t, s_scr, k_scr, osem, *sems):
+def head(groups, hd, x_ref, g1_ref, g2_ref, pos_ref, wq_ref, wk_ref, wv_ref, cos_ref, sin_ref, wg_ref, wu_ref, wo_ref, qkv_ref, u_scr, small_all, w_out, o_ref, stat_ref, wgu_ref, h_ref, m_ref,
+         full_w, acc_o, o_tok, o_send, small_ref, w_ref, full, acc, rot, g_scr, wg_t, wu_t, s_scr, k_scr, osem, *sems):
     me = lax.axis_index('sp')
     tokens, dim = x_ref.shape
     cols = w_ref.shape[0]
@@ -402,7 +405,7 @@
             w_ref[pl.ds(wq_ref.shape[0] + (2 * k + i) * hd, hd), :] = ref[k * hd:(k + 1) * hd, :]
     qw = tokens
     q_all = N_DEV * qw
-    gsems, ssems, usems, qsems, ksems, gate_sems, up_sems, osems = sems[:4], *(sems[i:i + 2] for i in range(4, len(sems) - 4, 2))
+    gsems, ssems, qsems, ksems, gate_sems, up_sems, osems = sems[:4], *(sems[i:i + 2] for i in range(4, len(sems) - 4, 2))
     gw = row_gather(wo_ref, full_w, sems[-4:], me, 1)
     feat = wg_ref.shape[1] // N_DEV
     enter(me, OTHERS)
@@ -432,7 +435,6 @@
     smalls.wait_recv()
     gain_row(g_scr, small_all, 0)
     norm_rows(x_ref, g_scr, u_scr)
-    ucols = Swap(lambda peer: u_scr.at[:, seg(peer)], lambda o: ucol_ref.at[seg(o, tokens), :], usems, me)
 
     def keep(mask):
         chip = flipped(me, mask) // 2
@@ -451,8 +453,8 @@
 
     for r in range(len(g.ROUNDS)):
         g.round(r)
-        if r in (1, 3, 5):
-            advance((r + 1) // 2)
+        if r in (2, 4):
+            advance(r // 2)
         for mask in g.READY[r]:
             use(mask)
 
@@ -478,13 +480,11 @@
     kvs = Swap(lambda peer: rot.at[kv_rows(peer), :], lambda o: qkv_ref.at[qw:, seg(o, tokens)], ksems, me)
     qs.start()
     kvs.start()
-    ucols.start()
     gw.start()
     keep_own(wo_ref, full_w, me)
     gain_row(g_scr, small_all, 1)
     qkv_ref[:qw, seg(me, tokens)] = rot[q_rows(me), :]
     qkv_ref[qw:, seg(me, tokens)] = rot[kv_rows(me), :]
-    ucol_ref[seg(me, tokens), :] = u_scr[:, seg(me)]
     wgu_ref[:feat, seg(me)] = wg_t[seg(me, feat), :]
     wgu_ref[feat:, seg(me)] = wu_t[seg(me, feat), :]
     gates.start((CORE,))
@@ -535,6 +535,7 @@
 
     loop(seq // QB, q_block)
     outs.start()
+    advance(3)
     o_tok[:, seg(me)] = o_send[seg(me), :]
     for r in (5, 6):
         gw.round(r)
@@ -552,7 +553,7 @@
         h_ref[rs, :] = (x_ref[rs, :].astype(F32) + acc_o[rs, :]).astype(BF16)
     loop(tokens // STRIP, residual)
     norm_rows(h_ref, g_scr, m_ref)
-    for swap in (gates, ups, ucols):
+    for swap in (gates, ups):
         swap.wait_recv()
     for mask in CHIP_MASKS:
         keep(mask).wait()
@@ -561,18 +562,20 @@
         swap.wait_send((CORE,) + SETS[3])
     g.finish()
     gw.finish()
-    for swap in (smalls, ucols, qs, kvs):
+    for swap in (smalls, qs, kvs):
         swap.wait_send()
 
 
-def mlp_local(m_ref, dout_ref, wgu_hbm, down_hbm, m_out, glu_out, dgu_out, ddown_ref,
+def mlp_local(m_ref, dout_ref, wgu_hbm, down_hbm, u_ref, ucol_ref, m_out, glu_out, dgu_out, ddown_ref,
               wgu_ref, down_ref, glu_ref, dgu_ref, isem, full_d, full_m, osem, *sems):
     me = lax.axis_index('sp')
     feat, dim = down_ref.shape
     loads = fetch_all(isem, (wgu_hbm, wgu_ref), (down_hbm, down_ref))
-    enter(me, NEAR)
+    enter(me, OTHERS)
     gd = row_gather(dout_ref, full_d, sems[:4], me, 0)
-    gm = row_gather(m_ref, full_m, sems[4:], me, 2)
+    gm = row_gather(m_ref, full_m, sems[4:8], me, 2)
+    ucols = Swap(lambda peer: u_ref.at[:, seg(peer)], lambda o: ucol_ref.at[seg(o), :], sems[8:], me)
+    ucol_ref[seg(me), :] = u_ref[:, seg(me)]
     gm.start()
     gd.start()
     keep_own(m_ref, full_m, me)
@@ -612,11 +615,15 @@
     for r in range(len(gm.ROUNDS)):
         gm.round(r)
         gd.round(r)
+        if r == 3:
+            ucols.start()
         for mask in gm.READY[r]:
             use(mask)
     for mask in CHIP_MASKS:
         for copy in keep(mask):
             copy.wait()
+    ucols.wait_recv()
+    ucols.wait_send()
     for g in (gd, gm):
         g.finish()
 
@@ -706,6 +713,7 @@
     gain_row(g_scr, small_all, 0)
 
     gates, ups = dw_swaps(lambda peer: stage.at[peer // 2], dg_hbm, du_hbm, sems[:4], me)
+    gq = row_gather(dq_scr, full, sems[6:10], me, 0)
     own = [pltpu.make_async_copy(swap.src(me), swap.dst(me), lsem.at[i]) for i, swap in enumerate((gates, ups))]
 
     def make(mask):
@@ -735,9 +743,9 @@
     key_rows(v_scr, qkv_ref, qw + hd, hd)
 
     def q_block(qb):
-        @pl.when(qb == 5)
-        def _():
-            advance(2)
+        for at, act in ((3, lambda: gq.start((0,))), (4, lambda: advance(2)), (5, lambda: gq.round(0, (0,))), (6, lambda: (gq.start((1,)), gq.round(1, (0,)))),
+                        (7, lambda: gq.round(2, (0,)))):
+            pl.when(qb == at)(lambda act=act: (act(), None)[1])
         qs = seg(qb, QB)
         q2 = side_by_side(qkv_ref, heads, hd, qs)
         do2 = side_by_side(do_ref, heads, hd, qs)
@@ -781,12 +789,11 @@
     per = N_DEV // groups
     q_all = dwq_ref.shape[0]
     sh = Swap(lambda peer: dkv_scr.at[seg(peer, tokens), :], lambda o: shares.at[o], sems[4:6], me)
-    gq = row_gather(dq_scr, full, sems[6:10], me)
     parts = thirds(dkv_own.shape[0], STRIP)
     gk = Gather(dkv_own, lambda o: full_kv.at[:, seg(o, tokens)], lambda view, c: [view.at[pl.ds(*parts[c]), :]], sems[10:14], me)
     gs = Swap(lambda peer: gains.at[:, seg(peer)], lambda o: gains_in.at[o], sems[14:], me)
     sh.start()
-    gq.start()
+    gq.start((2,))
     keep_own(dq_scr, full, me)
     shares[me] = dkv_scr[seg(me, tokens), :]
     sh.wait_recv()
@@ -809,8 +816,10 @@
         dwq_ref[seg(chip, WIDE), :] = mm(full[chip], ucol_ref[...], NN)
         dqkv[:, seg(chip, WIDE)] = full[chip, :, seg(me, tokens)].T
 
+    for r in range(3, len(gq.ROUNDS)):
+        gq.round(r, (0,))
     for r in range(len(gq.ROUNDS)):
-        gq.round(r)
+        gq.round(r, (1, 2))
         gk.round(r)
         if r == 3:
             advance(3)
@@ -917,21 +926,21 @@
         wo_own = w_o.reshape(qw, dim)
 
         args = (x_in, row(norm1_gain), row(norm2_gain), row(positions), by_head(w_q), by_head(w_k), by_head(w_v), cos_own, sin_own, w_gate, w_up, wo_own)
-        qkv, u_col, small_all, wqkv, attn_t, stat, wgu, hidden, mlp_in = call(
+        qkv, u, small_all, wqkv, attn_t, stat, wgu, hidden, mlp_in = call(
             functools.partial(head, n_kv, hd), 0, len(args),
-            (((qw + 2 * hd, seq), BF16), ((seq, rows), BF16), ((N_DEV, N_CHIP, rows), F32), ((N_CHIP, cols, WIDE), BF16),
+            (((qw + 2 * hd, seq), BF16), tok_shapes[0], ((N_DEV, N_CHIP, rows), F32), ((N_CHIP, cols, WIDE), BF16),
              ((qw, seq), BF16), ((seq // QB, 2, lanes), F32), ((2 * feat, dim), BF16), *tok_shapes),
             [full, vm((tokens, dim), F32), vm((tokens, dim), BF16), vm((seq, qw), BF16),
-             vm((N_CHIP, rows), F32), vm((cols, rows), BF16), vm((N_CHIP, cols, WIDE), BF16), vm((cols, tokens), F32), vm((cols, tokens), BF16), vm((tokens, dim), BF16), gain_scr,
+             vm((N_CHIP, rows), F32), vm((cols, rows), BF16), vm((N_CHIP, cols, WIDE), BF16), vm((cols, tokens), F32), vm((cols, tokens), BF16), gain_scr,
              vm((feat * N_DEV, rows), BF16), vm((feat * N_DEV, rows), BF16), vm((seq, lanes), F32), vm((seq, hd), BF16), dma(N_CHIP),
-             *Gather.sems, *(7 * Swap.sems), *Gather.sems], 4 * qw * seq * seq, far_out=(3,))(*args)
-        args = (mlp_in, d_out, wgu, w_down)
-        m_full, glu, dgu, d_down = call(
+             *Gather.sems, *(6 * Swap.sems), *Gather.sems], 4 * qw * seq * seq, far_out=(3,))(*args)
+        args = (mlp_in, d_out, wgu, w_down, u)
+        u_col, m_full, glu, dgu, d_down = call(
             mlp_local, 1, len(args),
-            (((N_CHIP, WIDE, dim), BF16), ((feat, seq), BF16), ((2 * feat, seq), BF16), ((feat, dim), F32)),
+            (((seq, rows), BF16), ((N_CHIP, WIDE, dim), BF16), ((feat, seq), BF16), ((2 * feat, seq), BF16), ((feat, dim), F32)),
             [vm((2 * feat, dim), BF16), vm((feat, dim), BF16), vm((feat, seq), BF16), vm((2 * feat, seq), BF16), dma(2),
-             full, full, dma(N_CHIP, 3), *(2 * Gather.sems)],
-            8 * feat * seq * dim, far_in=(2, 3), far_out=(0, 1, 2))(*args)
+             full, full, dma(N_CHIP, 3), *(2 * Gather.sems), *Swap.sems],
+            8 * feat * seq * dim, far_in=(2, 3), far_out=(1, 2, 3))(*args)
         args = (dgu, wgu, hidden, small_all, d_out, wo_own, attn_t, glu, w_down, m_full)
         y_out, d_hidden, d_attn, d_wo, d_g2, d_gate_t, d_up_t = call(
             mlp_back, 2, len(args),

time: 514 us -> 520 us (1.012)
  Pallas kernels: 498 us -> 504 us
    pallas_call x1, Pallas kernels: 106 us -> 116 us  [layer_step(): call(functools.partial(back, n_kv, hd), 3, len(args), (*dw_shapes, ((n_q...]
    pallas_call x1, Pallas kernels: 141 us -> 132 us  [layer_step(): call(functools.partial(head, n_kv, hd), 0, len(args), (((qw + 2 * hd, seq...]
    pallas_call x1, Pallas kernels: 70.7 us -> 76.2 us  [layer_step(): call(mlp_local, 1, len(args), (((seq, rows), BF16), ((N_CHIP, WIDE, dim),...]
where the time goes in v9:
time: 520 us; the launch traced here: 511 us
  Pallas kernels  504 us (97%)
    pallas_call x1, Pallas kernels, layer_step(): call(mlp_back, 2, len(args), (*tok_shapes, ((qw, seq), BF16), ((qw, dim),...  171 us
    pallas_call x1, Pallas kernels, layer_step(): call(functools.partial(head, n_kv, hd), 0, len(args), (((qw + 2 * hd, seq...  132 us
    pallas_call x1, Pallas kernels, layer_step(): call(functools.partial(back, n_kv, hd), 3, len(args), (*dw_shapes, ((n_q...  116 us
    pallas_call x1, Pallas kernels, layer_step(): call(mlp_local, 1, len(args), (((seq, rows), BF16), ((N_CHIP, WIDE, dim),...  76.2 us

profile of v9, /device:TPU:0, one launch (start us, length us, event | category | flops | bytes accessed | tf_op | source)
XLA Modules:
  0.0 510.8 jit_solution(12891197924229502305)
XLA Ops:
  0.7 0.7 convert_element_type.3
  1.3 0.8 multiply_sine_fusion.1
  2.1 131.7 %head.1 = (bf16[256,2048]{1,0:T(8,128)(2,1)}, bf16[128,2048]{1,0:T(8,128)(2,1)}, f32[16,8,128]{2,1,0:T(8,128)}, bf16[8,2560,256]{2,1,0:T(8,128)(2,1)}, bf16[128,...) custom-call(bf16[128,2048]{1,0:T(8,128)(2,1)} %x_ref.3, ...), custom_call_target="tpu_custom_call" | custom-call | flops 2147483648 | bytes 4194304 | tf_op jit(solution)/shard_map/head/pallas_call | solution.py:929
  133.7 0.8 slice.9
  134.6 1.8 multiply_sine_fusion
  136.4 76.2 %mlp_local.1 = (bf16[2048,128]{1,0:T(8,128)(2,1)}, bf16[8,256,2048]{2,1,0:T(8,128)(2,1)}, bf16[352,2048]{1,0:T(8,128)(2,1)}, bf16[704,2048]{1,0:T(8,128)(2,1)}, f32[352,2048]{1,0:T(8,128)}) custom-call(bf16[128,2048]{1,0:T(8,128)(2,1)} %get-tuple-element.49.m_ref, bf16[128,2048]{1,0:T(8,128)(2,1)} %dout_ref.3, bf16[704,2048]{1,0:T(8,128)(2,1)} %get-tuple-element.50.wgu_hbm, ...), custom_call_target="tpu_custom_call" | custom-call | flops 11811160064 | bytes 23068672 | tf_op jit(solution)/shard_map/mlp_local/pallas_call | solution.py:938
  212.6 171.0 %mlp_back.1 = (bf16[128,2048]{1,0:T(8,128)(2,1)}, bf16[128,2048]{1,0:T(8,128)(2,1)}, bf16[128,2048]{1,0:T(8,128)(2,1)}, f32[128,2048]{1,0:T(8,128)}, f32[8,2048]...) custom-call(bf16[704,2048]{1,0:T(8,128)(2,1)} %get-tuple-element.52.dgu_hbm.dgu_ref, ...), custom_call_target="tpu_custom_call" | custom-call | flops 5905580032 | bytes 11534336 | tf_op jit(solution)/shard_map/mlp_back/pallas_call | solution.py:945
  383.6 115.8 %back.1 = (f32[5632,128]{1,0:T(8,128)}, f32[5632,128]{1,0:T(8,128)}, f32[2048,128]{1,0:T(8,128)}, f32[512,128]{1,0:T(8,128)}, bf16[128,2048]{1,0:T(8,128)(2,1)}, /*index=5*/f32[8,128]{1,0:T(8,128)}) custom-call(bf16[256,2048]{1,0:T(8,128)(2,1)} %get-tuple-element.48.qkv_ref, ...), custom_call_target="tpu_custom_call", output_to_operand_aliasing={{0}: (15, {}), {1}: (16, {})} | custom-call | flops 5368709120 | bytes 10485760 | tf_op jit(solution)/shard_map/back/pallas_call | solution.py:955
  499.4 9.7 %finish.1 = (f32[128,5632]{1,0:T(8,128)}, f32[128,5632]{1,0:T(8,128)}, f32[256,128]{1,0:T(8,128)}, f32[256,128]{1,0:T(8,128)}, f32[2048,128]{1,0:T(8,128)}, /*in...) custom-call(f32[5632,128]{1,0:T(8,128)} %get-tuple-element.66.dg_hbm, ...), custom_call_target="tpu_custom_call" | custom-call | tf_op jit(solution)/shard_map/finish/pallas_call | solution.py:966
  509.1 1.3 slice_bitcast_fusion
  (1 shorter events, 0.0 us)

commit v10 on v9

--- a/solution.py
+++ b/solution.py
@@ -122,7 +122,7 @@
 class Gather:
     ROUNDS = ((0,), (1,), (2,), (0, 1), (0, 2), (1, 2), (0, 1, 2))
     READY = ((0,), (), (), (X, Y), (Z,), (X + Y, X + Z), (Y + Z, XYZ))
-    sems = (dma(N_COL, N_CHIP, 3, 2), dma(N_COL, N_CHIP, 2), dma(N_CHIP), dma(N_CHIP))
+    sems = (dma(N_COL, N_CHIP, 2), dma(N_COL, N_CHIP, 2), dma(N_CHIP), dma(N_CHIP))
 
     def __init__(self, own, block, cut, sems, me):
         self.own, self.block, self.cut, self.me = own, block, cut, me
@@ -133,8 +133,12 @@
 
     def unit(self, colour, mask, axis):
         ends = zip(self.cut(self.source(mask), colour), self.cut(self.block(flipped(self.me, mask)), colour))
-        return [remote(src, dst, self.send.at[colour, mask // 2, ORDERS[colour].index(axis), i], self.recv.at[colour, (mask + axis) // 2, i],
+        j = self.sends(colour).index((mask, axis))
+        return [remote(src, dst, self.send.at[colour, j, i], self.recv.at[colour, (mask + axis) // 2, i],
                        flipped(self.me, axis)) for i, (src, dst) in enumerate(ends)]
+
+    def sends(self, colour):
+        return [(0, axis) for axis in ORDERS[colour]] + [step[1:] for step in self.onward(colour)]
 
     def start_unit(self, colour, mask, axis):
         for copy in self.unit(colour, mask, axis):
@@ -154,32 +158,28 @@
             for axis in order[picks[-1] + 1:]:
                 yield picks, sum(order[p] for p in picks), axis
 
-    def start(self, colours=COLOURS):
+    def start(self):
         for pos in COLOURS:
-            for colour in colours:
+            for colour in COLOURS:
                 self.start_unit(colour, 0, ORDERS[colour][pos])
-        if 2 in colours:
-            self.pair(0).start()
-
-    def round(self, r, colours=COLOURS):
-        for colour in colours:
+        self.pair(0).start()
+
+    def round(self, r):
+        for colour in COLOURS:
             mask = sum(ORDERS[colour][p] for p in self.ROUNDS[r])
             for i, view in enumerate(self.cut(self.block(flipped(self.me, mask)), colour)):
-                remote(view, view, self.send.at[colour, 0, 0, i], self.recv.at[colour, mask // 2, i], self.me).wait_recv()
+                remote(view, view, self.send.at[colour, 0, i], self.recv.at[colour, mask // 2, i], self.me).wait_recv()
             for picks, at, axis in self.onward(colour):
                 if picks == self.ROUNDS[r]:
                     self.start_unit(colour, at, axis)
-        if 2 in colours:
-            for mask in {2: (X, Y, Z), 5: (X + Y, X + Z, Y + Z), 6: (XYZ,)}.get(r, ()):
-                self.pair(mask).start()
+        for mask in {2: (X, Y, Z), 5: (X + Y, X + Z, Y + Z), 6: (XYZ,)}.get(r, ()):
+            self.pair(mask).start()
 
     def finish(self):
         for colour in COLOURS:
-            for at, axis in [(0, axis) for axis in ORDERS[colour]] + [step[1:] for step in self.onward(colour)]:
-                for copy in self.unit(colour, at, axis):
-                    copy.wait_send()
-        for mask in CHIP_MASKS:
-            self.pair(mask).wait_send()
+            for i, view in enumerate(self.cut(self.own, colour)):
+                loop(len(self.sends(colour)), lambda j: remote(view, view, self.send.at[colour, j, i], self.recv.at[colour, j, i], self.me).wait_send())
+        loop(N_CHIP, lambda j: remote(self.own, self.own, self.pair_send.at[j], self.pair_recv.at[j], self.me).wait_send())
 
 
 def row_gather(own, full, sems, me, extra=None):
@@ -208,13 +208,12 @@
 
     @staticmethod
     def scratch(tokens, dim):
-        return [pltpu.VMEM((N_CHIP, 2, tokens, dim), F32), pltpu.VMEM((N_CHIP, tokens, dim), F32), pltpu.VMEM((N_CHIP - 1, tokens, dim), F32)]
-
-    def __init__(self, part, pair_in, link_in, sems, me):
-        self.part, self.pair_in, self.link_in, self.me = part, pair_in, link_in, me
+        return [pltpu.VMEM((n, tokens, dim), F32) for n in (N_CHIP, 2, N_CHIP, N_CHIP - 1)]
+
+    def __init__(self, part, other, pair_in, link_in, sems, me):
+        self.part, self.other, self.pair_in, self.link_in, self.me = part, other, pair_in, link_in, me
         self.pair_send, self.pair_recv, self.link_send, self.link_recv = sems
-        self.core = me % 2
-        self.tokens, self.dim = part.shape[2:]
+        self.tokens, self.dim = part.shape[1:]
         self.pieces = pieces(self.tokens, self.dim, STRIP // 2)
         self.ready, self.sent = set(), [0] * N_COL
 
@@ -227,13 +226,13 @@
         return slots.index((mask, axis))
 
     def pair(self, i):
-        return remote(self.part.at[i, 1 - self.core], self.pair_in.at[i], self.pair_send.at[i], self.pair_recv.at[i], flipped(self.me, CORE))
+        return remote(self.other.at[i % 2], self.pair_in.at[i], self.pair_send.at[i], self.pair_recv.at[i], flipped(self.me, CORE))
 
     def link(self, colour, mask):
         axis = ORDERS[colour][self.first(colour, mask)]
         slot = self.slot(colour, mask - axis, axis)
         i = self.ORDER.index(mask)
-        return [remote(self.part.at[i, self.core, rs, cs], self.link_in.at[slot, rs, cs], self.link_send.at[colour, i, k],
+        return [remote(self.part.at[i, rs, cs], self.link_in.at[slot, rs, cs], self.link_send.at[colour, i, k],
                        self.link_recv.at[colour, slot, k], flipped(self.me, axis)) for k, (rs, cs) in enumerate(self.pieces[colour])]
 
     def start_link(self, colour, mask):
@@ -245,7 +244,7 @@
 
         def step(r):
             rs = seg(r, STRIP)
-            self.part[i, self.core, rs, cs] += ref[rs, cs]
+            self.part[i, rs, cs] += ref[rs, cs]
         loop(self.tokens // STRIP, step)
 
     def finish_pair(self, i):
@@ -265,10 +264,12 @@
         ref = self.link_in.at[self.slot(colour, mask, axis)]
         (_, wide), (rs, cs) = self.pieces[colour]
         self.add(mask, ref, wide)
-        self.part[self.ORDER.index(mask), self.core, rs, cs] += ref[rs, cs]
+        self.part[self.ORDER.index(mask), rs, cs] += ref[rs, cs]
 
     def run(self, product, between=lambda i: None):
         for i, mask in enumerate(self.ORDER):
+            if i > 1:
+                self.pair(i - 2).wait_send()
             product(i, flipped(self.me, mask) // 2)
             self.pair(i).start()
             if i:
@@ -289,29 +290,28 @@
         for colour in COLOURS:
             for axis in ORDERS[colour]:
                 self.take(colour, 0, axis)
-        return self.part.at[N_CHIP - 1, self.core]
+        return self.part.at[N_CHIP - 1]
 
     def finish(self):
-        for i in range(N_CHIP):
+        for i in (N_CHIP - 2, N_CHIP - 1):
             self.pair(i).wait_send()
         for colour in COLOURS:
-            for mask in self.ORDER[:-1]:
-                for copy in self.link(colour, mask):
-                    copy.wait_send()
-
-
-def block_product(part, a_ref, w_ref, a_t):
-    tokens = part.shape[2]
+            for k, (rs, cs) in enumerate(self.pieces[colour]):
+                view = self.part.at[0, rs, cs]
+                loop(N_CHIP - 1, lambda i: remote(view, view, self.link_send.at[colour, i, k], self.link_recv.at[colour, i, k], self.me).wait_send())
+
+
+def block_product(s, a_ref, w_ref, a_t):
+    core = s.me % 2
 
     def product(i, chip):
-        a_t[...] = a_ref[:, seg(chip, 2 * tokens)].T
+        a_t[...] = a_ref[:, seg(chip, WIDE)].T
 
         def step(n):
             cs = seg(n, CHUNK)
-            r = mm(a_t[...], w_ref[:, cs], NN)
-            part[i, 0, :, cs] = r[:tokens]
-            part[i, 1, :, cs] = r[tokens:]
-        loop(part.shape[3] // CHUNK, step)
+            s.other[i % 2, :, cs] = mm(a_t[seg(1 - core), :], w_ref[:, cs], NN)
+            s.part[i, :, cs] = mm(a_t[seg(core), :], w_ref[:, cs], NN)
+        loop(s.dim // CHUNK, step)
     return product
 
 
@@ -566,26 +566,38 @@
         swap.wait_send()
 
 
-def mlp_local(m_ref, dout_ref, wgu_hbm, down_hbm, u_ref, ucol_ref, m_out, glu_out, dgu_out, ddown_ref,
-              wgu_ref, down_ref, glu_ref, dgu_ref, isem, full_d, full_m, osem, *sems):
+def dw_swaps(stage, gate_hbm, up_hbm, sems, me):
+    feat = gate_hbm.shape[0] // N_DEV
+    return [Swap(lambda peer, lo=lo: stage(peer).at[lo:lo + feat, seg(peer % 2)], lambda o, dst=dst: dst.at[seg(o, feat), :], sems[i:i + 2], me)
+            for lo, dst, i in ((0, gate_hbm, 0), (feat, up_hbm, 2))]
+
+
+def mlp(m_ref, dout_ref, wgu_hbm, down_hbm, u_ref, h_ref, small_all, wo_ref, o_ref,
+        ucol_ref, m_out, dgu_out, ddown_ref, y_ref, dh_ref, do_ref, dwo_ref, dg_ref, gate_hbm, up_hbm,
+        wgu_ref, down_ref, glu_ref, dgu_ref, isem, full_d, full_m, osem, stage, g_scr, dgu_t, glu_t, free, *scr):
     me = lax.axis_index('sp')
     feat, dim = down_ref.shape
     loads = fetch_all(isem, (wgu_hbm, wgu_ref), (down_hbm, down_ref))
     enter(me, OTHERS)
+    sems = scr[4:]
     gd = row_gather(dout_ref, full_d, sems[:4], me, 0)
     gm = row_gather(m_ref, full_m, sems[4:8], me, 2)
-    ucols = Swap(lambda peer: u_ref.at[:, seg(peer)], lambda o: ucol_ref.at[seg(o), :], sems[8:], me)
-    ucol_ref[seg(me), :] = u_ref[:, seg(me)]
+    g = row_gather(dh_ref, full_d, sems[8:12], me, 1)
+    ucols = Swap(lambda peer: u_ref.at[:, seg(peer)], lambda o: ucol_ref.at[seg(o), :], sems[12:14], me)
+    gates, ups = dw_swaps(lambda peer: stage, gate_hbm, up_hbm, sems[14:18], me)
     gm.start()
     gd.start()
+    ucol_ref[seg(me), :] = u_ref[:, seg(me)]
     keep_own(m_ref, full_m, me)
     keep_own(dout_ref, full_d, me)
+    gain_row(g_scr, small_all, 1)
+    dwo_ref[...] = jnp.zeros_like(dwo_ref)
     ddown_ref[...] = jnp.zeros_like(ddown_ref)
 
     def keep(mask):
         chip = flipped(me, mask) // 2
         ts = seg(chip, WIDE)
-        ends = ((full_m.at[chip], m_out.at[chip]), (glu_ref.at[:, ts], glu_out.at[:, ts]), (dgu_ref.at[:, ts], dgu_out.at[:, ts]))
+        ends = ((full_m.at[chip], m_out.at[chip]), (dgu_ref.at[:, ts], dgu_out.at[:, ts]))
         return [pltpu.make_async_copy(src, dst, osem.at[mask // 2, i]) for i, (src, dst) in enumerate(ends)]
 
     for load in loads:
@@ -619,73 +631,51 @@
             ucols.start()
         for mask in gm.READY[r]:
             use(mask)
-    for mask in CHIP_MASKS:
-        for copy in keep(mask):
-            copy.wait()
-    ucols.wait_recv()
-    ucols.wait_send()
-    for g in (gd, gm):
-        g.finish()
-
-
-def dw_swaps(stage, gate_hbm, up_hbm, sems, me):
-    feat = gate_hbm.shape[0] // N_DEV
-    return [Swap(lambda peer, lo=lo: stage(peer).at[lo:lo + feat, seg(peer % 2)], lambda o, dst=dst: dst.at[seg(o, feat), :], sems[i:i + 2], me)
-            for lo, dst, i in ((0, gate_hbm, 0), (feat, up_hbm, 2))]
-
-
-def mlp_back(dgu_hbm, wgu_hbm, h_ref, small_all, dout_ref, wo_ref, o_ref, glu_hbm, down_hbm, m_hbm,
-             y_ref, dh_ref, do_ref, dwo_ref, dg_ref, gate_hbm, up_hbm, m_cols, stage, dgu_ref, wgu_ref, glu_ref, down_ref, isem, full, g_scr, dgu_t, glu_t, free, *scr):
-    me = lax.axis_index('sp')
-    dim = wo_ref.shape[1]
     far = seg(flipped(me, XYZ) // 2, WIDE)
-    loads = fetch_all(isem, (dgu_hbm, dgu_ref), (m_hbm.at[:, :, far], m_cols), (wgu_hbm, wgu_ref), (glu_hbm, glu_ref), (down_hbm, down_ref))
-    enter(me, NEAR + SETS[0])
-    s = Scatter(*scr[:3], scr[3:7], me)
-    g = row_gather(dh_ref, full, scr[7:11], me)
-    gates, ups = dw_swaps(lambda peer: stage, gate_hbm, up_hbm, scr[11:], me)
-    gain_row(g_scr, small_all, 1)
-    dwo_ref[...] = jnp.zeros_like(dwo_ref)
-    for load in loads[:2]:
-        load.wait()
-    stage[...] = mm(dgu_ref[...], m_cols[...].reshape(dgu_ref.shape[1], WIDE), NN)
+    stage[...] = mm(dgu_ref[...], full_m[:, :, far].reshape(dgu_ref.shape[1], WIDE), NN)
     for swap in (gates, ups):
         swap.start(SETS[0])
-    for load in loads[2:]:
-        load.wait()
-    total = s.run(block_product(s.part, dgu_ref, wgu_ref, dgu_t))
+    for gather in (gd, gm):
+        gather.finish()
+    s = Scatter(*scr[:4], sems[18:], me)
+    total = s.run(block_product(s, dgu_ref, wgu_ref, dgu_t))
     for mask in NEAR:
         pl.semaphore_signal(free, inc=1, device_id=(flipped(me, mask),), device_id_type=MESH)
     norm_back(total, h_ref, g_scr, dout_ref, dh_ref, dg_ref)
     g.start()
-    keep_own(dh_ref, full, me)
+    keep_own(dh_ref, full_d, me)
     s.finish()
     pl.semaphore_wait(free, len(NEAR))
 
-    def use(mask):
+    def use_dh(mask):
         g.wait_pair(mask)
         chip = flipped(me, mask) // 2
-        do_ref[:, seg(chip, WIDE)] = mm(wo_ref[...], full[chip], NT).astype(BF16)
+        do_ref[:, seg(chip, WIDE)] = mm(wo_ref[...], full_d[chip], NT).astype(BF16)
         o = o_ref[:, seg(chip, WIDE)]
 
         def step(n):
-            dwo_ref[:, seg(n, CHUNK)] += mm(o, full[chip, :, seg(n, CHUNK)], NN)
+            dwo_ref[:, seg(n, CHUNK)] += mm(o, full_d[chip, :, seg(n, CHUNK)], NN)
         loop(dim // CHUNK, step)
 
     def between(i):
         if i < len(g.ROUNDS):
             g.round(i)
             for mask in g.READY[i]:
-                use(mask)
-
-    s = Scatter(*scr[:3], scr[3:7], me)
-    total = s.run(block_product(s.part, glu_ref, down_ref, glu_t), between)
+                use_dh(mask)
+
+    s = Scatter(*scr[:4], sems[18:], me)
+    total = s.run(block_product(s, glu_ref, down_ref, glu_t), between)
     y_ref[...] = (h_ref[...].astype(F32) + total[...]).astype(BF16)
     s.finish()
     g.finish()
     for swap in (gates, ups):
         swap.wait_recv(SETS[0])
         swap.wait_send(SETS[0])
+    ucols.wait_recv()
+    ucols.wait_send()
+    for mask in CHIP_MASKS:
+        for copy in keep(mask):
+            copy.wait()
 
 
 def back(groups, hd, qkv_ref, do_ref, stat_ref, cos_all, sin_all, dgu_ref, m_hbm, ucol_ref, cos_ref, sin_ref, w_hbm, x_ref, small_all, dh_ref, dg2_ref, dg_in, du_in,
@@ -713,7 +703,7 @@
     gain_row(g_scr, small_all, 0)
 
     gates, ups = dw_swaps(lambda peer: stage.at[peer // 2], dg_hbm, du_hbm, sems[:4], me)
-    gq = row_gather(dq_scr, full, sems[6:10], me, 0)
+    gq = row_gather(dq_scr, full, sems[6:10], me)
     own = [pltpu.make_async_copy(swap.src(me), swap.dst(me), lsem.at[i]) for i, swap in enumerate((gates, ups))]
 
     def make(mask):
@@ -743,9 +733,9 @@
     key_rows(v_scr, qkv_ref, qw + hd, hd)
 
     def q_block(qb):
-        for at, act in ((3, lambda: gq.start((0,))), (4, lambda: advance(2)), (5, lambda: gq.round(0, (0,))), (6, lambda: (gq.start((1,)), gq.round(1, (0,)))),
-                        (7, lambda: gq.round(2, (0,)))):
-            pl.when(qb == at)(lambda act=act: (act(), None)[1])
+        @pl.when(qb == 4)
+        def _():
+            advance(2)
         qs = seg(qb, QB)
         q2 = side_by_side(qkv_ref, heads, hd, qs)
         do2 = side_by_side(do_ref, heads, hd, qs)
@@ -793,7 +783,7 @@
     gk = Gather(dkv_own, lambda o: full_kv.at[:, seg(o, tokens)], lambda view, c: [view.at[pl.ds(*parts[c]), :]], sems[10:14], me)
     gs = Swap(lambda peer: gains.at[:, seg(peer)], lambda o: gains_in.at[o], sems[14:], me)
     sh.start()
-    gq.start((2,))
+    gq.start()
     keep_own(dq_scr, full, me)
     shares[me] = dkv_scr[seg(me, tokens), :]
     sh.wait_recv()
@@ -816,10 +806,8 @@
         dwq_ref[seg(chip, WIDE), :] = mm(full[chip], ucol_ref[...], NN)
         dqkv[:, seg(chip, WIDE)] = full[chip, :, seg(me, tokens)].T
 
-    for r in range(3, len(gq.ROUNDS)):
-        gq.round(r, (0,))
     for r in range(len(gq.ROUNDS)):
-        gq.round(r, (1, 2))
+        gq.round(r)
         gk.round(r)
         if r == 3:
             advance(3)
@@ -934,22 +922,15 @@
              vm((N_CHIP, rows), F32), vm((cols, rows), BF16), vm((N_CHIP, cols, WIDE), BF16), vm((cols, tokens), F32), vm((cols, tokens), BF16), gain_scr,
              vm((feat * N_DEV, rows), BF16), vm((feat * N_DEV, rows), BF16), vm((seq, lanes), F32), vm((seq, hd), BF16), dma(N_CHIP),
              *Gather.sems, *(6 * Swap.sems), *Gather.sems], 4 * qw * seq * seq, far_out=(3,))(*args)
-        args = (mlp_in, d_out, wgu, w_down, u)
-        u_col, m_full, glu, dgu, d_down = call(
-            mlp_local, 1, len(args),
-            (((seq, rows), BF16), ((N_CHIP, WIDE, dim), BF16), ((feat, seq), BF16), ((2 * feat, seq), BF16), ((feat, dim), F32)),
+        args = (mlp_in, d_out, wgu, w_down, u, hidden, small_all, wo_own, attn_t)
+        u_col, m_full, dgu, d_down, y_out, d_hidden, d_attn, d_wo, d_g2, d_gate_t, d_up_t = call(
+            mlp, 1, len(args),
+            (((seq, rows), BF16), ((N_CHIP, WIDE, dim), BF16), ((2 * feat, seq), BF16), ((feat, dim), F32),
+             *tok_shapes, ((qw, seq), BF16), ((qw, dim), F32), ((N_CHIP, dim), F32), *dw_shapes),
             [vm((2 * feat, dim), BF16), vm((feat, dim), BF16), vm((feat, seq), BF16), vm((2 * feat, seq), BF16), dma(2),
-             full, full, dma(N_CHIP, 3), *(2 * Gather.sems), *Swap.sems],
-            8 * feat * seq * dim, far_in=(2, 3), far_out=(1, 2, 3))(*args)
-        args = (dgu, wgu, hidden, small_all, d_out, wo_own, attn_t, glu, w_down, m_full)
-        y_out, d_hidden, d_attn, d_wo, d_g2, d_gate_t, d_up_t = call(
-            mlp_back, 2, len(args),
-            (*tok_shapes, ((qw, seq), BF16), ((qw, dim), F32), ((N_CHIP, dim), F32), *dw_shapes),
-            [vm((N_CHIP, WIDE, WIDE), BF16), vm((2 * feat, WIDE), F32),
-             vm((2 * feat, seq), BF16), vm((2 * feat, dim), BF16), vm((feat, seq), BF16), vm((feat, dim), BF16), dma(5),
-             full, gain_scr, vm((WIDE, 2 * feat), BF16), vm((WIDE, feat), BF16), pltpu.SemaphoreType.REGULAR,
-             *Scatter.scratch(tokens, dim), *Scatter.sems, *Gather.sems, *(2 * Swap.sems)], 4 * feat * seq * dim,
-            far_in=(0, 1, 7, 8, 9), far_out=(5, 6))(*args)
+             full, full, dma(N_CHIP, 2), vm((2 * feat, WIDE), F32), gain_scr, vm((WIDE, 2 * feat), BF16), vm((WIDE, feat), BF16), pltpu.SemaphoreType.REGULAR,
+             *Scatter.scratch(tokens, dim), *(3 * Gather.sems), *(3 * Swap.sems), *Scatter.sems], 12 * feat * seq * dim,
+            far_in=(2, 3), far_out=(1, 2, 9, 10))(*args)
         cos_all, sin_all = rope_tables(small_all[:, 2].reshape(-1), hd)
         args = (qkv, d_attn, stat, cos_all, sin_all, dgu, m_full, u_col, cos_own, sin_own, wqkv, x_in, small_all, d_hidden, d_g2, d_gate_t, d_up_t)
         d_gate_t, d_up_t, d_wq, d_wkv, d_x, gains = call(

time: 520 us -> 497 us (0.956)
  Pallas kernels: 504 us -> 482 us
    pallas_call x1, Pallas kernels: 116 us -> 104 us  [layer_step(): call(functools.partial(back, n_kv, hd), 3, len(args), (*dw_shapes, ((n_q...]
    pallas_call x2 -> x1, Pallas kernels: 247 us -> 237 us  [layer_step(): call(mlp, 1, len(args), (((seq, rows), BF16), ((N_CHIP, WIDE, dim), BF16)...]
where the time goes in v10:
time: 497 us; the launch traced here: 488 us
  Pallas kernels  482 us (97%)
    pallas_call x1, Pallas kernels, layer_step(): call(mlp, 1, len(args), (((seq, rows), BF16), ((N_CHIP, WIDE, dim), BF16)...  237 us
    pallas_call x1, Pallas kernels, layer_step(): call(functools.partial(head, n_kv, hd), 0, len(args), (((qw + 2 * hd, seq...  130 us
    pallas_call x1, Pallas kernels, layer_step(): call(functools.partial(back, n_kv, hd), 3, len(args), (*dw_shapes, ((n_q...  104 us

profile of v10, /device:TPU:0, one launch (start us, length us, event | category | flops | bytes accessed | tf_op | source)
XLA Modules:
  0.0 488.0 jit_solution(9702333703301398320)
XLA Ops:
  0.7 0.7 convert_element_type.3
  1.3 0.8 multiply_sine_fusion.1
  2.1 130.2 %head.1 = (bf16[256,2048]{1,0:T(8,128)(2,1)}, bf16[128,2048]{1,0:T(8,128)(2,1)}, f32[16,8,128]{2,1,0:T(8,128)}, bf16[8,2560,256]{2,1,0:T(8,128)(2,1)}, bf16[128,...) custom-call(bf16[128,2048]{1,0:T(8,128)(2,1)} %x_ref.3, ...), custom_call_target="tpu_custom_call" | custom-call | flops 2147483648 | bytes 4194304 | tf_op jit(solution)/shard_map/head/pallas_call | solution.py:917
  132.3 0.8 slice.9
  133.2 1.8 multiply_sine_fusion
  135.0 237.5 %mlp.1 = (bf16[2048,128]{1,0:T(8,128)(2,1)}, bf16[8,256,2048]{2,1,0:T(8,128)(2,1)}, bf16[704,2048]{1,0:T(8,128)(2,1)}, f32[352,2048]{1,0:T(8,128)}, bf16[128,204...) custom-call(bf16[128,2048]{1,0:T(8,128)(2,1)} %get-tuple-element.48., ...), custom_call_target="tpu_custom_call" | custom-call | flops 17716740096 | bytes 34603008 | tf_op jit(solution)/shard_map/mlp/pallas_call | solution.py:926
  372.4 104.1 %back.1 = (f32[5632,128]{1,0:T(8,128)}, f32[5632,128]{1,0:T(8,128)}, f32[2048,128]{1,0:T(8,128)}, f32[512,128]{1,0:T(8,128)}, bf16[128,2048]{1,0:T(8,128)(2,1)}, /*index=5*/f32[8,128]{1,0:T(8,128)}) custom-call(bf16[256,2048]{1,0:T(8,128)(2,1)} %get-tuple-element.47.qkv_ref, ...), custom_call_target="tpu_custom_call", output_to_operand_aliasing={{0}: (15, {}), {1}: (16, {})} | custom-call | flops 5368709120 | bytes 10485760 | tf_op jit(solution)/shard_map/back/pallas_call | solution.py:936
  476.6 9.7 %finish.1 = (f32[128,5632]{1,0:T(8,128)}, f32[128,5632]{1,0:T(8,128)}, f32[256,128]{1,0:T(8,128)}, f32[256,128]{1,0:T(8,128)}, f32[2048,128]{1,0:T(8,128)}, /*in...) custom-call(f32[5632,128]{1,0:T(8,128)} %get-tuple-element.64.dg_hbm, ...), custom_call_target="tpu_custom_call" | custom-call | tf_op jit(solution)/shard_map/finish/pallas_call | solution.py:947
  486.3 1.3 slice_bitcast_fusion
  (1 shorter events, 0.0 us)

commit v11 on v10

--- a/solution.py
+++ b/solution.py
@@ -393,7 +393,7 @@
     return jnp.concatenate([ref[h * hd:(h + 1) * hd, qs] for h in range(heads)], axis=1)
 
 
-def head(groups, hd, x_ref, g1_ref, g2_ref, pos_ref, wq_ref, wk_ref, wv_ref, cos_ref, sin_ref, wg_ref, wu_ref, wo_ref, qkv_ref, u_scr, small_all, w_out, o_ref, stat_ref, wgu_ref, h_ref, m_ref,
+def head(groups, hd, x_ref, g1_ref, g2_ref, pos_ref, wq_ref, wk_ref, wv_ref, freq_ref, wg_ref, wu_ref, wo_ref, qkv_ref, u_scr, small_all, w_out, o_ref, stat_ref, wgu_ref, h_ref, m_ref, cos_ref, sin_ref,
          full_w, acc_o, o_tok, o_send, small_ref, w_ref, full, acc, rot, g_scr, wg_t, wu_t, s_scr, k_scr, osem, *sems):
     me = lax.axis_index('sp')
     tokens, dim = x_ref.shape
@@ -451,15 +451,22 @@
             acc[rs, :] += mm(full[chip, rs, :], u, NT)
         loop(2, step)
 
+    def tables(o):
+        angles = freq_ref[...] * small_all[o, 2:3, :]
+        cos_ref[:, seg(o)] = jnp.cos(angles)
+        sin_ref[:, seg(o)] = jnp.sin(angles)
+
     for r in range(len(g.ROUNDS)):
         g.round(r)
         if r in (2, 4):
             advance(r // 2)
+        if r == 1:
+            loop(N_DEV, tables)
         for mask in g.READY[r]:
             use(mask)
 
     half = hd // 2
-    cos, sin = cos_ref[...], sin_ref[...]
+    cos, sin = cos_ref[:, seg(me)], sin_ref[:, seg(me)]
 
     def turn(h):
         first = seg(2 * h, half)
@@ -573,8 +580,8 @@
 
 
 def mlp(m_ref, dout_ref, wgu_hbm, down_hbm, u_ref, h_ref, small_all, wo_ref, o_ref,
-        ucol_ref, m_out, dgu_out, ddown_ref, y_ref, dh_ref, do_ref, dwo_ref, dg_ref, gate_hbm, up_hbm,
-        wgu_ref, down_ref, glu_ref, dgu_ref, isem, full_d, full_m, osem, stage, g_scr, dgu_t, glu_t, free, *scr):
+        ucol_ref, m_out, dgu_out, ddown_out, y_ref, dh_ref, do_ref, dwo_ref, dg_ref, gate_hbm, up_hbm,
+        wgu_ref, down_ref, glu_ref, dgu_ref, ddown_ref, isem, dsem, full_d, full_m, osem, stage, g_scr, dgu_t, glu_t, free, *scr):
     me = lax.axis_index('sp')
     feat, dim = down_ref.shape
     loads = fetch_all(isem, (wgu_hbm, wgu_ref), (down_hbm, down_ref))
@@ -637,6 +644,8 @@
         swap.start(SETS[0])
     for gather in (gd, gm):
         gather.finish()
+    leave = pltpu.make_async_copy(ddown_ref, ddown_out, dsem)
+    leave.start()
     s = Scatter(*scr[:4], sems[18:], me)
     total = s.run(block_product(s, dgu_ref, wgu_ref, dgu_t))
     for mask in NEAR:
@@ -673,12 +682,13 @@
         swap.wait_send(SETS[0])
     ucols.wait_recv()
     ucols.wait_send()
+    leave.wait()
     for mask in CHIP_MASKS:
         for copy in keep(mask):
             copy.wait()
 
 
-def back(groups, hd, qkv_ref, do_ref, stat_ref, cos_all, sin_all, dgu_ref, m_hbm, ucol_ref, cos_ref, sin_ref, w_hbm, x_ref, small_all, dh_ref, dg2_ref, dg_in, du_in,
+def back(groups, hd, qkv_ref, do_ref, stat_ref, cos_all, sin_all, dgu_ref, m_hbm, ucol_ref, w_hbm, x_ref, small_all, dh_ref, dg2_ref, dg_in, du_in,
          dg_hbm, du_hbm, dwq_ref, dwkv_ref, dx_ref, gain_ref,
          p_scr, dp_scr, k_scr, v_scr, dk_acc, dv_acc, stage, dq_scr, dkv_scr, m_scr,
          full, w_scr, shares, dkv_own, full_kv, dqkv, dn, g_scr, dg1, gains, gains_in, wsem, lsem, msem, *sems):
@@ -718,14 +728,12 @@
                 swap.wait_send(SETS[n - 1])
             swap.start(SETS[n])
 
-    for i, mask in enumerate(first):
+    for mask in first[:2]:
         make(mask)
-        if i == 1:
-            advance(1)
-    gates.start((CORE,))
-    ups.start((CORE,))
-    for copy in own:
-        copy.start()
+        for swap in (gates, ups):
+            swap.start((mask, mask + CORE))
+    for mask in first[2:4]:
+        make(mask)
 
     dk_acc[...] = jnp.zeros_like(dk_acc)
     dv_acc[...] = jnp.zeros_like(dv_acc)
@@ -784,10 +792,16 @@
     gs = Swap(lambda peer: gains.at[:, seg(peer)], lambda o: gains_in.at[o], sems[14:], me)
     sh.start()
     gq.start()
+    for mask in first[4:]:
+        make(mask)
+    for swap in (gates, ups):
+        swap.start((CORE,))
+    for copy in own:
+        copy.start()
     keep_own(dq_scr, full, me)
     shares[me] = dkv_scr[seg(me, tokens), :]
     sh.wait_recv()
-    cos, sin = cos_ref[...], sin_ref[...]
+    cos, sin = cos_all[:, seg(me)], sin_all[:, seg(me)]
     for k in range(groups):
         both = sum(shares[per * k + i].astype(F32) for i in range(per)).astype(BF16).astype(F32).T
         p, q = both[:half], both[half:hd]
@@ -861,10 +875,10 @@
     for w, i in starts:
         fetch(w, i).start()
     kv.start()
-    for load, _ in moves:
-        load.start()
-    for w, i in starts:
+    for k, (w, i) in enumerate(starts):
         fetch(w, i).wait()
+        if k < len(moves):
+            moves[k][0].start()
 
         at = pl.ds(i * step, step)
         g_out[w, :, at] = g_in[w, at, :].T
@@ -880,13 +894,6 @@
         put(w, i).wait()
     for _, store in moves:
         store.wait()
-
-
-def rope_tables(positions, head_dim):
-    half_dim = head_dim // 2
-    inv_freq = 1.0 / (ROPE_BASE ** (jnp.arange(half_dim, dtype=F32) * (2.0 / head_dim)))
-    angles = positions.astype(F32)[None, :] * inv_freq[:, None]
-    return jnp.cos(angles), jnp.sin(angles)
 
 
 def solution(mesh):
@@ -908,16 +915,17 @@
         tok_shapes = 2 * (((tokens, dim), BF16),)
         dw_shapes = 2 * (((feat * N_DEV, rows), F32),)
 
-        cos_own, sin_own = rope_tables(positions, hd)
+        inv_freq = 1.0 / (ROPE_BASE ** (jnp.arange(hd // 2, dtype=F32) * (2.0 / hd)))
+        freq = jnp.broadcast_to(inv_freq[:, None], (hd // 2, rows))
         row = lambda v: v.reshape(1, rows)
         by_head = lambda w: w.transpose(1, 2, 0).reshape(-1, rows)
         wo_own = w_o.reshape(qw, dim)
 
-        args = (x_in, row(norm1_gain), row(norm2_gain), row(positions), by_head(w_q), by_head(w_k), by_head(w_v), cos_own, sin_own, w_gate, w_up, wo_own)
-        qkv, u, small_all, wqkv, attn_t, stat, wgu, hidden, mlp_in = call(
+        args = (x_in, row(norm1_gain), row(norm2_gain), row(positions), by_head(w_q), by_head(w_k), by_head(w_v), freq, w_gate, w_up, wo_own)
+        qkv, u, small_all, wqkv, attn_t, stat, wgu, hidden, mlp_in, cos_all, sin_all = call(
             functools.partial(head, n_kv, hd), 0, len(args),
             (((qw + 2 * hd, seq), BF16), tok_shapes[0], ((N_DEV, N_CHIP, rows), F32), ((N_CHIP, cols, WIDE), BF16),
-             ((qw, seq), BF16), ((seq // QB, 2, lanes), F32), ((2 * feat, dim), BF16), *tok_shapes),
+             ((qw, seq), BF16), ((seq // QB, 2, lanes), F32), ((2 * feat, dim), BF16), *tok_shapes, *(2 * (((hd // 2, seq), F32),))),
             [full, vm((tokens, dim), F32), vm((tokens, dim), BF16), vm((seq, qw), BF16),
              vm((N_CHIP, rows), F32), vm((cols, rows), BF16), vm((N_CHIP, cols, WIDE), BF16), vm((cols, tokens), F32), vm((cols, tokens), BF16), gain_scr,
              vm((feat * N_DEV, rows), BF16), vm((feat * N_DEV, rows), BF16), vm((seq, lanes), F32), vm((seq, hd), BF16), dma(N_CHIP),
@@ -927,12 +935,11 @@
             mlp, 1, len(args),
             (((seq, rows), BF16), ((N_CHIP, WIDE, dim), BF16), ((2 * feat, seq), BF16), ((feat, dim), F32),
              *tok_shapes, ((qw, seq), BF16), ((qw, dim), F32), ((N_CHIP, dim), F32), *dw_shapes),
-            [vm((2 * feat, dim), BF16), vm((feat, dim), BF16), vm((feat, seq), BF16), vm((2 * feat, seq), BF16), dma(2),
+            [vm((2 * feat, dim), BF16), vm((feat, dim), BF16), vm((feat, seq), BF16), vm((2 * feat, seq), BF16), vm((feat, dim), F32), dma(2), dma(),
              full, full, dma(N_CHIP, 2), vm((2 * feat, WIDE), F32), gain_scr, vm((WIDE, 2 * feat), BF16), vm((WIDE, feat), BF16), pltpu.SemaphoreType.REGULAR,
              *Scatter.scratch(tokens, dim), *(3 * Gather.sems), *(3 * Swap.sems), *Scatter.sems], 12 * feat * seq * dim,
-            far_in=(2, 3), far_out=(1, 2, 9, 10))(*args)
-        cos_all, sin_all = rope_tables(small_all[:, 2].reshape(-1), hd)
-        args = (qkv, d_attn, stat, cos_all, sin_all, dgu, m_full, u_col, cos_own, sin_own, wqkv, x_in, small_all, d_hidden, d_g2, d_gate_t, d_up_t)
+            far_in=(2, 3), far_out=(1, 2, 3, 9, 10))(*args)
+        args = (qkv, d_attn, stat, cos_all, sin_all, dgu, m_full, u_col, wqkv, x_in, small_all, d_hidden, d_g2, d_gate_t, d_up_t)
         d_gate_t, d_up_t, d_wq, d_wkv, d_x, gains = call(
             functools.partial(back, n_kv, hd), 3, len(args),
             (*dw_shapes, ((n_q * hd, rows), F32), ((2 * n_kv * hd, rows), F32), tok_shapes[0], ((N_CHIP, rows), F32)),
@@ -940,7 +947,7 @@
              vm((N_CHIP, 2 * feat, WIDE), F32), vm((qw, seq), BF16), vm((seq, 2 * hd), BF16), full,
              full, vm((N_CHIP, cols, WIDE), BF16), vm((N_DEV, tokens, 2 * hd), BF16), vm((2 * n_kv * hd, tokens), BF16), vm((2 * n_kv * hd, seq), BF16),
              vm((tokens, cols), BF16), vm((tokens, dim), F32), gain_scr, gain_scr, gain_scr, vm((N_DEV, N_CHIP, rows), F32), dma(), dma(2), dma(N_CHIP),
-             *(3 * Swap.sems), *(2 * Gather.sems), *Swap.sems], 10 * qw * seq * seq, far_in=(6, 10, 15, 16), far_out=(0, 1), aliases={15: 0, 16: 1})(*args)
+             *(3 * Swap.sems), *(2 * Gather.sems), *Swap.sems], 10 * qw * seq * seq, far_in=(6, 8, 13, 14), far_out=(0, 1), aliases={13: 0, 14: 1})(*args)
         moved = (d_wq, d_wo, d_down, d_x, y_out, gains)
         half_kv = jax.ShapeDtypeStruct((n_kv * hd, rows), F32)
         wide = jax.ShapeDtypeStruct((rows, feat * N_DEV), F32)

time: 497 us -> 500 us (level)
  Pallas kernels: 482 us -> 489 us
    pallas_call x1, Pallas kernels: 104 us -> 112 us  [layer_step(): call(functools.partial(back, n_kv, hd), 3, len(args), (*dw_shapes, ((n_q...]
where the time goes in v11:
time: 500 us; the launch traced here: 492 us
  Pallas kernels  489 us (98%)
    pallas_call x1, Pallas kernels, layer_step(): call(mlp, 1, len(args), (((seq, rows), BF16), ((N_CHIP, WIDE, dim), BF16)...  237 us
    pallas_call x1, Pallas kernels, layer_step(): call(functools.partial(head, n_kv, hd), 0, len(args), (((qw + 2 * hd, seq...  130 us
    pallas_call x1, Pallas kernels, layer_step(): call(functools.partial(back, n_kv, hd), 3, len(args), (*dw_shapes, ((n_q...  112 us

profile of v11, /device:TPU:0, one launch (start us, length us, event | category | flops | bytes accessed | tf_op | source)
XLA Modules:
  0.0 492.1 jit_solution(13714759880040171431)
XLA Ops:
  0.7 0.7 broadcast_in_dim.2.freq_ref
  1.3 130.4 %head.1 = (bf16[256,2048]{1,0:T(8,128)(2,1)}, bf16[128,2048]{1,0:T(8,128)(2,1)}, f32[16,8,128]{2,1,0:T(8,128)}, bf16[8,2560,256]{2,1,0:T(8,128)(2,1)}, bf16[128,...) custom-call(bf16[128,2048]{1,0:T(8,128)(2,1)} %x_ref.3, ...), custom_call_target="tpu_custom_call" | custom-call | flops 2147483648 | bytes 4194304 | tf_op jit(solution)/shard_map/head/pallas_call | solution.py:925
  131.7 236.6 %mlp.1 = (bf16[2048,128]{1,0:T(8,128)(2,1)}, bf16[8,256,2048]{2,1,0:T(8,128)(2,1)}, bf16[704,2048]{1,0:T(8,128)(2,1)}, f32[352,2048]{1,0:T(8,128)}, bf16[128,204...) custom-call(bf16[128,2048]{1,0:T(8,128)(2,1)} %get-tuple-element.50., ...), custom_call_target="tpu_custom_call" | custom-call | flops 17716740096 | bytes 34603008 | tf_op jit(solution)/shard_map/mlp/pallas_call | solution.py:934
  368.3 112.2 %back.1 = (f32[5632,128]{1,0:T(8,128)}, f32[5632,128]{1,0:T(8,128)}, f32[2048,128]{1,0:T(8,128)}, f32[512,128]{1,0:T(8,128)}, bf16[128,2048]{1,0:T(8,128)(2,1)}, /*index=5*/f32[8,128]{1,0:T(8,128)}) custom-call(bf16[256,2048]{1,0:T(8,128)(2,1)} %get-tuple-element.49.qkv_ref, ...), custom_call_target="tpu_custom_call", output_to_operand_aliasing={{0}: (13, {}), {1}: (14, {})} | custom-call | flops 5368709120 | bytes 10485760 | tf_op jit(solution)/shard_map/back/pallas_call | solution.py:943
  480.6 9.8 %finish.1 = (f32[128,5632]{1,0:T(8,128)}, f32[128,5632]{1,0:T(8,128)}, f32[256,128]{1,0:T(8,128)}, f32[256,128]{1,0:T(8,128)}, f32[2048,128]{1,0:T(8,128)}, /*in...) custom-call(f32[5632,128]{1,0:T(8,128)} %get-tuple-element.68.dg_hbm, ...), custom_call_target="tpu_custom_call" | custom-call | tf_op jit(solution)/shard_map/finish/pallas_call | solution.py:954
  490.4 1.3 slice_bitcast_fusion
  (1 shorter events, 0.0 us)

commit v12 on v11

--- a/solution.py
+++ b/solution.py
@@ -16,7 +16,7 @@
 TN = (((0,), (0,)), ((), ()))
 NN = (((1,), (0,)), ((), ()))
 MESH = pl.DeviceIdType.MESH
-VMEM_CAP = 62 * 1024 * 1024
+VMEM_CAP = 67043328
 
 CORE, X, Y, Z = 1, 2, 4, 8
 XYZ = X + Y + Z
@@ -266,7 +266,7 @@
         self.add(mask, ref, wide)
         self.part[self.ORDER.index(mask), rs, cs] += ref[rs, cs]
 
-    def run(self, product, between=lambda i: None):
+    def run(self, product, between=lambda i: None, before_last=lambda: None):
         for i, mask in enumerate(self.ORDER):
             if i > 1:
                 self.pair(i - 2).wait_send()
@@ -282,6 +282,7 @@
                 mask = (b + c, b)[step]
                 self.take(colour, mask, a)
                 self.start_link(colour, mask)
+        before_last()
         for colour in COLOURS:
             a, b, c = ORDERS[colour]
             self.take(colour, c, a)
@@ -573,14 +574,12 @@
         swap.wait_send()
 
 
-def dw_swaps(stage, gate_hbm, up_hbm, sems, me):
-    feat = gate_hbm.shape[0] // N_DEV
-    return [Swap(lambda peer, lo=lo: stage(peer).at[lo:lo + feat, seg(peer % 2)], lambda o, dst=dst: dst.at[seg(o, feat), :], sems[i:i + 2], me)
-            for lo, dst, i in ((0, gate_hbm, 0), (feat, up_hbm, 2))]
+def dw_swap(stage, dw_hbm, sems, me):
+    return Swap(lambda peer: stage(peer).at[:, seg(peer % 2)], lambda o: dw_hbm.at[o], sems, me)
 
 
 def mlp(m_ref, dout_ref, wgu_hbm, down_hbm, u_ref, h_ref, small_all, wo_ref, o_ref,
-        ucol_ref, m_out, dgu_out, ddown_out, y_ref, dh_ref, do_ref, dwo_ref, dg_ref, gate_hbm, up_hbm,
+        ucol_ref, m_out, dgu_out, ddown_out, y_ref, dh_ref, do_ref, dwo_ref, dg_ref, dw_hbm,
         wgu_ref, down_ref, glu_ref, dgu_ref, ddown_ref, isem, dsem, full_d, full_m, osem, stage, g_scr, dgu_t, glu_t, free, *scr):
     me = lax.axis_index('sp')
     feat, dim = down_ref.shape
@@ -591,7 +590,12 @@
     gm = row_gather(m_ref, full_m, sems[4:8], me, 2)
     g = row_gather(dh_ref, full_d, sems[8:12], me, 1)
     ucols = Swap(lambda peer: u_ref.at[:, seg(peer)], lambda o: ucol_ref.at[seg(o), :], sems[12:14], me)
-    gates, ups = dw_swaps(lambda peer: stage, gate_hbm, up_hbm, sems[14:18], me)
+    def dw_part(slot, mask):
+        cols = full_m[:, :, seg(flipped(me, mask) // 2, WIDE)].reshape(dgu_ref.shape[1], WIDE)
+        stage[slot] = mm(dgu_ref[...], cols, NN)
+        swap = dw_swap(lambda peer: stage.at[slot], dw_hbm, sems[14:16], me)
+        loop(2, lambda core: swap.copy(mask + core).start())
+
     gm.start()
     gd.start()
     ucol_ref[seg(me), :] = u_ref[:, seg(me)]
@@ -638,15 +642,12 @@
             ucols.start()
         for mask in gm.READY[r]:
             use(mask)
-    far = seg(flipped(me, XYZ) // 2, WIDE)
-    stage[...] = mm(dgu_ref[...], full_m[:, :, far].reshape(dgu_ref.shape[1], WIDE), NN)
-    for swap in (gates, ups):
-        swap.start(SETS[0])
+    dw_part(0, XYZ)
     for gather in (gd, gm):
         gather.finish()
     leave = pltpu.make_async_copy(ddown_ref, ddown_out, dsem)
     leave.start()
-    s = Scatter(*scr[:4], sems[18:], me)
+    s = Scatter(*scr[:4], sems[16:], me)
     total = s.run(block_product(s, dgu_ref, wgu_ref, dgu_t))
     for mask in NEAR:
         pl.semaphore_signal(free, inc=1, device_id=(flipped(me, mask),), device_id_type=MESH)
@@ -672,24 +673,23 @@
             for mask in g.READY[i]:
                 use_dh(mask)
 
-    s = Scatter(*scr[:4], sems[18:], me)
-    total = s.run(block_product(s, glu_ref, down_ref, glu_t), between)
+    s = Scatter(*scr[:4], sems[16:], me)
+    total = s.run(block_product(s, glu_ref, down_ref, glu_t), between, lambda: (dw_part(1, X), dw_part(2, Y + Z)))
     y_ref[...] = (h_ref[...].astype(F32) + total[...]).astype(BF16)
     s.finish()
     g.finish()
-    for swap in (gates, ups):
-        swap.wait_recv(SETS[0])
-        swap.wait_send(SETS[0])
+    swap = dw_swap(lambda peer: stage.at[0], dw_hbm, sems[14:16], me)
+    for mask in (XYZ, X, Y + Z):
+        loop(2, lambda core: (swap.arrival(mask + core).wait_recv(), swap.copy(mask + core).wait_send()))
     ucols.wait_recv()
     ucols.wait_send()
     leave.wait()
-    for mask in CHIP_MASKS:
-        for copy in keep(mask):
-            copy.wait()
-
-
-def back(groups, hd, qkv_ref, do_ref, stat_ref, cos_all, sin_all, dgu_ref, m_hbm, ucol_ref, w_hbm, x_ref, small_all, dh_ref, dg2_ref, dg_in, du_in,
-         dg_hbm, du_hbm, dwq_ref, dwkv_ref, dx_ref, gain_ref,
+    loop(N_CHIP, lambda j: [pltpu.make_async_copy(src, dst, osem.at[j, i]).wait() for i, (src, dst) in enumerate(
+        ((full_m.at[0], m_out.at[0]), (dgu_ref.at[:, seg(0, WIDE)], dgu_out.at[:, seg(0, WIDE)])))])
+
+
+def back(groups, hd, qkv_ref, do_ref, stat_ref, cos_all, sin_all, dgu_ref, m_hbm, ucol_ref, w_hbm, x_ref, small_all, dh_ref, dg2_ref, dw_in,
+         dw_hbm, dwq_ref, dwkv_ref, dx_ref, gain_ref,
          p_scr, dp_scr, k_scr, v_scr, dk_acc, dv_acc, stage, dq_scr, dkv_scr, m_scr,
          full, w_scr, shares, dkv_own, full_kv, dqkv, dn, g_scr, dg1, gains, gains_in, wsem, lsem, msem, *sems):
     heads = qkv_ref.shape[0] // hd - 2
@@ -700,7 +700,7 @@
     half = hd // 2
     me = lax.axis_index('sp')
     feat = dgu_ref.shape[0] // 2
-    first = (X, Y + Z, Y, X + Z, Z, X + Y, 0)
+    first = (Y, X + Z, Z, X + Y, 0)
 
     def fetch(mask):
         cols = seg(flipped(me, mask) // 2, WIDE)
@@ -712,9 +712,9 @@
     enter(me, OTHERS)
     gain_row(g_scr, small_all, 0)
 
-    gates, ups = dw_swaps(lambda peer: stage.at[peer // 2], dg_hbm, du_hbm, sems[:4], me)
-    gq = row_gather(dq_scr, full, sems[6:10], me)
-    own = [pltpu.make_async_copy(swap.src(me), swap.dst(me), lsem.at[i]) for i, swap in enumerate((gates, ups))]
+    dws = dw_swap(lambda peer: stage.at[peer // 2], dw_hbm, sems[:2], me)
+    gq = row_gather(dq_scr, full, sems[4:8], me)
+    own = pltpu.make_async_copy(dws.src(me), dws.dst(me), lsem)
 
     def make(mask):
         chip = flipped(me, mask) // 2
@@ -723,17 +723,16 @@
         stage[chip] = mm(dgu_ref[...], cols, NN)
 
     def advance(n):
-        for swap in (gates, ups):
-            if n > 1:
-                swap.wait_send(SETS[n - 1])
-            swap.start(SETS[n])
-
-    for mask in first[:2]:
+        if n > 2:
+            dws.wait_send(SETS[n - 1])
+        dws.start(SETS[n])
+
+    for i, mask in enumerate(first):
         make(mask)
-        for swap in (gates, ups):
-            swap.start((mask, mask + CORE))
-    for mask in first[2:4]:
-        make(mask)
+        if i == 1:
+            advance(2)
+    dws.start((CORE,))
+    own.start()
 
     dk_acc[...] = jnp.zeros_like(dk_acc)
     dv_acc[...] = jnp.zeros_like(dv_acc)
@@ -741,9 +740,9 @@
     key_rows(v_scr, qkv_ref, qw + hd, hd)
 
     def q_block(qb):
-        @pl.when(qb == 4)
+        @pl.when(qb == 5)
         def _():
-            advance(2)
+            advance(3)
         qs = seg(qb, QB)
         q2 = side_by_side(qkv_ref, heads, hd, qs)
         do2 = side_by_side(do_ref, heads, hd, qs)
@@ -786,18 +785,12 @@
     tokens = ucol_ref.shape[1]
     per = N_DEV // groups
     q_all = dwq_ref.shape[0]
-    sh = Swap(lambda peer: dkv_scr.at[seg(peer, tokens), :], lambda o: shares.at[o], sems[4:6], me)
+    sh = Swap(lambda peer: dkv_scr.at[seg(peer, tokens), :], lambda o: shares.at[o], sems[2:4], me)
     parts = thirds(dkv_own.shape[0], STRIP)
-    gk = Gather(dkv_own, lambda o: full_kv.at[:, seg(o, tokens)], lambda view, c: [view.at[pl.ds(*parts[c]), :]], sems[10:14], me)
-    gs = Swap(lambda peer: gains.at[:, seg(peer)], lambda o: gains_in.at[o], sems[14:], me)
+    gk = Gather(dkv_own, lambda o: full_kv.at[:, seg(o, tokens)], lambda view, c: [view.at[pl.ds(*parts[c]), :]], sems[8:12], me)
+    gs = Swap(lambda peer: gains.at[:, seg(peer)], lambda o: gains_in.at[o], sems[12:], me)
     sh.start()
     gq.start()
-    for mask in first[4:]:
-        make(mask)
-    for swap in (gates, ups):
-        swap.start((CORE,))
-    for copy in own:
-        copy.start()
     keep_own(dq_scr, full, me)
     shares[me] = dkv_scr[seg(me, tokens), :]
     sh.wait_recv()
@@ -823,8 +816,6 @@
     for r in range(len(gq.ROUNDS)):
         gq.round(r)
         gk.round(r)
-        if r == 3:
-            advance(3)
         for mask in gq.READY[r]:
             use(mask)
     load.wait()
@@ -842,30 +833,29 @@
     dwkv_ref[...] = mm(full_kv[...], ucol_ref[...], NN)
     gs.wait_recv()
     gain_ref[...] = sum(gains_in[o] for o in range(N_DEV))
-    for swap in (gates, ups):
-        swap.wait_recv((CORE,) + SETS[1] + SETS[2] + SETS[3])
-        swap.wait_send((CORE,) + SETS[3])
-    for copy in own:
-        copy.wait()
+    dws.wait_recv((CORE,) + SETS[2] + SETS[3])
+    dws.wait_send((CORE,) + SETS[3])
+    own.wait()
     for c in (sh, gs):
         c.wait_send()
     for g in (gq, gk):
         g.finish()
 
 
-def finish(dg_hbm, du_hbm, dkv_hbm, *refs):
+def finish(dw_hbm, dkv_hbm, *refs):
     n = (len(refs) - 11) // 3
     srcs, (gate, up, dk, dv), dsts = refs[:n], refs[n:n + 4], refs[n + 4:2 * n + 4]
     (g_in, g_out, kv_in), holds, sems = refs[2 * n + 4:2 * n + 7], refs[2 * n + 7:3 * n + 7], refs[3 * n + 7:]
     t_in, t_out, p_in, p_out = sems
-    step = LANE * 11
-    cols = g_in.shape[1]
+    feat = g_in.shape[2]
+    four = N_DEV // 4
+    step = four * feat
     hd = dk.shape[0] // (kv_in.shape[0] // LANE)
-    starts = [(w, i) for i in range(cols // step) for w in range(2)]
+    starts = [(w, i) for i in range(4) for w in range(2)]
 
     def fetch(w, i):
-        rs = pl.ds(i * step, step)
-        return pltpu.make_async_copy((dg_hbm, du_hbm)[w].at[rs, :], g_in.at[w, rs, :], t_in.at[w, i])
+        at = pl.ds(i * four, four)
+        return pltpu.make_async_copy(dw_hbm.at[at, pl.ds(w * feat, feat), :], g_in.at[w, at], t_in.at[w, i])
 
     def put(w, i):
         cs = pl.ds(i * step, step)
@@ -880,8 +870,7 @@
         if k < len(moves):
             moves[k][0].start()
 
-        at = pl.ds(i * step, step)
-        g_out[w, :, at] = g_in[w, at, :].T
+        g_out[w, :, pl.ds(i * step, step)] = g_in[w, pl.ds(i * four, four)].reshape(step, LANE).T
         put(w, i).start()
     kv.wait()
     for k in range(dk.shape[0] // hd):
@@ -913,7 +902,7 @@
         full = vm((N_CHIP, WIDE, dim), BF16)
         gain_scr = vm((N_CHIP, dim), F32)
         tok_shapes = 2 * (((tokens, dim), BF16),)
-        dw_shapes = 2 * (((feat * N_DEV, rows), F32),)
+        dw_shape = ((N_DEV, 2 * feat, rows), F32)
 
         inv_freq = 1.0 / (ROPE_BASE ** (jnp.arange(hd // 2, dtype=F32) * (2.0 / hd)))
         freq = jnp.broadcast_to(inv_freq[:, None], (hd // 2, rows))
@@ -931,34 +920,34 @@
              vm((feat * N_DEV, rows), BF16), vm((feat * N_DEV, rows), BF16), vm((seq, lanes), F32), vm((seq, hd), BF16), dma(N_CHIP),
              *Gather.sems, *(6 * Swap.sems), *Gather.sems], 4 * qw * seq * seq, far_out=(3,))(*args)
         args = (mlp_in, d_out, wgu, w_down, u, hidden, small_all, wo_own, attn_t)
-        u_col, m_full, dgu, d_down, y_out, d_hidden, d_attn, d_wo, d_g2, d_gate_t, d_up_t = call(
+        u_col, m_full, dgu, d_down, y_out, d_hidden, d_attn, d_wo, d_g2, d_gu = call(
             mlp, 1, len(args),
             (((seq, rows), BF16), ((N_CHIP, WIDE, dim), BF16), ((2 * feat, seq), BF16), ((feat, dim), F32),
-             *tok_shapes, ((qw, seq), BF16), ((qw, dim), F32), ((N_CHIP, dim), F32), *dw_shapes),
+             *tok_shapes, ((qw, seq), BF16), ((qw, dim), F32), ((N_CHIP, dim), F32), dw_shape),
             [vm((2 * feat, dim), BF16), vm((feat, dim), BF16), vm((feat, seq), BF16), vm((2 * feat, seq), BF16), vm((feat, dim), F32), dma(2), dma(),
-             full, full, dma(N_CHIP, 2), vm((2 * feat, WIDE), F32), gain_scr, vm((WIDE, 2 * feat), BF16), vm((WIDE, feat), BF16), pltpu.SemaphoreType.REGULAR,
-             *Scatter.scratch(tokens, dim), *(3 * Gather.sems), *(3 * Swap.sems), *Scatter.sems], 12 * feat * seq * dim,
-            far_in=(2, 3), far_out=(1, 2, 3, 9, 10))(*args)
-        args = (qkv, d_attn, stat, cos_all, sin_all, dgu, m_full, u_col, wqkv, x_in, small_all, d_hidden, d_g2, d_gate_t, d_up_t)
-        d_gate_t, d_up_t, d_wq, d_wkv, d_x, gains = call(
+             full, full, dma(N_CHIP, 2), vm((3, 2 * feat, WIDE), F32), gain_scr, vm((WIDE, 2 * feat), BF16), vm((WIDE, feat), BF16), pltpu.SemaphoreType.REGULAR,
+             *Scatter.scratch(tokens, dim), *(3 * Gather.sems), *(2 * Swap.sems), *Scatter.sems], 12 * feat * seq * dim,
+            far_in=(2, 3), far_out=(1, 2, 3, 9))(*args)
+        args = (qkv, d_attn, stat, cos_all, sin_all, dgu, m_full, u_col, wqkv, x_in, small_all, d_hidden, d_g2, d_gu)
+        d_gu, d_wq, d_wkv, d_x, gains = call(
             functools.partial(back, n_kv, hd), 3, len(args),
-            (*dw_shapes, ((n_q * hd, rows), F32), ((2 * n_kv * hd, rows), F32), tok_shapes[0], ((N_CHIP, rows), F32)),
+            (dw_shape, ((n_q * hd, rows), F32), ((2 * n_kv * hd, rows), F32), tok_shapes[0], ((N_CHIP, rows), F32)),
             [vm((seq, lanes), F32), vm((seq, lanes), BF16), vm((seq, hd), BF16), vm((seq, hd), BF16), vm((seq, hd), F32), vm((seq, hd), F32),
              vm((N_CHIP, 2 * feat, WIDE), F32), vm((qw, seq), BF16), vm((seq, 2 * hd), BF16), full,
              full, vm((N_CHIP, cols, WIDE), BF16), vm((N_DEV, tokens, 2 * hd), BF16), vm((2 * n_kv * hd, tokens), BF16), vm((2 * n_kv * hd, seq), BF16),
-             vm((tokens, cols), BF16), vm((tokens, dim), F32), gain_scr, gain_scr, gain_scr, vm((N_DEV, N_CHIP, rows), F32), dma(), dma(2), dma(N_CHIP),
-             *(3 * Swap.sems), *(2 * Gather.sems), *Swap.sems], 10 * qw * seq * seq, far_in=(6, 8, 13, 14), far_out=(0, 1), aliases={13: 0, 14: 1})(*args)
+             vm((tokens, cols), BF16), vm((tokens, dim), F32), gain_scr, gain_scr, gain_scr, vm((N_DEV, N_CHIP, rows), F32), dma(), dma(), dma(N_CHIP),
+             *(2 * Swap.sems), *(2 * Gather.sems), *Swap.sems], 10 * qw * seq * seq, far_in=(6, 8, 13), far_out=(0,), aliases={13: 0})(*args)
         moved = (d_wq, d_wo, d_down, d_x, y_out, gains)
         half_kv = jax.ShapeDtypeStruct((n_kv * hd, rows), F32)
         wide = jax.ShapeDtypeStruct((rows, feat * N_DEV), F32)
         d_gate, d_up, d_wk, d_wv, d_wq, d_wo, d_down, d_x, y_out, gains = pl.pallas_call(
             finish,
             out_shape=[wide, wide, half_kv, half_kv] + [jax.ShapeDtypeStruct(v.shape, v.dtype) for v in moved],
-            in_specs=[IN_HBM] * (3 + len(moved)), out_specs=[IN_HBM] * 2 + on_chip(2) + [IN_HBM] * len(moved),
-            scratch_shapes=[vm((2, feat * N_DEV, rows), F32), vm((2, rows, feat * N_DEV), F32), vm(d_wkv.shape, F32)]
+            in_specs=[IN_HBM] * (2 + len(moved)), out_specs=[IN_HBM] * 2 + on_chip(2) + [IN_HBM] * len(moved),
+            scratch_shapes=[vm((2, N_DEV, feat, rows), F32), vm((2, rows, feat * N_DEV), F32), vm(d_wkv.shape, F32)]
             + [vm(v.shape, v.dtype) for v in moved] + [dma(2, 4), dma(2, 4), dma(len(moved) + 1), dma(len(moved))],
             compiler_params=pltpu.CompilerParams(vmem_limit_bytes=VMEM_CAP), name='finish',
-        )(d_gate_t, d_up_t, d_wkv, *moved)
+        )(d_gu, d_wkv, *moved)
         by_row = lambda g, heads: g.reshape(heads, hd, rows).transpose(2, 0, 1)
         return (y_out, d_x, gains[0], gains[1], by_row(d_wq, n_q), by_row(d_wk, n_kv), by_row(d_wv, n_kv),
                 d_wo.reshape(w_o.shape), d_gate, d_up, d_down)

time: 500 us -> 500 us (level)
    pallas_call x1, Pallas kernels: 112 us -> 96.3 us  [layer_step(): call(functools.partial(back, n_kv, hd), 3, len(args), (dw_shape, ((n_q *...]
    pallas_call x1, Pallas kernels: 237 us -> 252 us  [layer_step(): call(mlp, 1, len(args), (((seq, rows), BF16), ((N_CHIP, WIDE, dim), BF16)...]
where the time goes in v12:
time: 500 us; the launch traced here: 491 us
  Pallas kernels  488 us (98%)
    pallas_call x1, Pallas kernels, layer_step(): call(mlp, 1, len(args), (((seq, rows), BF16), ((N_CHIP, WIDE, dim), BF16)...  252 us
    pallas_call x1, Pallas kernels, layer_step(): call(functools.partial(head, n_kv, hd), 0, len(args), (((qw + 2 * hd, seq...  130 us
    pallas_call x1, Pallas kernels, layer_step(): call(functools.partial(back, n_kv, hd), 3, len(args), (dw_shape, ((n_q *...  96.3 us

profile of v12, /device:TPU:0, one launch (start us, length us, event | category | flops | bytes accessed | tf_op | source)
XLA Modules:
  0.0 491.4 jit_solution(11011762816059623624)
XLA Ops:
  0.7 0.7 broadcast_in_dim.2.freq_ref
  1.3 130.4 %head.1 = (bf16[256,2048]{1,0:T(8,128)(2,1)}, bf16[128,2048]{1,0:T(8,128)(2,1)}, f32[16,8,128]{2,1,0:T(8,128)}, bf16[8,2560,256]{2,1,0:T(8,128)(2,1)}, bf16[128,...) custom-call(bf16[128,2048]{1,0:T(8,128)(2,1)} %x_ref.3, ...), custom_call_target="tpu_custom_call" | custom-call | flops 2147483648 | bytes 4194304 | tf_op jit(solution)/shard_map/head/pallas_call | solution.py:914
  131.7 251.8 %mlp.1 = (bf16[2048,128]{1,0:T(8,128)(2,1)}, bf16[8,256,2048]{2,1,0:T(8,128)(2,1)}, bf16[704,2048]{1,0:T(8,128)(2,1)}, f32[352,2048]{1,0:T(8,128)}, bf16[128,204...) custom-call(bf16[128,2048]{1,0:T(8,128)(2,1)} %get-tuple-element.48., ...), custom_call_target="tpu_custom_call" | custom-call | flops 17716740096 | bytes 34603008 | tf_op jit(solution)/shard_map/mlp/pallas_call | solution.py:923
  383.6 96.3 %back.1 = (f32[16,704,128]{2,1,0:T(8,128)}, f32[2048,128]{1,0:T(8,128)}, f32[512,128]{1,0:T(8,128)}, bf16[128,2048]{1,0:T(8,128)(2,1)}, f32[8,128]{1,0:T(8,128)}) custom-call(bf16[256,2048]{1,0:T(8,128)(2,1)} %get-tuple-element.47.qkv_ref, bf16[128,2048]{1,0:T(8,128)(2,1)} %get-tuple-element.54.do_ref, ...), custom_call_target="tpu_custom_call", output_to_operand_aliasing={{0}: (13, {})} | custom-call | flops 5368709120 | bytes 10485760 | tf_op jit(solution)/shard_map/back/pallas_call | solution.py:932
  479.8 9.8 %finish.1 = (f32[128,5632]{1,0:T(8,128)}, f32[128,5632]{1,0:T(8,128)}, f32[256,128]{1,0:T(8,128)}, f32[256,128]{1,0:T(8,128)}, f32[2048,128]{1,0:T(8,128)}, /*in...) custom-call(f32[16,704,128]{2,1,0:T(8,128)} %get-tuple-element.65.dw, ...), custom_call_target="tpu_custom_call" | custom-call | tf_op jit(solution)/shard_map/finish/pallas_call | solution.py:943
  489.7 1.3 slice_bitcast_fusion
  (1 shorter events, 0.0 us)

commit v13 on v12

--- a/solution.py
+++ b/solution.py
@@ -266,7 +266,7 @@
         self.add(mask, ref, wide)
         self.part[self.ORDER.index(mask), rs, cs] += ref[rs, cs]
 
-    def run(self, product, between=lambda i: None, before_last=lambda: None):
+    def run(self, product, between=lambda i: None):
         for i, mask in enumerate(self.ORDER):
             if i > 1:
                 self.pair(i - 2).wait_send()
@@ -282,7 +282,6 @@
                 mask = (b + c, b)[step]
                 self.take(colour, mask, a)
                 self.start_link(colour, mask)
-        before_last()
         for colour in COLOURS:
             a, b, c = ORDERS[colour]
             self.take(colour, c, a)
@@ -590,10 +589,10 @@
     gm = row_gather(m_ref, full_m, sems[4:8], me, 2)
     g = row_gather(dh_ref, full_d, sems[8:12], me, 1)
     ucols = Swap(lambda peer: u_ref.at[:, seg(peer)], lambda o: ucol_ref.at[seg(o), :], sems[12:14], me)
-    def dw_part(slot, mask):
+    def dw_part(mask):
         cols = full_m[:, :, seg(flipped(me, mask) // 2, WIDE)].reshape(dgu_ref.shape[1], WIDE)
-        stage[slot] = mm(dgu_ref[...], cols, NN)
-        swap = dw_swap(lambda peer: stage.at[slot], dw_hbm, sems[14:16], me)
+        stage[...] = mm(dgu_ref[...], cols, NN)
+        swap = dw_swap(lambda peer: stage, dw_hbm, sems[14:16], me)
         loop(2, lambda core: swap.copy(mask + core).start())
 
     gm.start()
@@ -642,7 +641,7 @@
             ucols.start()
         for mask in gm.READY[r]:
             use(mask)
-    dw_part(0, XYZ)
+    dw_part(XYZ)
     for gather in (gd, gm):
         gather.finish()
     leave = pltpu.make_async_copy(ddown_ref, ddown_out, dsem)
@@ -674,13 +673,12 @@
                 use_dh(mask)
 
     s = Scatter(*scr[:4], sems[16:], me)
-    total = s.run(block_product(s, glu_ref, down_ref, glu_t), between, lambda: (dw_part(1, X), dw_part(2, Y + Z)))
+    total = s.run(block_product(s, glu_ref, down_ref, glu_t), between)
     y_ref[...] = (h_ref[...].astype(F32) + total[...]).astype(BF16)
     s.finish()
     g.finish()
-    swap = dw_swap(lambda peer: stage.at[0], dw_hbm, sems[14:16], me)
-    for mask in (XYZ, X, Y + Z):
-        loop(2, lambda core: (swap.arrival(mask + core).wait_recv(), swap.copy(mask + core).wait_send()))
+    swap = dw_swap(lambda peer: stage, dw_hbm, sems[14:16], me)
+    loop(2, lambda core: (swap.arrival(XYZ + core).wait_recv(), swap.copy(XYZ + core).wait_send()))
     ucols.wait_recv()
     ucols.wait_send()
     leave.wait()
@@ -700,7 +698,7 @@
     half = hd // 2
     me = lax.axis_index('sp')
     feat = dgu_ref.shape[0] // 2
-    first = (Y, X + Z, Z, X + Y, 0)
+    first = (X, Y + Z, Y, X + Z, Z, X + Y, 0)
 
     def fetch(mask):
         cols = seg(flipped(me, mask) // 2, WIDE)
@@ -723,16 +721,14 @@
         stage[chip] = mm(dgu_ref[...], cols, NN)
 
     def advance(n):
-        if n > 2:
+        if n > 1:
             dws.wait_send(SETS[n - 1])
         dws.start(SETS[n])
 
-    for i, mask in enumerate(first):
+    for i, mask in enumerate(first[:4]):
         make(mask)
         if i == 1:
-            advance(2)
-    dws.start((CORE,))
-    own.start()
+            advance(1)
 
     dk_acc[...] = jnp.zeros_like(dk_acc)
     dv_acc[...] = jnp.zeros_like(dv_acc)
@@ -742,7 +738,7 @@
     def q_block(qb):
         @pl.when(qb == 5)
         def _():
-            advance(3)
+            advance(2)
         qs = seg(qb, QB)
         q2 = side_by_side(qkv_ref, heads, hd, qs)
         do2 = side_by_side(do_ref, heads, hd, qs)
@@ -791,6 +787,10 @@
     gs = Swap(lambda peer: gains.at[:, seg(peer)], lambda o: gains_in.at[o], sems[12:], me)
     sh.start()
     gq.start()
+    for mask in first[4:]:
+        make(mask)
+    dws.start((CORE,))
+    own.start()
     keep_own(dq_scr, full, me)
     shares[me] = dkv_scr[seg(me, tokens), :]
     sh.wait_recv()
@@ -807,22 +807,33 @@
     for k in range(groups):
         dqkv[:, q_all + 2 * hd * k:q_all + 2 * hd * (k + 1)] = dkv_own[2 * hd * k:2 * hd * (k + 1), :].T
 
+    def spread(cols):
+        part = dqkv[:, cols]
+
+        def step(i):
+            dn[:, seg(i, WIDE)] += mm(part, w_scr[i, cols, :], NN)
+        loop(N_CHIP, step)
+
     def use(mask):
         gq.wait_pair(mask)
         chip = flipped(me, mask) // 2
         dwq_ref[seg(chip, WIDE), :] = mm(full[chip], ucol_ref[...], NN)
         dqkv[:, seg(chip, WIDE)] = full[chip, :, seg(me, tokens)].T
-
+        spread(seg(chip, WIDE))
+
+    load.wait()
+    dn[...] = jnp.zeros_like(dn)
+    spread(pl.ds(q_all, dqkv.shape[1] - q_all))
     for r in range(len(gq.ROUNDS)):
         gq.round(r)
-        gk.round(r)
+        if r == 3:
+            advance(3)
+            for i in range(4):
+                gk.round(i)
+        if r > 3:
+            gk.round(r)
         for mask in gq.READY[r]:
             use(mask)
-    load.wait()
-
-    def normed(i):
-        dn[:, seg(i, WIDE)] = mm(dqkv[...], w_scr[i], NN)
-    loop(N_CHIP, normed)
     norm_back(dn, x_ref, g_scr, dh_ref, dx_ref, dg1)
     gains[...] = jnp.concatenate([jnp.sum(dg1[...], axis=0, keepdims=True), jnp.sum(dg2_ref[...], axis=0, keepdims=True),
                                   jnp.zeros((N_CHIP - 2, dg1.shape[1]), F32)], axis=0)
@@ -833,7 +844,7 @@
     dwkv_ref[...] = mm(full_kv[...], ucol_ref[...], NN)
     gs.wait_recv()
     gain_ref[...] = sum(gains_in[o] for o in range(N_DEV))
-    dws.wait_recv((CORE,) + SETS[2] + SETS[3])
+    dws.wait_recv((CORE,) + SETS[1] + SETS[2] + SETS[3])
     dws.wait_send((CORE,) + SETS[3])
     own.wait()
     for c in (sh, gs):
@@ -925,7 +936,7 @@
             (((seq, rows), BF16), ((N_CHIP, WIDE, dim), BF16), ((2 * feat, seq), BF16), ((feat, dim), F32),
              *tok_shapes, ((qw, seq), BF16), ((qw, dim), F32), ((N_CHIP, dim), F32), dw_shape),
             [vm((2 * feat, dim), BF16), vm((feat, dim), BF16), vm((feat, seq), BF16), vm((2 * feat, seq), BF16), vm((feat, dim), F32), dma(2), dma(),
-             full, full, dma(N_CHIP, 2), vm((3, 2 * feat, WIDE), F32), gain_scr, vm((WIDE, 2 * feat), BF16), vm((WIDE, feat), BF16), pltpu.SemaphoreType.REGULAR,
+             full, full, dma(N_CHIP, 2), vm((2 * feat, WIDE), F32), gain_scr, vm((WIDE, 2 * feat), BF16), vm((WIDE, feat), BF16), pltpu.SemaphoreType.REGULAR,
              *Scatter.scratch(tokens, dim), *(3 * Gather.sems), *(2 * Swap.sems), *Scatter.sems], 12 * feat * seq * dim,
             far_in=(2, 3), far_out=(1, 2, 3, 9))(*args)
         args = (qkv, d_attn, stat, cos_all, sin_all, dgu, m_full, u_col, wqkv, x_in, small_all, d_hidden, d_g2, d_gu)

time: 500 us -> 507 us (1.014)
  Pallas kernels: 488 us -> 496 us
    pallas_call x1, Pallas kernels: 96.3 us -> 119 us  [layer_step(): call(functools.partial(back, n_kv, hd), 3, len(args), (dw_shape, ((n_q *...]
    pallas_call x1, Pallas kernels: 252 us -> 236 us  [layer_step(): call(mlp, 1, len(args), (((seq, rows), BF16), ((N_CHIP, WIDE, dim), BF16)...]
where the time goes in v13:
time: 507 us; the launch traced here: 499 us
  Pallas kernels  496 us (98%)
    pallas_call x1, Pallas kernels, layer_step(): call(mlp, 1, len(args), (((seq, rows), BF16), ((N_CHIP, WIDE, dim), BF16)...  236 us
    pallas_call x1, Pallas kernels, layer_step(): call(functools.partial(head, n_kv, hd), 0, len(args), (((qw + 2 * hd, seq...  130 us
    pallas_call x1, Pallas kernels, layer_step(): call(functools.partial(back, n_kv, hd), 3, len(args), (dw_shape, ((n_q *...  119 us

profile of v13, /device:TPU:0, one launch (start us, length us, event | category | flops | bytes accessed | tf_op | source)
XLA Modules:
  0.0 499.1 jit_solution(12498940954322755044)
XLA Ops:
  0.7 0.7 broadcast_in_dim.2.freq_ref
  1.3 130.4 %head.1 = (bf16[256,2048]{1,0:T(8,128)(2,1)}, bf16[128,2048]{1,0:T(8,128)(2,1)}, f32[16,8,128]{2,1,0:T(8,128)}, bf16[8,2560,256]{2,1,0:T(8,128)(2,1)}, bf16[128,...) custom-call(bf16[128,2048]{1,0:T(8,128)(2,1)} %x_ref.3, ...), custom_call_target="tpu_custom_call" | custom-call | flops 2147483648 | bytes 4194304 | tf_op jit(solution)/shard_map/head/pallas_call | solution.py:925
  131.7 236.4 %mlp.1 = (bf16[2048,128]{1,0:T(8,128)(2,1)}, bf16[8,256,2048]{2,1,0:T(8,128)(2,1)}, bf16[704,2048]{1,0:T(8,128)(2,1)}, f32[352,2048]{1,0:T(8,128)}, bf16[128,204...) custom-call(bf16[128,2048]{1,0:T(8,128)(2,1)} %get-tuple-element.48., ...), custom_call_target="tpu_custom_call" | custom-call | flops 17716740096 | bytes 34603008 | tf_op jit(solution)/shard_map/mlp/pallas_call | solution.py:934
  368.1 119.4 %back.1 = (f32[16,704,128]{2,1,0:T(8,128)}, f32[2048,128]{1,0:T(8,128)}, f32[512,128]{1,0:T(8,128)}, bf16[128,2048]{1,0:T(8,128)(2,1)}, f32[8,128]{1,0:T(8,128)}) custom-call(bf16[256,2048]{1,0:T(8,128)(2,1)} %get-tuple-element.47.qkv_ref, bf16[128,2048]{1,0:T(8,128)(2,1)} %get-tuple-element.54.do_ref, ...), custom_call_target="tpu_custom_call", output_to_operand_aliasing={{0}: (13, {})} | custom-call | flops 5368709120 | bytes 10485760 | tf_op jit(solution)/shard_map/back/pallas_call | solution.py:943
  487.6 9.8 %finish.1 = (f32[128,5632]{1,0:T(8,128)}, f32[128,5632]{1,0:T(8,128)}, f32[256,128]{1,0:T(8,128)}, f32[256,128]{1,0:T(8,128)}, f32[2048,128]{1,0:T(8,128)}, /*in...) custom-call(f32[16,704,128]{2,1,0:T(8,128)} %get-tuple-element.65.dw, ...), custom_call_target="tpu_custom_call" | custom-call | tf_op jit(solution)/shard_map/finish/pallas_call | solution.py:954
  497.4 1.3 slice_bitcast_fusion
  (1 shorter events, 0.0 us)

commit v14 on v11

--- a/solution.py
+++ b/solution.py
@@ -277,16 +277,19 @@
             between(i)
         self.finish_pair(N_CHIP - 1)
         for step in range(2):
+            between(N_CHIP + step)
             for colour in COLOURS:
                 a, b, c = ORDERS[colour]
                 mask = (b + c, b)[step]
                 self.take(colour, mask, a)
                 self.start_link(colour, mask)
+        between(N_CHIP + 2)
         for colour in COLOURS:
             a, b, c = ORDERS[colour]
             self.take(colour, c, a)
             self.take(colour, c, b)
             self.start_link(colour, c)
+        between(N_CHIP + 3)
         for colour in COLOURS:
             for axis in ORDERS[colour]:
                 self.take(colour, 0, axis)
@@ -667,9 +670,10 @@
         loop(dim // CHUNK, step)
 
     def between(i):
-        if i < len(g.ROUNDS):
-            g.round(i)
-            for mask in g.READY[i]:
+        r = i if i < 3 else i - N_CHIP + 3
+        if i < 3 or i >= N_CHIP:
+            g.round(r)
+            for mask in g.READY[r]:
                 use_dh(mask)
 
     s = Scatter(*scr[:4], sems[18:], me)
@@ -728,12 +732,14 @@
                 swap.wait_send(SETS[n - 1])
             swap.start(SETS[n])
 
-    for mask in first[:2]:
+    for i, mask in enumerate(first):
         make(mask)
-        for swap in (gates, ups):
-            swap.start((mask, mask + CORE))
-    for mask in first[2:4]:
-        make(mask)
+        if i == 1:
+            advance(1)
+    gates.start((CORE,))
+    ups.start((CORE,))
+    for copy in own:
+        copy.start()
 
     dk_acc[...] = jnp.zeros_like(dk_acc)
     dv_acc[...] = jnp.zeros_like(dv_acc)
@@ -792,12 +798,6 @@
     gs = Swap(lambda peer: gains.at[:, seg(peer)], lambda o: gains_in.at[o], sems[14:], me)
     sh.start()
     gq.start()
-    for mask in first[4:]:
-        make(mask)
-    for swap in (gates, ups):
-        swap.start((CORE,))
-    for copy in own:
-        copy.start()
     keep_own(dq_scr, full, me)
     shares[me] = dkv_scr[seg(me, tokens), :]
     sh.wait_recv()
@@ -875,10 +875,10 @@
     for w, i in starts:
         fetch(w, i).start()
     kv.start()
-    for k, (w, i) in enumerate(starts):
+    for load, _ in moves:
+        load.start()
+    for w, i in starts:
         fetch(w, i).wait()
-        if k < len(moves):
-            moves[k][0].start()
 
         at = pl.ds(i * step, step)
         g_out[w, :, at] = g_in[w, at, :].T

time: 500 us -> 488 us (0.976)
  Pallas kernels: 489 us -> 477 us
    pallas_call x1, Pallas kernels: 112 us -> 104 us  [layer_step(): call(functools.partial(back, n_kv, hd), 3, len(args), (*dw_shapes, ((n_q...]
where the time goes in v14:
time: 488 us; the launch traced here: 480 us
  Pallas kernels  477 us (98%)
    pallas_call x1, Pallas kernels, layer_step(): call(mlp, 1, len(args), (((seq, rows), BF16), ((N_CHIP, WIDE, dim), BF16)...  233 us
    pallas_call x1, Pallas kernels, layer_step(): call(functools.partial(head, n_kv, hd), 0, len(args), (((qw + 2 * hd, seq...  130 us
    pallas_call x1, Pallas kernels, layer_step(): call(functools.partial(back, n_kv, hd), 3, len(args), (*dw_shapes, ((n_q...  104 us

profile of v14, /device:TPU:0, one launch (start us, length us, event | category | flops | bytes accessed | tf_op | source)
XLA Modules:
  0.0 479.9 jit_solution(9450985736564378177)
XLA Ops:
  0.7 0.7 broadcast_in_dim.2.freq_ref
  1.3 130.4 %head.1 = (bf16[256,2048]{1,0:T(8,128)(2,1)}, bf16[128,2048]{1,0:T(8,128)(2,1)}, f32[16,8,128]{2,1,0:T(8,128)}, bf16[8,2560,256]{2,1,0:T(8,128)(2,1)}, bf16[128,...) custom-call(bf16[128,2048]{1,0:T(8,128)(2,1)} %x_ref.3, ...), custom_call_target="tpu_custom_call" | custom-call | flops 2147483648 | bytes 4194304 | tf_op jit(solution)/shard_map/head/pallas_call | solution.py:925
  131.7 233.0 %mlp.1 = (bf16[2048,128]{1,0:T(8,128)(2,1)}, bf16[8,256,2048]{2,1,0:T(8,128)(2,1)}, bf16[704,2048]{1,0:T(8,128)(2,1)}, f32[352,2048]{1,0:T(8,128)}, bf16[128,204...) custom-call(bf16[128,2048]{1,0:T(8,128)(2,1)} %get-tuple-element.50., ...), custom_call_target="tpu_custom_call" | custom-call | flops 17716740096 | bytes 34603008 | tf_op jit(solution)/shard_map/mlp/pallas_call | solution.py:934
  364.7 103.8 %back.1 = (f32[5632,128]{1,0:T(8,128)}, f32[5632,128]{1,0:T(8,128)}, f32[2048,128]{1,0:T(8,128)}, f32[512,128]{1,0:T(8,128)}, bf16[128,2048]{1,0:T(8,128)(2,1)}, /*index=5*/f32[8,128]{1,0:T(8,128)}) custom-call(bf16[256,2048]{1,0:T(8,128)(2,1)} %get-tuple-element.49.qkv_ref, ...), custom_call_target="tpu_custom_call", output_to_operand_aliasing={{0}: (13, {}), {1}: (14, {})} | custom-call | flops 5368709120 | bytes 10485760 | tf_op jit(solution)/shard_map/back/pallas_call | solution.py:943
  468.5 9.7 %finish.1 = (f32[128,5632]{1,0:T(8,128)}, f32[128,5632]{1,0:T(8,128)}, f32[256,128]{1,0:T(8,128)}, f32[256,128]{1,0:T(8,128)}, f32[2048,128]{1,0:T(8,128)}, /*in...) custom-call(f32[5632,128]{1,0:T(8,128)} %get-tuple-element.68.dg_hbm, ...), custom_call_target="tpu_custom_call" | custom-call | tf_op jit(solution)/shard_map/finish/pallas_call | solution.py:954
  478.2 1.3 slice_bitcast_fusion
  (1 shorter events, 0.0 us)

commit v15 on v14

--- a/solution.py
+++ b/solution.py
@@ -105,7 +105,14 @@
                 act(mask)
 
     def start(self, masks=None):
-        self.each(masks, lambda mask: self.copy(mask).start())
+        if masks is not None:
+            return self.each(masks, lambda mask: self.copy(mask).start())
+
+        def step(i):
+            turn = (i // 2 + 5 + self.me % 2) % 6 + 1
+            self.copy(2 * (2 * turn % 7) + i % 2).start()
+        loop(12, step)
+        self.each((XYZ, XYZ + CORE, CORE), lambda mask: self.copy(mask).start())
 
     def advance(self, n):
         if n:
@@ -396,7 +403,8 @@
     return jnp.concatenate([ref[h * hd:(h + 1) * hd, qs] for h in range(heads)], axis=1)
 
 
-def head(groups, hd, x_ref, g1_ref, g2_ref, pos_ref, wq_ref, wk_ref, wv_ref, freq_ref, wg_ref, wu_ref, wo_ref, qkv_ref, u_scr, small_all, w_out, o_ref, stat_ref, wgu_ref, h_ref, m_ref, cos_ref, sin_ref,
+def head(groups, hd, x_ref, g1_ref, g2_ref, pos_ref, wq_ref, wk_ref, wv_ref, freq_ref, wg_hbm, wu_hbm, wo_hbm, qkv_out, u_out, small_all, w_out, o_ref, stat_ref, wgu_ref, h_ref, m_ref, cos_out, sin_out,
+         wg_ref, wu_ref, wo_ref, qkv_ref, u_scr, cos_ref, sin_ref, isem, esem,
          full_w, acc_o, o_tok, o_send, small_ref, w_ref, full, acc, rot, g_scr, wg_t, wu_t, s_scr, k_scr, osem, *sems):
     me = lax.axis_index('sp')
     tokens, dim = x_ref.shape
@@ -411,6 +419,7 @@
     gsems, ssems, qsems, ksems, gate_sems, up_sems, osems = sems[:4], *(sems[i:i + 2] for i in range(4, len(sems) - 4, 2))
     gw = row_gather(wo_ref, full_w, sems[-4:], me, 1)
     feat = wg_ref.shape[1] // N_DEV
+    loads = fetch_all(isem, (wg_hbm, wg_ref), (wu_hbm, wu_ref), (wo_hbm, wo_ref))
     enter(me, OTHERS)
     smalls = Swap(lambda peer: small_ref, lambda o: small_all.at[o], ssems, me)
     smalls.start()
@@ -427,6 +436,8 @@
     def transpose(i):
         wg_t[seg(i, CHUNK), :] = wg_ref[:, seg(i, CHUNK)].T
         wu_t[seg(i, CHUNK), :] = wu_ref[:, seg(i, CHUNK)].T
+    for load in loads:
+        load.wait()
     loop(wg_ref.shape[1] // CHUNK, transpose)
     advance(0)
 
@@ -501,6 +512,7 @@
     ups.start((CORE,))
     for swap in (qs, kvs):
         swap.wait_recv()
+    stores = fetch_all(esem, (qkv_ref, qkv_out), (u_scr, u_out), (cos_ref, cos_out), (sin_ref, sin_out))
     heads = qkv_ref.shape[0] // hd - 2
     seq = qkv_ref.shape[1]
     scale = hd ** -0.5
@@ -570,6 +582,8 @@
     outs.wait_send()
     for swap in (gates, ups):
         swap.wait_send((CORE,) + SETS[3])
+    for store in stores:
+        store.wait()
     g.finish()
     gw.finish()
     for swap in (smalls, qs, kvs):
@@ -597,7 +611,6 @@
     gates, ups = dw_swaps(lambda peer: stage, gate_hbm, up_hbm, sems[14:18], me)
     gm.start()
     gd.start()
-    ucol_ref[seg(me), :] = u_ref[:, seg(me)]
     keep_own(m_ref, full_m, me)
     keep_own(dout_ref, full_d, me)
     gain_row(g_scr, small_all, 1)
@@ -612,6 +625,7 @@
 
     for load in loads:
         load.wait()
+    ucol_ref[seg(me), :] = u_ref[:, seg(me)]
 
     def use(mask):
         gd.wait_pair(mask)
@@ -687,13 +701,13 @@
     ucols.wait_recv()
     ucols.wait_send()
     leave.wait()
-    for mask in CHIP_MASKS:
-        for copy in keep(mask):
-            copy.wait()
-
-
-def back(groups, hd, qkv_ref, do_ref, stat_ref, cos_all, sin_all, dgu_ref, m_hbm, ucol_ref, w_hbm, x_ref, small_all, dh_ref, dg2_ref, dg_in, du_in,
+    ends = ((full_m.at[0], m_out.at[0]), (dgu_ref.at[:, seg(0, WIDE)], dgu_out.at[:, seg(0, WIDE)]))
+    loop(N_CHIP, lambda j: [pltpu.make_async_copy(src, dst, osem.at[j, i]).wait() for i, (src, dst) in enumerate(ends)])
+
+
+def back(groups, hd, qkv_hbm, do_hbm, stat_ref, cos_all, sin_all, dgu_hbm, m_hbm, ucol_ref, w_hbm, x_ref, small_all, dh_ref, dg2_ref, dg_in, du_in,
          dg_hbm, du_hbm, dwq_ref, dwkv_ref, dx_ref, gain_ref,
+         dgu_ref, qkv_ref, do_ref, isem,
          p_scr, dp_scr, k_scr, v_scr, dk_acc, dv_acc, stage, dq_scr, dkv_scr, m_scr,
          full, w_scr, shares, dkv_own, full_kv, dqkv, dn, g_scr, dg1, gains, gains_in, wsem, lsem, msem, *sems):
     heads = qkv_ref.shape[0] // hd - 2
@@ -711,6 +725,7 @@
         return pltpu.make_async_copy(m_hbm.at[:, :, cols], m_scr.at[:, :, cols], msem.at[mask // 2])
     for mask in first:
         fetch(mask).start()
+    loads = fetch_all(isem, (dgu_hbm, dgu_ref), (qkv_hbm, qkv_ref), (do_hbm, do_ref))
     load = pltpu.make_async_copy(w_hbm, w_scr, wsem)
     load.start()
     enter(me, OTHERS)
@@ -732,6 +747,8 @@
                 swap.wait_send(SETS[n - 1])
             swap.start(SETS[n])
 
+    for copy in loads:
+        copy.wait()
     for i, mask in enumerate(first):
         make(mask)
         if i == 1:
@@ -854,9 +871,12 @@
 
 
 def finish(dg_hbm, du_hbm, dkv_hbm, *refs):
-    n = (len(refs) - 11) // 3
-    srcs, (gate, up, dk, dv), dsts = refs[:n], refs[n:n + 4], refs[n + 4:2 * n + 4]
-    (g_in, g_out, kv_in), holds, sems = refs[2 * n + 4:2 * n + 7], refs[2 * n + 7:3 * n + 7], refs[3 * n + 7:]
+    n = (len(refs) - 14) // 3
+    gains, refs = refs[0], refs[1:]
+    srcs, (gate, up, dk, dv, dg1, dg2), refs = refs[:n], refs[n:n + 6], refs[n + 6:]
+    dsts, (g_in, g_out, kv_in), holds, sems = refs[:n], refs[n:n + 3], refs[n + 3:2 * n + 3], refs[2 * n + 3:]
+    dg1[...] = gains[:1, :]
+    dg2[...] = gains[1:2, :]
     t_in, t_out, p_in, p_out = sems
     step = LANE * 11
     cols = g_in.shape[1]
@@ -926,16 +946,19 @@
             functools.partial(head, n_kv, hd), 0, len(args),
             (((qw + 2 * hd, seq), BF16), tok_shapes[0], ((N_DEV, N_CHIP, rows), F32), ((N_CHIP, cols, WIDE), BF16),
              ((qw, seq), BF16), ((seq // QB, 2, lanes), F32), ((2 * feat, dim), BF16), *tok_shapes, *(2 * (((hd // 2, seq), F32),))),
-            [full, vm((tokens, dim), F32), vm((tokens, dim), BF16), vm((seq, qw), BF16),
+            [vm(w_gate.shape, BF16), vm(w_up.shape, BF16), vm((qw, dim), BF16), vm((qw + 2 * hd, seq), BF16), vm((tokens, dim), BF16),
+             vm((hd // 2, seq), F32), vm((hd // 2, seq), F32), dma(3), dma(4),
+             full, vm((tokens, dim), F32), vm((tokens, dim), BF16), vm((seq, qw), BF16),
              vm((N_CHIP, rows), F32), vm((cols, rows), BF16), vm((N_CHIP, cols, WIDE), BF16), vm((cols, tokens), F32), vm((cols, tokens), BF16), gain_scr,
              vm((feat * N_DEV, rows), BF16), vm((feat * N_DEV, rows), BF16), vm((seq, lanes), F32), vm((seq, hd), BF16), dma(N_CHIP),
-             *Gather.sems, *(6 * Swap.sems), *Gather.sems], 4 * qw * seq * seq, far_out=(3,))(*args)
+             *Gather.sems, *(6 * Swap.sems), *Gather.sems], 4 * qw * seq * seq, far_in=(8, 9, 10), far_out=(0, 1, 3, 9, 10))(*args)
         args = (mlp_in, d_out, wgu, w_down, u, hidden, small_all, wo_own, attn_t)
         u_col, m_full, dgu, d_down, y_out, d_hidden, d_attn, d_wo, d_g2, d_gate_t, d_up_t = call(
             mlp, 1, len(args),
             (((seq, rows), BF16), ((N_CHIP, WIDE, dim), BF16), ((2 * feat, seq), BF16), ((feat, dim), F32),
              *tok_shapes, ((qw, seq), BF16), ((qw, dim), F32), ((N_CHIP, dim), F32), *dw_shapes),
-            [vm((2 * feat, dim), BF16), vm((feat, dim), BF16), vm((feat, seq), BF16), vm((2 * feat, seq), BF16), vm((feat, dim), F32), dma(2), dma(),
+            [vm((2 * feat, dim), BF16), vm((feat, dim), BF16),
+             vm((feat, seq), BF16), vm((2 * feat, seq), BF16), vm((feat, dim), F32), dma(2), dma(),
              full, full, dma(N_CHIP, 2), vm((2 * feat, WIDE), F32), gain_scr, vm((WIDE, 2 * feat), BF16), vm((WIDE, feat), BF16), pltpu.SemaphoreType.REGULAR,
              *Scatter.scratch(tokens, dim), *(3 * Gather.sems), *(3 * Swap.sems), *Scatter.sems], 12 * feat * seq * dim,
             far_in=(2, 3), far_out=(1, 2, 3, 9, 10))(*args)
@@ -943,24 +966,26 @@
         d_gate_t, d_up_t, d_wq, d_wkv, d_x, gains = call(
             functools.partial(back, n_kv, hd), 3, len(args),
             (*dw_shapes, ((n_q * hd, rows), F32), ((2 * n_kv * hd, rows), F32), tok_shapes[0], ((N_CHIP, rows), F32)),
-            [vm((seq, lanes), F32), vm((seq, lanes), BF16), vm((seq, hd), BF16), vm((seq, hd), BF16), vm((seq, hd), F32), vm((seq, hd), F32),
+            [vm((2 * feat, seq), BF16), vm((qw + 2 * hd, seq), BF16), vm((qw, seq), BF16), dma(3),
+             vm((seq, lanes), F32), vm((seq, lanes), BF16), vm((seq, hd), BF16), vm((seq, hd), BF16), vm((seq, hd), F32), vm((seq, hd), F32),
              vm((N_CHIP, 2 * feat, WIDE), F32), vm((qw, seq), BF16), vm((seq, 2 * hd), BF16), full,
              full, vm((N_CHIP, cols, WIDE), BF16), vm((N_DEV, tokens, 2 * hd), BF16), vm((2 * n_kv * hd, tokens), BF16), vm((2 * n_kv * hd, seq), BF16),
              vm((tokens, cols), BF16), vm((tokens, dim), F32), gain_scr, gain_scr, gain_scr, vm((N_DEV, N_CHIP, rows), F32), dma(), dma(2), dma(N_CHIP),
-             *(3 * Swap.sems), *(2 * Gather.sems), *Swap.sems], 10 * qw * seq * seq, far_in=(6, 8, 13, 14), far_out=(0, 1), aliases={13: 0, 14: 1})(*args)
-        moved = (d_wq, d_wo, d_down, d_x, y_out, gains)
+             *(3 * Swap.sems), *(2 * Gather.sems), *Swap.sems], 10 * qw * seq * seq, far_in=(0, 1, 5, 6, 8, 13, 14), far_out=(0, 1), aliases={13: 0, 14: 1})(*args)
+        moved = (d_wq, d_wo, d_down, d_x, y_out)
+        one_row = jax.ShapeDtypeStruct((1, rows), F32)
         half_kv = jax.ShapeDtypeStruct((n_kv * hd, rows), F32)
         wide = jax.ShapeDtypeStruct((rows, feat * N_DEV), F32)
-        d_gate, d_up, d_wk, d_wv, d_wq, d_wo, d_down, d_x, y_out, gains = pl.pallas_call(
+        d_gate, d_up, d_wk, d_wv, d_g1, d_g2, d_wq, d_wo, d_down, d_x, y_out = pl.pallas_call(
             finish,
-            out_shape=[wide, wide, half_kv, half_kv] + [jax.ShapeDtypeStruct(v.shape, v.dtype) for v in moved],
-            in_specs=[IN_HBM] * (3 + len(moved)), out_specs=[IN_HBM] * 2 + on_chip(2) + [IN_HBM] * len(moved),
+            out_shape=[wide, wide, half_kv, half_kv, one_row, one_row] + [jax.ShapeDtypeStruct(v.shape, v.dtype) for v in moved],
+            in_specs=[IN_HBM] * 3 + on_chip(1) + [IN_HBM] * len(moved), out_specs=[IN_HBM] * 2 + on_chip(4) + [IN_HBM] * len(moved),
             scratch_shapes=[vm((2, feat * N_DEV, rows), F32), vm((2, rows, feat * N_DEV), F32), vm(d_wkv.shape, F32)]
             + [vm(v.shape, v.dtype) for v in moved] + [dma(2, 4), dma(2, 4), dma(len(moved) + 1), dma(len(moved))],
             compiler_params=pltpu.CompilerParams(vmem_limit_bytes=VMEM_CAP), name='finish',
-        )(d_gate_t, d_up_t, d_wkv, *moved)
+        )(d_gate_t, d_up_t, d_wkv, gains, *moved)
         by_row = lambda g, heads: g.reshape(heads, hd, rows).transpose(2, 0, 1)
-        return (y_out, d_x, gains[0], gains[1], by_row(d_wq, n_q), by_row(d_wk, n_kv), by_row(d_wv, n_kv),
+        return (y_out, d_x, d_g1.reshape(rows), d_g2.reshape(rows), by_row(d_wq, n_q), by_row(d_wk, n_kv), by_row(d_wv, n_kv),
                 d_wo.reshape(w_o.shape), d_gate, d_up, d_down)
 
     all_rows = P('sp')

time: 488 us -> 485 us (level)
  no operation moved by 1% of the time
where the time goes in v15:
time: 485 us; the launch traced here: 477 us
  Pallas kernels  475 us (98%)
    pallas_call x1, Pallas kernels, layer_step(): call(mlp, 1, len(args), (((seq, rows), BF16), ((N_CHIP, WIDE, dim), BF16)...  232 us
    pallas_call x1, Pallas kernels, layer_step(): call(functools.partial(head, n_kv, hd), 0, len(args), (((qw + 2 * hd, seq...  129 us
    pallas_call x1, Pallas kernels, layer_step(): call(functools.partial(back, n_kv, hd), 3, len(args), (*dw_shapes, ((n_q...  104 us
    pallas_call x1, Pallas kernels, layer_step(): pl.pallas_call(finish, out_shape=[wide, wide, half_kv, half_kv, one_row,...  10.5 us

profile of v15, /device:TPU:0, one launch (start us, length us, event | category | flops | bytes accessed | tf_op | source)
XLA Modules:
  0.0 477.1 jit_solution(2430512758415801930)
XLA Ops:
  0.7 0.7 broadcast_in_dim.2.freq_ref
  1.3 129.2 %head.1 = (bf16[256,2048]{1,0:T(8,128)(2,1)}, bf16[128,2048]{1,0:T(8,128)(2,1)}, f32[16,8,128]{2,1,0:T(8,128)}, bf16[8,2560,256]{2,1,0:T(8,128)(2,1)}, bf16[128,...) custom-call(bf16[128,2048]{1,0:T(8,128)(2,1)} %x_ref.3, ...), custom_call_target="tpu_custom_call" | custom-call | flops 2147483648 | bytes 4194304 | tf_op jit(solution)/shard_map/head/pallas_call | solution.py:945
  130.5 231.7 %mlp.1 = (bf16[2048,128]{1,0:T(8,128)(2,1)}, bf16[8,256,2048]{2,1,0:T(8,128)(2,1)}, bf16[704,2048]{1,0:T(8,128)(2,1)}, f32[352,2048]{1,0:T(8,128)}, bf16[128,204...) custom-call(bf16[128,2048]{1,0:T(8,128)(2,1)} %get-tuple-element.51., ...), custom_call_target="tpu_custom_call" | custom-call | flops 17716740096 | bytes 34603008 | tf_op jit(solution)/shard_map/mlp/pallas_call | solution.py:956
  362.2 103.8 %back.1 = (f32[5632,128]{1,0:T(8,128)}, f32[5632,128]{1,0:T(8,128)}, f32[2048,128]{1,0:T(8,128)}, f32[512,128]{1,0:T(8,128)}, bf16[128,2048]{1,0:T(8,128)(2,1)}, /*index=5*/f32[8,128]{1,0:T(8,128)}) custom-call(bf16[256,2048]{1,0:T(8,128)(2,1)} %get-tuple-element.50.qkv_hbm, ...), custom_call_target="tpu_custom_call", output_to_operand_aliasing={{0}: (13, {}), {1}: (14, {})} | custom-call | flops 5368709120 | bytes 10485760 | tf_op jit(solution)/shard_map/back/pallas_call | solution.py:966
  466.0 10.5 %finish.1 = (f32[128,5632]{1,0:T(8,128)}, f32[128,5632]{1,0:T(8,128)}, f32[256,128]{1,0:T(8,128)}, f32[256,128]{1,0:T(8,128)}, f32[1,128]{1,0:T(1,128)}, /*index...) custom-call(f32[5632,128]{1,0:T(8,128)} %get-tuple-element.69.dg_hbm, ...), custom_call_target="tpu_custom_call" | custom-call | tf_op jit(solution)/shard_map/finish/pallas_call | solution.py:979
  (1 shorter events, 0.0 us)

commit v16 on v15

--- a/solution.py
+++ b/solution.py
@@ -105,14 +105,7 @@
                 act(mask)
 
     def start(self, masks=None):
-        if masks is not None:
-            return self.each(masks, lambda mask: self.copy(mask).start())
-
-        def step(i):
-            turn = (i // 2 + 5 + self.me % 2) % 6 + 1
-            self.copy(2 * (2 * turn % 7) + i % 2).start()
-        loop(12, step)
-        self.each((XYZ, XYZ + CORE, CORE), lambda mask: self.copy(mask).start())
+        self.each(masks, lambda mask: self.copy(mask).start())
 
     def advance(self, n):
         if n:
@@ -472,7 +465,7 @@
 
     for r in range(len(g.ROUNDS)):
         g.round(r)
-        if r in (2, 4):
+        if r in (2, 5):
             advance(r // 2)
         if r == 1:
             loop(N_DEV, tables)

time: 485 us -> 492 us (1.014)
  Pallas kernels: 475 us -> 482 us
    pallas_call x1, Pallas kernels: 104 us -> 109 us  [layer_step(): call(functools.partial(back, n_kv, hd), 3, len(args), (*dw_shapes, ((n_q...]
where the time goes in v16:
time: 492 us; the launch traced here: 484 us
  Pallas kernels  482 us (98%)
    pallas_call x1, Pallas kernels, layer_step(): call(mlp, 1, len(args), (((seq, rows), BF16), ((N_CHIP, WIDE, dim), BF16)...  233 us
    pallas_call x1, Pallas kernels, layer_step(): call(functools.partial(head, n_kv, hd), 0, len(args), (((qw + 2 * hd, seq...  129 us
    pallas_call x1, Pallas kernels, layer_step(): call(functools.partial(back, n_kv, hd), 3, len(args), (*dw_shapes, ((n_q...  109 us
    pallas_call x1, Pallas kernels, layer_step(): pl.pallas_call(finish, out_shape=[wide, wide, half_kv, half_kv, one_row,...  10.5 us

profile of v16, /device:TPU:0, one launch (start us, length us, event | category | flops | bytes accessed | tf_op | source)
XLA Modules:
  0.0 483.5 jit_solution(10827568598608126259)
XLA Ops:
  0.7 0.7 broadcast_in_dim.2.freq_ref
  1.3 128.8 %head.1 = (bf16[256,2048]{1,0:T(8,128)(2,1)}, bf16[128,2048]{1,0:T(8,128)(2,1)}, f32[16,8,128]{2,1,0:T(8,128)}, bf16[8,2560,256]{2,1,0:T(8,128)(2,1)}, bf16[128,...) custom-call(bf16[128,2048]{1,0:T(8,128)(2,1)} %x_ref.3, ...), custom_call_target="tpu_custom_call" | custom-call | flops 2147483648 | bytes 4194304 | tf_op jit(solution)/shard_map/head/pallas_call | solution.py:938
  130.1 233.0 %mlp.1 = (bf16[2048,128]{1,0:T(8,128)(2,1)}, bf16[8,256,2048]{2,1,0:T(8,128)(2,1)}, bf16[704,2048]{1,0:T(8,128)(2,1)}, f32[352,2048]{1,0:T(8,128)}, bf16[128,204...) custom-call(bf16[128,2048]{1,0:T(8,128)(2,1)} %get-tuple-element.51., ...), custom_call_target="tpu_custom_call" | custom-call | flops 17716740096 | bytes 34603008 | tf_op jit(solution)/shard_map/mlp/pallas_call | solution.py:949
  363.2 109.3 %back.1 = (f32[5632,128]{1,0:T(8,128)}, f32[5632,128]{1,0:T(8,128)}, f32[2048,128]{1,0:T(8,128)}, f32[512,128]{1,0:T(8,128)}, bf16[128,2048]{1,0:T(8,128)(2,1)}, /*index=5*/f32[8,128]{1,0:T(8,128)}) custom-call(bf16[256,2048]{1,0:T(8,128)(2,1)} %get-tuple-element.50.qkv_hbm, ...), custom_call_target="tpu_custom_call", output_to_operand_aliasing={{0}: (13, {}), {1}: (14, {})} | custom-call | flops 5368709120 | bytes 10485760 | tf_op jit(solution)/shard_map/back/pallas_call | solution.py:959
  472.5 10.5 %finish.1 = (f32[128,5632]{1,0:T(8,128)}, f32[128,5632]{1,0:T(8,128)}, f32[256,128]{1,0:T(8,128)}, f32[256,128]{1,0:T(8,128)}, f32[1,128]{1,0:T(1,128)}, /*index...) custom-call(f32[5632,128]{1,0:T(8,128)} %get-tuple-element.69.dg_hbm, ...), custom_call_target="tpu_custom_call" | custom-call | tf_op jit(solution)/shard_map/finish/pallas_call | solution.py:972
  (1 shorter events, 0.0 us)

commit v17 on v16

--- a/solution.py
+++ b/solution.py
@@ -700,7 +700,7 @@
 
 def back(groups, hd, qkv_hbm, do_hbm, stat_ref, cos_all, sin_all, dgu_hbm, m_hbm, ucol_ref, w_hbm, x_ref, small_all, dh_ref, dg2_ref, dg_in, du_in,
          dg_hbm, du_hbm, dwq_ref, dwkv_ref, dx_ref, gain_ref,
-         dgu_ref, qkv_ref, do_ref, isem,
+         dgu_ref, qkv_ref, do_ref, isem, qsem,
          p_scr, dp_scr, k_scr, v_scr, dk_acc, dv_acc, stage, dq_scr, dkv_scr, m_scr,
          full, w_scr, shares, dkv_own, full_kv, dqkv, dn, g_scr, dg1, gains, gains_in, wsem, lsem, msem, *sems):
     heads = qkv_ref.shape[0] // hd - 2
@@ -716,12 +716,14 @@
     def fetch(mask):
         cols = seg(flipped(me, mask) // 2, WIDE)
         return pltpu.make_async_copy(m_hbm.at[:, :, cols], m_scr.at[:, :, cols], msem.at[mask // 2])
-    for mask in first:
+    needed, = fetch_all(isem, (dgu_hbm, dgu_ref))
+    for mask in first[:2]:
         fetch(mask).start()
-    loads = fetch_all(isem, (dgu_hbm, dgu_ref), (qkv_hbm, qkv_ref), (do_hbm, do_ref))
     load = pltpu.make_async_copy(w_hbm, w_scr, wsem)
-    load.start()
     enter(me, OTHERS)
+    for mask in first[2:]:
+        fetch(mask).start()
+    loads = fetch_all(qsem, (qkv_hbm, qkv_ref), (do_hbm, do_ref))
     gain_row(g_scr, small_all, 0)
 
     gates, ups = dw_swaps(lambda peer: stage.at[peer // 2], dg_hbm, du_hbm, sems[:4], me)
@@ -740,12 +742,14 @@
                 swap.wait_send(SETS[n - 1])
             swap.start(SETS[n])
 
-    for copy in loads:
-        copy.wait()
+    needed.wait()
     for i, mask in enumerate(first):
         make(mask)
         if i == 1:
             advance(1)
+    load.start()
+    for copy in loads:
+        copy.wait()
     gates.start((CORE,))
     ups.start((CORE,))
     for copy in own:
@@ -959,7 +963,7 @@
         d_gate_t, d_up_t, d_wq, d_wkv, d_x, gains = call(
             functools.partial(back, n_kv, hd), 3, len(args),
             (*dw_shapes, ((n_q * hd, rows), F32), ((2 * n_kv * hd, rows), F32), tok_shapes[0], ((N_CHIP, rows), F32)),
-            [vm((2 * feat, seq), BF16), vm((qw + 2 * hd, seq), BF16), vm((qw, seq), BF16), dma(3),
+            [vm((2 * feat, seq), BF16), vm((qw + 2 * hd, seq), BF16), vm((qw, seq), BF16), dma(1), dma(2),
              vm((seq, lanes), F32), vm((seq, lanes), BF16), vm((seq, hd), BF16), vm((seq, hd), BF16), vm((seq, hd), F32), vm((seq, hd), F32),
              vm((N_CHIP, 2 * feat, WIDE), F32), vm((qw, seq), BF16), vm((seq, 2 * hd), BF16), full,
              full, vm((N_CHIP, cols, WIDE), BF16), vm((N_DEV, tokens, 2 * hd), BF16), vm((2 * n_kv * hd, tokens), BF16), vm((2 * n_kv * hd, seq), BF16),

time: 492 us -> 485 us (0.986)
  Pallas kernels: 482 us -> 475 us
    pallas_call x1, Pallas kernels: 109 us -> 102 us  [layer_step(): call(functools.partial(back, n_kv, hd), 3, len(args), (*dw_shapes, ((n_q...]
where the time goes in v17:
time: 485 us; the launch traced here: 477 us
  Pallas kernels  475 us (98%)
    pallas_call x1, Pallas kernels, layer_step(): call(mlp, 1, len(args), (((seq, rows), BF16), ((N_CHIP, WIDE, dim), BF16)...  233 us
    pallas_call x1, Pallas kernels, layer_step(): call(functools.partial(head, n_kv, hd), 0, len(args), (((qw + 2 * hd, seq...  129 us
    pallas_call x1, Pallas kernels, layer_step(): call(functools.partial(back, n_kv, hd), 3, len(args), (*dw_shapes, ((n_q...  102 us
    pallas_call x1, Pallas kernels, layer_step(): pl.pallas_call(finish, out_shape=[wide, wide, half_kv, half_kv, one_row,...  10.5 us

profile of v17, /device:TPU:0, one launch (start us, length us, event | category | flops | bytes accessed | tf_op | source)
XLA Modules:
  0.0 476.6 jit_solution(1645654563082667013)
XLA Ops:
  0.7 0.7 broadcast_in_dim.2.freq_ref
  1.3 128.8 %head.1 = (bf16[256,2048]{1,0:T(8,128)(2,1)}, bf16[128,2048]{1,0:T(8,128)(2,1)}, f32[16,8,128]{2,1,0:T(8,128)}, bf16[8,2560,256]{2,1,0:T(8,128)(2,1)}, bf16[128,...) custom-call(bf16[128,2048]{1,0:T(8,128)(2,1)} %x_ref.3, ...), custom_call_target="tpu_custom_call" | custom-call | flops 2147483648 | bytes 4194304 | tf_op jit(solution)/shard_map/head/pallas_call | solution.py:942
  130.1 233.0 %mlp.1 = (bf16[2048,128]{1,0:T(8,128)(2,1)}, bf16[8,256,2048]{2,1,0:T(8,128)(2,1)}, bf16[704,2048]{1,0:T(8,128)(2,1)}, f32[352,2048]{1,0:T(8,128)}, bf16[128,204...) custom-call(bf16[128,2048]{1,0:T(8,128)(2,1)} %get-tuple-element.51., ...), custom_call_target="tpu_custom_call" | custom-call | flops 17716740096 | bytes 34603008 | tf_op jit(solution)/shard_map/mlp/pallas_call | solution.py:953
  363.2 102.5 %back.1 = (f32[5632,128]{1,0:T(8,128)}, f32[5632,128]{1,0:T(8,128)}, f32[2048,128]{1,0:T(8,128)}, f32[512,128]{1,0:T(8,128)}, bf16[128,2048]{1,0:T(8,128)(2,1)}, /*index=5*/f32[8,128]{1,0:T(8,128)}) custom-call(bf16[256,2048]{1,0:T(8,128)(2,1)} %get-tuple-element.50.qkv_hbm, ...), custom_call_target="tpu_custom_call", output_to_operand_aliasing={{0}: (13, {}), {1}: (14, {})} | custom-call | flops 5368709120 | bytes 10485760 | tf_op jit(solution)/shard_map/back/pallas_call | solution.py:963
  465.6 10.5 %finish.1 = (f32[128,5632]{1,0:T(8,128)}, f32[128,5632]{1,0:T(8,128)}, f32[256,128]{1,0:T(8,128)}, f32[256,128]{1,0:T(8,128)}, f32[1,128]{1,0:T(1,128)}, /*index...) custom-call(f32[5632,128]{1,0:T(8,128)} %get-tuple-element.69.dg_hbm, ...), custom_call_target="tpu_custom_call" | custom-call | tf_op jit(solution)/shard_map/finish/pallas_call | solution.py:976
  (1 shorter events, 0.0 us)

commit v18 on v17

--- a/solution.py
+++ b/solution.py
@@ -16,7 +16,7 @@
 TN = (((0,), (0,)), ((), ()))
 NN = (((1,), (0,)), ((), ()))
 MESH = pl.DeviceIdType.MESH
-VMEM_CAP = 62 * 1024 * 1024
+VMEM_CAP = 67043328
 
 CORE, X, Y, Z = 1, 2, 4, 8
 XYZ = X + Y + Z
@@ -46,11 +46,21 @@
 
 
 def flipped(index, mask):
+    if not isinstance(mask, int):
+        return differing(index, mask)
     out = index
     for bit in NEAR:
         if mask & bit:
             out = out + (1 - 2 * ((index // bit) % 2)) * bit
     return out
+
+
+def run_ready(masks, use):
+    if len(masks) == 2:
+        loop(2, lambda j: use(masks[0] + (masks[1] - masks[0]) * j))
+    else:
+        for mask in masks:
+            use(mask)
 
 
 def thirds(total, unit):
@@ -469,8 +479,7 @@
             advance(r // 2)
         if r == 1:
             loop(N_DEV, tables)
-        for mask in g.READY[r]:
-            use(mask)
+        run_ready(g.READY[r], use)
 
     half = hd // 2
     cos, sin = cos_ref[:, seg(me)], sin_ref[:, seg(me)]
@@ -646,8 +655,7 @@
         gd.round(r)
         if r == 3:
             ucols.start()
-        for mask in gm.READY[r]:
-            use(mask)
+        run_ready(gm.READY[r], use)
     far = seg(flipped(me, XYZ) // 2, WIDE)
     stage[...] = mm(dgu_ref[...], full_m[:, :, far].reshape(dgu_ref.shape[1], WIDE), NN)
     for swap in (gates, ups):
@@ -680,8 +688,7 @@
         r = i if i < 3 else i - N_CHIP + 3
         if i < 3 or i >= N_CHIP:
             g.round(r)
-            for mask in g.READY[r]:
-                use_dh(mask)
+            run_ready(g.READY[r], use_dh)
 
     s = Scatter(*scr[:4], sems[18:], me)
     total = s.run(block_product(s, glu_ref, down_ref, glu_t), between)
@@ -743,10 +750,10 @@
             swap.start(SETS[n])
 
     needed.wait()
-    for i, mask in enumerate(first):
+    for mask in first[:2]:
         make(mask)
-        if i == 1:
-            advance(1)
+    advance(1)
+    loop(5, lambda j: make(2 * ((j + 2) % 6)))
     load.start()
     for copy in loads:
         copy.wait()
@@ -839,8 +846,7 @@
         gk.round(r)
         if r == 3:
             advance(3)
-        for mask in gq.READY[r]:
-            use(mask)
+        run_ready(gq.READY[r], use)
     load.wait()
 
     def normed(i):

time: 485 us -> 483 us (level); the launches traced: 477 us -> 483 us
  Pallas kernels: 475 us -> 482 us
    pallas_call x1, Pallas kernels: 102 us -> 109 us  [layer_step(): call(functools.partial(back, n_kv, hd), 3, len(args), (*dw_shapes, ((n_q...]
where the time goes in v18:
time: 483 us
  Pallas kernels  482 us (100%)
    pallas_call x1, Pallas kernels, layer_step(): call(mlp, 1, len(args), (((seq, rows), BF16), ((N_CHIP, WIDE, dim), BF16)...  233 us
    pallas_call x1, Pallas kernels, layer_step(): call(functools.partial(head, n_kv, hd), 0, len(args), (((qw + 2 * hd, seq...  129 us
    pallas_call x1, Pallas kernels, layer_step(): call(functools.partial(back, n_kv, hd), 3, len(args), (*dw_shapes, ((n_q...  109 us
    pallas_call x1, Pallas kernels, layer_step(): pl.pallas_call(finish, out_shape=[wide, wide, half_kv, half_kv, one_row,...  10.5 us

profile of v18, /device:TPU:0, one launch (start us, length us, event | category | flops | bytes accessed | tf_op | source)
XLA Modules:
  0.0 483.3 jit_solution(11613483755424940716)
XLA Ops:
  0.7 0.7 broadcast_in_dim.2.freq_ref
  1.3 128.8 %head.1 = (bf16[256,2048]{1,0:T(8,128)(2,1)}, bf16[128,2048]{1,0:T(8,128)(2,1)}, f32[16,8,128]{2,1,0:T(8,128)}, bf16[8,2560,256]{2,1,0:T(8,128)(2,1)}, bf16[128,...) custom-call(bf16[128,2048]{1,0:T(8,128)(2,1)} %x_ref.3, ...), custom_call_target="tpu_custom_call" | custom-call | flops 2147483648 | bytes 4194304 | tf_op jit(solution)/shard_map/head/pallas_call | solution.py:948
  130.1 233.0 %mlp.1 = (bf16[2048,128]{1,0:T(8,128)(2,1)}, bf16[8,256,2048]{2,1,0:T(8,128)(2,1)}, bf16[704,2048]{1,0:T(8,128)(2,1)}, f32[352,2048]{1,0:T(8,128)}, bf16[128,204...) custom-call(bf16[128,2048]{1,0:T(8,128)(2,1)} %get-tuple-element.51., ...), custom_call_target="tpu_custom_call" | custom-call | flops 17716740096 | bytes 34603008 | tf_op jit(solution)/shard_map/mlp/pallas_call | solution.py:959
  363.1 109.4 %back.1 = (f32[5632,128]{1,0:T(8,128)}, f32[5632,128]{1,0:T(8,128)}, f32[2048,128]{1,0:T(8,128)}, f32[512,128]{1,0:T(8,128)}, bf16[128,2048]{1,0:T(8,128)(2,1)}, /*index=5*/f32[8,128]{1,0:T(8,128)}) custom-call(bf16[256,2048]{1,0:T(8,128)(2,1)} %get-tuple-element.50.qkv_hbm, ...), custom_call_target="tpu_custom_call", output_to_operand_aliasing={{0}: (13, {}), {1}: (14, {})} | custom-call | flops 5368709120 | bytes 10485760 | tf_op jit(solution)/shard_map/back/pallas_call | solution.py:969
  472.6 10.5 %finish.1 = (f32[128,5632]{1,0:T(8,128)}, f32[128,5632]{1,0:T(8,128)}, f32[256,128]{1,0:T(8,128)}, f32[256,128]{1,0:T(8,128)}, f32[1,128]{1,0:T(1,128)}, /*index...) custom-call(f32[5632,128]{1,0:T(8,128)} %get-tuple-element.69.dg_hbm, ...), custom_call_target="tpu_custom_call" | custom-call | tf_op jit(solution)/shard_map/finish/pallas_call | solution.py:982
  (1 shorter events, 0.0 us)

commit v19 on v18

--- a/solution.py
+++ b/solution.py
@@ -750,10 +750,10 @@
             swap.start(SETS[n])
 
     needed.wait()
-    for mask in first[:2]:
+    for i, mask in enumerate(first):
         make(mask)
-    advance(1)
-    loop(5, lambda j: make(2 * ((j + 2) % 6)))
+        if i == 1:
+            advance(1)
     load.start()
     for copy in loads:
         copy.wait()

time: 483 us -> 477 us (0.988)
  Pallas kernels: 482 us -> 475 us
    pallas_call x1, Pallas kernels: 109 us -> 103 us  [layer_step(): call(functools.partial(back, n_kv, hd), 3, len(args), (*dw_shapes, ((n_q...]
where the time goes in v19:
time: 477 us
  Pallas kernels  475 us (100%)
    pallas_call x1, Pallas kernels, layer_step(): call(mlp, 1, len(args), (((seq, rows), BF16), ((N_CHIP, WIDE, dim), BF16)...  233 us
    pallas_call x1, Pallas kernels, layer_step(): call(functools.partial(head, n_kv, hd), 0, len(args), (((qw + 2 * hd, seq...  129 us
    pallas_call x1, Pallas kernels, layer_step(): call(functools.partial(back, n_kv, hd), 3, len(args), (*dw_shapes, ((n_q...  103 us
    pallas_call x1, Pallas kernels, layer_step(): pl.pallas_call(finish, out_shape=[wide, wide, half_kv, half_kv, one_row,...  10.5 us

profile of v19, /device:TPU:0, one launch (start us, length us, event | category | flops | bytes accessed | tf_op | source)
XLA Modules:
  0.0 476.8 jit_solution(7731395560863751640)
XLA Ops:
  0.7 0.7 broadcast_in_dim.2.freq_ref
  1.3 128.8 %head.1 = (bf16[256,2048]{1,0:T(8,128)(2,1)}, bf16[128,2048]{1,0:T(8,128)(2,1)}, f32[16,8,128]{2,1,0:T(8,128)}, bf16[8,2560,256]{2,1,0:T(8,128)(2,1)}, bf16[128,...) custom-call(bf16[128,2048]{1,0:T(8,128)(2,1)} %x_ref.3, ...), custom_call_target="tpu_custom_call" | custom-call | flops 2147483648 | bytes 4194304 | tf_op jit(solution)/shard_map/head/pallas_call | solution.py:948
  130.1 233.2 %mlp.1 = (bf16[2048,128]{1,0:T(8,128)(2,1)}, bf16[8,256,2048]{2,1,0:T(8,128)(2,1)}, bf16[704,2048]{1,0:T(8,128)(2,1)}, f32[352,2048]{1,0:T(8,128)}, bf16[128,204...) custom-call(bf16[128,2048]{1,0:T(8,128)(2,1)} %get-tuple-element.51., ...), custom_call_target="tpu_custom_call" | custom-call | flops 17716740096 | bytes 34603008 | tf_op jit(solution)/shard_map/mlp/pallas_call | solution.py:959
  363.4 102.7 %back.1 = (f32[5632,128]{1,0:T(8,128)}, f32[5632,128]{1,0:T(8,128)}, f32[2048,128]{1,0:T(8,128)}, f32[512,128]{1,0:T(8,128)}, bf16[128,2048]{1,0:T(8,128)(2,1)}, /*index=5*/f32[8,128]{1,0:T(8,128)}) custom-call(bf16[256,2048]{1,0:T(8,128)(2,1)} %get-tuple-element.50.qkv_hbm, ...), custom_call_target="tpu_custom_call", output_to_operand_aliasing={{0}: (13, {}), {1}: (14, {})} | custom-call | flops 5368709120 | bytes 10485760 | tf_op jit(solution)/shard_map/back/pallas_call | solution.py:969
  466.1 10.5 %finish.1 = (f32[128,5632]{1,0:T(8,128)}, f32[128,5632]{1,0:T(8,128)}, f32[256,128]{1,0:T(8,128)}, f32[256,128]{1,0:T(8,128)}, f32[1,128]{1,0:T(1,128)}, /*index...) custom-call(f32[5632,128]{1,0:T(8,128)} %get-tuple-element.69.dg_hbm, ...), custom_call_target="tpu_custom_call" | custom-call | tf_op jit(solution)/shard_map/finish/pallas_call | solution.py:982
  (1 shorter events, 0.0 us)

commit v20 on v19

--- a/solution.py
+++ b/solution.py
@@ -768,7 +768,7 @@
     key_rows(v_scr, qkv_ref, qw + hd, hd)
 
     def q_block(qb):
-        @pl.when(qb == 4)
+        @pl.when(qb == 5)
         def _():
             advance(2)
         qs = seg(qb, QB)

time: 477 us -> 478 us (level)
  no operation moved by 1% of the time
where the time goes in v20:
time: 478 us
  Pallas kernels  477 us (100%)
    pallas_call x1, Pallas kernels, layer_step(): call(mlp, 1, len(args), (((seq, rows), BF16), ((N_CHIP, WIDE, dim), BF16)...  233 us
    pallas_call x1, Pallas kernels, layer_step(): call(functools.partial(head, n_kv, hd), 0, len(args), (((qw + 2 * hd, seq...  129 us
    pallas_call x1, Pallas kernels, layer_step(): call(functools.partial(back, n_kv, hd), 3, len(args), (*dw_shapes, ((n_q...  104 us
    pallas_call x1, Pallas kernels, layer_step(): pl.pallas_call(finish, out_shape=[wide, wide, half_kv, half_kv, one_row,...  10.5 us

profile of v20, /device:TPU:0, one launch (start us, length us, event | category | flops | bytes accessed | tf_op | source)
XLA Modules:
  0.0 478.2 jit_solution(10778517453048105724)
XLA Ops:
  0.7 0.7 broadcast_in_dim.2.freq_ref
  1.3 128.8 %head.1 = (bf16[256,2048]{1,0:T(8,128)(2,1)}, bf16[128,2048]{1,0:T(8,128)(2,1)}, f32[16,8,128]{2,1,0:T(8,128)}, bf16[8,2560,256]{2,1,0:T(8,128)(2,1)}, bf16[128,...) custom-call(bf16[128,2048]{1,0:T(8,128)(2,1)} %x_ref.3, ...), custom_call_target="tpu_custom_call" | custom-call | flops 2147483648 | bytes 4194304 | tf_op jit(solution)/shard_map/head/pallas_call | solution.py:948
  130.1 233.2 %mlp.1 = (bf16[2048,128]{1,0:T(8,128)(2,1)}, bf16[8,256,2048]{2,1,0:T(8,128)(2,1)}, bf16[704,2048]{1,0:T(8,128)(2,1)}, f32[352,2048]{1,0:T(8,128)}, bf16[128,204...) custom-call(bf16[128,2048]{1,0:T(8,128)(2,1)} %get-tuple-element.51., ...), custom_call_target="tpu_custom_call" | custom-call | flops 17716740096 | bytes 34603008 | tf_op jit(solution)/shard_map/mlp/pallas_call | solution.py:959
  363.4 104.1 %back.1 = (f32[5632,128]{1,0:T(8,128)}, f32[5632,128]{1,0:T(8,128)}, f32[2048,128]{1,0:T(8,128)}, f32[512,128]{1,0:T(8,128)}, bf16[128,2048]{1,0:T(8,128)(2,1)}, /*index=5*/f32[8,128]{1,0:T(8,128)}) custom-call(bf16[256,2048]{1,0:T(8,128)(2,1)} %get-tuple-element.50.qkv_hbm, ...), custom_call_target="tpu_custom_call", output_to_operand_aliasing={{0}: (13, {}), {1}: (14, {})} | custom-call | flops 5368709120 | bytes 10485760 | tf_op jit(solution)/shard_map/back/pallas_call | solution.py:969
  467.5 10.5 %finish.1 = (f32[128,5632]{1,0:T(8,128)}, f32[128,5632]{1,0:T(8,128)}, f32[256,128]{1,0:T(8,128)}, f32[256,128]{1,0:T(8,128)}, f32[1,128]{1,0:T(1,128)}, /*index...) custom-call(f32[5632,128]{1,0:T(8,128)} %get-tuple-element.69.dg_hbm, ...), custom_call_target="tpu_custom_call" | custom-call | tf_op jit(solution)/shard_map/finish/pallas_call | solution.py:982
  (1 shorter events, 0.0 us)
